TPU v7x, 512 devices: a whole 4x8x8 slice. The times are simulated.
512 devices in a mesh: row: 8 (over y_hi, core), col: 8 (over y_lo, x), depth: 8 (over z).
Axes of the slice: x: 4, y: 8 (y_hi: 4, y_lo: 2; y = y_hi * 2 + y_lo), z: 8, core: 2. Of those that a mesh axis runs over, the one named last changes fastest.
Arguments:
- inputs: bfloat16 [8, 512, 5120], P('depth', 'col', 'row'), may hold values from -6 to 6
- pre_act: bfloat16 [8, 512, 10240], P('depth', 'row', 'col'), may hold values from -8 to 8
- grad_out: bfloat16 [8, 512, 5120], P('depth', 'col', 'row'), may hold values from -6 to 6
- weight_up: bfloat16 [5120, 10240], P('row', 'col'), may hold values from -0.078125 to 0.078125
- weight_down: bfloat16 [10240, 5120], P('col', 'row'), may hold values from -0.0625 to 0.0625
Outputs:
- grad_inputs: bfloat16 [8, 512, 5120], P('depth', 'col', 'row')
- grad_up: float32 [5120, 10240], P('row', ('col', 'depth'))
- grad_down: float32 [10240, 5120], P(('col', 'depth'), 'row')
All inputs are finite; a program needn't handle non-finite values.
Results may differ from a plain program's by a relative error of at most 0.02.
Values may be sent and summed in bfloat16 or wider, within the bound.
No kernel may reach another device: no remote copies, remote signals or barrier semaphores. Data moves between devices by JAX's collectives and lax.ppermute only.
A program may use at most 128 MiB of HBM per device.

v0:
```python
import jax
import jax.numpy as jnp
from jax import lax
from jax.sharding import PartitionSpec as P

root_coeff = 0.7978845608028654
cubic_coeff = 0.044715


def side_by_side(arrays, axis, dim, along):
    widths = [a.shape[along] for a in arrays]
    both = jnp.concatenate(arrays, axis=along)
    whole = lax.all_gather(both, axis, axis=dim, tiled=True)
    return tuple(jnp.split(whole, [sum(widths[:k]) for k in range(1, len(widths))], axis=along))


def in_blocks(value, dim, length):
    before, after = (value.shape[:dim], value.shape[dim + 1 :])
    return jnp.moveaxis(value.reshape(*before, length, -1, *after), dim, 0)


def sent_and_summed(value, axis, dim):
    length = lax.axis_size(axis)
    pieces = lax.all_to_all(in_blocks(value, dim, length), axis, 0, 0, tiled=True)
    return jnp.sum(pieces.astype(jnp.float32), axis=0)


def sent_to_all(value, axis):
    copies = jnp.broadcast_to(value, (lax.axis_size(axis), *value.shape))
    return lax.all_to_all(copies, axis, split_axis=0, concat_axis=0, tiled=True)


def in_order(pieces, dim):
    pieces = jnp.moveaxis(pieces, 0, dim)
    lengths = pieces.shape
    return pieces.reshape(*lengths[:dim], lengths[dim] * lengths[dim + 1], *lengths[dim + 2 :])


def gathered_copies(value, axis, dim):
    pieces = sent_to_all(value, axis)
    return in_order(pieces, dim)


def sent_together(arrays, axis, dim, along):
    widths = [a.shape[along] for a in arrays]
    both = jnp.concatenate(arrays, axis=along)
    whole = gathered_copies(both, axis, dim)
    return tuple(jnp.split(whole, [sum(widths[:k]) for k in range(1, len(widths))], axis=along))


def gelu_parts(values):
    inner = root_coeff * (values + cubic_coeff * values * values * values)
    tangent = jnp.tanh(inner)
    active = 0.5 * values * (1.0 + tangent)
    slope = 0.5 * (1.0 + tangent) + 0.5 * values * (1.0 - tangent * tangent) * root_coeff * (
        1.0 + 3.0 * cubic_coeff * values * values
    )
    return (active, slope)


def contract_last(left, right):
    return lax.dot_general(
        left, right, (((1,), (1,)), ((), ())), preferred_element_type=jnp.float32
    )


def layer_lower(slice_active, every_grads, layers):
    active_three = slice_active.reshape(layers, -1, slice_active.shape[1])
    grads_three = every_grads.reshape(layers, -1, every_grads.shape[1])
    lower_parts = jnp.einsum(
        "ntf,ntk->nfk", active_three, grads_three, preferred_element_type=jnp.float32
    )
    lower_round = lax.optimization_barrier(lower_parts.astype(jnp.bfloat16)).astype(jnp.float32)
    return jnp.sum(lower_round, axis=0)


def local(inputs, pre_act, grad_out, weight_up, weight_down):
    own_inputs = inputs[0]
    own_grads = grad_out[0]
    layer_inputs, layer_grads = side_by_side((own_inputs, own_grads), "col", 0, 1)
    picked = layer_grads
    hidden_grad = sent_and_summed(contract_last(picked, weight_down).astype(jnp.bfloat16), "row", 0)
    active, slope = gelu_parts(pre_act[0].astype(jnp.float32))
    active_own = active.astype(jnp.bfloat16)
    delta_own = (hidden_grad * slope).astype(jnp.bfloat16)
    layer_active, layer_delta = sent_together((active_own, delta_own), "row", 0, 1)
    picked = layer_delta
    input_grad = sent_and_summed(contract_last(picked, weight_up).astype(jnp.bfloat16), "col", 0)
    grad_inputs = input_grad.astype(jnp.bfloat16)[None]
    layers = lax.axis_size("depth")
    every_inputs, every_grads = side_by_side((layer_inputs, layer_grads), "depth", 0, 1)
    slice_active, slice_delta = (
        lax.all_to_all(layer_active, "depth", split_axis=1, concat_axis=0, tiled=True),
        lax.all_to_all(layer_delta, "depth", split_axis=1, concat_axis=0, tiled=True),
    )
    inputs_three = every_inputs.reshape(layers, -1, every_inputs.shape[1])
    delta_three = slice_delta.reshape(layers, -1, slice_delta.shape[1])
    upper_parts = jnp.einsum(
        "ntk,ntf->nkf", inputs_three, delta_three, preferred_element_type=jnp.float32
    )
    upper_round = lax.optimization_barrier(upper_parts.astype(jnp.bfloat16)).astype(jnp.float32)
    grad_up = jnp.sum(upper_round, axis=0)
    grad_down = layer_lower(slice_active, every_grads, layers)
    return (grad_inputs, grad_up, grad_down)


def solution(mesh):
    placed = (
        P("depth", "col", "row"),
        P("depth", "row", "col"),
        P("depth", "col", "row"),
        P("row", "col"),
        P("col", "row"),
    )
    return jax.shard_map(
        local,
        mesh=mesh,
        in_specs=placed,
        out_specs=(
            P("depth", "col", "row"),
            P("row", ("col", "depth")),
            P(("col", "depth"), "row"),
        ),
        check_vma=False,
    )
```

profile of v0, /device:TPU:9, one launch (start us, length us, event | category | flops | bytes accessed | tf_op | source)
XLA Modules:
  0.0 279.0 jit_solution(130414984939236571)
XLA Ops:
  7.2 0.0 copy-start
  7.2 0.0 all-gather.3.cloned.1.call-start
  7.2 1.7 pad_maximum_fusion.1
  8.9 0.0 all-gather.3.cloned.1.call-update
  9.0 0.0 all-gather.5.cloned.1.call-start
  9.0 43.8 %all-gather.3.cloned.1.call-done = bf16[512,1280]{1,0:T(8,128)(2,1)} async-done(((bf16[64,1280]{1,0:T(8,128)(2,1)}), bf16[512,1280]{1,0:T(8,128)(2,1)}) %all-gather.3.cloned.1.call-update) | async-done | bytes 1310736 | tf_op jit(solution)/shard_map/all_gather | solution.py:13
  52.8 0.0 all-gather.5.cloned.1.call-update
  52.8 0.0 copy-done
  52.8 2.3 convolution_convert_fusion
  55.1 0.0 copy-start.2
  55.1 47.0 %all_to_all.47 = bf16[8,64,1280]{2,1,0:T(8,128)(2,1)S(1)} all-to-all(bf16[8,64,1280]{2,1,0:T(8,128)(2,1)S(1)} %bitcast.30), channel_id=1, replica_groups=mesh['row'=8,'col'=8,'depth'=8] {'row'}, dimensions={0} | all-to-all | bytes 2621440 | tf_op jit(solution)/shard_map/all_to_all | solution.py:24
  102.1 0.2 convert_reduce_fusion.2
  102.3 0.2 fusion.5
  102.6 0.2 broadcast_in_dim.6
  102.8 0.0 copy-start.3
  102.8 51.9 %all_to_all.48 = bf16[8,64,2560]{2,1,0:T(8,128)(2,1)S(1)} all-to-all(bf16[8,64,2560]{2,1,0:T(8,128)(2,1)S(1)} %broadcast_in_dim.6), channel_id=1, replica_groups=mesh['row'=8,'col'=8,'depth'=8] {'row'}, dimensions={0} | all-to-all | bytes 5242880 | tf_op jit(solution)/shard_map/all_to_all | solution.py:30
  154.7 2.1 convolution_convert_fusion.3
  156.8 18.5 %all-to-all-start.2 = ((bf16[8,64,640]{2,1,0:T(8,128)(2,1)}), bf16[8,64,640]{2,1,0:T(8,128)(2,1)}, u32[]{:S(2)}, u32[]{:S(2)}) async-start(bf16[8,64,640]{2,1,0:T(8,128)(2,1)} %bitcast.6), calls=%async_computation.2 | async-start | bytes 1310720 | tf_op jit(solution)/shard_map/all_to_all | solution.py:24
  175.3 3.0 %fusion.16 = (bf16[512,1280]{1,0:T(8,128)(2,1)S(1)}, bf16[512,1280]{1,0:T(8,128)(2,1)}) fusion(bf16[512,2560]{1,0:T(8,128)(2,1)} %bitcast.27), kind=kLoop, calls=%fused_computation.32 | loop fusion | bytes 5242880 | tf_op jit(solution)/shard_map/split | solution.py:48
  178.3 1.5 copy.10
  179.7 6.2 %all-to-all-done.2 = bf16[8,64,640]{2,1,0:T(8,128)(2,1)} async-done(((bf16[8,64,640]{2,1,0:T(8,128)(2,1)}), bf16[8,64,640]{2,1,0:T(8,128)(2,1)}, u32[]{:S(2)}, u32[]{:S(2)}) %all-to-all-start.2) | async-done | bytes 655392 | tf_op jit(solution)/shard_map/all_to_all | solution.py:24
  185.9 7.2 %all-to-all-start.4 = ((bf16[512,8,160]{0,2,1:T(8,128)(2,1)}), bf16[512,8,160]{0,2,1:T(8,128)(2,1)S(1)}, u32[]{:S(2)}, u32[]{:S(2)}) async-start(bf16[512,8,160]{0,2,1:T(8,128)(2,1)} %bitcast.29), calls=%async_computation.4 | async-start | bytes 2621440 | tf_op jit(solution)/shard_map/all_to_all | solution.py:93
  193.1 2.4 copy.9
  195.5 32.5 %all-to-all-done.4 = bf16[512,8,160]{0,2,1:T(8,128)(2,1)S(1)} async-done(((bf16[512,8,160]{0,2,1:T(8,128)(2,1)}), bf16[512,8,160]{0,2,1:T(8,128)(2,1)S(1)}, u32[]{:S(2)}, u32[]{:S(2)}) %all-to-all-start.4) | async-done | bytes 1310752 | tf_op jit(solution)/shard_map/all_to_all | solution.py:93
  228.0 4.3 %all-to-all-start.3 = ((bf16[512,8,160]{0,2,1:T(8,128)(2,1)}), bf16[512,8,160]{0,2,1:T(8,128)(2,1)}, u32[]{:S(2)}, u32[]{:S(2)}) async-start(bf16[512,8,160]{0,2,1:T(8,128)(2,1)} %bitcast.28), calls=%async_computation.3 | async-start | bytes 2621440 | tf_op jit(solution)/shard_map/all_to_all | solution.py:94
  232.2 1.8 reduce_sum.40
  234.1 8.9 %fusion.15 = (bf16[4096,640]{1,0:T(8,128)(2,1)}, bf16[4096,640]{1,0:T(8,128)(2,1)}) fusion(bf16[4096,1280]{1,0:T(8,128)(2,1)} %all-gather.5.cloned.1.call-done), kind=kLoop, calls=%fused_computation.31 | loop fusion | bytes 20971520 | tf_op jit(solution)/shard_map/split | solution.py:14
  243.0 3.7 %convolution_convert_fusion.2 = bf16[8,160,640]{2,1,0:T(8,128)(2,1)S(1)} fusion(bf16[8,512,640]{2,1,0:T(8,128)(2,1)} %bitcast.25, bf16[512,8,160]{0,2,1:T(8,128)(2,1)S(1)} %all-to-all-done.4), kind=kOutput, calls=%fused_computation.5 | convolution fusion | flops 839680000 | bytes 8192000 | tf_op jit(solution)/shard_map/ntf,ntk->nfk/dot_general | solution.py:70
  246.7 1.0 convert_reduce_fusion
  247.6 19.4 %all-to-all-done.3 = bf16[512,8,160]{0,2,1:T(8,128)(2,1)} async-done(((bf16[512,8,160]{0,2,1:T(8,128)(2,1)}), bf16[512,8,160]{0,2,1:T(8,128)(2,1)}, u32[]{:S(2)}, u32[]{:S(2)}) %all-to-all-start.3) | async-done | bytes 1310752 | tf_op jit(solution)/shard_map/all_to_all | solution.py:94
  267.1 4.1 %convolution_convert_fusion.1 = bf16[8,640,160]{1,2,0:T(8,128)(2,1)S(1)} fusion(bf16[8,512,640]{2,1,0:T(8,128)(2,1)} %bitcast.24, bf16[512,8,160]{0,2,1:T(8,128)(2,1)} %all-to-all-done.3), kind=kOutput, calls=%fused_computation.4 | convolution fusion | flops 839680000 | bytes 8192000 | tf_op jit(solution)/shard_map/ntk,ntf->nkf/dot_general | solution.py:98
  271.1 1.0 convert_reduce_fusion.1
  (6 shorter events, 0.0 us)
Async XLA Ops:
  7.2 45.6 %copy-start = (bf16[1280,640]{1,0:T(8,128)(2,1)S(1)}, bf16[1280,640]{1,0:T(8,128)(2,1)}, u32[]{:S(2)}) copy-start(bf16[1280,640]{1,0:T(8,128)(2,1)} %param.9) | copy-start | bytes 4915204
  7.2 45.6 %all-gather.3.cloned.1.call-start = ((), (), s32[]{:S(2)}) async-start(), calls=%async_computation.5 | async-start | bytes 1474560 | tf_op jit(solution)/shard_map/all_gather | solution.py:13
  9.0 225.1 %all-gather.5.cloned.1.call-start = ((), (), s32[]{:S(2)}) async-start(), calls=%async_computation.6 | async-start | bytes 11796480 | tf_op jit(solution)/shard_map/all_gather | solution.py:13
  55.1 47.2 %copy-start.2 = (bf16[1,64,1280]{2,1,0:T(8,128)(2,1)S(1)}, bf16[1,64,1280]{2,1,0:T(8,128)(2,1)}, u32[]{:S(2)}) copy-start(bf16[1,64,1280]{2,1,0:T(8,128)(2,1)} %param.6) | copy-start | bytes 491524
  102.8 51.9 %copy-start.3 = (bf16[640,1280]{1,0:T(8,128)(2,1)S(1)}, bf16[640,1280]{1,0:T(8,128)(2,1)}, u32[]{:S(2)}) copy-start(bf16[640,1280]{1,0:T(8,128)(2,1)} %param.8) | copy-start | bytes 4915204
  154.7 2.1 copy-start.1
  156.8 29.1 %all-to-all-start.2 = ((bf16[8,64,640]{2,1,0:T(8,128)(2,1)}), bf16[8,64,640]{2,1,0:T(8,128)(2,1)}, u32[]{:S(2)}, u32[]{:S(2)}) async-start(bf16[8,64,640]{2,1,0:T(8,128)(2,1)} %bitcast.6), calls=%async_computation.2 | async-start | bytes 1310720 | tf_op jit(solution)/shard_map/all_to_all | solution.py:24
  185.9 42.1 %all-to-all-start.4 = ((bf16[512,8,160]{0,2,1:T(8,128)(2,1)}), bf16[512,8,160]{0,2,1:T(8,128)(2,1)S(1)}, u32[]{:S(2)}, u32[]{:S(2)}) async-start(bf16[512,8,160]{0,2,1:T(8,128)(2,1)} %bitcast.29), calls=%async_computation.4 | async-start | bytes 2621440 | tf_op jit(solution)/shard_map/all_to_all | solution.py:93
  228.0 39.1 %all-to-all-start.3 = ((bf16[512,8,160]{0,2,1:T(8,128)(2,1)}), bf16[512,8,160]{0,2,1:T(8,128)(2,1)}, u32[]{:S(2)}, u32[]{:S(2)}) async-start(bf16[512,8,160]{0,2,1:T(8,128)(2,1)} %bitcast.28), calls=%async_computation.3 | async-start | bytes 2621440 | tf_op jit(solution)/shard_map/all_to_all | solution.py:94
Sparse Core Ops, SparseCore 0:
  10.6 42.0 all-gather.2
  54.9 123.6 all-gather.4
where the time goes:
time: 280 us; the launch traced here: 279 us
  waiting for transfers between devices  102 us (36%)
  blocking collectives  98.9 us (35%)
  starting transfers between devices  30 us (11%)
  local copies, waits for them, and re-layouts  16 us (6%)
  between operations  14.1 us (5%)
  matrix products  12.1 us (4%)
  other arithmetic  5.94 us (2%)
    all_to_all x1, blocking collectives, sent_to_all(): return lax.all_to_all(copies, axis, split_axis=0, concat_axis=0, tiled=True)  51.9 us
    all_to_all x1, blocking collectives, sent_and_summed(): lax.all_to_all(in_blocks(value, dim, length), axis, 0, 0, tiled=True)  47 us
    all_gather x2, waiting for transfers between devices, side_by_side(): whole = lax.all_gather(both, axis, axis=dim, tiled=True)  43.8 us
    all_to_all x1, waiting for transfers between devices, local(): lax.all_to_all(layer_active, 'depth', split_axis=1, concat_axis=0, tiled=...  32.5 us
    all_to_all x1, waiting for transfers between devices, local(): lax.all_to_all(layer_delta, 'depth', split_axis=1, concat_axis=0, tiled=T...  19.4 us
    all_to_all x1, starting transfers between devices, sent_and_summed(): lax.all_to_all(in_blocks(value, dim, length), axis, 0, 0, tiled=True)  18.5 us
    split x1, local copies, waits for them, and re-layouts, side_by_side(): jnp.split(whole, [sum(widths[:k]) for k in range(1, len(widths))], axis=a...  8.89 us
    all_to_all x1, starting transfers between devices, local(): lax.all_to_all(layer_active, 'depth', split_axis=1, concat_axis=0, tiled=...  7.16 us
  transfers between devices with their start and end apart: 5, of which 4 were waited for; matrix products, arithmetic and copies ran while one was open for 10% of the time, Pallas kernels for 0%

commit v1 on v0

v1 whole, which is shorter than its diff:
```python
import jax
import jax.numpy as jnp
from jax import lax
from jax.sharding import Mesh, PartitionSpec as P

root_coeff = 0.7978845608028654
cubic_coeff = 0.044715

ROW = ("yhi", "core")
COL = ("ylo", "x")
SWAP = [(0, 1), (1, 0)]


def spread(value, axis):
    copies = jnp.broadcast_to(value, (lax.axis_size(axis), *value.shape))
    return lax.all_to_all(copies, axis, split_axis=0, concat_axis=0, tiled=True)


def exchanged(value, axis):
    return lax.all_to_all(value, axis, split_axis=0, concat_axis=0, tiled=True)


def summed(pieces):
    return jnp.sum(pieces.astype(jnp.float32), axis=0)


def gelu_parts(values):
    inner = root_coeff * (values + cubic_coeff * values * values * values)
    tangent = jnp.tanh(inner)
    active = 0.5 * values * (1.0 + tangent)
    slope = 0.5 * (1.0 + tangent) + 0.5 * values * (1.0 - tangent * tangent) * root_coeff * (
        1.0 + 3.0 * cubic_coeff * values * values
    )
    return (active, slope)


def contract_last(left, right):
    return lax.dot_general(
        left, right, (((1,), (1,)), ((), ())), preferred_element_type=jnp.float32
    )


def contract_first(left, right):
    return lax.dot_general(
        left, right, (((0,), (0,)), ((), ())), preferred_element_type=jnp.float32
    )


def halves(pieces, core):
    split = pieces.reshape(4, 2, *pieces.shape[1:])
    mine = lax.dynamic_index_in_dim(split, core, 1, keepdims=False)
    other = lax.dynamic_index_in_dim(split, 1 - core, 1, keepdims=False)
    return mine.reshape(-1, mine.shape[-1]), other.reshape(-1, other.shape[-1])


def swapped(value):
    return lax.ppermute(value, "core", SWAP)


def local(inputs, pre_act, grad_out, weight_up, weight_down):
    core = lax.axis_index("core")
    layer_grads = spread(grad_out[0], COL)
    active, slope = gelu_parts(pre_act[0].astype(jnp.float32))
    active_own = active.astype(jnp.bfloat16)
    grads_mine, grads_other = halves(layer_grads, core)
    away = contract_last(grads_other, weight_down).astype(jnp.bfloat16)
    back = swapped(away)
    kept = contract_last(grads_mine, weight_down)
    pair = (kept + back.astype(jnp.float32)).astype(jnp.bfloat16)
    hidden_grad = summed(exchanged(pair.reshape(4, -1, pair.shape[1]), "yhi"))
    delta_own = (hidden_grad * slope).astype(jnp.bfloat16)

    active_mine = spread(active_own, "yhi").reshape(-1, active_own.shape[1])
    active_other = swapped(active_mine)
    lower = contract_first(active_mine, grads_mine) + contract_first(active_other, grads_other)
    lower = lower.astype(jnp.bfloat16).reshape(8, -1, lower.shape[1])
    grad_down = summed(exchanged(lower, "depth"))

    layer_inputs = spread(inputs[0], COL)
    inputs_mine, inputs_other = halves(layer_inputs, core)
    delta_mine = spread(delta_own, "yhi").reshape(-1, delta_own.shape[1])
    delta_other = swapped(delta_mine)
    upper = contract_first(delta_mine, inputs_mine) + contract_first(delta_other, inputs_other)
    upper = upper.astype(jnp.bfloat16).reshape(8, -1, upper.shape[1])
    grad_up = summed(exchanged(upper, "depth")).T

    part_mine = contract_last(delta_mine, weight_up).astype(jnp.bfloat16)
    part_other = contract_last(delta_other, weight_up).astype(jnp.bfloat16)
    first = jnp.where(core == 0, part_mine, part_other).reshape(4, 64, -1)
    second = jnp.where(core == 0, part_other, part_mine).reshape(4, 64, -1)
    parts = jnp.stack([first, second], axis=1).reshape(8, 64, -1)
    grad_inputs = summed(exchanged(parts, COL)).astype(jnp.bfloat16)[None]
    return (grad_inputs, grad_up, grad_down)


def solution(mesh):
    fine = Mesh(mesh.devices.reshape(4, 2, 2, 4, 8), ("yhi", "core", "ylo", "x", "depth"))
    placed = (
        P("depth", COL, ROW),
        P("depth", ROW, COL),
        P("depth", COL, ROW),
        P(ROW, COL),
        P(COL, ROW),
    )
    return jax.shard_map(
        local,
        mesh=fine,
        in_specs=placed,
        out_specs=(
            P("depth", COL, ROW),
            P(ROW, (*COL, "depth")),
            P((*COL, "depth"), ROW),
        ),
        check_vma=False,
    )
```

time: 280 us -> 230 us (0.82)
  the two profiles are of different devices: /device:TPU:9 before, /device:TPU:24 now
where the time goes in v1:
time: 230 us; the launch traced here: 229 us
  waiting for transfers between devices  105 us (46%)
  blocking collectives  60.8 us (26%)
  starting transfers between devices  35.6 us (15%)
  matrix products  14 us (6%)
  other arithmetic  6.47 us (3%)
  local copies, waits for them, and re-layouts  6.19 us (3%)
    all_to_all x3, waiting for transfers between devices, exchanged(): return lax.all_to_all(value, axis, split_axis=0, concat_axis=0, tiled=True)  79.6 us
    all_to_all x2, blocking collectives, spread(): return lax.all_to_all(copies, axis, split_axis=0, concat_axis=0, tiled=True)  37 us
    all_to_all x1, blocking collectives, exchanged(): return lax.all_to_all(value, axis, split_axis=0, concat_axis=0, tiled=True)  23.8 us
    all_to_all x2, waiting for transfers between devices, spread(): return lax.all_to_all(copies, axis, split_axis=0, concat_axis=0, tiled=True)  22.8 us
    all_to_all x3, starting transfers between devices, exchanged(): return lax.all_to_all(value, axis, split_axis=0, concat_axis=0, tiled=True)  20.2 us
    all_to_all x2, starting transfers between devices, spread(): return lax.all_to_all(copies, axis, split_axis=0, concat_axis=0, tiled=True)  9.52 us
    dot_general x4, matrix products, contract_first(): lax.dot_general(left, right, (((0,), (0,)), ((), ())), preferred_element_...  8.47 us
    ppermute x3, starting transfers between devices, swapped(): return lax.ppermute(value, 'core', SWAP)  5.88 us
  transfers between devices with their start and end apart: 8, of which 7 were waited for; matrix products, arithmetic and copies ran while one was open for 7% of the time, Pallas kernels for 0%

profile of v1, /device:TPU:24, one launch (start us, length us, event | category | flops | bytes accessed | tf_op | source)
XLA Modules:
  0.0 228.7 jit_solution(2548732637590369696)
XLA Ops:
  0.7 1.1 broadcast_in_dim.18
  1.7 15.7 %all_to_all.40 = bf16[8,64,640]{2,1,0:T(8,128)(2,1)S(1)} all-to-all(bf16[8,64,640]{2,1,0:T(8,128)(2,1)S(1)} %broadcast_in_dim.18), channel_id=1, replica_groups=mesh['yhi'=4,'core'=2,'ylo'=2,'x'=4,'depth'=8] {'ylo','x'}, dimensions={0} | all-to-all | bytes 1310720 | tf_op jit(solution)/shard_map/all_to_all | solution.py:16
  17.4 0.9 broadcast_in_dim.15
  18.3 4.9 %all-to-all-start = ((bf16[8,64,640]{2,1,0:T(8,128)(2,1)}), bf16[8,64,640]{2,1,0:T(8,128)(2,1)S(1)}, u32[]{:S(2)}, u32[]{:S(2)}) async-start(bf16[8,64,640]{2,1,0:T(8,128)(2,1)} %broadcast_in_dim.15), calls=%async_computation | async-start | bytes 1310720 | tf_op jit(solution)/shard_map/all_to_all | solution.py:16
  23.2 8.8 %all-to-all-done = bf16[8,64,640]{2,1,0:T(8,128)(2,1)S(1)} async-done(((bf16[8,64,640]{2,1,0:T(8,128)(2,1)}), bf16[8,64,640]{2,1,0:T(8,128)(2,1)S(1)}, u32[]{:S(2)}, u32[]{:S(2)}) %all-to-all-start) | async-done | bytes 655392 | tf_op jit(solution)/shard_map/all_to_all | solution.py:16
  34.3 1.9 collective-permute-start
  36.3 2.1 collective-permute-done
  39.1 23.8 %all_to_all.41 = bf16[4,64,1280]{2,1,0:T(8,128)(2,1)S(1)} all-to-all(bf16[4,64,1280]{2,1,0:T(8,128)(2,1)S(1)} %bitcast.50), channel_id=1, replica_groups=mesh['yhi'=4,'core'=2,'ylo'=2,'x'=4,'depth'=8] {'yhi'}, dimensions={0} | all-to-all | bytes 1310720 | tf_op jit(solution)/shard_map/all_to_all | solution.py:20
  63.3 21.3 %all_to_all.42 = bf16[4,64,1280]{2,1,0:T(8,128)(2,1)S(1)} all-to-all(bf16[4,64,1280]{2,1,0:T(8,128)(2,1)S(1)} %broadcast_in_dim.16), channel_id=1, replica_groups=mesh['yhi'=4,'core'=2,'ylo'=2,'x'=4,'depth'=8] {'yhi'}, dimensions={0} | all-to-all | bytes 1310720 | tf_op jit(solution)/shard_map/all_to_all | solution.py:16
  84.6 1.9 collective-permute-start.1
  86.5 0.9 broadcast_in_dim.19
  87.4 4.7 %all-to-all-start.6 = ((bf16[4,64,1280]{2,1,0:T(8,128)(2,1)}), bf16[4,64,1280]{2,1,0:T(8,128)(2,1)S(1)}, u32[]{:S(2)}, u32[]{:S(2)}) async-start(bf16[4,64,1280]{2,1,0:T(8,128)(2,1)} %broadcast_in_dim.19), calls=%async_computation.6 | async-start | bytes 1310720 | tf_op jit(solution)/shard_map/all_to_all | solution.py:16
  92.1 2.3 convolution_convert_fusion.2
  94.4 1.8 broadcast_select_fusion.1
  96.2 0.9 pad_maximum_fusion
  97.1 13.9 %all-to-all-done.6 = bf16[4,64,1280]{2,1,0:T(8,128)(2,1)S(1)} async-done(((bf16[4,64,1280]{2,1,0:T(8,128)(2,1)}), bf16[4,64,1280]{2,1,0:T(8,128)(2,1)S(1)}, u32[]{:S(2)}, u32[]{:S(2)}) %all-to-all-start.6) | async-done | bytes 655392 | tf_op jit(solution)/shard_map/all_to_all | solution.py:16
  111.0 0.8 copy-done.5
  111.9 5.5 %all-to-all-start.3 = ((bf16[8,64,640]{2,1,0:T(8,128)(2,1)}), bf16[8,64,640]{2,1,0:T(8,128)(2,1)S(1)}, u32[]{:S(2)}, u32[]{:S(2)}) async-start(bf16[8,64,640]{2,1,0:T(8,128)(2,1)} %bitcast.12), calls=%async_computation.3 | async-start | bytes 1310720 | tf_op jit(solution)/shard_map/all_to_all | solution.py:20
  117.4 1.7 fusion.13
  119.1 3.0 %fusion = bf16[1280,640]{1,0:T(8,128)(2,1)} fusion(f32[1280,640]{1,0:T(8,128)S(1)} %fusion.13, bf16[256,1280]{1,0:T(8,128)(2,1)} %collective-permute-done.1, bf16[256,640]{1,0:T(8,128)(2,1)S(1)} %bitcast.56), kind=kOutput, calls=%fused_computation.4 | convolution fusion | flops 421068800 | bytes 5898240 | tf_op jit(solution)/shard_map/dot_general | solution.py:44
  122.1 5.6 %all-to-all-done.3 = bf16[8,64,640]{2,1,0:T(8,128)(2,1)S(1)} async-done(((bf16[8,64,640]{2,1,0:T(8,128)(2,1)}), bf16[8,64,640]{2,1,0:T(8,128)(2,1)S(1)}, u32[]{:S(2)}, u32[]{:S(2)}) %all-to-all-start.3) | async-done | bytes 655392 | tf_op jit(solution)/shard_map/all_to_all | solution.py:20
  127.7 0.9 copy-done.4
  128.6 10.3 %all-to-all-start.5 = ((bf16[8,160,640]{2,1,0:T(8,128)(2,1)}), bf16[8,160,640]{2,1,0:T(8,128)(2,1)S(1)}, u32[]{:S(2)}, u32[]{:S(2)}) async-start(bf16[8,160,640]{2,1,0:T(8,128)(2,1)} %bitcast.42), calls=%async_computation.5 | async-start | bytes 3276800 | tf_op jit(solution)/shard_map/all_to_all | solution.py:20
  138.9 2.1 collective-permute-start.2
  140.9 1.9 fusion.14
  143.2 1.9 fusion.1
  145.1 35.0 %all-to-all-done.5 = bf16[8,160,640]{2,1,0:T(8,128)(2,1)S(1)} async-done(((bf16[8,160,640]{2,1,0:T(8,128)(2,1)}), bf16[8,160,640]{2,1,0:T(8,128)(2,1)S(1)}, u32[]{:S(2)}, u32[]{:S(2)}) %all-to-all-start.5) | async-done | bytes 1638432 | tf_op jit(solution)/shard_map/all_to_all | solution.py:20
  180.1 4.3 %all-to-all-start.7 = ((bf16[8,160,640]{2,1,0:T(8,128)(2,1)}), bf16[8,160,640]{2,1,0:T(8,128)(2,1)}, u32[]{:S(2)}, u32[]{:S(2)}) async-start(bf16[8,160,640]{2,1,0:T(8,128)(2,1)} %bitcast.43), calls=%async_computation.7 | async-start | bytes 3276800 | tf_op jit(solution)/shard_map/all_to_all | solution.py:20
  184.4 1.8 reduce_sum.40
  186.3 1.0 convert_reduce_fusion.1
  187.2 39.0 %all-to-all-done.7 = bf16[8,160,640]{2,1,0:T(8,128)(2,1)} async-done(((bf16[8,160,640]{2,1,0:T(8,128)(2,1)}), bf16[8,160,640]{2,1,0:T(8,128)(2,1)}, u32[]{:S(2)}, u32[]{:S(2)}) %all-to-all-start.7) | async-done | bytes 1638432 | tf_op jit(solution)/shard_map/all_to_all | solution.py:20
  226.3 2.4 %convert_reduce_fusion = f32[160,640]{1,0:T(8,128)} fusion(bf16[8,160,640]{2,1,0:T(8,128)(2,1)} %all-to-all-done.7), kind=kLoop, calls=%fused_computation.2 | loop fusion | flops 1536000 | bytes 2048000 | tf_op jit(solution)/shard_map/reduce_sum | solution.py:24
  (24 shorter events, 3.8 us)
Async XLA Ops:
  0.6 33.0 %copy-start = (bf16[1280,640]{1,0:T(8,128)(2,1)S(1)}, bf16[1280,640]{1,0:T(8,128)(2,1)}, u32[]{:S(2)}) copy-start(bf16[1280,640]{1,0:T(8,128)(2,1)} %param.9) | copy-start | bytes 4915204
  0.6 16.8 %copy-start.7 = (bf16[1,64,640]{2,1,0:T(8,128)(2,1)S(1)}, bf16[1,64,640]{2,1,0:T(8,128)(2,1)}, u32[]{:S(2)}) copy-start(bf16[1,64,640]{2,1,0:T(8,128)(2,1)} %param.7) | copy-start | bytes 245764
  18.3 13.7 %all-to-all-start = ((bf16[8,64,640]{2,1,0:T(8,128)(2,1)}), bf16[8,64,640]{2,1,0:T(8,128)(2,1)S(1)}, u32[]{:S(2)}, u32[]{:S(2)}) async-start(bf16[8,64,640]{2,1,0:T(8,128)(2,1)} %broadcast_in_dim.15), calls=%async_computation | async-start | bytes 1310720 | tf_op jit(solution)/shard_map/all_to_all | solution.py:16
  32.9 0.7 copy-start.1
  32.9 6.2 %copy-start.3 = (bf16[4,1,64,640]{3,2,1,0:T(8,128)(2,1)}, bf16[4,1,64,640]{3,2,1,0:T(8,128)(2,1)S(1)}, u32[]{:S(2)}) copy-start(bf16[4,1,64,640]{3,2,1,0:T(8,128)(2,1)S(1)} %get-tuple-element.11) | copy-start | bytes 983044
  34.3 4.0 %collective-permute-start = (bf16[256,1280]{1,0:T(8,128)(2,1)S(1)}, bf16[256,1280]{1,0:T(8,128)(2,1)S(1)}, u32[]{:S(2)}, u32[]{:S(2)}) collective-permute-start(bf16[256,1280]{1,0:T(8,128)(2,1)S(1)} %convolution_convert_fusion), channel_id=1, source_target_pairs={{0,64},{64,0},{1,65},{65,1},{2,66},{66,2},{3,67},{67,3},{4,68},{68... | collective-permute-start | bytes 1966088 | tf_op jit(solution)/shard_map/ppermute | solution.py:57
  39.1 23.9 %copy-start.6 = (bf16[1,64,1280]{2,1,0:T(8,128)(2,1)S(1)}, bf16[1,64,1280]{2,1,0:T(8,128)(2,1)}, u32[]{:S(2)}) copy-start(bf16[1,64,1280]{2,1,0:T(8,128)(2,1)} %param.6) | copy-start | bytes 491524
  84.6 9.7 %collective-permute-start.1 = (bf16[256,1280]{1,0:T(8,128)(2,1)S(1)}, bf16[256,1280]{1,0:T(8,128)(2,1)}, u32[]{:S(2)}, u32[]{:S(2)}) collective-permute-start(bf16[256,1280]{1,0:T(8,128)(2,1)S(1)} %bitcast.53), channel_id=1, source_target_pairs={{0,64},{64,0},{1,65},{65,1},{2,66},{66,2},{3,67},{67,3},{4,68},{68... | collective-permute-start | bytes 1966088 | tf_op jit(solution)/shard_map/ppermute | solution.py:57
  87.4 23.6 %all-to-all-start.6 = ((bf16[4,64,1280]{2,1,0:T(8,128)(2,1)}), bf16[4,64,1280]{2,1,0:T(8,128)(2,1)S(1)}, u32[]{:S(2)}, u32[]{:S(2)}) async-start(bf16[4,64,1280]{2,1,0:T(8,128)(2,1)} %broadcast_in_dim.19), calls=%async_computation.6 | async-start | bytes 1310720 | tf_op jit(solution)/shard_map/all_to_all | solution.py:16
  92.1 2.3 copy-start.8
  111.0 0.8 copy-start.5
  111.9 15.8 %all-to-all-start.3 = ((bf16[8,64,640]{2,1,0:T(8,128)(2,1)}), bf16[8,64,640]{2,1,0:T(8,128)(2,1)S(1)}, u32[]{:S(2)}, u32[]{:S(2)}) async-start(bf16[8,64,640]{2,1,0:T(8,128)(2,1)} %bitcast.12), calls=%async_computation.3 | async-start | bytes 1310720 | tf_op jit(solution)/shard_map/all_to_all | solution.py:20
  127.7 0.9 copy-start.4
  128.6 51.6 %all-to-all-start.5 = ((bf16[8,160,640]{2,1,0:T(8,128)(2,1)}), bf16[8,160,640]{2,1,0:T(8,128)(2,1)S(1)}, u32[]{:S(2)}, u32[]{:S(2)}) async-start(bf16[8,160,640]{2,1,0:T(8,128)(2,1)} %bitcast.42), calls=%async_computation.5 | async-start | bytes 3276800 | tf_op jit(solution)/shard_map/all_to_all | solution.py:20
  138.9 4.3 %copy-start.2 = (bf16[4,1,64,640]{3,2,1,0:T(8,128)(2,1)S(1)}, bf16[4,1,64,640]{3,2,1,0:T(8,128)(2,1)}, u32[]{:S(2)}) copy-start(bf16[4,1,64,640]{3,2,1,0:T(8,128)(2,1)} %copy-done.1) | copy-start | bytes 983044
  138.9 4.3 %collective-permute-start.2 = (bf16[256,1280]{1,0:T(8,128)(2,1)}, bf16[256,1280]{1,0:T(8,128)(2,1)S(1)}, u32[]{:S(2)}, u32[]{:S(2)}) collective-permute-start(bf16[256,1280]{1,0:T(8,128)(2,1)} %bitcast.51), channel_id=1, source_target_pairs={{0,64},{64,0},{1,65},{65,1},{2,66},{66,2},{3,67},{67,3},{4,68},{68... | collective-permute-start | bytes 1966088 | tf_op jit(solution)/shard_map/ppermute | solution.py:57
  180.1 46.1 %all-to-all-start.7 = ((bf16[8,160,640]{2,1,0:T(8,128)(2,1)}), bf16[8,160,640]{2,1,0:T(8,128)(2,1)}, u32[]{:S(2)}, u32[]{:S(2)}) async-start(bf16[8,160,640]{2,1,0:T(8,128)(2,1)} %bitcast.43), calls=%async_computation.7 | async-start | bytes 3276800 | tf_op jit(solution)/shard_map/all_to_all | solution.py:20

commit v2 on v1

v2 whole, which is shorter than its diff:
```python
import jax
import jax.numpy as jnp
from jax import lax
from jax.experimental import pallas as pl
from jax.experimental.pallas import tpu as pltpu
from jax.sharding import Mesh, PartitionSpec as P

root_coeff = 0.7978845608028654
cubic_coeff = 0.044715

ROW = ("yhi", "core")
COL = ("ylo", "x")
SWAP = [(0, 1), (1, 0)]


def spread(value, axis):
    copies = jnp.broadcast_to(value, (lax.axis_size(axis), *value.shape))
    return lax.all_to_all(copies, axis, split_axis=0, concat_axis=0, tiled=True)


def exchanged(value, axis):
    return lax.all_to_all(value, axis, split_axis=0, concat_axis=0, tiled=True)


def summed(pieces):
    return jnp.sum(pieces.astype(jnp.float32), axis=0)


def gelu_parts(values):
    inner = root_coeff * (values + cubic_coeff * values * values * values)
    tangent = jnp.tanh(inner)
    active = 0.5 * values * (1.0 + tangent)
    slope = 0.5 * (1.0 + tangent) + 0.5 * values * (1.0 - tangent * tangent) * root_coeff * (
        1.0 + 3.0 * cubic_coeff * values * values
    )
    return (active, slope)


def contract_last(left, right):
    return lax.dot_general(
        left, right, (((1,), (1,)), ((), ())), preferred_element_type=jnp.float32
    )


def contract_first(left, right):
    return lax.dot_general(
        left, right, (((0,), (0,)), ((), ())), preferred_element_type=jnp.float32
    )


def shifted(value, axis, by):
    length = lax.axis_size(axis)
    return lax.ppermute(value, axis, [(k, (k + by) % length) for k in range(length)])


def swapped(value):
    return lax.ppermute(value, "core", SWAP)


def block_at(blocks, index):
    return lax.dynamic_index_in_dim(blocks, index, 0, keepdims=False)


def gathered(own):
    return jnp.concatenate([own] + [shifted(own, "yhi", 4 - u) for u in (1, 2, 3)], axis=0)


def depth_sum(blocks):
    here = lax.axis_index("depth")
    pick = lambda by: block_at(blocks, (here + by) % 8)
    half = blocks.shape[1] // 2
    far = pick(4)
    near_up = shifted(jnp.stack([pick(1), pick(3)]), "depth", 1)
    near_down = shifted(jnp.stack([pick(7), pick(5)]), "depth", 7)
    far_up = shifted(far[:half], "depth", 2)
    far_down = shifted(far[half:], "depth", 6)
    wide = lambda v: v.astype(jnp.float32)
    up = wide(pick(2)) + wide(near_up[1])
    up = jnp.concatenate([up[:half] + wide(far_up), up[half:]], axis=0).astype(jnp.bfloat16)
    down = wide(pick(6)) + wide(near_down[1])
    down = jnp.concatenate([down[:half], down[half:] + wide(far_down)], axis=0).astype(jnp.bfloat16)
    last_up = shifted(up, "depth", 2)
    last_down = shifted(down, "depth", 6)
    near = wide(pick(0)) + wide(near_up[0]) + wide(near_down[0])
    return near + wide(last_up) + wide(last_down)


def pick_kernel(order, blocks, *outs):
    for k in range(blocks.shape[0]):
        start = 0
        for out in outs:
            width = out.shape[-1]
            out[k] = blocks[order[k], :, start : start + width]
            start += width


def picked(blocks, order, ways=1):
    n, m, w = blocks.shape
    whole = pl.BlockSpec(memory_space=pltpu.VMEM)
    outs = pl.pallas_call(
        pick_kernel,
        out_shape=[jax.ShapeDtypeStruct((n, m, w // ways), blocks.dtype)] * ways,
        in_specs=[pl.BlockSpec(memory_space=pltpu.SMEM), whole],
        out_specs=[whole] * ways,
        name="pick",
    )(jnp.stack(order).astype(jnp.int32), blocks)
    return [out.reshape(n * m, w // ways) for out in outs]


def together(*values):
    return lax.optimization_barrier(values)


def local(inputs, pre_act, grad_out, weight_up, weight_down):
    core = lax.axis_index("core")
    high = lax.axis_index("yhi")
    active, slope = gelu_parts(pre_act[0].astype(jnp.float32))
    active_mine = gathered(active.astype(jnp.bfloat16))

    both = spread(jnp.concatenate([grad_out[0], inputs[0]], axis=1), COL)
    both, active_mine = together(both, active_mine)
    active_all = jnp.concatenate([active_mine, swapped(active_mine)], axis=0)
    order = [((high + u) % 4) * 2 + c for c in (core, 1 - core) for u in range(4)]
    grads, layer_inputs = picked(both, order, 2)

    away = contract_last(grads[256:], weight_down).astype(jnp.bfloat16)
    back = swapped(away)
    kept = contract_last(grads[:256], weight_down)
    pair = (kept + back.astype(jnp.float32)).astype(jnp.bfloat16).reshape(4, 64, -1)

    lower = contract_first(active_all, grads).astype(jnp.bfloat16)
    pair, lower = together(pair, lower)
    lower_pieces = exchanged(lower.reshape(8, -1, lower.shape[1]), "depth")

    came = [pair[0]] + [shifted(pair[u], "yhi", u) for u in (1, 2, 3)]
    hidden_grad = sum(piece.astype(jnp.float32) for piece in came)
    delta_mine = gathered((hidden_grad * slope).astype(jnp.bfloat16))
    delta_all = jnp.concatenate([delta_mine, swapped(delta_mine)], axis=0)
    delta_all, lower_pieces = together(delta_all, lower_pieces)
    grad_down = summed(lower_pieces)

    upper = contract_first(delta_all, layer_inputs).astype(jnp.bfloat16)
    grad_up = depth_sum(upper.reshape(8, -1, upper.shape[1])).T

    parts = contract_last(delta_all, weight_up).astype(jnp.bfloat16).reshape(8, 64, -1)
    spot = [(k // 2 - high) % 4 + 4 * ((k + core) % 2) for k in range(8)]
    parts = picked(parts, spot)[0].reshape(8, 64, -1)
    grad_inputs = summed(exchanged(parts, COL)).astype(jnp.bfloat16)[None]
    return (grad_inputs, grad_up, grad_down)


def solution(mesh):
    fine = Mesh(mesh.devices.reshape(4, 2, 2, 4, 8), ("yhi", "core", "ylo", "x", "depth"))
    placed = (
        P("depth", COL, ROW),
        P("depth", ROW, COL),
        P("depth", COL, ROW),
        P(ROW, COL),
        P(COL, ROW),
    )
    return jax.shard_map(
        local,
        mesh=fine,
        in_specs=placed,
        out_specs=(
            P("depth", COL, ROW),
            P(ROW, (*COL, "depth")),
            P((*COL, "depth"), ROW),
        ),
        check_vma=False,
    )
```

time: 230 us -> 187 us (0.81)
  the two profiles are of different devices: /device:TPU:24 before, /device:TPU:2 now
where the time goes in v2:
time: 187 us; the launch traced here: 186 us
  starting transfers between devices  89.8 us (48%)
  waiting for transfers between devices  52 us (28%)
  other arithmetic  14.7 us (8%)
  local copies, waits for them, and re-layouts  12.5 us (7%)
  matrix products  10.8 us (6%)
  Pallas kernels  4.51 us (2%)
    ppermute x15, starting transfers between devices, shifted(): lax.ppermute(value, axis, [(k, (k + by) % length) for k in range(length)])  56.8 us
    ppermute x15, waiting for transfers between devices, shifted(): lax.ppermute(value, axis, [(k, (k + by) % length) for k in range(length)])  51.9 us
    all_to_all x2, starting transfers between devices, exchanged(): return lax.all_to_all(value, axis, split_axis=0, concat_axis=0, tiled=True)  17.3 us
    all_to_all x1, starting transfers between devices, spread(): return lax.all_to_all(copies, axis, split_axis=0, concat_axis=0, tiled=True)  9.48 us
    ppermute x3, starting transfers between devices, swapped(): return lax.ppermute(value, 'core', SWAP)  6.25 us
    unnamed x17, local copies, waits for them, and re-layouts  5.89 us
    dot_general x3, matrix products, contract_last(): lax.dot_general(left, right, (((1,), (1,)), ((), ())), preferred_element_...  5.67 us
    dot_general x2, matrix products, contract_first(): lax.dot_general(left, right, (((0,), (0,)), ((), ())), preferred_element_...  5.11 us
  transfers between devices with their start and end apart: 21, of which 12 were waited for; matrix products, arithmetic and copies ran while one was open for 13% of the time, Pallas kernels for 1%

profile of v2, /device:TPU:2, one launch (start us, length us, event | category | flops | bytes accessed | tf_op | source)
XLA Modules:
  0.0 185.7 jit_solution(14377604483371924742)
XLA Ops:
  2.9 9.5 %all-to-all-start = ((bf16[8,64,1280]{2,1,0:T(8,128)(2,1)}), bf16[8,64,1280]{2,1,0:T(8,128)(2,1)S(1)}, u32[]{:S(2)}, u32[]{:S(2)}) async-start(bf16[8,64,1280]{2,1,0:T(8,128)(2,1)} %broadcast_in_dim.6), calls=%async_computation | async-start | bytes 2621440 | tf_op jit(solution)/shard_map/all_to_all | solution.py:18
  14.4 4.1 %collective-permute-start.1 = (bf16[64,1280]{1,0:T(8,128)(2,1)S(1)}, bf16[64,1280]{1,0:T(8,128)(2,1)S(1)}, u32[]{:S(2)}, u32[]{:S(2)}) collective-permute-start(bf16[64,1280]{1,0:T(8,128)(2,1)S(1)} %fusion.7), channel_id=1, source_target_pairs={{0,256},{128,384},{256,0},{384,128},{1,257},{129,385},{257,1},{385... | collective-permute-start | bytes 491528 | tf_op jit(solution)/shard_map/ppermute | solution.py:53
  18.5 5.3 %collective-permute-start = (bf16[64,1280]{1,0:T(8,128)(2,1)S(1)}, bf16[64,1280]{1,0:T(8,128)(2,1)}, u32[]{:S(2)}, u32[]{:S(2)}) collective-permute-start(bf16[64,1280]{1,0:T(8,128)(2,1)S(1)} %fusion.7), channel_id=1, source_target_pairs={{0,384},{128,0},{256,128},{384,256},{1,385},{129,1},{257,129},{385... | collective-permute-start | bytes 491528 | tf_op jit(solution)/shard_map/ppermute | solution.py:53
  24.5 11.9 %collective-permute-done.2 = bf16[64,1280]{1,0:T(8,128)(2,1)S(1)} collective-permute-done((bf16[64,1280]{1,0:T(8,128)(2,1)S(1)}, bf16[64,1280]{1,0:T(8,128)(2,1)S(1)}, u32[]{:S(2)}, u32[]{:S(2)}) %collective-permute-start.2) | collective-permute-done | bytes 163872 | tf_op jit(solution)/shard_map/ppermute | solution.py:53
  36.3 3.5 %collective-permute-done.1 = bf16[64,1280]{1,0:T(8,128)(2,1)S(1)} collective-permute-done((bf16[64,1280]{1,0:T(8,128)(2,1)S(1)}, bf16[64,1280]{1,0:T(8,128)(2,1)S(1)}, u32[]{:S(2)}, u32[]{:S(2)}) %collective-permute-start.1) | collective-permute-done | bytes 163872 | tf_op jit(solution)/shard_map/ppermute | solution.py:53
  42.8 2.5 %pick.2 = (bf16[8,64,640]{2,1,0:T(8,128)(2,1)}, bf16[8,64,640]{2,1,0:T(8,128)(2,1)}) custom-call(s32[8]{0:T(128)} %stack.81.order, bf16[8,64,1280]{2,1,0:T(8,128)(2,1)} %copy-done.1), custom_call_target="tpu_custom_call" | custom-call | tf_op jit(solution)/shard_map/pick/pallas_call | solution.py:100
  49.1 2.4 %collective-permute-start.4 = (bf16[256,1280]{1,0:T(8,128)(2,1)S(1)}, bf16[256,1280]{1,0:T(8,128)(2,1)S(1)}, u32[]{:S(2)}, u32[]{:S(2)}) collective-permute-start(bf16[256,1280]{1,0:T(8,128)(2,1)S(1)} %copy-done.4), channel_id=1, source_target_pairs={{0,64},{64,0},{1,65},{65,1},{2,66},{66,2},{3,67},{67,3},{4,68},{68... | collective-permute-start | bytes 1966088 | tf_op jit(solution)/shard_map/ppermute | solution.py:57
  53.2 2.4 %convolution_convert_fusion.1 = bf16[1280,640]{1,0:T(8,128)(2,1)} fusion(bf16[512,640]{1,0:T(8,128)(2,1)S(1)} %bitcast.88, bf16[256,1280]{1,0:T(8,128)(2,1)S(1)} %collective-permute-done.4, bf16[256,1280]{1,0:T(8,128)(2,1)S(1)} %copy-done.4), kind=kOutput, calls=%fused_computation.2 | convolution fusion | flops 842301440 | bytes 3604480 | tf_op jit(solution)/shard_map/dot_general | solution.py:46
  55.6 10.3 %all-to-all-start.1 = ((bf16[8,160,640]{2,1,0:T(8,128)(2,1)}), bf16[8,160,640]{2,1,0:T(8,128)(2,1)S(1)}, u32[]{:S(2)}, u32[]{:S(2)}) async-start(bf16[8,160,640]{2,1,0:T(8,128)(2,1)} %bitcast.81), calls=%async_computation.1 | async-start | bytes 3276800 | tf_op jit(solution)/shard_map/all_to_all | solution.py:22
  67.0 5.6 %collective-permute-start.7 = (bf16[64,1280]{1,0:T(8,128)(2,1)S(1)}, bf16[64,1280]{1,0:T(8,128)(2,1)S(1)}, u32[]{:S(2)}, u32[]{:S(2)}) collective-permute-start(bf16[64,1280]{1,0:T(8,128)(2,1)S(1)} %get-tuple-element.30), channel_id=1, source_target_pairs={{0,384},{128,0},{256,128},{384,256},{1,385},{129,1},{257,129},{385... | collective-permute-start | bytes 491528 | tf_op jit(solution)/shard_map/ppermute | solution.py:53
  72.6 5.0 %collective-permute-start.6 = (bf16[64,1280]{1,0:T(8,128)(2,1)S(1)}, bf16[64,1280]{1,0:T(8,128)(2,1)S(1)}, u32[]{:S(2)}, u32[]{:S(2)}) collective-permute-start(bf16[64,1280]{1,0:T(8,128)(2,1)S(1)} %get-tuple-element.31), channel_id=1, source_target_pairs={{0,256},{128,384},{256,0},{384,128},{1,257},{129,385},{257,1},{385... | collective-permute-start | bytes 491528 | tf_op jit(solution)/shard_map/ppermute | solution.py:53
  79.6 6.8 %collective-permute-done.7 = bf16[64,1280]{1,0:T(8,128)(2,1)S(1)} collective-permute-done((bf16[64,1280]{1,0:T(8,128)(2,1)S(1)}, bf16[64,1280]{1,0:T(8,128)(2,1)S(1)}, u32[]{:S(2)}, u32[]{:S(2)}) %collective-permute-start.7) | collective-permute-done | bytes 163872 | tf_op jit(solution)/shard_map/ppermute | solution.py:53
  86.4 4.8 %collective-permute-done.6 = bf16[64,1280]{1,0:T(8,128)(2,1)S(1)} collective-permute-done((bf16[64,1280]{1,0:T(8,128)(2,1)S(1)}, bf16[64,1280]{1,0:T(8,128)(2,1)S(1)}, u32[]{:S(2)}, u32[]{:S(2)}) %collective-permute-start.6) | collective-permute-done | bytes 163872 | tf_op jit(solution)/shard_map/ppermute | solution.py:53
  91.2 2.9 %collective-permute-done.5 = bf16[64,1280]{1,0:T(8,128)(2,1)S(1)} collective-permute-done((bf16[64,1280]{1,0:T(8,128)(2,1)S(1)}, bf16[64,1280]{1,0:T(8,128)(2,1)S(1)}, u32[]{:S(2)}, u32[]{:S(2)}) %collective-permute-start.5) | collective-permute-done | bytes 163872 | tf_op jit(solution)/shard_map/ppermute | solution.py:53
  94.1 2.0 %constant_dynamic-update-slice_fusion.4 = (bf16[512,1280]{1,0:T(8,128)(2,1)}, bf16[64,1280]{1,0:T(8,128)(2,1)S(1)}) fusion(bf16[1,64,1280]{2,1,0:T(8,128)(2,1)} %param.6, bf16[64,1280]{1,0:T(8,128)(2,1)S(1)} %collective-permute-done.7, bf16[64,1280]{1,0:T(8,128)(2,1)S(1)} %collective-permute-done.6, bf16[64,1280]{1,0:T(8,128)(2,1)S(1)} %collective-permute-done.5, ...), kind=kLoop, calls=%fused_computation.61 | loop fusion | flops 2211839 | bytes 1146880
  96.1 3.0 %collective-permute-start.8 = (bf16[64,1280]{1,0:T(8,128)(2,1)S(1)}, bf16[64,1280]{1,0:T(8,128)(2,1)}, u32[]{:S(2)}, u32[]{:S(2)}) collective-permute-start(bf16[64,1280]{1,0:T(8,128)(2,1)S(1)} %get-tuple-element.20), channel_id=1, source_target_pairs={{0,384},{128,0},{256,128},{384,256},{1,385},{129,1},{257,129},{385... | collective-permute-start | bytes 491528 | tf_op jit(solution)/shard_map/ppermute | solution.py:53
  99.1 5.1 %collective-permute-start.9 = (bf16[64,1280]{1,0:T(8,128)(2,1)S(1)}, bf16[64,1280]{1,0:T(8,128)(2,1)}, u32[]{:S(2)}, u32[]{:S(2)}) collective-permute-start(bf16[64,1280]{1,0:T(8,128)(2,1)S(1)} %get-tuple-element.20), channel_id=1, source_target_pairs={{0,256},{128,384},{256,0},{384,128},{1,257},{129,385},{257,1},{385... | collective-permute-start | bytes 491528 | tf_op jit(solution)/shard_map/ppermute | solution.py:53
  104.2 3.4 %collective-permute-start.10 = (bf16[64,1280]{1,0:T(8,128)(2,1)S(1)}, bf16[64,1280]{1,0:T(8,128)(2,1)}, u32[]{:S(2)}, u32[]{:S(2)}) collective-permute-start(bf16[64,1280]{1,0:T(8,128)(2,1)S(1)} %get-tuple-element.20), channel_id=1, source_target_pairs={{0,128},{128,256},{256,384},{384,0},{1,129},{129,257},{257,385},{3... | collective-permute-start | bytes 491528 | tf_op jit(solution)/shard_map/ppermute | solution.py:53
  109.8 6.7 %collective-permute-done.9 = bf16[64,1280]{1,0:T(8,128)(2,1)} collective-permute-done((bf16[64,1280]{1,0:T(8,128)(2,1)S(1)}, bf16[64,1280]{1,0:T(8,128)(2,1)}, u32[]{:S(2)}, u32[]{:S(2)}) %collective-permute-start.9) | collective-permute-done | bytes 163872 | tf_op jit(solution)/shard_map/ppermute | solution.py:53
  116.5 2.6 %collective-permute-done.10 = bf16[64,1280]{1,0:T(8,128)(2,1)} collective-permute-done((bf16[64,1280]{1,0:T(8,128)(2,1)S(1)}, bf16[64,1280]{1,0:T(8,128)(2,1)}, u32[]{:S(2)}, u32[]{:S(2)}) %collective-permute-start.10) | collective-permute-done | bytes 163872 | tf_op jit(solution)/shard_map/ppermute | solution.py:53
  127.8 2.7 %convolution_convert_fusion = bf16[1280,640]{1,0:T(8,128)(2,1)S(1)} fusion(bf16[512,1280]{1,0:T(8,128)(2,1)} %constant_dynamic-update-slice_fusion, bf16[512,640]{1,0:T(8,128)(2,1)} %bitcast.93), kind=kOutput, calls=%fused_computation.1 | convolution fusion | flops 839680000 | bytes 3604480 | tf_op jit(solution)/shard_map/dot_general | solution.py:46
  131.5 3.8 %collective-permute-start.12 = (bf16[2,160,640]{2,1,0:T(8,128)(2,1)}, bf16[2,160,640]{2,1,0:T(8,128)(2,1)}, u32[]{:S(2)}, u32[]{:S(2)}) collective-permute-start(bf16[2,160,640]{2,1,0:T(8,128)(2,1)} %pad_maximum_fusion.2), channel_id=1, source_target_pairs={{0,1},{1,2},{2,3},{3,4},{4,5},{5,6},{6,7},{7,0},{8,9},{9,10},{10,1... | collective-permute-start | bytes 1228808 | tf_op jit(solution)/shard_map/ppermute | solution.py:53
  136.0 3.4 %collective-permute-start.13 = (bf16[2,160,640]{2,1,0:T(8,128)(2,1)}, bf16[2,160,640]{2,1,0:T(8,128)(2,1)}, u32[]{:S(2)}, u32[]{:S(2)}) collective-permute-start(bf16[2,160,640]{2,1,0:T(8,128)(2,1)} %pad_maximum_fusion.3), channel_id=1, source_target_pairs={{0,7},{1,0},{2,1},{3,2},{4,3},{5,4},{6,5},{7,6},{8,15},{9,8},{10,9... | collective-permute-start | bytes 1228808 | tf_op jit(solution)/shard_map/ppermute | solution.py:53
  139.5 3.4 %convolution_convert_fusion.3 = bf16[512,640]{1,0:T(8,128)(2,1)} fusion(bf16[512,1280]{1,0:T(8,128)(2,1)} %constant_dynamic-update-slice_fusion, bf16[640,1280]{1,0:T(8,128)(2,1)S(1)} %copy-done.6), kind=kOutput, calls=%fused_computation.4 | convolution fusion | flops 839188480 | bytes 3604480 | tf_op jit(solution)/shard_map/dot_general | solution.py:40
  142.8 2.0 %pick.3 = bf16[8,64,640]{2,1,0:T(8,128)(2,1)} custom-call(s32[8]{0:T(128)} %stack.72.order, bf16[8,64,640]{2,1,0:T(8,128)(2,1)} %bitcast.89), custom_call_target="tpu_custom_call" | custom-call | tf_op jit(solution)/shard_map/pick/pallas_call | solution.py:100
  144.9 7.0 %all-to-all-start.2 = ((bf16[8,64,640]{2,1,0:T(8,128)(2,1)}), bf16[8,64,640]{2,1,0:T(8,128)(2,1)}, u32[]{:S(2)}, u32[]{:S(2)}) async-start(bf16[8,64,640]{2,1,0:T(8,128)(2,1)} %pick.3), calls=%async_computation.2 | async-start | bytes 1310720 | tf_op jit(solution)/shard_map/all_to_all | solution.py:22
  152.8 4.6 %collective-permute-start.16 = (bf16[80,640]{1,0:T(8,128)(2,1)S(1)}, bf16[80,640]{1,0:T(8,128)(2,1)S(1)}, u32[]{:S(2)}, u32[]{:S(2)}) collective-permute-start(bf16[80,640]{1,0:T(8,128)(2,1)S(1)} %get-tuple-element.22), channel_id=1, source_target_pairs={{0,6},{1,7},{2,0},{3,1},{4,2},{5,3},{6,4},{7,5},{8,14},{9,15},{10,... | collective-permute-start | bytes 307208 | tf_op jit(solution)/shard_map/ppermute | solution.py:53
  157.3 2.2 %collective-permute-start.14 = (bf16[80,640]{1,0:T(8,128)(2,1)S(1)}, bf16[80,640]{1,0:T(8,128)(2,1)S(1)}, u32[]{:S(2)}, u32[]{:S(2)}) collective-permute-start(bf16[80,640]{1,0:T(8,128)(2,1)S(1)} %get-tuple-element.21), channel_id=1, source_target_pairs={{0,2},{1,3},{2,4},{3,5},{4,6},{5,7},{6,0},{7,1},{8,10},{9,11},{10,... | collective-permute-start | bytes 307208 | tf_op jit(solution)/shard_map/ppermute | solution.py:53
  162.1 5.7 %collective-permute-start.17 = (bf16[160,640]{1,0:T(8,128)(2,1)S(1)}, bf16[160,640]{1,0:T(8,128)(2,1)}, u32[]{:S(2)}, u32[]{:S(2)}) collective-permute-start(bf16[160,640]{1,0:T(8,128)(2,1)S(1)} %pad_maximum_fusion.5), channel_id=1, source_target_pairs={{0,6},{1,7},{2,0},{3,1},{4,2},{5,3},{6,4},{7,5},{8,14},{9,15},{10,... | collective-permute-start | bytes 614408 | tf_op jit(solution)/shard_map/ppermute | solution.py:53
  171.4 4.3 %collective-permute-done.17 = bf16[160,640]{1,0:T(8,128)(2,1)} collective-permute-done((bf16[160,640]{1,0:T(8,128)(2,1)S(1)}, bf16[160,640]{1,0:T(8,128)(2,1)}, u32[]{:S(2)}, u32[]{:S(2)}) %collective-permute-start.17) | collective-permute-done | bytes 204832 | tf_op jit(solution)/shard_map/ppermute | solution.py:53
  175.8 5.9 %collective-permute-done.15 = bf16[160,640]{1,0:T(8,128)(2,1)} collective-permute-done((bf16[160,640]{1,0:T(8,128)(2,1)}, bf16[160,640]{1,0:T(8,128)(2,1)}, u32[]{:S(2)}, u32[]{:S(2)}) %collective-permute-start.15) | collective-permute-done | bytes 204832 | tf_op jit(solution)/shard_map/ppermute | solution.py:53
  181.7 2.2 %fusion.4 = f32[640,160]{0,1:T(8,128)} fusion(bf16[160,640]{1,0:T(8,128)(2,1)} %collective-permute-done.17, bf16[160,640]{1,0:T(8,128)(2,1)} %collective-permute-done.15, bf16[2,160,640]{2,1,0:T(8,128)(2,1)} %collective-permute-done.13, bf16[2,160,640]{2,1,0:T(8,128)(2,1)} %collective-permute-done.12, bf16[8,160,640]{2,1,0:T(8,128)(2,1)} %bitcast.85, ...), kind=kLoop, calls=%fused_computation.22 | loop fusion | flops 921600 | bytes 1433604 | tf_op jit(solution)/shard_map/transpose | solution.py:143
  (59 shorter events, 37.5 us)
Async XLA Ops:
  0.6 45.8 %copy-start = (bf16[1280,640]{1,0:T(8,128)(2,1)S(1)}, bf16[1280,640]{1,0:T(8,128)(2,1)}, u32[]{:S(2)}) copy-start(bf16[1280,640]{1,0:T(8,128)(2,1)} %param.9) | copy-start | bytes 4915204
  2.9 9.5 %copy-start.3 = (bf16[1,64,1280]{2,1,0:T(8,128)(2,1)S(1)}, bf16[1,64,1280]{2,1,0:T(8,128)(2,1)}, u32[]{:S(2)}) copy-start(bf16[1,64,1280]{2,1,0:T(8,128)(2,1)} %param.6) | copy-start | bytes 491524
  2.9 38.8 %all-to-all-start = ((bf16[8,64,1280]{2,1,0:T(8,128)(2,1)}), bf16[8,64,1280]{2,1,0:T(8,128)(2,1)S(1)}, u32[]{:S(2)}, u32[]{:S(2)}) async-start(bf16[8,64,1280]{2,1,0:T(8,128)(2,1)} %broadcast_in_dim.6), calls=%async_computation | async-start | bytes 2621440 | tf_op jit(solution)/shard_map/all_to_all | solution.py:18
  12.5 23.9 %collective-permute-start.2 = (bf16[64,1280]{1,0:T(8,128)(2,1)S(1)}, bf16[64,1280]{1,0:T(8,128)(2,1)S(1)}, u32[]{:S(2)}, u32[]{:S(2)}) collective-permute-start(bf16[64,1280]{1,0:T(8,128)(2,1)S(1)} %fusion.7), channel_id=1, source_target_pairs={{0,128},{128,256},{256,384},{384,0},{1,129},{129,257},{257,385},{3... | collective-permute-start | bytes 491528 | tf_op jit(solution)/shard_map/ppermute | solution.py:53
  14.4 25.5 %collective-permute-start.1 = (bf16[64,1280]{1,0:T(8,128)(2,1)S(1)}, bf16[64,1280]{1,0:T(8,128)(2,1)S(1)}, u32[]{:S(2)}, u32[]{:S(2)}) collective-permute-start(bf16[64,1280]{1,0:T(8,128)(2,1)S(1)} %fusion.7), channel_id=1, source_target_pairs={{0,256},{128,384},{256,0},{384,128},{1,257},{129,385},{257,1},{385... | collective-permute-start | bytes 491528 | tf_op jit(solution)/shard_map/ppermute | solution.py:53
  18.5 21.3 %collective-permute-start = (bf16[64,1280]{1,0:T(8,128)(2,1)S(1)}, bf16[64,1280]{1,0:T(8,128)(2,1)}, u32[]{:S(2)}, u32[]{:S(2)}) collective-permute-start(bf16[64,1280]{1,0:T(8,128)(2,1)S(1)} %fusion.7), channel_id=1, source_target_pairs={{0,384},{128,0},{256,128},{384,256},{1,385},{129,1},{257,129},{385... | collective-permute-start | bytes 491528 | tf_op jit(solution)/shard_map/ppermute | solution.py:53
  41.7 1.1 copy-start.1
  46.4 2.7 %copy-start.4 = (bf16[256,1280]{1,0:T(8,128)(2,1)S(1)}, bf16[256,1280]{1,0:T(8,128)(2,1)}, u32[]{:S(2)}) copy-start(bf16[256,1280]{1,0:T(8,128)(2,1)} %pad_maximum_fusion) | copy-start | bytes 1966084
  47.1 4.4 %collective-permute-start.3 = (bf16[256,1280]{1,0:T(8,128)(2,1)S(1)}, bf16[256,1280]{1,0:T(8,128)(2,1)S(1)}, u32[]{:S(2)}, u32[]{:S(2)}) collective-permute-start(bf16[256,1280]{1,0:T(8,128)(2,1)S(1)} %convolution_convert_fusion.2), channel_id=1, source_target_pairs={{0,64},{64,0},{1,65},{65,1},{2,66},{66,2},{3,67},{67,3},{4,68},{68... | collective-permute-start | bytes 1966088 | tf_op jit(solution)/shard_map/ppermute | solution.py:57
  49.1 4.1 %collective-permute-start.4 = (bf16[256,1280]{1,0:T(8,128)(2,1)S(1)}, bf16[256,1280]{1,0:T(8,128)(2,1)S(1)}, u32[]{:S(2)}, u32[]{:S(2)}) collective-permute-start(bf16[256,1280]{1,0:T(8,128)(2,1)S(1)} %copy-done.4), channel_id=1, source_target_pairs={{0,64},{64,0},{1,65},{65,1},{2,66},{66,2},{3,67},{67,3},{4,68},{68... | collective-permute-start | bytes 1966088 | tf_op jit(solution)/shard_map/ppermute | solution.py:57
  51.5 1.7 copy-start.5
  55.6 72.3 %all-to-all-start.1 = ((bf16[8,160,640]{2,1,0:T(8,128)(2,1)}), bf16[8,160,640]{2,1,0:T(8,128)(2,1)S(1)}, u32[]{:S(2)}, u32[]{:S(2)}) async-start(bf16[8,160,640]{2,1,0:T(8,128)(2,1)} %bitcast.81), calls=%async_computation.1 | async-start | bytes 3276800 | tf_op jit(solution)/shard_map/all_to_all | solution.py:22
  67.0 19.4 %collective-permute-start.7 = (bf16[64,1280]{1,0:T(8,128)(2,1)S(1)}, bf16[64,1280]{1,0:T(8,128)(2,1)S(1)}, u32[]{:S(2)}, u32[]{:S(2)}) collective-permute-start(bf16[64,1280]{1,0:T(8,128)(2,1)S(1)} %get-tuple-element.30), channel_id=1, source_target_pairs={{0,384},{128,0},{256,128},{384,256},{1,385},{129,1},{257,129},{385... | collective-permute-start | bytes 491528 | tf_op jit(solution)/shard_map/ppermute | solution.py:53
  72.6 18.6 %collective-permute-start.6 = (bf16[64,1280]{1,0:T(8,128)(2,1)S(1)}, bf16[64,1280]{1,0:T(8,128)(2,1)S(1)}, u32[]{:S(2)}, u32[]{:S(2)}) collective-permute-start(bf16[64,1280]{1,0:T(8,128)(2,1)S(1)} %get-tuple-element.31), channel_id=1, source_target_pairs={{0,256},{128,384},{256,0},{384,128},{1,257},{129,385},{257,1},{385... | collective-permute-start | bytes 491528 | tf_op jit(solution)/shard_map/ppermute | solution.py:53
  77.6 16.5 %collective-permute-start.5 = (bf16[64,1280]{1,0:T(8,128)(2,1)S(1)}, bf16[64,1280]{1,0:T(8,128)(2,1)S(1)}, u32[]{:S(2)}, u32[]{:S(2)}) collective-permute-start(bf16[64,1280]{1,0:T(8,128)(2,1)S(1)} %get-tuple-element.29), channel_id=1, source_target_pairs={{0,128},{128,256},{256,384},{384,0},{1,129},{129,257},{257,385},{3... | collective-permute-start | bytes 491528 | tf_op jit(solution)/shard_map/ppermute | solution.py:53
  96.1 13.7 %collective-permute-start.8 = (bf16[64,1280]{1,0:T(8,128)(2,1)S(1)}, bf16[64,1280]{1,0:T(8,128)(2,1)}, u32[]{:S(2)}, u32[]{:S(2)}) collective-permute-start(bf16[64,1280]{1,0:T(8,128)(2,1)S(1)} %get-tuple-element.20), channel_id=1, source_target_pairs={{0,384},{128,0},{256,128},{384,256},{1,385},{129,1},{257,129},{385... | collective-permute-start | bytes 491528 | tf_op jit(solution)/shard_map/ppermute | solution.py:53
  99.1 17.4 %collective-permute-start.9 = (bf16[64,1280]{1,0:T(8,128)(2,1)S(1)}, bf16[64,1280]{1,0:T(8,128)(2,1)}, u32[]{:S(2)}, u32[]{:S(2)}) collective-permute-start(bf16[64,1280]{1,0:T(8,128)(2,1)S(1)} %get-tuple-element.20), channel_id=1, source_target_pairs={{0,256},{128,384},{256,0},{384,128},{1,257},{129,385},{257,1},{385... | collective-permute-start | bytes 491528 | tf_op jit(solution)/shard_map/ppermute | solution.py:53
  104.2 15.0 %collective-permute-start.10 = (bf16[64,1280]{1,0:T(8,128)(2,1)S(1)}, bf16[64,1280]{1,0:T(8,128)(2,1)}, u32[]{:S(2)}, u32[]{:S(2)}) collective-permute-start(bf16[64,1280]{1,0:T(8,128)(2,1)S(1)} %get-tuple-element.20), channel_id=1, source_target_pairs={{0,128},{128,256},{256,384},{384,0},{1,129},{129,257},{257,385},{3... | collective-permute-start | bytes 491528 | tf_op jit(solution)/shard_map/ppermute | solution.py:53
  120.2 6.7 %collective-permute-start.11 = (bf16[256,1280]{1,0:T(8,128)(2,1)S(1)}, bf16[256,1280]{1,0:T(8,128)(2,1)S(1)}, u32[]{:S(2)}, u32[]{:S(2)}) collective-permute-start(bf16[256,1280]{1,0:T(8,128)(2,1)S(1)} %pad_maximum_fusion.1), channel_id=1, source_target_pairs={{0,64},{64,0},{1,65},{65,1},{2,66},{66,2},{3,67},{67,3},{4,68},{68... | collective-permute-start | bytes 1966088 | tf_op jit(solution)/shard_map/ppermute | solution.py:57
  130.6 5.5 %copy-start.2 = (bf16[1280,640]{1,0:T(8,128)(2,1)}, bf16[1280,640]{1,0:T(8,128)(2,1)S(1)}, u32[]{:S(2)}) copy-start(bf16[1280,640]{1,0:T(8,128)(2,1)S(1)} %convolution_convert_fusion) | copy-start | bytes 4915204
  130.6 8.9 %copy-start.6 = (bf16[640,1280]{1,0:T(8,128)(2,1)S(1)}, bf16[640,1280]{1,0:T(8,128)(2,1)}, u32[]{:S(2)}) copy-start(bf16[640,1280]{1,0:T(8,128)(2,1)} %param.8) | copy-start | bytes 4915204
  131.5 28.1 %collective-permute-start.12 = (bf16[2,160,640]{2,1,0:T(8,128)(2,1)}, bf16[2,160,640]{2,1,0:T(8,128)(2,1)}, u32[]{:S(2)}, u32[]{:S(2)}) collective-permute-start(bf16[2,160,640]{2,1,0:T(8,128)(2,1)} %pad_maximum_fusion.2), channel_id=1, source_target_pairs={{0,1},{1,2},{2,3},{3,4},{4,5},{5,6},{6,7},{7,0},{8,9},{9,10},{10,1... | collective-permute-start | bytes 1228808 | tf_op jit(solution)/shard_map/ppermute | solution.py:53
  136.0 23.5 %collective-permute-start.13 = (bf16[2,160,640]{2,1,0:T(8,128)(2,1)}, bf16[2,160,640]{2,1,0:T(8,128)(2,1)}, u32[]{:S(2)}, u32[]{:S(2)}) collective-permute-start(bf16[2,160,640]{2,1,0:T(8,128)(2,1)} %pad_maximum_fusion.3), channel_id=1, source_target_pairs={{0,7},{1,0},{2,1},{3,2},{4,3},{5,4},{6,5},{7,6},{8,15},{9,8},{10,9... | collective-permute-start | bytes 1228808 | tf_op jit(solution)/shard_map/ppermute | solution.py:53
  144.9 39.0 %all-to-all-start.2 = ((bf16[8,64,640]{2,1,0:T(8,128)(2,1)}), bf16[8,64,640]{2,1,0:T(8,128)(2,1)}, u32[]{:S(2)}, u32[]{:S(2)}) async-start(bf16[8,64,640]{2,1,0:T(8,128)(2,1)} %pick.3), calls=%async_computation.2 | async-start | bytes 1310720 | tf_op jit(solution)/shard_map/all_to_all | solution.py:22
  152.8 9.2 %collective-permute-start.16 = (bf16[80,640]{1,0:T(8,128)(2,1)S(1)}, bf16[80,640]{1,0:T(8,128)(2,1)S(1)}, u32[]{:S(2)}, u32[]{:S(2)}) collective-permute-start(bf16[80,640]{1,0:T(8,128)(2,1)S(1)} %get-tuple-element.22), channel_id=1, source_target_pairs={{0,6},{1,7},{2,0},{3,1},{4,2},{5,3},{6,4},{7,5},{8,14},{9,15},{10,... | collective-permute-start | bytes 307208 | tf_op jit(solution)/shard_map/ppermute | solution.py:53
  157.3 10.4 %collective-permute-start.14 = (bf16[80,640]{1,0:T(8,128)(2,1)S(1)}, bf16[80,640]{1,0:T(8,128)(2,1)S(1)}, u32[]{:S(2)}, u32[]{:S(2)}) collective-permute-start(bf16[80,640]{1,0:T(8,128)(2,1)S(1)} %get-tuple-element.21), channel_id=1, source_target_pairs={{0,2},{1,3},{2,4},{3,5},{4,6},{5,7},{6,0},{7,1},{8,10},{9,11},{10,... | collective-permute-start | bytes 307208 | tf_op jit(solution)/shard_map/ppermute | solution.py:53
  162.1 13.7 %collective-permute-start.17 = (bf16[160,640]{1,0:T(8,128)(2,1)S(1)}, bf16[160,640]{1,0:T(8,128)(2,1)}, u32[]{:S(2)}, u32[]{:S(2)}) collective-permute-start(bf16[160,640]{1,0:T(8,128)(2,1)S(1)} %pad_maximum_fusion.5), channel_id=1, source_target_pairs={{0,6},{1,7},{2,0},{3,1},{4,2},{5,3},{6,4},{7,5},{8,14},{9,15},{10,... | collective-permute-start | bytes 614408 | tf_op jit(solution)/shard_map/ppermute | solution.py:53
  168.5 13.1 %collective-permute-start.15 = (bf16[160,640]{1,0:T(8,128)(2,1)}, bf16[160,640]{1,0:T(8,128)(2,1)}, u32[]{:S(2)}, u32[]{:S(2)}) collective-permute-start(bf16[160,640]{1,0:T(8,128)(2,1)} %pad_maximum_fusion.4), channel_id=1, source_target_pairs={{0,2},{1,3},{2,4},{3,5},{4,6},{5,7},{6,0},{7,1},{8,10},{9,11},{10,... | collective-permute-start | bytes 614408 | tf_op jit(solution)/shard_map/ppermute | solution.py:53

commit v3 on v2

v3 whole, which is shorter than its diff:
```python
import jax
import jax.numpy as jnp
from jax import lax
from jax.experimental import pallas as pl
from jax.experimental.pallas import tpu as pltpu
from jax.sharding import Mesh, PartitionSpec as P


root_coeff = 0.7978845608028654
cubic_coeff = 0.044715

ROW = ("yhi", "core")
COL = ("ylo", "x")
SWAP = [(0, 1), (1, 0)]


def spread(value, axis):
    copies = jnp.broadcast_to(value, (lax.axis_size(axis), *value.shape))
    return lax.all_to_all(copies, axis, split_axis=0, concat_axis=0, tiled=True)


def exchanged(value, axis):
    return lax.all_to_all(value, axis, split_axis=0, concat_axis=0, tiled=True)


def summed(pieces):
    return jnp.sum(pieces.astype(jnp.float32), axis=0)


def gelu_parts(values):
    inner = root_coeff * (values + cubic_coeff * values * values * values)
    tangent = jnp.tanh(inner)
    active = 0.5 * values * (1.0 + tangent)
    slope = 0.5 * (1.0 + tangent) + 0.5 * values * (1.0 - tangent * tangent) * root_coeff * (
        1.0 + 3.0 * cubic_coeff * values * values
    )
    return (active, slope)


def contract_last(left, right):
    return lax.dot_general(
        left, right, (((1,), (1,)), ((), ())), preferred_element_type=jnp.float32
    )


def contract_first(left, right):
    return lax.dot_general(
        left, right, (((0,), (0,)), ((), ())), preferred_element_type=jnp.float32
    )


def shifted(value, axis, by):
    length = lax.axis_size(axis)
    return lax.ppermute(value, axis, [(k, (k + by) % length) for k in range(length)])


def swapped(value):
    return lax.ppermute(value, "core", SWAP)


def block_at(blocks, index):
    return lax.dynamic_index_in_dim(blocks, index, 0, keepdims=False)


def gathered(own):
    return jnp.concatenate([own] + [shifted(own, "yhi", 4 - u) for u in (1, 2, 3)], axis=0)


def wide(value):
    return value.astype(jnp.float32)


def depth_sum(blocks):
    here = lax.axis_index("depth")
    pick = lambda by: block_at(blocks, (here + by) % 8)
    half = blocks.shape[1] // 2
    near_up = shifted(jnp.stack([pick(1), pick(3)]), "depth", 1)
    near_down = shifted(jnp.stack([pick(7), pick(5)]), "depth", 7)
    far = pick(4)
    far_up = shifted(far[:half], "depth", 2)
    far_down = shifted(far[half:], "depth", 6)
    up = wide(pick(2)) + wide(near_up[1])
    up = jnp.concatenate([up[:half] + wide(far_up), up[half:]], axis=0).astype(jnp.bfloat16)
    down = wide(pick(6)) + wide(near_down[1])
    down = jnp.concatenate([down[:half], down[half:] + wide(far_down)], axis=0).astype(jnp.bfloat16)
    last_up = shifted(up, "depth", 2)
    last_down = shifted(down, "depth", 6)
    near = wide(pick(0)) + wide(near_up[0]) + wide(near_down[0])
    return near + wide(last_up) + wide(last_down)


def pick_kernel(spot, blocks, *outs):
    width = outs[0].shape[-1]
    for u in range(4):
        row = 2 * ((spot[0] + u) % 4)
        for c, core in enumerate((spot[1], 1 - spot[1])):
            for k in range(2):
                outs[2 * c + k][u] = blocks[row + core, :, k * width : (k + 1) * width]


def picked(blocks, high, core):
    width = blocks.shape[2] // 2
    whole = pl.BlockSpec(memory_space=pltpu.VMEM)
    outs = pl.pallas_call(
        pick_kernel,
        out_shape=[jax.ShapeDtypeStruct((4, 64, width), blocks.dtype)] * 4,
        in_specs=[pl.BlockSpec(memory_space=pltpu.SMEM), whole],
        out_specs=[whole] * 4,
        name="pick",
    )(jnp.stack([high, core]).astype(jnp.int32), blocks)
    return [out.reshape(256, width) for out in outs]


def place_kernel(spot, mine, other, out):
    for u in range(4):
        row = 2 * ((spot[0] + u) % 4)
        out[row + spot[1]] = mine[u]
        out[row + 1 - spot[1]] = other[u]


def placed_by_row(mine, other, high, core):
    width = mine.shape[1]
    whole = pl.BlockSpec(memory_space=pltpu.VMEM)
    return pl.pallas_call(
        place_kernel,
        out_shape=jax.ShapeDtypeStruct((8, 64, width), mine.dtype),
        in_specs=[pl.BlockSpec(memory_space=pltpu.SMEM), whole, whole],
        out_specs=whole,
        name="place",
    )(jnp.stack([high, core]).astype(jnp.int32), mine.reshape(4, 64, width), other.reshape(4, 64, width))


def step(inputs, pre_act, grad_out, weight_up, weight_down):
    core = lax.axis_index("core")
    high = lax.axis_index("yhi")
    active, slope = gelu_parts(pre_act[0].astype(jnp.float32))
    active, slope = lax.optimization_barrier((active.astype(jnp.bfloat16), slope))
    active_mine = gathered(active)

    both = spread(jnp.concatenate([grad_out[0], inputs[0]], axis=1), COL)
    grads_mine, inputs_mine, grads_other, inputs_other = picked(both, high, core)

    away = contract_last(grads_other, weight_down).astype(jnp.bfloat16)
    back = swapped(away)
    kept = contract_last(grads_mine, weight_down)
    pair = (kept + wide(back)).astype(jnp.bfloat16).reshape(4, 64, -1)
    came = [shifted(pair[u], "yhi", u) for u in (1, 2, 3)]

    active_other = swapped(active_mine)
    lower_mine = lax.optimization_barrier(contract_first(active_mine, grads_mine))
    lower = (contract_first(active_other, grads_other) + lower_mine).astype(jnp.bfloat16)
    lower_pieces = exchanged(lower.reshape(8, -1, lower.shape[1]), "depth")

    hidden_grad = wide(pair[0]) + sum(wide(piece) for piece in came)
    delta_own = (hidden_grad * slope).astype(jnp.bfloat16)
    delta_mine = gathered(delta_own)
    delta_other = swapped(delta_mine)

    upper_mine = lax.optimization_barrier(contract_first(delta_mine, inputs_mine))
    upper = (contract_first(delta_other, inputs_other) + upper_mine).astype(jnp.bfloat16)
    grad_up = depth_sum(upper.reshape(8, -1, upper.shape[1]))

    parts_mine = contract_last(delta_mine, weight_up).astype(jnp.bfloat16)
    parts_other = contract_last(delta_other, weight_up).astype(jnp.bfloat16)
    parts = placed_by_row(parts_mine, parts_other, high, core)
    parts = exchanged(parts, COL)
    grad_inputs = summed(parts).astype(jnp.bfloat16)[None]
    grad_down = summed(lower_pieces)
    return (grad_inputs, grad_up.T, grad_down)


def solution(mesh):
    fine = Mesh(mesh.devices.reshape(4, 2, 2, 4, 8), ("yhi", "core", "ylo", "x", "depth"))
    placed = (
        P("depth", COL, ROW),
        P("depth", ROW, COL),
        P("depth", COL, ROW),
        P(ROW, COL),
        P(COL, ROW),
    )
    return jax.shard_map(
        step,
        mesh=fine,
        in_specs=placed,
        out_specs=(
            P("depth", COL, ROW),
            P(ROW, (*COL, "depth")),
            P((*COL, "depth"), ROW),
        ),
        check_vma=False,
    )
```

time: 187 us -> 207 us (1.11)
  the two profiles are of different devices: /device:TPU:2 before, /device:TPU:8 now
where the time goes in v3:
time: 207 us; the launch traced here: 206 us
  starting transfers between devices  93.8 us (45%)
  waiting for transfers between devices  76.2 us (37%)
  matrix products  14.4 us (7%)
  other arithmetic  10.9 us (5%)
  local copies, waits for them, and re-layouts  5.39 us (3%)
  Pallas kernels  4.49 us (2%)
    ppermute x15, starting transfers between devices, shifted(): lax.ppermute(value, axis, [(k, (k + by) % length) for k in range(length)])  59.6 us
    ppermute x15, waiting for transfers between devices, shifted(): lax.ppermute(value, axis, [(k, (k + by) % length) for k in range(length)])  59.1 us
    all_to_all x2, starting transfers between devices, exchanged(): return lax.all_to_all(value, axis, split_axis=0, concat_axis=0, tiled=True)  18.6 us
    all_to_all x1, waiting for transfers between devices, spread(): return lax.all_to_all(copies, axis, split_axis=0, concat_axis=0, tiled=True)  12.9 us
    all_to_all x1, starting transfers between devices, spread(): return lax.all_to_all(copies, axis, split_axis=0, concat_axis=0, tiled=True)  9.29 us
    dot_general x4, matrix products, contract_first(): lax.dot_general(left, right, (((0,), (0,)), ((), ())), preferred_element_...  9.08 us
    ppermute x3, starting transfers between devices, swapped(): return lax.ppermute(value, 'core', SWAP)  6.25 us
    dot_general x4, matrix products, contract_last(): lax.dot_general(left, right, (((1,), (1,)), ((), ())), preferred_element_...  5.34 us
  transfers between devices with their start and end apart: 21, of which 10 were waited for; matrix products, arithmetic and copies ran while one was open for 11% of the time, Pallas kernels for 1%

profile of v3, /device:TPU:8, one launch (start us, length us, event | category | flops | bytes accessed | tf_op | source)
XLA Modules:
  0.0 206.2 jit_solution(554935160051311690)
XLA Ops:
  2.9 9.3 %all-to-all-start = ((bf16[8,64,1280]{2,1,0:T(8,128)(2,1)}), bf16[8,64,1280]{2,1,0:T(8,128)(2,1)S(1)}, u32[]{:S(2)}, u32[]{:S(2)}) async-start(bf16[8,64,1280]{2,1,0:T(8,128)(2,1)} %broadcast_in_dim.6), calls=%async_computation | async-start | bytes 2621440 | tf_op jit(solution)/shard_map/all_to_all | solution.py:19
  12.8 12.9 %all-to-all-done.blocks = bf16[8,64,1280]{2,1,0:T(8,128)(2,1)S(1)} async-done(((bf16[8,64,1280]{2,1,0:T(8,128)(2,1)}), bf16[8,64,1280]{2,1,0:T(8,128)(2,1)S(1)}, u32[]{:S(2)}, u32[]{:S(2)}) %all-to-all-start) | async-done | bytes 1310752 | tf_op jit(solution)/shard_map/all_to_all | solution.py:19
  26.8 2.5 %pick.1 = (bf16[4,64,640]{2,1,0:T(8,128)(2,1)}, bf16[4,64,640]{2,1,0:T(8,128)(2,1)}, bf16[4,64,640]{2,1,0:T(8,128)(2,1)}, bf16[4,64,640]{2,1,0:T(8,128)(2,1)}) custom-call(s32[2]{0:T(128)} %pad_add_fusion.spot, bf16[8,64,1280]{2,1,0:T(8,128)(2,1)} %copy-done.2), custom_call_target="tpu_custom_call" | custom-call | tf_op jit(solution)/shard_map/pick/pallas_call | solution.py:104
  31.0 1.9 collective-permute-start
  33.2 5.3 %collective-permute-start.14 = (bf16[64,1280]{1,0:T(8,128)(2,1)S(1)}, bf16[64,1280]{1,0:T(8,128)(2,1)S(1)}, u32[]{:S(2)}, u32[]{:S(2)}) collective-permute-start(bf16[64,1280]{1,0:T(8,128)(2,1)S(1)} %get-tuple-element.14), channel_id=1, source_target_pairs={{0,384},{128,0},{256,128},{384,256},{1,385},{129,1},{257,129},{385... | collective-permute-start | bytes 491528 | tf_op jit(solution)/shard_map/ppermute | solution.py:54
  38.5 4.7 %collective-permute-start.15 = (bf16[64,1280]{1,0:T(8,128)(2,1)S(1)}, bf16[64,1280]{1,0:T(8,128)(2,1)S(1)}, u32[]{:S(2)}, u32[]{:S(2)}) collective-permute-start(bf16[64,1280]{1,0:T(8,128)(2,1)S(1)} %get-tuple-element.14), channel_id=1, source_target_pairs={{0,256},{128,384},{256,0},{384,128},{1,257},{129,385},{257,1},{385... | collective-permute-start | bytes 491528 | tf_op jit(solution)/shard_map/ppermute | solution.py:54
  44.0 2.2 %collective-permute-start.3 = (bf16[64,1280]{1,0:T(8,128)(2,1)S(1)}, bf16[64,1280]{1,0:T(8,128)(2,1)S(1)}, u32[]{:S(2)}, u32[]{:S(2)}) collective-permute-start(bf16[64,1280]{1,0:T(8,128)(2,1)S(1)} %get-tuple-element.24), channel_id=1, source_target_pairs={{0,384},{128,0},{256,128},{384,256},{1,385},{129,1},{257,129},{385... | collective-permute-start | bytes 491528 | tf_op jit(solution)/shard_map/ppermute | solution.py:54
  46.2 6.8 %collective-permute-start.2 = (bf16[64,1280]{1,0:T(8,128)(2,1)S(1)}, bf16[64,1280]{1,0:T(8,128)(2,1)S(1)}, u32[]{:S(2)}, u32[]{:S(2)}) collective-permute-start(bf16[64,1280]{1,0:T(8,128)(2,1)S(1)} %get-tuple-element.25), channel_id=1, source_target_pairs={{0,256},{128,384},{256,0},{384,128},{1,257},{129,385},{257,1},{385... | collective-permute-start | bytes 491528 | tf_op jit(solution)/shard_map/ppermute | solution.py:54
  53.1 2.7 %collective-permute-start.1 = (bf16[64,1280]{1,0:T(8,128)(2,1)S(1)}, bf16[64,1280]{1,0:T(8,128)(2,1)S(1)}, u32[]{:S(2)}, u32[]{:S(2)}) collective-permute-start(bf16[64,1280]{1,0:T(8,128)(2,1)S(1)} %get-tuple-element.23), channel_id=1, source_target_pairs={{0,128},{128,256},{256,384},{384,0},{1,129},{129,257},{257,385},{3... | collective-permute-start | bytes 491528 | tf_op jit(solution)/shard_map/ppermute | solution.py:54
  57.5 5.3 %collective-permute-start.16 = (bf16[64,1280]{1,0:T(8,128)(2,1)S(1)}, bf16[64,1280]{1,0:T(8,128)(2,1)S(1)}, u32[]{:S(2)}, u32[]{:S(2)}) collective-permute-start(bf16[64,1280]{1,0:T(8,128)(2,1)S(1)} %get-tuple-element.14), channel_id=1, source_target_pairs={{0,128},{128,256},{256,384},{384,0},{1,129},{129,257},{257,385},{3... | collective-permute-start | bytes 491528 | tf_op jit(solution)/shard_map/ppermute | solution.py:54
  62.8 7.6 %collective-permute-done.2 = bf16[64,1280]{1,0:T(8,128)(2,1)S(1)} collective-permute-done((bf16[64,1280]{1,0:T(8,128)(2,1)S(1)}, bf16[64,1280]{1,0:T(8,128)(2,1)S(1)}, u32[]{:S(2)}, u32[]{:S(2)}) %collective-permute-start.2) | collective-permute-done | bytes 163872 | tf_op jit(solution)/shard_map/ppermute | solution.py:54
  72.4 4.1 %collective-permute-start.5 = (bf16[64,1280]{1,0:T(8,128)(2,1)S(1)}, bf16[64,1280]{1,0:T(8,128)(2,1)S(1)}, u32[]{:S(2)}, u32[]{:S(2)}) collective-permute-start(bf16[64,1280]{1,0:T(8,128)(2,1)S(1)} %multiply_convert_fusion), channel_id=1, source_target_pairs={{0,256},{128,384},{256,0},{384,128},{1,257},{129,385},{257,1},{385... | collective-permute-start | bytes 491528 | tf_op jit(solution)/shard_map/ppermute | solution.py:54
  76.5 6.0 %collective-permute-start.4 = (bf16[64,1280]{1,0:T(8,128)(2,1)S(1)}, bf16[64,1280]{1,0:T(8,128)(2,1)S(1)}, u32[]{:S(2)}, u32[]{:S(2)}) collective-permute-start(bf16[64,1280]{1,0:T(8,128)(2,1)S(1)} %multiply_convert_fusion), channel_id=1, source_target_pairs={{0,384},{128,0},{256,128},{384,256},{1,385},{129,1},{257,129},{385... | collective-permute-start | bytes 491528 | tf_op jit(solution)/shard_map/ppermute | solution.py:54
  84.4 6.9 %collective-permute-done.4 = bf16[64,1280]{1,0:T(8,128)(2,1)S(1)} collective-permute-done((bf16[64,1280]{1,0:T(8,128)(2,1)S(1)}, bf16[64,1280]{1,0:T(8,128)(2,1)S(1)}, u32[]{:S(2)}, u32[]{:S(2)}) %collective-permute-start.4) | collective-permute-done | bytes 163872 | tf_op jit(solution)/shard_map/ppermute | solution.py:54
  91.4 1.9 collective-permute-start.7
  93.4 2.4 %collective-permute-start.17 = (bf16[256,1280]{1,0:T(8,128)(2,1)S(1)}, bf16[256,1280]{1,0:T(8,128)(2,1)}, u32[]{:S(2)}, u32[]{:S(2)}) collective-permute-start(bf16[256,1280]{1,0:T(8,128)(2,1)S(1)} %constant_dynamic-update-slice_fusion), channel_id=1, source_target_pairs={{0,64},{64,0},{1,65},{65,1},{2,66},{66,2},{3,67},{67,3},{4,68},{68... | collective-permute-start | bytes 1966088 | tf_op jit(solution)/shard_map/ppermute | solution.py:58
  99.6 2.0 place.1
  101.6 8.3 %all-to-all-start.1 = ((bf16[8,64,640]{2,1,0:T(8,128)(2,1)}), bf16[8,64,640]{2,1,0:T(8,128)(2,1)S(1)}, u32[]{:S(2)}, u32[]{:S(2)}) async-start(bf16[8,64,640]{2,1,0:T(8,128)(2,1)} %place.1), calls=%async_computation.1 | async-start | bytes 1310720 | tf_op jit(solution)/shard_map/all_to_all | solution.py:23
  110.8 3.0 %fusion.1 = bf16[1280,640]{1,0:T(8,128)(2,1)} fusion(f32[1280,640]{1,0:T(8,128)S(1)} %fusion.21, bf16[256,1280]{1,0:T(8,128)(2,1)} %collective-permute-done.17, bf16[256,640]{1,0:T(8,128)(2,1)S(1)} %bitcast.64), kind=kOutput, calls=%fused_computation.4 | convolution fusion | flops 421068800 | bytes 5898240 | tf_op jit(solution)/shard_map/dot_general | solution.py:47
  113.9 2.4 %fusion.19 = f32[1280,640]{1,0:T(8,128)} fusion(bf16[256,640]{1,0:T(8,128)(2,1)S(1)} %bitcast.68, bf16[64,1280]{1,0:T(8,128)(2,1)S(1)} %copy-done.7, bf16[64,1280]{1,0:T(8,128)(2,1)S(1)} %copy-done.9, bf16[64,1280]{1,0:T(8,128)(2,1)S(1)} %copy-done.11, bf16[64,1280]{1,0:T(8,128)(2,1)S(1)} %multiply_convert_fusion), kind=kOutput, calls=%fused_computation.58 | convolution fusion | flops 422051840 | bytes 4259840 | tf_op jit(solution)/shard_map/dot_general | solution.py:47
  116.3 4.1 %all-to-all-done.1 = bf16[8,64,640]{2,1,0:T(8,128)(2,1)S(1)} async-done(((bf16[8,64,640]{2,1,0:T(8,128)(2,1)}), bf16[8,64,640]{2,1,0:T(8,128)(2,1)S(1)}, u32[]{:S(2)}, u32[]{:S(2)}) %all-to-all-start.1) | async-done | bytes 655392 | tf_op jit(solution)/shard_map/all_to_all | solution.py:23
  121.2 10.3 %all-to-all-start.2 = ((bf16[8,160,640]{2,1,0:T(8,128)(2,1)}), bf16[8,160,640]{2,1,0:T(8,128)(2,1)S(1)}, u32[]{:S(2)}, u32[]{:S(2)}) async-start(bf16[8,160,640]{2,1,0:T(8,128)(2,1)} %bitcast.22), calls=%async_computation.2 | async-start | bytes 3276800 | tf_op jit(solution)/shard_map/all_to_all | solution.py:23
  131.6 2.9 %fusion = bf16[1280,640]{1,0:T(8,128)(2,1)S(1)} fusion(f32[1280,640]{1,0:T(8,128)} %fusion.19, bf16[256,1280]{1,0:T(8,128)(2,1)} %copy-done.12, bf16[256,640]{1,0:T(8,128)(2,1)} %bitcast.67), kind=kOutput, calls=%fused_computation.3 | convolution fusion | flops 421068800 | bytes 5898240 | tf_op jit(solution)/shard_map/dot_general | solution.py:47
  135.6 3.9 %collective-permute-start.8 = (bf16[2,160,640]{2,1,0:T(8,128)(2,1)}, bf16[2,160,640]{2,1,0:T(8,128)(2,1)}, u32[]{:S(2)}, u32[]{:S(2)}) collective-permute-start(bf16[2,160,640]{2,1,0:T(8,128)(2,1)} %pad_maximum_fusion.1), channel_id=1, source_target_pairs={{0,1},{1,2},{2,3},{3,4},{4,5},{5,6},{6,7},{7,0},{8,9},{9,10},{10,1... | collective-permute-start | bytes 1228808 | tf_op jit(solution)/shard_map/ppermute | solution.py:54
  140.3 3.1 %collective-permute-start.9 = (bf16[2,160,640]{2,1,0:T(8,128)(2,1)}, bf16[2,160,640]{2,1,0:T(8,128)(2,1)}, u32[]{:S(2)}, u32[]{:S(2)}) collective-permute-start(bf16[2,160,640]{2,1,0:T(8,128)(2,1)} %pad_maximum_fusion.2), channel_id=1, source_target_pairs={{0,7},{1,0},{2,1},{3,2},{4,3},{5,4},{6,5},{7,6},{8,15},{9,8},{10,9... | collective-permute-start | bytes 1228808 | tf_op jit(solution)/shard_map/ppermute | solution.py:54
  144.5 4.8 %collective-permute-start.12 = (bf16[80,640]{1,0:T(8,128)(2,1)S(1)}, bf16[80,640]{1,0:T(8,128)(2,1)S(1)}, u32[]{:S(2)}, u32[]{:S(2)}) collective-permute-start(bf16[80,640]{1,0:T(8,128)(2,1)S(1)} %get-tuple-element.16), channel_id=1, source_target_pairs={{0,6},{1,7},{2,0},{3,1},{4,2},{5,3},{6,4},{7,5},{8,14},{9,15},{10,... | collective-permute-start | bytes 307208 | tf_op jit(solution)/shard_map/ppermute | solution.py:54
  151.2 29.4 %collective-permute-done.8 = bf16[2,160,640]{2,1,0:T(8,128)(2,1)} collective-permute-done((bf16[2,160,640]{2,1,0:T(8,128)(2,1)}, bf16[2,160,640]{2,1,0:T(8,128)(2,1)}, u32[]{:S(2)}, u32[]{:S(2)}) %collective-permute-start.8) | collective-permute-done | bytes 409632 | tf_op jit(solution)/shard_map/ppermute | solution.py:54
  183.1 4.0 %collective-permute-start.13 = (bf16[160,640]{1,0:T(8,128)(2,1)S(1)}, bf16[160,640]{1,0:T(8,128)(2,1)}, u32[]{:S(2)}, u32[]{:S(2)}) collective-permute-start(bf16[160,640]{1,0:T(8,128)(2,1)S(1)} %pad_maximum_fusion.4), channel_id=1, source_target_pairs={{0,6},{1,7},{2,0},{3,1},{4,2},{5,3},{6,4},{7,5},{8,14},{9,15},{10,... | collective-permute-start | bytes 614408 | tf_op jit(solution)/shard_map/ppermute | solution.py:54
  187.8 2.7 %collective-permute-start.11 = (bf16[160,640]{1,0:T(8,128)(2,1)}, bf16[160,640]{1,0:T(8,128)(2,1)}, u32[]{:S(2)}, u32[]{:S(2)}) collective-permute-start(bf16[160,640]{1,0:T(8,128)(2,1)} %pad_maximum_fusion.3), channel_id=1, source_target_pairs={{0,2},{1,3},{2,4},{3,5},{4,6},{5,7},{6,0},{7,1},{8,10},{9,11},{10,... | collective-permute-start | bytes 614408 | tf_op jit(solution)/shard_map/ppermute | solution.py:54
  190.6 4.9 %collective-permute-done.13 = bf16[160,640]{1,0:T(8,128)(2,1)} collective-permute-done((bf16[160,640]{1,0:T(8,128)(2,1)S(1)}, bf16[160,640]{1,0:T(8,128)(2,1)}, u32[]{:S(2)}, u32[]{:S(2)}) %collective-permute-start.13) | collective-permute-done | bytes 204832 | tf_op jit(solution)/shard_map/ppermute | solution.py:54
  195.5 5.7 %collective-permute-done.11 = bf16[160,640]{1,0:T(8,128)(2,1)} collective-permute-done((bf16[160,640]{1,0:T(8,128)(2,1)}, bf16[160,640]{1,0:T(8,128)(2,1)}, u32[]{:S(2)}, u32[]{:S(2)}) %collective-permute-start.11) | collective-permute-done | bytes 204832 | tf_op jit(solution)/shard_map/ppermute | solution.py:54
  201.2 2.2 %fusion.3 = f32[640,160]{0,1:T(8,128)} fusion(bf16[160,640]{1,0:T(8,128)(2,1)} %collective-permute-done.13, bf16[160,640]{1,0:T(8,128)(2,1)} %collective-permute-done.11, bf16[2,160,640]{2,1,0:T(8,128)(2,1)} %collective-permute-done.9, bf16[2,160,640]{2,1,0:T(8,128)(2,1)} %collective-permute-done.8, bf16[8,160,640]{2,1,0:T(8,128)(2,1)} %bitcast.62, ...), kind=kLoop, calls=%fused_computation.21 | loop fusion | flops 921600 | bytes 1433604 | tf_op jit(solution)/shard_map/transpose | solution.py:169
  (77 shorter events, 28.5 us)
Async XLA Ops:
  0.6 28.6 %copy-start = (bf16[1280,640]{1,0:T(8,128)(2,1)S(1)}, bf16[1280,640]{1,0:T(8,128)(2,1)}, u32[]{:S(2)}) copy-start(bf16[1280,640]{1,0:T(8,128)(2,1)} %param.9) | copy-start | bytes 4915204
  2.9 22.8 %all-to-all-start = ((bf16[8,64,1280]{2,1,0:T(8,128)(2,1)}), bf16[8,64,1280]{2,1,0:T(8,128)(2,1)S(1)}, u32[]{:S(2)}, u32[]{:S(2)}) async-start(bf16[8,64,1280]{2,1,0:T(8,128)(2,1)} %broadcast_in_dim.6), calls=%async_computation | async-start | bytes 2621440 | tf_op jit(solution)/shard_map/all_to_all | solution.py:19
  29.3 3.7 %copy-start.14 = (bf16[1,64,1280]{2,1,0:T(8,128)(2,1)S(1)}, bf16[1,64,1280]{2,1,0:T(8,128)(2,1)}, u32[]{:S(2)}) copy-start(bf16[1,64,1280]{2,1,0:T(8,128)(2,1)} %param.6) | copy-start | bytes 491524
  29.3 13.9 %copy-start.5 = (bf16[4,64,640]{2,1,0:T(8,128)(2,1)S(1)}, bf16[4,64,640]{2,1,0:T(8,128)(2,1)}, u32[]{:S(2)}) copy-start(bf16[4,64,640]{2,1,0:T(8,128)(2,1)} %get-tuple-element.9) | copy-start | bytes 983044
  31.0 12.2 %collective-permute-start = (bf16[256,1280]{1,0:T(8,128)(2,1)S(1)}, bf16[256,1280]{1,0:T(8,128)(2,1)S(1)}, u32[]{:S(2)}, u32[]{:S(2)}) collective-permute-start(bf16[256,1280]{1,0:T(8,128)(2,1)S(1)} %convolution_convert_fusion), channel_id=1, source_target_pairs={{0,64},{64,0},{1,65},{65,1},{2,66},{66,2},{3,67},{67,3},{4,68},{68... | collective-permute-start | bytes 1966088 | tf_op jit(solution)/shard_map/ppermute | solution.py:58
  33.2 43.4 %collective-permute-start.14 = (bf16[64,1280]{1,0:T(8,128)(2,1)S(1)}, bf16[64,1280]{1,0:T(8,128)(2,1)S(1)}, u32[]{:S(2)}, u32[]{:S(2)}) collective-permute-start(bf16[64,1280]{1,0:T(8,128)(2,1)S(1)} %get-tuple-element.14), channel_id=1, source_target_pairs={{0,384},{128,0},{256,128},{384,256},{1,385},{129,1},{257,129},{385... | collective-permute-start | bytes 491528 | tf_op jit(solution)/shard_map/ppermute | solution.py:54
  38.5 54.9 %collective-permute-start.15 = (bf16[64,1280]{1,0:T(8,128)(2,1)S(1)}, bf16[64,1280]{1,0:T(8,128)(2,1)S(1)}, u32[]{:S(2)}, u32[]{:S(2)}) collective-permute-start(bf16[64,1280]{1,0:T(8,128)(2,1)S(1)} %get-tuple-element.14), channel_id=1, source_target_pairs={{0,256},{128,384},{256,0},{384,128},{1,257},{129,385},{257,1},{385... | collective-permute-start | bytes 491528 | tf_op jit(solution)/shard_map/ppermute | solution.py:54
  44.0 13.5 %collective-permute-start.3 = (bf16[64,1280]{1,0:T(8,128)(2,1)S(1)}, bf16[64,1280]{1,0:T(8,128)(2,1)S(1)}, u32[]{:S(2)}, u32[]{:S(2)}) collective-permute-start(bf16[64,1280]{1,0:T(8,128)(2,1)S(1)} %get-tuple-element.24), channel_id=1, source_target_pairs={{0,384},{128,0},{256,128},{384,256},{1,385},{129,1},{257,129},{385... | collective-permute-start | bytes 491528 | tf_op jit(solution)/shard_map/ppermute | solution.py:54
  46.2 24.2 %collective-permute-start.2 = (bf16[64,1280]{1,0:T(8,128)(2,1)S(1)}, bf16[64,1280]{1,0:T(8,128)(2,1)S(1)}, u32[]{:S(2)}, u32[]{:S(2)}) collective-permute-start(bf16[64,1280]{1,0:T(8,128)(2,1)S(1)} %get-tuple-element.25), channel_id=1, source_target_pairs={{0,256},{128,384},{256,0},{384,128},{1,257},{129,385},{257,1},{385... | collective-permute-start | bytes 491528 | tf_op jit(solution)/shard_map/ppermute | solution.py:54
  53.1 17.3 %collective-permute-start.1 = (bf16[64,1280]{1,0:T(8,128)(2,1)S(1)}, bf16[64,1280]{1,0:T(8,128)(2,1)S(1)}, u32[]{:S(2)}, u32[]{:S(2)}) collective-permute-start(bf16[64,1280]{1,0:T(8,128)(2,1)S(1)} %get-tuple-element.23), channel_id=1, source_target_pairs={{0,128},{128,256},{256,384},{384,0},{1,129},{129,257},{257,385},{3... | collective-permute-start | bytes 491528 | tf_op jit(solution)/shard_map/ppermute | solution.py:54
  55.8 40.0 %copy-start.15 = (bf16[640,1280]{1,0:T(8,128)(2,1)S(1)}, bf16[640,1280]{1,0:T(8,128)(2,1)}, u32[]{:S(2)}) copy-start(bf16[640,1280]{1,0:T(8,128)(2,1)} %param.8) | copy-start | bytes 4915204
  57.5 35.9 %collective-permute-start.16 = (bf16[64,1280]{1,0:T(8,128)(2,1)S(1)}, bf16[64,1280]{1,0:T(8,128)(2,1)S(1)}, u32[]{:S(2)}, u32[]{:S(2)}) collective-permute-start(bf16[64,1280]{1,0:T(8,128)(2,1)S(1)} %get-tuple-element.14), channel_id=1, source_target_pairs={{0,128},{128,256},{256,384},{384,0},{1,129},{129,257},{257,385},{3... | collective-permute-start | bytes 491528 | tf_op jit(solution)/shard_map/ppermute | solution.py:54
  70.5 13.9 %collective-permute-start.6 = (bf16[64,1280]{1,0:T(8,128)(2,1)S(1)}, bf16[64,1280]{1,0:T(8,128)(2,1)S(1)}, u32[]{:S(2)}, u32[]{:S(2)}) collective-permute-start(bf16[64,1280]{1,0:T(8,128)(2,1)S(1)} %multiply_convert_fusion), channel_id=1, source_target_pairs={{0,128},{128,256},{256,384},{384,0},{1,129},{129,257},{257,385},{3... | collective-permute-start | bytes 491528 | tf_op jit(solution)/shard_map/ppermute | solution.py:54
  72.4 12.0 %collective-permute-start.5 = (bf16[64,1280]{1,0:T(8,128)(2,1)S(1)}, bf16[64,1280]{1,0:T(8,128)(2,1)S(1)}, u32[]{:S(2)}, u32[]{:S(2)}) collective-permute-start(bf16[64,1280]{1,0:T(8,128)(2,1)S(1)} %multiply_convert_fusion), channel_id=1, source_target_pairs={{0,256},{128,384},{256,0},{384,128},{1,257},{129,385},{257,1},{385... | collective-permute-start | bytes 491528 | tf_op jit(solution)/shard_map/ppermute | solution.py:54
  76.5 14.8 %collective-permute-start.4 = (bf16[64,1280]{1,0:T(8,128)(2,1)S(1)}, bf16[64,1280]{1,0:T(8,128)(2,1)S(1)}, u32[]{:S(2)}, u32[]{:S(2)}) collective-permute-start(bf16[64,1280]{1,0:T(8,128)(2,1)S(1)} %multiply_convert_fusion), channel_id=1, source_target_pairs={{0,384},{128,0},{256,128},{384,256},{1,385},{129,1},{257,129},{385... | collective-permute-start | bytes 491528 | tf_op jit(solution)/shard_map/ppermute | solution.py:54
  84.4 12.8 %copy-start.6 = (bf16[64,1280]{1,0:T(8,128)(2,1)}, bf16[64,1280]{1,0:T(8,128)(2,1)S(1)}, u32[]{:S(2)}) copy-start(bf16[64,1280]{1,0:T(8,128)(2,1)S(1)} %collective-permute-done.6) | copy-start | bytes 491524
  84.4 12.8 %copy-start.8 = (bf16[64,1280]{1,0:T(8,128)(2,1)}, bf16[64,1280]{1,0:T(8,128)(2,1)S(1)}, u32[]{:S(2)}) copy-start(bf16[64,1280]{1,0:T(8,128)(2,1)S(1)} %collective-permute-done.5) | copy-start | bytes 491524
  91.3 5.9 %copy-start.10 = (bf16[64,1280]{1,0:T(8,128)(2,1)}, bf16[64,1280]{1,0:T(8,128)(2,1)S(1)}, u32[]{:S(2)}) copy-start(bf16[64,1280]{1,0:T(8,128)(2,1)S(1)} %collective-permute-done.4) | copy-start | bytes 491524
  91.4 5.9 %collective-permute-start.7 = (bf16[256,1280]{1,0:T(8,128)(2,1)S(1)}, bf16[256,1280]{1,0:T(8,128)(2,1)S(1)}, u32[]{:S(2)}, u32[]{:S(2)}) collective-permute-start(bf16[256,1280]{1,0:T(8,128)(2,1)S(1)} %pad_maximum_fusion), channel_id=1, source_target_pairs={{0,64},{64,0},{1,65},{65,1},{2,66},{66,2},{3,67},{67,3},{4,68},{68... | collective-permute-start | bytes 1966088 | tf_op jit(solution)/shard_map/ppermute | solution.py:58
  93.4 17.2 %collective-permute-start.17 = (bf16[256,1280]{1,0:T(8,128)(2,1)S(1)}, bf16[256,1280]{1,0:T(8,128)(2,1)}, u32[]{:S(2)}, u32[]{:S(2)}) collective-permute-start(bf16[256,1280]{1,0:T(8,128)(2,1)S(1)} %constant_dynamic-update-slice_fusion), channel_id=1, source_target_pairs={{0,64},{64,0},{1,65},{65,1},{2,66},{66,2},{3,67},{67,3},{4,68},{68... | collective-permute-start | bytes 1966088 | tf_op jit(solution)/shard_map/ppermute | solution.py:58
  101.6 18.8 %all-to-all-start.1 = ((bf16[8,64,640]{2,1,0:T(8,128)(2,1)}), bf16[8,64,640]{2,1,0:T(8,128)(2,1)S(1)}, u32[]{:S(2)}, u32[]{:S(2)}) async-start(bf16[8,64,640]{2,1,0:T(8,128)(2,1)} %place.1), calls=%async_computation.1 | async-start | bytes 1310720 | tf_op jit(solution)/shard_map/all_to_all | solution.py:23
  110.6 3.3 %copy-start.7 = (bf16[64,1280]{1,0:T(8,128)(2,1)S(1)}, bf16[64,1280]{1,0:T(8,128)(2,1)}, u32[]{:S(2)}) copy-start(bf16[64,1280]{1,0:T(8,128)(2,1)} %copy-done.6) | copy-start | bytes 491524
  110.6 3.3 %copy-start.9 = (bf16[64,1280]{1,0:T(8,128)(2,1)S(1)}, bf16[64,1280]{1,0:T(8,128)(2,1)}, u32[]{:S(2)}) copy-start(bf16[64,1280]{1,0:T(8,128)(2,1)} %copy-done.8) | copy-start | bytes 491524
  110.6 3.3 %copy-start.11 = (bf16[64,1280]{1,0:T(8,128)(2,1)S(1)}, bf16[64,1280]{1,0:T(8,128)(2,1)}, u32[]{:S(2)}) copy-start(bf16[64,1280]{1,0:T(8,128)(2,1)} %copy-done.10) | copy-start | bytes 491524
  121.2 84.0 %all-to-all-start.2 = ((bf16[8,160,640]{2,1,0:T(8,128)(2,1)}), bf16[8,160,640]{2,1,0:T(8,128)(2,1)S(1)}, u32[]{:S(2)}, u32[]{:S(2)}) async-start(bf16[8,160,640]{2,1,0:T(8,128)(2,1)} %bitcast.22), calls=%async_computation.2 | async-start | bytes 3276800 | tf_op jit(solution)/shard_map/all_to_all | solution.py:23
  134.5 5.8 %copy-start.1 = (bf16[1280,640]{1,0:T(8,128)(2,1)}, bf16[1280,640]{1,0:T(8,128)(2,1)S(1)}, u32[]{:S(2)}) copy-start(bf16[1280,640]{1,0:T(8,128)(2,1)S(1)} %fusion) | copy-start | bytes 4915204
  135.6 45.0 %collective-permute-start.8 = (bf16[2,160,640]{2,1,0:T(8,128)(2,1)}, bf16[2,160,640]{2,1,0:T(8,128)(2,1)}, u32[]{:S(2)}, u32[]{:S(2)}) collective-permute-start(bf16[2,160,640]{2,1,0:T(8,128)(2,1)} %pad_maximum_fusion.1), channel_id=1, source_target_pairs={{0,1},{1,2},{2,3},{3,4},{4,5},{5,6},{6,7},{7,0},{8,9},{9,10},{10,1... | collective-permute-start | bytes 1228808 | tf_op jit(solution)/shard_map/ppermute | solution.py:54
  140.3 40.3 %collective-permute-start.9 = (bf16[2,160,640]{2,1,0:T(8,128)(2,1)}, bf16[2,160,640]{2,1,0:T(8,128)(2,1)}, u32[]{:S(2)}, u32[]{:S(2)}) collective-permute-start(bf16[2,160,640]{2,1,0:T(8,128)(2,1)} %pad_maximum_fusion.2), channel_id=1, source_target_pairs={{0,7},{1,0},{2,1},{3,2},{4,3},{5,4},{6,5},{7,6},{8,15},{9,8},{10,9... | collective-permute-start | bytes 1228808 | tf_op jit(solution)/shard_map/ppermute | solution.py:54
  144.5 38.5 %collective-permute-start.12 = (bf16[80,640]{1,0:T(8,128)(2,1)S(1)}, bf16[80,640]{1,0:T(8,128)(2,1)S(1)}, u32[]{:S(2)}, u32[]{:S(2)}) collective-permute-start(bf16[80,640]{1,0:T(8,128)(2,1)S(1)} %get-tuple-element.16), channel_id=1, source_target_pairs={{0,6},{1,7},{2,0},{3,1},{4,2},{5,3},{6,4},{7,5},{8,14},{9,15},{10,... | collective-permute-start | bytes 307208 | tf_op jit(solution)/shard_map/ppermute | solution.py:54
  149.3 37.8 %collective-permute-start.10 = (bf16[80,640]{1,0:T(8,128)(2,1)S(1)}, bf16[80,640]{1,0:T(8,128)(2,1)S(1)}, u32[]{:S(2)}, u32[]{:S(2)}) collective-permute-start(bf16[80,640]{1,0:T(8,128)(2,1)S(1)} %get-tuple-element.15), channel_id=1, source_target_pairs={{0,2},{1,3},{2,4},{3,5},{4,6},{5,7},{6,0},{7,1},{8,10},{9,11},{10,... | collective-permute-start | bytes 307208 | tf_op jit(solution)/shard_map/ppermute | solution.py:54
  183.1 12.4 %collective-permute-start.13 = (bf16[160,640]{1,0:T(8,128)(2,1)S(1)}, bf16[160,640]{1,0:T(8,128)(2,1)}, u32[]{:S(2)}, u32[]{:S(2)}) collective-permute-start(bf16[160,640]{1,0:T(8,128)(2,1)S(1)} %pad_maximum_fusion.4), channel_id=1, source_target_pairs={{0,6},{1,7},{2,0},{3,1},{4,2},{5,3},{6,4},{7,5},{8,14},{9,15},{10,... | collective-permute-start | bytes 614408 | tf_op jit(solution)/shard_map/ppermute | solution.py:54
  187.8 13.4 %collective-permute-start.11 = (bf16[160,640]{1,0:T(8,128)(2,1)}, bf16[160,640]{1,0:T(8,128)(2,1)}, u32[]{:S(2)}, u32[]{:S(2)}) collective-permute-start(bf16[160,640]{1,0:T(8,128)(2,1)} %pad_maximum_fusion.3), channel_id=1, source_target_pairs={{0,2},{1,3},{2,4},{3,5},{4,6},{5,7},{6,0},{7,1},{8,10},{9,11},{10,... | collective-permute-start | bytes 614408 | tf_op jit(solution)/shard_map/ppermute | solution.py:54
  (5 other events, 7.1 us)

commit v4 on v1

v4 whole, which is shorter than its diff:
```python
import jax
import jax.numpy as jnp
from jax import lax
from jax.sharding import Mesh, PartitionSpec as P


root_coeff = 0.7978845608028654
cubic_coeff = 0.044715

ROW = ("yhi", "core")
COL = ("ylo", "x")
SWAP = [(0, 1), (1, 0)]


def spread(value, axis):
    copies = jnp.broadcast_to(value, (lax.axis_size(axis), *value.shape))
    return lax.all_to_all(copies, axis, split_axis=0, concat_axis=0, tiled=True)


def exchanged(value, axis):
    return lax.all_to_all(value, axis, split_axis=0, concat_axis=0, tiled=True)


def summed(pieces):
    return jnp.sum(pieces.astype(jnp.float32), axis=0)


def gelu_parts(values):
    inner = root_coeff * (values + cubic_coeff * values * values * values)
    tangent = jnp.tanh(inner)
    active = 0.5 * values * (1.0 + tangent)
    slope = 0.5 * (1.0 + tangent) + 0.5 * values * (1.0 - tangent * tangent) * root_coeff * (
        1.0 + 3.0 * cubic_coeff * values * values
    )
    return (active, slope)


def contract_last(left, right):
    return lax.dot_general(
        left, right, (((1,), (1,)), ((), ())), preferred_element_type=jnp.float32
    )


def contract_first(left, right):
    return lax.dot_general(
        left, right, (((0,), (0,)), ((), ())), preferred_element_type=jnp.float32
    )


def shifted(value, axis, by):
    length = lax.axis_size(axis)
    return lax.ppermute(value, axis, [(k, (k + by) % length) for k in range(length)])


def swapped(value):
    return lax.ppermute(value, "core", SWAP)


def block_at(blocks, index):
    return lax.dynamic_index_in_dim(blocks, index, 0, keepdims=False)


def gathered(own):
    return jnp.concatenate([own] + [shifted(own, "yhi", 4 - u) for u in (1, 2, 3)], axis=0)


def wide(value):
    return value.astype(jnp.float32)


def depth_parts(blocks):
    here = lax.axis_index("depth")
    pick = lambda by: block_at(blocks, (here + by) % 8)
    even = here % 2 == 0
    near_up = shifted(jnp.stack([pick(1), pick(3)]), "depth", 1)
    near_down = shifted(jnp.stack([pick(7), pick(5)]), "depth", 7)
    turns = [(k, (k + 2) % 8 if k % 2 == 0 else (k - 2) % 8) for k in range(8)]
    far = wide(lax.ppermute(pick(4), "depth", turns))
    up = wide(pick(2)) + wide(near_up[1]) + jnp.where(even, far, 0.0)
    down = wide(pick(6)) + wide(near_down[1]) + jnp.where(even, 0.0, far)
    last_up = shifted(up.astype(jnp.bfloat16), "depth", 2)
    last_down = shifted(down.astype(jnp.bfloat16), "depth", 6)
    near = wide(pick(0)) + wide(near_up[0]) + wide(near_down[0])
    return near, last_up, last_down


def total(parts):
    near, last_up, last_down = parts
    return near + wide(last_up) + wide(last_down)


def step(inputs, pre_act, grad_out, weight_up, weight_down):
    core = lax.axis_index("core")
    high = lax.axis_index("yhi")
    active, slope = gelu_parts(wide(pre_act[0]))
    active, slope = lax.optimization_barrier((active.astype(jnp.bfloat16), slope))
    active_mine = gathered(active)

    both = spread(jnp.concatenate([grad_out[0], inputs[0]], axis=1), COL)
    width = inputs.shape[2]
    both = both.reshape(4, 2, *both.shape[1:])
    of = lambda c: lax.dynamic_index_in_dim(both, c, 1, keepdims=False)
    mine, other = of(core), of(1 - core)
    flat = lambda blocks: blocks.reshape(-1, blocks.shape[-1])
    away = contract_last(flat(other[..., :width]), weight_down).astype(jnp.bfloat16)
    back = swapped(away)
    kept = contract_last(flat(mine[..., :width]), weight_down)
    pair = (kept + wide(back)).astype(jnp.bfloat16).reshape(4, 64, -1)
    came = exchanged(pair, "yhi")

    active_other = swapped(active_mine)
    turned = lambda blocks: jnp.concatenate([block_at(blocks, (high + u) % 4) for u in range(4)], axis=0)
    lower_mine = lax.optimization_barrier(contract_first(active_mine, turned(mine[..., :width])))
    lower = contract_first(active_other, turned(other[..., :width])) + lower_mine
    lower = lower.astype(jnp.bfloat16)
    lower_parts = depth_parts(lower.reshape(8, -1, lower.shape[1]))

    delta_own = (summed(came) * slope).astype(jnp.bfloat16)
    delta_mine = flat(spread(delta_own, "yhi"))
    delta_other = swapped(delta_mine)

    upper_mine = lax.optimization_barrier(contract_first(delta_mine, flat(mine[..., width:])))
    upper = contract_first(delta_other, flat(other[..., width:])) + upper_mine
    upper = upper.astype(jnp.bfloat16)
    near, last_up, last_down = depth_parts(upper.reshape(8, -1, upper.shape[1]))

    parts_mine = contract_last(delta_mine, weight_up).astype(jnp.bfloat16)
    parts_other = contract_last(delta_other, weight_up).astype(jnp.bfloat16)
    first = jnp.where(core == 0, parts_mine, parts_other).reshape(4, 64, -1)
    second = jnp.where(core == 0, parts_other, parts_mine).reshape(4, 64, -1)
    parts = jnp.stack([first, second], axis=1).reshape(8, 64, -1)
    parts = exchanged(parts, COL)
    grad_inputs = summed(parts).astype(jnp.bfloat16)[None]
    grad_down = total(lower_parts)
    grad_inputs, grad_down, last_up = lax.optimization_barrier((grad_inputs, grad_down, last_up))
    grad_up = total((near, last_up, last_down))
    return (grad_inputs, grad_up.T, grad_down)


def solution(mesh):
    fine = Mesh(mesh.devices.reshape(4, 2, 2, 4, 8), ("yhi", "core", "ylo", "x", "depth"))
    placed = (
        P("depth", COL, ROW),
        P("depth", ROW, COL),
        P("depth", COL, ROW),
        P(ROW, COL),
        P(COL, ROW),
    )
    return jax.shard_map(
        step,
        mesh=fine,
        in_specs=placed,
        out_specs=(
            P("depth", COL, ROW),
            P(ROW, (*COL, "depth")),
            P((*COL, "depth"), ROW),
        ),
        check_vma=False,
    )
```

time: 230 us -> 173 us (0.75)
  the two profiles are of different devices: /device:TPU:24 before, /device:TPU:2 now
where the time goes in v4:
time: 173 us; the launch traced here: 171 us
  starting transfers between devices  92.6 us (54%)
  waiting for transfers between devices  36.3 us (21%)
  other arithmetic  17.1 us (10%)
  matrix products  15.7 us (9%)
  local copies, waits for them, and re-layouts  8.45 us (5%)
    ppermute x11, starting transfers between devices, shifted(): lax.ppermute(value, axis, [(k, (k + by) % length) for k in range(length)])  54.1 us
    all_to_all x2, starting transfers between devices, spread(): return lax.all_to_all(copies, axis, split_axis=0, concat_axis=0, tiled=True)  15.4 us
    all_to_all x2, waiting for transfers between devices, exchanged(): return lax.all_to_all(value, axis, split_axis=0, concat_axis=0, tiled=True)  13.8 us
    all_to_all x2, waiting for transfers between devices, spread(): return lax.all_to_all(copies, axis, split_axis=0, concat_axis=0, tiled=True)  12.9 us
    all_to_all x2, starting transfers between devices, exchanged(): return lax.all_to_all(value, axis, split_axis=0, concat_axis=0, tiled=True)  9.39 us
    dot_general x4, matrix products, contract_first(): lax.dot_general(left, right, (((0,), (0,)), ((), ())), preferred_element_...  9.04 us
    ppermute x2, starting transfers between devices, depth_parts(): far = wide(lax.ppermute(pick(4), 'depth', turns))  7.99 us
    dot_general x4, matrix products, contract_last(): lax.dot_general(left, right, (((1,), (1,)), ((), ())), preferred_element_...  6.71 us
  transfers between devices with their start and end apart: 20, of which 5 were waited for; matrix products, arithmetic and copies ran while one was open for 20% of the time, Pallas kernels for 0%

profile of v4, /device:TPU:2, one launch (start us, length us, event | category | flops | bytes accessed | tf_op | source)
XLA Modules:
  0.0 171.3 jit_solution(2623822889460283734)
XLA Ops:
  2.9 9.4 %all-to-all-start = ((bf16[8,64,1280]{2,1,0:T(8,128)(2,1)}), bf16[8,64,1280]{2,1,0:T(8,128)(2,1)S(1)}, u32[]{:S(2)}, u32[]{:S(2)}) async-start(bf16[8,64,1280]{2,1,0:T(8,128)(2,1)} %broadcast_in_dim.17), calls=%async_computation | async-start | bytes 2621440 | tf_op jit(solution)/shard_map/all_to_all | solution.py:17
  12.2 12.9 %all-to-all-done = bf16[8,64,1280]{2,1,0:T(8,128)(2,1)S(1)} async-done(((bf16[8,64,1280]{2,1,0:T(8,128)(2,1)}), bf16[8,64,1280]{2,1,0:T(8,128)(2,1)S(1)}, u32[]{:S(2)}, u32[]{:S(2)}) %all-to-all-start) | async-done | bytes 1310752 | tf_op jit(solution)/shard_map/all_to_all | solution.py:17
  28.4 1.9 %collective-permute-start = (bf16[256,1280]{1,0:T(8,128)(2,1)}, bf16[256,1280]{1,0:T(8,128)(2,1)}, u32[]{:S(2)}, u32[]{:S(2)}) collective-permute-start(bf16[256,1280]{1,0:T(8,128)(2,1)} %convolution_convert_fusion), channel_id=1, source_target_pairs={{0,64},{64,0},{1,65},{65,1},{2,66},{66,2},{3,67},{67,3},{4,68},{68... | collective-permute-start | bytes 1966088 | tf_op jit(solution)/shard_map/ppermute | solution.py:56
  30.6 5.3 %collective-permute-start.2 = (bf16[64,1280]{1,0:T(8,128)(2,1)S(1)}, bf16[64,1280]{1,0:T(8,128)(2,1)}, u32[]{:S(2)}, u32[]{:S(2)}) collective-permute-start(bf16[64,1280]{1,0:T(8,128)(2,1)S(1)} %get-tuple-element.9), channel_id=1, source_target_pairs={{0,384},{128,0},{256,128},{384,256},{1,385},{129,1},{257,129},{385... | collective-permute-start | bytes 491528 | tf_op jit(solution)/shard_map/ppermute | solution.py:52
  35.9 4.7 %collective-permute-start.3 = (bf16[64,1280]{1,0:T(8,128)(2,1)S(1)}, bf16[64,1280]{1,0:T(8,128)(2,1)}, u32[]{:S(2)}, u32[]{:S(2)}) collective-permute-start(bf16[64,1280]{1,0:T(8,128)(2,1)S(1)} %get-tuple-element.9), channel_id=1, source_target_pairs={{0,256},{128,384},{256,0},{384,128},{1,257},{129,385},{257,1},{385... | collective-permute-start | bytes 491528 | tf_op jit(solution)/shard_map/ppermute | solution.py:52
  40.6 3.6 %collective-permute-start.4 = (bf16[64,1280]{1,0:T(8,128)(2,1)S(1)}, bf16[64,1280]{1,0:T(8,128)(2,1)}, u32[]{:S(2)}, u32[]{:S(2)}) collective-permute-start(bf16[64,1280]{1,0:T(8,128)(2,1)S(1)} %get-tuple-element.9), channel_id=1, source_target_pairs={{0,128},{128,256},{256,384},{384,0},{1,129},{129,257},{257,385},{3... | collective-permute-start | bytes 491528 | tf_op jit(solution)/shard_map/ppermute | solution.py:52
  44.4 2.6 %add_convert_fusion = bf16[256,1280]{1,0:T(8,128)(2,1)} fusion(bf16[256,1280]{1,0:T(8,128)(2,1)} %collective-permute-done, bf16[256,640]{1,0:T(8,128)(2,1)S(1)} %bitcast.89, bf16[1280,640]{1,0:T(8,128)(2,1)S(1)} %copy-done), kind=kOutput, calls=%fused_computation.7 | convolution fusion | flops 420413440 | bytes 3276800 | tf_op jit(solution)/shard_map/dot_general | solution.py:39
  47.0 4.2 %all-to-all-start.1 = ((bf16[4,64,1280]{2,1,0:T(8,128)(2,1)}), bf16[4,64,1280]{2,1,0:T(8,128)(2,1)}, u32[]{:S(2)}, u32[]{:S(2)}) async-start(bf16[4,64,1280]{2,1,0:T(8,128)(2,1)} %bitcast.7), calls=%async_computation.1 | async-start | bytes 1310720 | tf_op jit(solution)/shard_map/all_to_all | solution.py:21
  54.4 1.9 %collective-permute-start.5 = (bf16[256,1280]{1,0:T(8,128)(2,1)S(1)}, bf16[256,1280]{1,0:T(8,128)(2,1)}, u32[]{:S(2)}, u32[]{:S(2)}) collective-permute-start(bf16[256,1280]{1,0:T(8,128)(2,1)S(1)} %constant_dynamic-update-slice_fusion), channel_id=1, source_target_pairs={{0,64},{64,0},{1,65},{65,1},{2,66},{66,2},{3,67},{67,3},{4,68},{68... | collective-permute-start | bytes 1966088 | tf_op jit(solution)/shard_map/ppermute | solution.py:56
  57.0 13.8 %all-to-all-done.1 = bf16[4,64,1280]{2,1,0:T(8,128)(2,1)} async-done(((bf16[4,64,1280]{2,1,0:T(8,128)(2,1)}), bf16[4,64,1280]{2,1,0:T(8,128)(2,1)}, u32[]{:S(2)}, u32[]{:S(2)}) %all-to-all-start.1) | async-done | bytes 655392 | tf_op jit(solution)/shard_map/all_to_all | solution.py:21
  73.0 6.0 %all-to-all-start.2 = ((bf16[4,64,1280]{2,1,0:T(8,128)(2,1)}), bf16[4,64,1280]{2,1,0:T(8,128)(2,1)}, u32[]{:S(2)}, u32[]{:S(2)}) async-start(bf16[4,64,1280]{2,1,0:T(8,128)(2,1)} %broadcast_in_dim.18), calls=%async_computation.2 | async-start | bytes 1310720 | tf_op jit(solution)/shard_map/all_to_all | solution.py:17
  79.8 1.8 %fusion = bf16[1280,640]{1,0:T(8,128)(2,1)S(1)} fusion(f32[1280,640]{1,0:T(8,128)S(1)} %fusion.30, bf16[256,1280]{1,0:T(8,128)(2,1)} %collective-permute-done.5, bf16[64,640]{1,0:T(8,128)(2,1)S(1)} %get-tuple-element.34, bf16[64,640]{1,0:T(8,128)(2,1)S(1)} %get-tuple-element.35, bf16[64,640]{1,0:T(8,128)(2,1)S(1)} %get-tuple-element.36, ...), kind=kOutput, calls=%fused_computation.3 | convolution fusion | flops 422379520 | bytes 5898240 | tf_op jit(solution)/shard_map/dot_general | solution.py:45
  82.5 6.1 %collective-permute-start.8 = (bf16[160,640]{1,0:T(8,128)(2,1)}, bf16[160,640]{1,0:T(8,128)(2,1)}, u32[]{:S(2)}, u32[]{:S(2)}) collective-permute-start(bf16[160,640]{1,0:T(8,128)(2,1)} %get-tuple-element.23), channel_id=1, source_target_pairs={{0,2},{1,7},{2,4},{3,1},{4,6},{5,3},{6,0},{7,5},{8,10},{9,15},{10,... | collective-permute-start | bytes 614408 | tf_op jit(solution)/shard_map/ppermute | solution.py:78
  89.3 8.2 %collective-permute-start.6 = (bf16[2,160,640]{2,1,0:T(8,128)(2,1)}, bf16[2,160,640]{2,1,0:T(8,128)(2,1)}, u32[]{:S(2)}, u32[]{:S(2)}) collective-permute-start(bf16[2,160,640]{2,1,0:T(8,128)(2,1)} %pad_maximum_fusion.1), channel_id=1, source_target_pairs={{0,1},{1,2},{2,3},{3,4},{4,5},{5,6},{6,7},{7,0},{8,9},{9,10},{10,1... | collective-permute-start | bytes 1228808 | tf_op jit(solution)/shard_map/ppermute | solution.py:52
  97.6 1.9 %collective-permute-start.1 = (bf16[256,1280]{1,0:T(8,128)(2,1)}, bf16[256,1280]{1,0:T(8,128)(2,1)S(1)}, u32[]{:S(2)}, u32[]{:S(2)}) collective-permute-start(bf16[256,1280]{1,0:T(8,128)(2,1)} %bitcast.10), channel_id=1, source_target_pairs={{0,64},{64,0},{1,65},{65,1},{2,66},{66,2},{3,67},{67,3},{4,68},{68... | collective-permute-start | bytes 1966088 | tf_op jit(solution)/shard_map/ppermute | solution.py:56
  101.2 10.6 %collective-permute-start.7 = (bf16[2,160,640]{2,1,0:T(8,128)(2,1)}, bf16[2,160,640]{2,1,0:T(8,128)(2,1)}, u32[]{:S(2)}, u32[]{:S(2)}) collective-permute-start(bf16[2,160,640]{2,1,0:T(8,128)(2,1)} %pad_maximum_fusion.2), channel_id=1, source_target_pairs={{0,7},{1,0},{2,1},{3,2},{4,3},{5,4},{6,5},{7,6},{8,15},{9,8},{10,9... | collective-permute-start | bytes 1228808 | tf_op jit(solution)/shard_map/ppermute | solution.py:52
  111.8 3.6 %convolution_bitcast_fusion = f32[1280,640]{1,0:T(8,128)} fusion(bf16[4,64,1280]{2,1,0:T(8,128)(2,1)} %all-to-all-done.2, bf16[4,64,1280]{2,1,0:T(8,128)(2,1)} %get-tuple-element.28), kind=kOutput, calls=%fused_computation.2 | convolution fusion | flops 419430400 | bytes 4259840 | tf_op jit(solution)/shard_map/dot_general | solution.py:45
  119.0 5.2 %all-to-all-start.3 = ((bf16[8,64,640]{2,1,0:T(8,128)(2,1)}), bf16[8,64,640]{2,1,0:T(8,128)(2,1)}, u32[]{:S(2)}, u32[]{:S(2)}) async-start(bf16[8,64,640]{2,1,0:T(8,128)(2,1)} %bitcast.90), calls=%async_computation.3 | async-start | bytes 1310720 | tf_op jit(solution)/shard_map/all_to_all | solution.py:21
  124.2 2.9 %fusion.1 = bf16[1280,640]{1,0:T(8,128)(2,1)S(1)} fusion(f32[1280,640]{1,0:T(8,128)} %convolution_bitcast_fusion, bf16[256,1280]{1,0:T(8,128)(2,1)} %copy-done.3, bf16[256,640]{1,0:T(8,128)(2,1)} %bitcast.91), kind=kOutput, calls=%fused_computation.4 | convolution fusion | flops 421068800 | bytes 5898240 | tf_op jit(solution)/shard_map/dot_general | solution.py:45
  128.3 2.5 %collective-permute-start.14 = (bf16[2,160,640]{2,1,0:T(8,128)(2,1)}, bf16[2,160,640]{2,1,0:T(8,128)(2,1)}, u32[]{:S(2)}, u32[]{:S(2)}) collective-permute-start(bf16[2,160,640]{2,1,0:T(8,128)(2,1)} %pad_maximum_fusion.4), channel_id=1, source_target_pairs={{0,7},{1,0},{2,1},{3,2},{4,3},{5,4},{6,5},{7,6},{8,15},{9,8},{10,9... | collective-permute-start | bytes 1228808 | tf_op jit(solution)/shard_map/ppermute | solution.py:52
  131.6 3.4 %collective-permute-start.11 = (bf16[2,160,640]{2,1,0:T(8,128)(2,1)}, bf16[2,160,640]{2,1,0:T(8,128)(2,1)}, u32[]{:S(2)}, u32[]{:S(2)}) collective-permute-start(bf16[2,160,640]{2,1,0:T(8,128)(2,1)} %pad_maximum_fusion.3), channel_id=1, source_target_pairs={{0,1},{1,2},{2,3},{3,4},{4,5},{5,6},{6,7},{7,0},{8,9},{9,10},{10,1... | collective-permute-start | bytes 1228808 | tf_op jit(solution)/shard_map/ppermute | solution.py:52
  135.0 1.9 %collective-permute-start.12 = (bf16[160,640]{1,0:T(8,128)(2,1)S(1)}, bf16[160,640]{1,0:T(8,128)(2,1)S(1)}, u32[]{:S(2)}, u32[]{:S(2)}) collective-permute-start(bf16[160,640]{1,0:T(8,128)(2,1)S(1)} %get-tuple-element.19), channel_id=1, source_target_pairs={{0,2},{1,7},{2,4},{3,1},{4,6},{5,3},{6,0},{7,5},{8,10},{9,15},{10,... | collective-permute-start | bytes 614408 | tf_op jit(solution)/shard_map/ppermute | solution.py:78
  138.2 6.0 %collective-permute-start.10 = (bf16[160,640]{1,0:T(8,128)(2,1)S(1)}, bf16[160,640]{1,0:T(8,128)(2,1)S(1)}, u32[]{:S(2)}, u32[]{:S(2)}) collective-permute-start(bf16[160,640]{1,0:T(8,128)(2,1)S(1)} %get-tuple-element.16), channel_id=1, source_target_pairs={{0,6},{1,7},{2,0},{3,1},{4,2},{5,3},{6,4},{7,5},{8,14},{9,15},{10,... | collective-permute-start | bytes 614408 | tf_op jit(solution)/shard_map/ppermute | solution.py:52
  144.3 1.9 %collective-permute-start.9 = (bf16[160,640]{1,0:T(8,128)(2,1)S(1)}, bf16[160,640]{1,0:T(8,128)(2,1)S(1)}, u32[]{:S(2)}, u32[]{:S(2)}) collective-permute-start(bf16[160,640]{1,0:T(8,128)(2,1)S(1)} %get-tuple-element.15), channel_id=1, source_target_pairs={{0,2},{1,3},{2,4},{3,5},{4,6},{5,7},{6,0},{7,1},{8,10},{9,11},{10,... | collective-permute-start | bytes 614408 | tf_op jit(solution)/shard_map/ppermute | solution.py:52
  146.2 3.5 %collective-permute-done.12 = bf16[160,640]{1,0:T(8,128)(2,1)S(1)} collective-permute-done((bf16[160,640]{1,0:T(8,128)(2,1)S(1)}, bf16[160,640]{1,0:T(8,128)(2,1)S(1)}, u32[]{:S(2)}, u32[]{:S(2)}) %collective-permute-start.12) | collective-permute-done | bytes 204832 | tf_op jit(solution)/shard_map/ppermute | solution.py:78
  149.7 5.6 %collective-permute-done.11 = bf16[2,160,640]{2,1,0:T(8,128)(2,1)} collective-permute-done((bf16[2,160,640]{2,1,0:T(8,128)(2,1)}, bf16[2,160,640]{2,1,0:T(8,128)(2,1)}, u32[]{:S(2)}, u32[]{:S(2)}) %collective-permute-start.11) | collective-permute-done | bytes 409632 | tf_op jit(solution)/shard_map/ppermute | solution.py:52
  155.3 2.1 %fusion.9 = (bf16[160,640]{1,0:T(8,128)(2,1)S(1)}, bf16[160,640]{1,0:T(8,128)(2,1)}) fusion(bf16[160,640]{1,0:T(8,128)(2,1)S(1)} %collective-permute-done.12, bf16[2,160,640]{2,1,0:T(8,128)(2,1)} %collective-permute-done.14, bf16[8,160,640]{2,1,0:T(8,128)(2,1)} %bitcast.85, s32[]{:T(128)S(6)} %select_n.203, pred[]{:T(512)S(6)} %eq.36, ...), kind=kLoop, calls=%fused_computation.31 | loop fusion | flops 1331200 | bytes 1433609 | tf_op jit(solution)/shard_map/convert_element_type | solution.py:82
  157.4 1.9 %collective-permute-start.13 = (bf16[160,640]{1,0:T(8,128)(2,1)}, bf16[160,640]{1,0:T(8,128)(2,1)}, u32[]{:S(2)}, u32[]{:S(2)}) collective-permute-start(bf16[160,640]{1,0:T(8,128)(2,1)} %get-tuple-element.14), channel_id=1, source_target_pairs={{0,2},{1,3},{2,4},{3,5},{4,6},{5,7},{6,0},{7,1},{8,10},{9,11},{10,... | collective-permute-start | bytes 614408 | tf_op jit(solution)/shard_map/ppermute | solution.py:52
  159.3 6.0 %collective-permute-start.15 = (bf16[160,640]{1,0:T(8,128)(2,1)S(1)}, bf16[160,640]{1,0:T(8,128)(2,1)}, u32[]{:S(2)}, u32[]{:S(2)}) collective-permute-start(bf16[160,640]{1,0:T(8,128)(2,1)S(1)} %get-tuple-element.13), channel_id=1, source_target_pairs={{0,6},{1,7},{2,0},{3,1},{4,2},{5,3},{6,4},{7,5},{8,14},{9,15},{10,... | collective-permute-start | bytes 614408 | tf_op jit(solution)/shard_map/ppermute | solution.py:52
  165.4 1.9 %fusion.12 = f32[160,640]{1,0:T(8,128)} fusion(bf16[160,640]{1,0:T(8,128)(2,1)S(1)} %collective-permute-done.10, bf16[160,640]{1,0:T(8,128)(2,1)S(1)} %collective-permute-done.9, bf16[2,160,640]{2,1,0:T(8,128)(2,1)} %collective-permute-done.7, bf16[2,160,640]{2,1,0:T(8,128)(2,1)} %collective-permute-done.6, bf16[8,160,640]{2,1,0:T(8,128)(2,1)S(1)} %bitcast.83, ...), kind=kLoop, calls=%fused_computation.40 | loop fusion | flops 921600 | bytes 1433604 | tf_op jit(solution)/shard_map/add | solution.py:89
  167.3 1.8 %reduce_sum.22 = bf16[64,640]{1,0:T(8,128)(2,1)} reduce(bf16[8,64,640]{2,1,0:T(8,128)(2,1)} %all-to-all-done.3, bf16[]{:T(256)} %constant.187.clone.1), dimensions={0}, to_apply=%region_1.2 | reduce | flops 286720 | bytes 737282 | tf_op jit(solution)/shard_map/reduce_sum | solution.py:25
  169.1 2.2 %fusion.11 = f32[640,160]{0,1:T(8,128)} fusion(bf16[160,640]{1,0:T(8,128)(2,1)} %collective-permute-done.15, bf16[160,640]{1,0:T(8,128)(2,1)} %collective-permute-done.13, bf16[2,160,640]{2,1,0:T(8,128)(2,1)} %collective-permute-done.14, bf16[2,160,640]{2,1,0:T(8,128)(2,1)} %collective-permute-done.11, bf16[8,160,640]{2,1,0:T(8,128)(2,1)} %bitcast.86, ...), kind=kLoop, calls=%fused_computation.38 | loop fusion | flops 921600 | bytes 1433604 | tf_op jit(solution)/shard_map/transpose | solution.py:137
  (57 shorter events, 22.8 us)
Async XLA Ops:
  0.6 26.2 %copy-start = (bf16[1280,640]{1,0:T(8,128)(2,1)S(1)}, bf16[1280,640]{1,0:T(8,128)(2,1)}, u32[]{:S(2)}) copy-start(bf16[1280,640]{1,0:T(8,128)(2,1)} %param.9) | copy-start | bytes 4915204
  2.9 22.3 %all-to-all-start = ((bf16[8,64,1280]{2,1,0:T(8,128)(2,1)}), bf16[8,64,1280]{2,1,0:T(8,128)(2,1)S(1)}, u32[]{:S(2)}, u32[]{:S(2)}) async-start(bf16[8,64,1280]{2,1,0:T(8,128)(2,1)} %broadcast_in_dim.17), calls=%async_computation | async-start | bytes 2621440 | tf_op jit(solution)/shard_map/all_to_all | solution.py:17
  26.9 3.5 %copy-start.5 = (bf16[1,64,1280]{2,1,0:T(8,128)(2,1)S(1)}, bf16[1,64,1280]{2,1,0:T(8,128)(2,1)}, u32[]{:S(2)}) copy-start(bf16[1,64,1280]{2,1,0:T(8,128)(2,1)} %param.6) | copy-start | bytes 491524
  26.9 17.4 %copy-start.2 = (bf16[4,64,1280]{2,1,0:T(8,128)(2,1)S(1)}, bf16[4,64,1280]{2,1,0:T(8,128)(2,1)}, u32[]{:S(2)}) copy-start(bf16[4,64,1280]{2,1,0:T(8,128)(2,1)} %get-tuple-element.28) | copy-start | bytes 1966084
  28.4 15.9 %collective-permute-start = (bf16[256,1280]{1,0:T(8,128)(2,1)}, bf16[256,1280]{1,0:T(8,128)(2,1)}, u32[]{:S(2)}, u32[]{:S(2)}) collective-permute-start(bf16[256,1280]{1,0:T(8,128)(2,1)} %convolution_convert_fusion), channel_id=1, source_target_pairs={{0,64},{64,0},{1,65},{65,1},{2,66},{66,2},{3,67},{67,3},{4,68},{68... | collective-permute-start | bytes 1966088 | tf_op jit(solution)/shard_map/ppermute | solution.py:56
  30.6 20.6 %collective-permute-start.2 = (bf16[64,1280]{1,0:T(8,128)(2,1)S(1)}, bf16[64,1280]{1,0:T(8,128)(2,1)}, u32[]{:S(2)}, u32[]{:S(2)}) collective-permute-start(bf16[64,1280]{1,0:T(8,128)(2,1)S(1)} %get-tuple-element.9), channel_id=1, source_target_pairs={{0,384},{128,0},{256,128},{384,256},{1,385},{129,1},{257,129},{385... | collective-permute-start | bytes 491528 | tf_op jit(solution)/shard_map/ppermute | solution.py:52
  35.9 16.7 %collective-permute-start.3 = (bf16[64,1280]{1,0:T(8,128)(2,1)S(1)}, bf16[64,1280]{1,0:T(8,128)(2,1)}, u32[]{:S(2)}, u32[]{:S(2)}) collective-permute-start(bf16[64,1280]{1,0:T(8,128)(2,1)S(1)} %get-tuple-element.9), channel_id=1, source_target_pairs={{0,256},{128,384},{256,0},{384,128},{1,257},{129,385},{257,1},{385... | collective-permute-start | bytes 491528 | tf_op jit(solution)/shard_map/ppermute | solution.py:52
  40.6 12.9 %collective-permute-start.4 = (bf16[64,1280]{1,0:T(8,128)(2,1)S(1)}, bf16[64,1280]{1,0:T(8,128)(2,1)}, u32[]{:S(2)}, u32[]{:S(2)}) collective-permute-start(bf16[64,1280]{1,0:T(8,128)(2,1)S(1)} %get-tuple-element.9), channel_id=1, source_target_pairs={{0,128},{128,256},{256,384},{384,0},{1,129},{129,257},{257,385},{3... | collective-permute-start | bytes 491528 | tf_op jit(solution)/shard_map/ppermute | solution.py:52
  47.0 23.8 %all-to-all-start.1 = ((bf16[4,64,1280]{2,1,0:T(8,128)(2,1)}), bf16[4,64,1280]{2,1,0:T(8,128)(2,1)}, u32[]{:S(2)}, u32[]{:S(2)}) async-start(bf16[4,64,1280]{2,1,0:T(8,128)(2,1)} %bitcast.7), calls=%async_computation.1 | async-start | bytes 1310720 | tf_op jit(solution)/shard_map/all_to_all | solution.py:21
  54.4 25.3 %collective-permute-start.5 = (bf16[256,1280]{1,0:T(8,128)(2,1)S(1)}, bf16[256,1280]{1,0:T(8,128)(2,1)}, u32[]{:S(2)}, u32[]{:S(2)}) collective-permute-start(bf16[256,1280]{1,0:T(8,128)(2,1)S(1)} %constant_dynamic-update-slice_fusion), channel_id=1, source_target_pairs={{0,64},{64,0},{1,65},{65,1},{2,66},{66,2},{3,67},{67,3},{4,68},{68... | collective-permute-start | bytes 1966088 | tf_op jit(solution)/shard_map/ppermute | solution.py:56
  72.1 6.9 %copy-start.4 = (bf16[64,640]{1,0:T(8,128)(2,1)S(1)}, bf16[64,640]{1,0:T(8,128)(2,1)}, u32[]{:S(2)}) copy-start(bf16[64,640]{1,0:T(8,128)(2,1)} %get-tuple-element.40) | copy-start | bytes 245764
  73.0 24.6 %all-to-all-start.2 = ((bf16[4,64,1280]{2,1,0:T(8,128)(2,1)}), bf16[4,64,1280]{2,1,0:T(8,128)(2,1)}, u32[]{:S(2)}, u32[]{:S(2)}) async-start(bf16[4,64,1280]{2,1,0:T(8,128)(2,1)} %broadcast_in_dim.18), calls=%async_computation.2 | async-start | bytes 1310720 | tf_op jit(solution)/shard_map/all_to_all | solution.py:17
  82.5 52.5 %collective-permute-start.8 = (bf16[160,640]{1,0:T(8,128)(2,1)}, bf16[160,640]{1,0:T(8,128)(2,1)}, u32[]{:S(2)}, u32[]{:S(2)}) collective-permute-start(bf16[160,640]{1,0:T(8,128)(2,1)} %get-tuple-element.23), channel_id=1, source_target_pairs={{0,2},{1,7},{2,4},{3,1},{4,6},{5,3},{6,0},{7,5},{8,10},{9,15},{10,... | collective-permute-start | bytes 614408 | tf_op jit(solution)/shard_map/ppermute | solution.py:78
  89.3 47.6 %collective-permute-start.6 = (bf16[2,160,640]{2,1,0:T(8,128)(2,1)}, bf16[2,160,640]{2,1,0:T(8,128)(2,1)}, u32[]{:S(2)}, u32[]{:S(2)}) collective-permute-start(bf16[2,160,640]{2,1,0:T(8,128)(2,1)} %pad_maximum_fusion.1), channel_id=1, source_target_pairs={{0,1},{1,2},{2,3},{3,4},{4,5},{5,6},{6,7},{7,0},{8,9},{9,10},{10,1... | collective-permute-start | bytes 1228808 | tf_op jit(solution)/shard_map/ppermute | solution.py:52
  97.6 19.6 %collective-permute-start.1 = (bf16[256,1280]{1,0:T(8,128)(2,1)}, bf16[256,1280]{1,0:T(8,128)(2,1)S(1)}, u32[]{:S(2)}, u32[]{:S(2)}) collective-permute-start(bf16[256,1280]{1,0:T(8,128)(2,1)} %bitcast.10), channel_id=1, source_target_pairs={{0,64},{64,0},{1,65},{65,1},{2,66},{66,2},{3,67},{67,3},{4,68},{68... | collective-permute-start | bytes 1966088 | tf_op jit(solution)/shard_map/ppermute | solution.py:56
  101.2 14.2 %copy-start.6 = (bf16[640,1280]{1,0:T(8,128)(2,1)S(1)}, bf16[640,1280]{1,0:T(8,128)(2,1)}, u32[]{:S(2)}) copy-start(bf16[640,1280]{1,0:T(8,128)(2,1)} %param.8) | copy-start | bytes 4915204
  101.2 35.7 %collective-permute-start.7 = (bf16[2,160,640]{2,1,0:T(8,128)(2,1)}, bf16[2,160,640]{2,1,0:T(8,128)(2,1)}, u32[]{:S(2)}, u32[]{:S(2)}) collective-permute-start(bf16[2,160,640]{2,1,0:T(8,128)(2,1)} %pad_maximum_fusion.2), channel_id=1, source_target_pairs={{0,7},{1,0},{2,1},{3,2},{4,3},{5,4},{6,5},{7,6},{8,15},{9,8},{10,9... | collective-permute-start | bytes 1228808 | tf_op jit(solution)/shard_map/ppermute | solution.py:52
  117.2 0.9 copy-start.3
  119.0 48.3 %all-to-all-start.3 = ((bf16[8,64,640]{2,1,0:T(8,128)(2,1)}), bf16[8,64,640]{2,1,0:T(8,128)(2,1)}, u32[]{:S(2)}, u32[]{:S(2)}) async-start(bf16[8,64,640]{2,1,0:T(8,128)(2,1)} %bitcast.90), calls=%async_computation.3 | async-start | bytes 1310720 | tf_op jit(solution)/shard_map/all_to_all | solution.py:21
  127.2 4.4 %copy-start.1 = (bf16[1280,640]{1,0:T(8,128)(2,1)}, bf16[1280,640]{1,0:T(8,128)(2,1)S(1)}, u32[]{:S(2)}) copy-start(bf16[1280,640]{1,0:T(8,128)(2,1)S(1)} %fusion.1) | copy-start | bytes 4915204
  128.3 21.4 %collective-permute-start.14 = (bf16[2,160,640]{2,1,0:T(8,128)(2,1)}, bf16[2,160,640]{2,1,0:T(8,128)(2,1)}, u32[]{:S(2)}, u32[]{:S(2)}) collective-permute-start(bf16[2,160,640]{2,1,0:T(8,128)(2,1)} %pad_maximum_fusion.4), channel_id=1, source_target_pairs={{0,7},{1,0},{2,1},{3,2},{4,3},{5,4},{6,5},{7,6},{8,15},{9,8},{10,9... | collective-permute-start | bytes 1228808 | tf_op jit(solution)/shard_map/ppermute | solution.py:52
  131.6 23.8 %collective-permute-start.11 = (bf16[2,160,640]{2,1,0:T(8,128)(2,1)}, bf16[2,160,640]{2,1,0:T(8,128)(2,1)}, u32[]{:S(2)}, u32[]{:S(2)}) collective-permute-start(bf16[2,160,640]{2,1,0:T(8,128)(2,1)} %pad_maximum_fusion.3), channel_id=1, source_target_pairs={{0,1},{1,2},{2,3},{3,4},{4,5},{5,6},{6,7},{7,0},{8,9},{9,10},{10,1... | collective-permute-start | bytes 1228808 | tf_op jit(solution)/shard_map/ppermute | solution.py:52
  135.0 14.7 %collective-permute-start.12 = (bf16[160,640]{1,0:T(8,128)(2,1)S(1)}, bf16[160,640]{1,0:T(8,128)(2,1)S(1)}, u32[]{:S(2)}, u32[]{:S(2)}) collective-permute-start(bf16[160,640]{1,0:T(8,128)(2,1)S(1)} %get-tuple-element.19), channel_id=1, source_target_pairs={{0,2},{1,7},{2,4},{3,1},{4,6},{5,3},{6,0},{7,5},{8,10},{9,15},{10,... | collective-permute-start | bytes 614408 | tf_op jit(solution)/shard_map/ppermute | solution.py:78
  138.2 27.1 %collective-permute-start.10 = (bf16[160,640]{1,0:T(8,128)(2,1)S(1)}, bf16[160,640]{1,0:T(8,128)(2,1)S(1)}, u32[]{:S(2)}, u32[]{:S(2)}) collective-permute-start(bf16[160,640]{1,0:T(8,128)(2,1)S(1)} %get-tuple-element.16), channel_id=1, source_target_pairs={{0,6},{1,7},{2,0},{3,1},{4,2},{5,3},{6,4},{7,5},{8,14},{9,15},{10,... | collective-permute-start | bytes 614408 | tf_op jit(solution)/shard_map/ppermute | solution.py:52
  144.3 21.1 %collective-permute-start.9 = (bf16[160,640]{1,0:T(8,128)(2,1)S(1)}, bf16[160,640]{1,0:T(8,128)(2,1)S(1)}, u32[]{:S(2)}, u32[]{:S(2)}) collective-permute-start(bf16[160,640]{1,0:T(8,128)(2,1)S(1)} %get-tuple-element.15), channel_id=1, source_target_pairs={{0,2},{1,3},{2,4},{3,5},{4,6},{5,7},{6,0},{7,1},{8,10},{9,11},{10,... | collective-permute-start | bytes 614408 | tf_op jit(solution)/shard_map/ppermute | solution.py:52
  157.4 11.7 %collective-permute-start.13 = (bf16[160,640]{1,0:T(8,128)(2,1)}, bf16[160,640]{1,0:T(8,128)(2,1)}, u32[]{:S(2)}, u32[]{:S(2)}) collective-permute-start(bf16[160,640]{1,0:T(8,128)(2,1)} %get-tuple-element.14), channel_id=1, source_target_pairs={{0,2},{1,3},{2,4},{3,5},{4,6},{5,7},{6,0},{7,1},{8,10},{9,11},{10,... | collective-permute-start | bytes 614408 | tf_op jit(solution)/shard_map/ppermute | solution.py:52
  159.3 9.8 %collective-permute-start.15 = (bf16[160,640]{1,0:T(8,128)(2,1)S(1)}, bf16[160,640]{1,0:T(8,128)(2,1)}, u32[]{:S(2)}, u32[]{:S(2)}) collective-permute-start(bf16[160,640]{1,0:T(8,128)(2,1)S(1)} %get-tuple-element.13), channel_id=1, source_target_pairs={{0,6},{1,7},{2,0},{3,1},{4,2},{5,3},{6,4},{7,5},{8,14},{9,15},{10,... | collective-permute-start | bytes 614408 | tf_op jit(solution)/shard_map/ppermute | solution.py:52

commit v5 on v4

--- a/solution.py
+++ b/solution.py
@@ -75,10 +75,11 @@
     near_up = shifted(jnp.stack([pick(1), pick(3)]), "depth", 1)
     near_down = shifted(jnp.stack([pick(7), pick(5)]), "depth", 7)
     turns = [(k, (k + 2) % 8 if k % 2 == 0 else (k - 2) % 8) for k in range(8)]
-    far = wide(lax.ppermute(pick(4), "depth", turns))
-    up = wide(pick(2)) + wide(near_up[1]) + jnp.where(even, far, 0.0)
-    down = wide(pick(6)) + wide(near_down[1]) + jnp.where(even, 0.0, far)
-    last_up = shifted(up.astype(jnp.bfloat16), "depth", 2)
+    far = lax.ppermute(pick(4), "depth", turns)
+    up = wide(pick(2)) + wide(near_up[1]) + jnp.where(even, wide(far), 0.0)
+    up, far = lax.optimization_barrier((up.astype(jnp.bfloat16), far))
+    down = wide(pick(6)) + wide(near_down[1]) + jnp.where(even, 0.0, wide(far))
+    last_up = shifted(up, "depth", 2)
     last_down = shifted(down.astype(jnp.bfloat16), "depth", 6)
     near = wide(pick(0)) + wide(near_up[0]) + wide(near_down[0])
     return near, last_up, last_down
@@ -115,7 +116,7 @@
     lower = lower.astype(jnp.bfloat16)
     lower_parts = depth_parts(lower.reshape(8, -1, lower.shape[1]))
 
-    delta_own = (summed(came) * slope).astype(jnp.bfloat16)
+    delta_own = (sum(wide(came[k]) for k in range(4)) * slope).astype(jnp.bfloat16)
     delta_mine = flat(spread(delta_own, "yhi"))
     delta_other = swapped(delta_mine)
 
@@ -123,6 +124,7 @@
     upper = contract_first(delta_other, flat(other[..., width:])) + upper_mine
     upper = upper.astype(jnp.bfloat16)
     near, last_up, last_down = depth_parts(upper.reshape(8, -1, upper.shape[1]))
+    near = lax.optimization_barrier(near)
 
     parts_mine = contract_last(delta_mine, weight_up).astype(jnp.bfloat16)
     parts_other = contract_last(delta_other, weight_up).astype(jnp.bfloat16)

time: 173 us -> 176 us (1.017)
  the two profiles are of different devices: /device:TPU:2 before, /device:TPU:104 now
where the time goes in v5:
time: 176 us; the launch traced here: 174 us
  starting transfers between devices  89.8 us (51%)
  waiting for transfers between devices  40.1 us (23%)
  other arithmetic  19.3 us (11%)
  matrix products  14.7 us (8%)
  local copies, waits for them, and re-layouts  9.27 us (5%)
    ppermute x11, starting transfers between devices, shifted(): lax.ppermute(value, axis, [(k, (k + by) % length) for k in range(length)])  36 us
    all_to_all x2, starting transfers between devices, exchanged(): return lax.all_to_all(value, axis, split_axis=0, concat_axis=0, tiled=True)  19.3 us
    all_to_all x2, waiting for transfers between devices, spread(): return lax.all_to_all(copies, axis, split_axis=0, concat_axis=0, tiled=True)  17.1 us
    all_to_all x2, starting transfers between devices, spread(): return lax.all_to_all(copies, axis, split_axis=0, concat_axis=0, tiled=True)  15.1 us
    ppermute x2, starting transfers between devices, depth_parts(): far = lax.ppermute(pick(4), 'depth', turns)  13.6 us
    ppermute x11, waiting for transfers between devices, shifted(): lax.ppermute(value, axis, [(k, (k + by) % length) for k in range(length)])  11.1 us
    ppermute x2, waiting for transfers between devices, depth_parts(): far = lax.ppermute(pick(4), 'depth', turns)  9.34 us
    dot_general x4, matrix products, contract_first(): lax.dot_general(left, right, (((0,), (0,)), ((), ())), preferred_element_...  7.87 us
  transfers between devices with their start and end apart: 20, of which 7 were waited for; matrix products, arithmetic and copies ran while one was open for 21% of the time, Pallas kernels for 0%

profile of v5, /device:TPU:104, one launch (start us, length us, event | category | flops | bytes accessed | tf_op | source)
XLA Modules:
  0.0 174.4 jit_solution(14433534904899117133)
XLA Ops:
  2.9 5.8 %all-to-all-start = ((bf16[8,64,1280]{2,1,0:T(8,128)(2,1)}), bf16[8,64,1280]{2,1,0:T(8,128)(2,1)S(1)}, u32[]{:S(2)}, u32[]{:S(2)}) async-start(bf16[8,64,1280]{2,1,0:T(8,128)(2,1)} %broadcast_in_dim.17), calls=%async_computation | async-start | bytes 2621440 | tf_op jit(solution)/shard_map/all_to_all | solution.py:17
  8.6 17.1 %all-to-all-done = bf16[8,64,1280]{2,1,0:T(8,128)(2,1)S(1)} async-done(((bf16[8,64,1280]{2,1,0:T(8,128)(2,1)}), bf16[8,64,1280]{2,1,0:T(8,128)(2,1)S(1)}, u32[]{:S(2)}, u32[]{:S(2)}) %all-to-all-start) | async-done | bytes 1310752 | tf_op jit(solution)/shard_map/all_to_all | solution.py:17
  29.0 1.9 %collective-permute-start = (bf16[256,1280]{1,0:T(8,128)(2,1)}, bf16[256,1280]{1,0:T(8,128)(2,1)}, u32[]{:S(2)}, u32[]{:S(2)}) collective-permute-start(bf16[256,1280]{1,0:T(8,128)(2,1)} %convolution_convert_fusion), channel_id=1, source_target_pairs={{0,64},{64,0},{1,65},{65,1},{2,66},{66,2},{3,67},{67,3},{4,68},{68... | collective-permute-start | bytes 1966088 | tf_op jit(solution)/shard_map/ppermute | solution.py:56
  31.2 3.1 %collective-permute-start.2 = (bf16[64,1280]{1,0:T(8,128)(2,1)S(1)}, bf16[64,1280]{1,0:T(8,128)(2,1)S(1)}, u32[]{:S(2)}, u32[]{:S(2)}) collective-permute-start(bf16[64,1280]{1,0:T(8,128)(2,1)S(1)} %get-tuple-element.13), channel_id=1, source_target_pairs={{0,384},{128,0},{256,128},{384,256},{1,385},{129,1},{257,129},{385... | collective-permute-start | bytes 491528 | tf_op jit(solution)/shard_map/ppermute | solution.py:52
  34.3 5.0 %collective-permute-start.3 = (bf16[64,1280]{1,0:T(8,128)(2,1)S(1)}, bf16[64,1280]{1,0:T(8,128)(2,1)}, u32[]{:S(2)}, u32[]{:S(2)}) collective-permute-start(bf16[64,1280]{1,0:T(8,128)(2,1)S(1)} %get-tuple-element.13), channel_id=1, source_target_pairs={{0,256},{128,384},{256,0},{384,128},{1,257},{129,385},{257,1},{385... | collective-permute-start | bytes 491528 | tf_op jit(solution)/shard_map/ppermute | solution.py:52
  39.4 1.9 %collective-permute-start.4 = (bf16[64,1280]{1,0:T(8,128)(2,1)S(1)}, bf16[64,1280]{1,0:T(8,128)(2,1)}, u32[]{:S(2)}, u32[]{:S(2)}) collective-permute-start(bf16[64,1280]{1,0:T(8,128)(2,1)S(1)} %get-tuple-element.13), channel_id=1, source_target_pairs={{0,128},{128,256},{256,384},{384,0},{1,129},{129,257},{257,385},{3... | collective-permute-start | bytes 491528 | tf_op jit(solution)/shard_map/ppermute | solution.py:52
  41.4 3.1 %collective-permute-done.2 = bf16[64,1280]{1,0:T(8,128)(2,1)S(1)} collective-permute-done((bf16[64,1280]{1,0:T(8,128)(2,1)S(1)}, bf16[64,1280]{1,0:T(8,128)(2,1)S(1)}, u32[]{:S(2)}, u32[]{:S(2)}) %collective-permute-start.2) | collective-permute-done | bytes 163872 | tf_op jit(solution)/shard_map/ppermute | solution.py:52
  45.6 2.6 %add_convert_fusion = bf16[256,1280]{1,0:T(8,128)(2,1)} fusion(bf16[256,1280]{1,0:T(8,128)(2,1)} %collective-permute-done, bf16[256,640]{1,0:T(8,128)(2,1)S(1)} %bitcast.99, bf16[1280,640]{1,0:T(8,128)(2,1)S(1)} %copy-done), kind=kOutput, calls=%fused_computation.6 | convolution fusion | flops 420413440 | bytes 3276800 | tf_op jit(solution)/shard_map/dot_general | solution.py:39
  48.2 8.9 %all-to-all-start.1 = ((bf16[4,64,1280]{2,1,0:T(8,128)(2,1)}), bf16[4,64,1280]{2,1,0:T(8,128)(2,1)}, u32[]{:S(2)}, u32[]{:S(2)}) async-start(bf16[4,64,1280]{2,1,0:T(8,128)(2,1)} %bitcast.101), calls=%async_computation.1 | async-start | bytes 1310720 | tf_op jit(solution)/shard_map/all_to_all | solution.py:21
  59.1 1.9 %collective-permute-start.5 = (bf16[256,1280]{1,0:T(8,128)(2,1)S(1)}, bf16[256,1280]{1,0:T(8,128)(2,1)}, u32[]{:S(2)}, u32[]{:S(2)}) collective-permute-start(bf16[256,1280]{1,0:T(8,128)(2,1)S(1)} %constant_dynamic-update-slice_fusion), channel_id=1, source_target_pairs={{0,64},{64,0},{1,65},{65,1},{2,66},{66,2},{3,67},{67,3},{4,68},{68... | collective-permute-start | bytes 1966088 | tf_op jit(solution)/shard_map/ppermute | solution.py:56
  61.0 2.4 %fusion.24 = f32[1280,640]{1,0:T(8,128)} fusion(bf16[256,1280]{1,0:T(8,128)(2,1)S(1)} %constant_dynamic-update-slice_fusion, bf16[64,640]{1,0:T(8,128)(2,1)S(1)} %get-tuple-element.42, bf16[64,640]{1,0:T(8,128)(2,1)S(1)} %get-tuple-element.43, bf16[64,640]{1,0:T(8,128)(2,1)S(1)} %get-tuple-element.44, bf16[64,640]{1,0:T(8,128)(2,1)S(1)} %get-tuple-element.41), kind=kOutput, calls=%fused_computation.52 | convolution fusion | flops 420741120 | bytes 4259840 | tf_op jit(solution)/shard_map/dot_general | solution.py:45
  64.1 2.6 %all-to-all-done.1 = bf16[4,64,1280]{2,1,0:T(8,128)(2,1)} async-done(((bf16[4,64,1280]{2,1,0:T(8,128)(2,1)}), bf16[4,64,1280]{2,1,0:T(8,128)(2,1)}, u32[]{:S(2)}, u32[]{:S(2)}) %all-to-all-start.1) | async-done | bytes 655392 | tf_op jit(solution)/shard_map/all_to_all | solution.py:21
  68.9 9.4 %all-to-all-start.2 = ((bf16[4,64,1280]{2,1,0:T(8,128)(2,1)}), bf16[4,64,1280]{2,1,0:T(8,128)(2,1)}, u32[]{:S(2)}, u32[]{:S(2)}) async-start(bf16[4,64,1280]{2,1,0:T(8,128)(2,1)} %broadcast_in_dim.18), calls=%async_computation.2 | async-start | bytes 1310720 | tf_op jit(solution)/shard_map/all_to_all | solution.py:17
  78.3 2.9 %fusion = bf16[1280,640]{1,0:T(8,128)(2,1)S(1)} fusion(f32[1280,640]{1,0:T(8,128)} %fusion.24, bf16[256,1280]{1,0:T(8,128)(2,1)} %collective-permute-done.5, bf16[64,640]{1,0:T(8,128)(2,1)S(1)} %get-tuple-element.38, bf16[64,640]{1,0:T(8,128)(2,1)S(1)} %get-tuple-element.39, bf16[64,640]{1,0:T(8,128)(2,1)} %get-tuple-element.40, ...), kind=kOutput, calls=%fused_computation.3 | convolution fusion | flops 422379520 | bytes 5898240 | tf_op jit(solution)/shard_map/dot_general | solution.py:45
  82.8 4.3 %collective-permute-start.6 = (bf16[2,160,640]{2,1,0:T(8,128)(2,1)}, bf16[2,160,640]{2,1,0:T(8,128)(2,1)}, u32[]{:S(2)}, u32[]{:S(2)}) collective-permute-start(bf16[2,160,640]{2,1,0:T(8,128)(2,1)} %pad_maximum_fusion.1), channel_id=1, source_target_pairs={{0,1},{1,2},{2,3},{3,4},{4,5},{5,6},{6,7},{7,0},{8,9},{9,10},{10,1... | collective-permute-start | bytes 1228808 | tf_op jit(solution)/shard_map/ppermute | solution.py:52
  87.0 7.7 %collective-permute-start.8 = (bf16[160,640]{1,0:T(8,128)(2,1)}, bf16[160,640]{1,0:T(8,128)(2,1)S(1)}, u32[]{:S(2)}, u32[]{:S(2)}) collective-permute-start(bf16[160,640]{1,0:T(8,128)(2,1)} %get-tuple-element.27), channel_id=1, source_target_pairs={{0,2},{1,7},{2,4},{3,1},{4,6},{5,3},{6,0},{7,5},{8,10},{9,15},{10,... | collective-permute-start | bytes 614408 | tf_op jit(solution)/shard_map/ppermute | solution.py:78
  95.5 1.9 %collective-permute-start.7 = (bf16[2,160,640]{2,1,0:T(8,128)(2,1)}, bf16[2,160,640]{2,1,0:T(8,128)(2,1)}, u32[]{:S(2)}, u32[]{:S(2)}) collective-permute-start(bf16[2,160,640]{2,1,0:T(8,128)(2,1)} %pad_maximum_fusion.2), channel_id=1, source_target_pairs={{0,7},{1,0},{2,1},{3,2},{4,3},{5,4},{6,5},{7,6},{8,15},{9,8},{10,9... | collective-permute-start | bytes 1228808 | tf_op jit(solution)/shard_map/ppermute | solution.py:52
  97.5 3.0 %collective-permute-done.8 = bf16[160,640]{1,0:T(8,128)(2,1)S(1)} collective-permute-done((bf16[160,640]{1,0:T(8,128)(2,1)}, bf16[160,640]{1,0:T(8,128)(2,1)S(1)}, u32[]{:S(2)}, u32[]{:S(2)}) %collective-permute-start.8) | collective-permute-done | bytes 204832 | tf_op jit(solution)/shard_map/ppermute | solution.py:78
  102.2 1.9 %collective-permute-start.1 = (bf16[256,1280]{1,0:T(8,128)(2,1)}, bf16[256,1280]{1,0:T(8,128)(2,1)S(1)}, u32[]{:S(2)}, u32[]{:S(2)}) collective-permute-start(bf16[256,1280]{1,0:T(8,128)(2,1)} %bitcast.11), channel_id=1, source_target_pairs={{0,64},{64,0},{1,65},{65,1},{2,66},{66,2},{3,67},{67,3},{4,68},{68... | collective-permute-start | bytes 1966088 | tf_op jit(solution)/shard_map/ppermute | solution.py:56
  104.1 2.3 %collective-permute-done.7 = bf16[2,160,640]{2,1,0:T(8,128)(2,1)} collective-permute-done((bf16[2,160,640]{2,1,0:T(8,128)(2,1)}, bf16[2,160,640]{2,1,0:T(8,128)(2,1)}, u32[]{:S(2)}, u32[]{:S(2)}) %collective-permute-start.7) | collective-permute-done | bytes 409632 | tf_op jit(solution)/shard_map/ppermute | solution.py:52
  108.1 5.0 %collective-permute-start.10 = (bf16[160,640]{1,0:T(8,128)(2,1)}, bf16[160,640]{1,0:T(8,128)(2,1)}, u32[]{:S(2)}, u32[]{:S(2)}) collective-permute-start(bf16[160,640]{1,0:T(8,128)(2,1)} %fusion.4), channel_id=1, source_target_pairs={{0,6},{1,7},{2,0},{3,1},{4,2},{5,3},{6,4},{7,5},{8,14},{9,15},{10,... | collective-permute-start | bytes 614408 | tf_op jit(solution)/shard_map/ppermute | solution.py:52
  113.1 1.9 %collective-permute-start.9 = (bf16[160,640]{1,0:T(8,128)(2,1)}, bf16[160,640]{1,0:T(8,128)(2,1)}, u32[]{:S(2)}, u32[]{:S(2)}) collective-permute-start(bf16[160,640]{1,0:T(8,128)(2,1)} %fusion.5), channel_id=1, source_target_pairs={{0,2},{1,3},{2,4},{3,5},{4,6},{5,7},{6,0},{7,1},{8,10},{9,11},{10,... | collective-permute-start | bytes 614408 | tf_op jit(solution)/shard_map/ppermute | solution.py:52
  115.0 1.9 %convolution_bitcast_fusion = f32[1280,640]{1,0:T(8,128)S(1)} fusion(bf16[4,64,1280]{2,1,0:T(8,128)(2,1)} %all-to-all-done.2, bf16[4,64,1280]{2,1,0:T(8,128)(2,1)} %get-tuple-element.32), kind=kOutput, calls=%fused_computation.2 | convolution fusion | flops 419430400 | bytes 4259840 | tf_op jit(solution)/shard_map/dot_general | solution.py:45
  122.2 10.4 %all-to-all-start.3 = ((bf16[8,64,640]{2,1,0:T(8,128)(2,1)}), bf16[8,64,640]{2,1,0:T(8,128)(2,1)}, u32[]{:S(2)}, u32[]{:S(2)}) async-start(bf16[8,64,640]{2,1,0:T(8,128)(2,1)} %bitcast.100), calls=%async_computation.3 | async-start | bytes 1310720 | tf_op jit(solution)/shard_map/all_to_all | solution.py:21
  134.4 2.6 %collective-permute-start.11 = (bf16[2,160,640]{2,1,0:T(8,128)(2,1)}, bf16[2,160,640]{2,1,0:T(8,128)(2,1)}, u32[]{:S(2)}, u32[]{:S(2)}) collective-permute-start(bf16[2,160,640]{2,1,0:T(8,128)(2,1)} %pad_maximum_fusion.3), channel_id=1, source_target_pairs={{0,1},{1,2},{2,3},{3,4},{4,5},{5,6},{6,7},{7,0},{8,9},{9,10},{10,1... | collective-permute-start | bytes 1228808 | tf_op jit(solution)/shard_map/ppermute | solution.py:52
  138.0 3.4 %collective-permute-start.14 = (bf16[2,160,640]{2,1,0:T(8,128)(2,1)S(1)}, bf16[2,160,640]{2,1,0:T(8,128)(2,1)S(1)}, u32[]{:S(2)}, u32[]{:S(2)}) collective-permute-start(bf16[2,160,640]{2,1,0:T(8,128)(2,1)S(1)} %pad_maximum_fusion.4), channel_id=1, source_target_pairs={{0,7},{1,0},{2,1},{3,2},{4,3},{5,4},{6,5},{7,6},{8,15},{9,8},{10,9... | collective-permute-start | bytes 1228808 | tf_op jit(solution)/shard_map/ppermute | solution.py:52
  141.4 5.9 %collective-permute-start.12 = (bf16[160,640]{1,0:T(8,128)(2,1)}, bf16[160,640]{1,0:T(8,128)(2,1)S(1)}, u32[]{:S(2)}, u32[]{:S(2)}) collective-permute-start(bf16[160,640]{1,0:T(8,128)(2,1)} %get-tuple-element.23), channel_id=1, source_target_pairs={{0,2},{1,7},{2,4},{3,1},{4,6},{5,3},{6,0},{7,5},{8,10},{9,15},{10,... | collective-permute-start | bytes 614408 | tf_op jit(solution)/shard_map/ppermute | solution.py:78
  147.3 2.1 %fusion.6 = f32[160,640]{1,0:T(8,128)} fusion(bf16[160,640]{1,0:T(8,128)(2,1)} %collective-permute-done.10, bf16[160,640]{1,0:T(8,128)(2,1)} %collective-permute-done.9, bf16[2,160,640]{2,1,0:T(8,128)(2,1)} %collective-permute-done.7, bf16[2,160,640]{2,1,0:T(8,128)(2,1)} %collective-permute-done.6, bf16[8,160,640]{2,1,0:T(8,128)(2,1)S(1)} %bitcast.92, ...), kind=kLoop, calls=%fused_computation.32 | loop fusion | flops 921600 | bytes 1433604 | tf_op jit(solution)/shard_map/add | solution.py:90
  149.4 6.4 %collective-permute-done.12 = bf16[160,640]{1,0:T(8,128)(2,1)S(1)} collective-permute-done((bf16[160,640]{1,0:T(8,128)(2,1)}, bf16[160,640]{1,0:T(8,128)(2,1)S(1)}, u32[]{:S(2)}, u32[]{:S(2)}) %collective-permute-start.12) | collective-permute-done | bytes 204832 | tf_op jit(solution)/shard_map/ppermute | solution.py:78
  158.0 5.0 %collective-permute-start.15 = (bf16[160,640]{1,0:T(8,128)(2,1)S(1)}, bf16[160,640]{1,0:T(8,128)(2,1)S(1)}, u32[]{:S(2)}, u32[]{:S(2)}) collective-permute-start(bf16[160,640]{1,0:T(8,128)(2,1)S(1)} %fusion.2), channel_id=1, source_target_pairs={{0,6},{1,7},{2,0},{3,1},{4,2},{5,3},{6,4},{7,5},{8,14},{9,15},{10,... | collective-permute-start | bytes 614408 | tf_op jit(solution)/shard_map/ppermute | solution.py:52
  163.0 1.9 %collective-permute-start.13 = (bf16[160,640]{1,0:T(8,128)(2,1)S(1)}, bf16[160,640]{1,0:T(8,128)(2,1)S(1)}, u32[]{:S(2)}, u32[]{:S(2)}) collective-permute-start(bf16[160,640]{1,0:T(8,128)(2,1)S(1)} %fusion.3), channel_id=1, source_target_pairs={{0,2},{1,3},{2,4},{3,5},{4,6},{5,7},{6,0},{7,1},{8,10},{9,11},{10,... | collective-permute-start | bytes 614408 | tf_op jit(solution)/shard_map/ppermute | solution.py:52
  167.9 5.6 %collective-permute-done.13 = bf16[160,640]{1,0:T(8,128)(2,1)S(1)} collective-permute-done((bf16[160,640]{1,0:T(8,128)(2,1)S(1)}, bf16[160,640]{1,0:T(8,128)(2,1)S(1)}, u32[]{:S(2)}, u32[]{:S(2)}) %collective-permute-start.13) | collective-permute-done | bytes 204832 | tf_op jit(solution)/shard_map/ppermute | solution.py:52
  (55 shorter events, 31.4 us)
Async XLA Ops:
  0.6 26.8 %copy-start = (bf16[1280,640]{1,0:T(8,128)(2,1)S(1)}, bf16[1280,640]{1,0:T(8,128)(2,1)}, u32[]{:S(2)}) copy-start(bf16[1280,640]{1,0:T(8,128)(2,1)} %param.9) | copy-start | bytes 4915204
  2.9 22.8 %all-to-all-start = ((bf16[8,64,1280]{2,1,0:T(8,128)(2,1)}), bf16[8,64,1280]{2,1,0:T(8,128)(2,1)S(1)}, u32[]{:S(2)}, u32[]{:S(2)}) async-start(bf16[8,64,1280]{2,1,0:T(8,128)(2,1)} %broadcast_in_dim.17), calls=%async_computation | async-start | bytes 2621440 | tf_op jit(solution)/shard_map/all_to_all | solution.py:17
  27.4 3.5 %copy-start.3 = (bf16[1,64,1280]{2,1,0:T(8,128)(2,1)S(1)}, bf16[1,64,1280]{2,1,0:T(8,128)(2,1)}, u32[]{:S(2)}) copy-start(bf16[1,64,1280]{2,1,0:T(8,128)(2,1)} %param.6) | copy-start | bytes 491524
  29.0 16.6 %collective-permute-start = (bf16[256,1280]{1,0:T(8,128)(2,1)}, bf16[256,1280]{1,0:T(8,128)(2,1)}, u32[]{:S(2)}, u32[]{:S(2)}) collective-permute-start(bf16[256,1280]{1,0:T(8,128)(2,1)} %convolution_convert_fusion), channel_id=1, source_target_pairs={{0,64},{64,0},{1,65},{65,1},{2,66},{66,2},{3,67},{67,3},{4,68},{68... | collective-permute-start | bytes 1966088 | tf_op jit(solution)/shard_map/ppermute | solution.py:56
  31.2 13.4 %collective-permute-start.2 = (bf16[64,1280]{1,0:T(8,128)(2,1)S(1)}, bf16[64,1280]{1,0:T(8,128)(2,1)S(1)}, u32[]{:S(2)}, u32[]{:S(2)}) collective-permute-start(bf16[64,1280]{1,0:T(8,128)(2,1)S(1)} %get-tuple-element.13), channel_id=1, source_target_pairs={{0,384},{128,0},{256,128},{384,256},{1,385},{129,1},{257,129},{385... | collective-permute-start | bytes 491528 | tf_op jit(solution)/shard_map/ppermute | solution.py:52
  34.3 22.9 %collective-permute-start.3 = (bf16[64,1280]{1,0:T(8,128)(2,1)S(1)}, bf16[64,1280]{1,0:T(8,128)(2,1)}, u32[]{:S(2)}, u32[]{:S(2)}) collective-permute-start(bf16[64,1280]{1,0:T(8,128)(2,1)S(1)} %get-tuple-element.13), channel_id=1, source_target_pairs={{0,256},{128,384},{256,0},{384,128},{1,257},{129,385},{257,1},{385... | collective-permute-start | bytes 491528 | tf_op jit(solution)/shard_map/ppermute | solution.py:52
  39.4 18.8 %collective-permute-start.4 = (bf16[64,1280]{1,0:T(8,128)(2,1)S(1)}, bf16[64,1280]{1,0:T(8,128)(2,1)}, u32[]{:S(2)}, u32[]{:S(2)}) collective-permute-start(bf16[64,1280]{1,0:T(8,128)(2,1)S(1)} %get-tuple-element.13), channel_id=1, source_target_pairs={{0,128},{128,256},{256,384},{384,0},{1,129},{129,257},{257,385},{3... | collective-permute-start | bytes 491528 | tf_op jit(solution)/shard_map/ppermute | solution.py:52
  48.2 18.5 %all-to-all-start.1 = ((bf16[4,64,1280]{2,1,0:T(8,128)(2,1)}), bf16[4,64,1280]{2,1,0:T(8,128)(2,1)}, u32[]{:S(2)}, u32[]{:S(2)}) async-start(bf16[4,64,1280]{2,1,0:T(8,128)(2,1)} %bitcast.101), calls=%async_computation.1 | async-start | bytes 1310720 | tf_op jit(solution)/shard_map/all_to_all | solution.py:21
  59.1 19.2 %collective-permute-start.5 = (bf16[256,1280]{1,0:T(8,128)(2,1)S(1)}, bf16[256,1280]{1,0:T(8,128)(2,1)}, u32[]{:S(2)}, u32[]{:S(2)}) collective-permute-start(bf16[256,1280]{1,0:T(8,128)(2,1)S(1)} %constant_dynamic-update-slice_fusion), channel_id=1, source_target_pairs={{0,64},{64,0},{1,65},{65,1},{2,66},{66,2},{3,67},{67,3},{4,68},{68... | collective-permute-start | bytes 1966088 | tf_op jit(solution)/shard_map/ppermute | solution.py:56
  68.9 33.3 %all-to-all-start.2 = ((bf16[4,64,1280]{2,1,0:T(8,128)(2,1)}), bf16[4,64,1280]{2,1,0:T(8,128)(2,1)}, u32[]{:S(2)}, u32[]{:S(2)}) async-start(bf16[4,64,1280]{2,1,0:T(8,128)(2,1)} %broadcast_in_dim.18), calls=%async_computation.2 | async-start | bytes 1310720 | tf_op jit(solution)/shard_map/all_to_all | solution.py:17
  82.8 17.7 %collective-permute-start.6 = (bf16[2,160,640]{2,1,0:T(8,128)(2,1)}, bf16[2,160,640]{2,1,0:T(8,128)(2,1)}, u32[]{:S(2)}, u32[]{:S(2)}) collective-permute-start(bf16[2,160,640]{2,1,0:T(8,128)(2,1)} %pad_maximum_fusion.1), channel_id=1, source_target_pairs={{0,1},{1,2},{2,3},{3,4},{4,5},{5,6},{6,7},{7,0},{8,9},{9,10},{10,1... | collective-permute-start | bytes 1228808 | tf_op jit(solution)/shard_map/ppermute | solution.py:52
  87.0 13.5 %collective-permute-start.8 = (bf16[160,640]{1,0:T(8,128)(2,1)}, bf16[160,640]{1,0:T(8,128)(2,1)S(1)}, u32[]{:S(2)}, u32[]{:S(2)}) collective-permute-start(bf16[160,640]{1,0:T(8,128)(2,1)} %get-tuple-element.27), channel_id=1, source_target_pairs={{0,2},{1,7},{2,4},{3,1},{4,6},{5,3},{6,0},{7,5},{8,10},{9,15},{10,... | collective-permute-start | bytes 614408 | tf_op jit(solution)/shard_map/ppermute | solution.py:78
  95.5 10.9 %collective-permute-start.7 = (bf16[2,160,640]{2,1,0:T(8,128)(2,1)}, bf16[2,160,640]{2,1,0:T(8,128)(2,1)}, u32[]{:S(2)}, u32[]{:S(2)}) collective-permute-start(bf16[2,160,640]{2,1,0:T(8,128)(2,1)} %pad_maximum_fusion.2), channel_id=1, source_target_pairs={{0,7},{1,0},{2,1},{3,2},{4,3},{5,4},{6,5},{7,6},{8,15},{9,8},{10,9... | collective-permute-start | bytes 1228808 | tf_op jit(solution)/shard_map/ppermute | solution.py:52
  102.2 16.6 %collective-permute-start.1 = (bf16[256,1280]{1,0:T(8,128)(2,1)}, bf16[256,1280]{1,0:T(8,128)(2,1)S(1)}, u32[]{:S(2)}, u32[]{:S(2)}) collective-permute-start(bf16[256,1280]{1,0:T(8,128)(2,1)} %bitcast.11), channel_id=1, source_target_pairs={{0,64},{64,0},{1,65},{65,1},{2,66},{66,2},{3,67},{67,3},{4,68},{68... | collective-permute-start | bytes 1966088 | tf_op jit(solution)/shard_map/ppermute | solution.py:56
  108.1 8.8 %copy-start.4 = (bf16[640,1280]{1,0:T(8,128)(2,1)S(1)}, bf16[640,1280]{1,0:T(8,128)(2,1)}, u32[]{:S(2)}) copy-start(bf16[640,1280]{1,0:T(8,128)(2,1)} %param.8) | copy-start | bytes 4915204
  108.1 39.2 %collective-permute-start.10 = (bf16[160,640]{1,0:T(8,128)(2,1)}, bf16[160,640]{1,0:T(8,128)(2,1)}, u32[]{:S(2)}, u32[]{:S(2)}) collective-permute-start(bf16[160,640]{1,0:T(8,128)(2,1)} %fusion.4), channel_id=1, source_target_pairs={{0,6},{1,7},{2,0},{3,1},{4,2},{5,3},{6,4},{7,5},{8,14},{9,15},{10,... | collective-permute-start | bytes 614408 | tf_op jit(solution)/shard_map/ppermute | solution.py:52
  113.1 34.2 %collective-permute-start.9 = (bf16[160,640]{1,0:T(8,128)(2,1)}, bf16[160,640]{1,0:T(8,128)(2,1)}, u32[]{:S(2)}, u32[]{:S(2)}) collective-permute-start(bf16[160,640]{1,0:T(8,128)(2,1)} %fusion.5), channel_id=1, source_target_pairs={{0,2},{1,3},{2,4},{3,5},{4,6},{5,7},{6,0},{7,1},{8,10},{9,11},{10,... | collective-permute-start | bytes 614408 | tf_op jit(solution)/shard_map/ppermute | solution.py:52
  116.9 1.9 %copy-start.2 = (bf16[4,64,640]{2,1,0:T(8,128)(2,1)S(1)}, bf16[4,64,640]{2,1,0:T(8,128)(2,1)}, u32[]{:S(2)}) copy-start(bf16[4,64,640]{2,1,0:T(8,128)(2,1)} %get-tuple-element.33) | copy-start | bytes 983044
  119.5 1.8 %copy-start.1 = (bf16[1280,640]{1,0:T(8,128)(2,1)}, bf16[1280,640]{1,0:T(8,128)(2,1)S(1)}, u32[]{:S(2)}) copy-start(bf16[1280,640]{1,0:T(8,128)(2,1)S(1)} %fusion.1) | copy-start | bytes 4915204
  122.2 43.8 %all-to-all-start.3 = ((bf16[8,64,640]{2,1,0:T(8,128)(2,1)}), bf16[8,64,640]{2,1,0:T(8,128)(2,1)}, u32[]{:S(2)}, u32[]{:S(2)}) async-start(bf16[8,64,640]{2,1,0:T(8,128)(2,1)} %bitcast.100), calls=%async_computation.3 | async-start | bytes 1310720 | tf_op jit(solution)/shard_map/all_to_all | solution.py:21
  134.4 21.4 %collective-permute-start.11 = (bf16[2,160,640]{2,1,0:T(8,128)(2,1)}, bf16[2,160,640]{2,1,0:T(8,128)(2,1)}, u32[]{:S(2)}, u32[]{:S(2)}) collective-permute-start(bf16[2,160,640]{2,1,0:T(8,128)(2,1)} %pad_maximum_fusion.3), channel_id=1, source_target_pairs={{0,1},{1,2},{2,3},{3,4},{4,5},{5,6},{6,7},{7,0},{8,9},{9,10},{10,1... | collective-permute-start | bytes 1228808 | tf_op jit(solution)/shard_map/ppermute | solution.py:52
  138.0 18.9 %collective-permute-start.14 = (bf16[2,160,640]{2,1,0:T(8,128)(2,1)S(1)}, bf16[2,160,640]{2,1,0:T(8,128)(2,1)S(1)}, u32[]{:S(2)}, u32[]{:S(2)}) collective-permute-start(bf16[2,160,640]{2,1,0:T(8,128)(2,1)S(1)} %pad_maximum_fusion.4), channel_id=1, source_target_pairs={{0,7},{1,0},{2,1},{3,2},{4,3},{5,4},{6,5},{7,6},{8,15},{9,8},{10,9... | collective-permute-start | bytes 1228808 | tf_op jit(solution)/shard_map/ppermute | solution.py:52
  141.4 14.4 %collective-permute-start.12 = (bf16[160,640]{1,0:T(8,128)(2,1)}, bf16[160,640]{1,0:T(8,128)(2,1)S(1)}, u32[]{:S(2)}, u32[]{:S(2)}) collective-permute-start(bf16[160,640]{1,0:T(8,128)(2,1)} %get-tuple-element.23), channel_id=1, source_target_pairs={{0,2},{1,7},{2,4},{3,1},{4,6},{5,3},{6,0},{7,5},{8,10},{9,15},{10,... | collective-permute-start | bytes 614408 | tf_op jit(solution)/shard_map/ppermute | solution.py:78
  158.0 15.6 %collective-permute-start.15 = (bf16[160,640]{1,0:T(8,128)(2,1)S(1)}, bf16[160,640]{1,0:T(8,128)(2,1)S(1)}, u32[]{:S(2)}, u32[]{:S(2)}) collective-permute-start(bf16[160,640]{1,0:T(8,128)(2,1)S(1)} %fusion.2), channel_id=1, source_target_pairs={{0,6},{1,7},{2,0},{3,1},{4,2},{5,3},{6,4},{7,5},{8,14},{9,15},{10,... | collective-permute-start | bytes 614408 | tf_op jit(solution)/shard_map/ppermute | solution.py:52
  163.0 10.5 %collective-permute-start.13 = (bf16[160,640]{1,0:T(8,128)(2,1)S(1)}, bf16[160,640]{1,0:T(8,128)(2,1)S(1)}, u32[]{:S(2)}, u32[]{:S(2)}) collective-permute-start(bf16[160,640]{1,0:T(8,128)(2,1)S(1)} %fusion.3), channel_id=1, source_target_pairs={{0,2},{1,3},{2,4},{3,5},{4,6},{5,7},{6,0},{7,1},{8,10},{9,11},{10,... | collective-permute-start | bytes 614408 | tf_op jit(solution)/shard_map/ppermute | solution.py:52

commit v6 on v5

--- a/solution.py
+++ b/solution.py
@@ -61,7 +61,11 @@
 
 
 def gathered(own):
-    return jnp.concatenate([own] + [shifted(own, "yhi", 4 - u) for u in (1, 2, 3)], axis=0)
+    pieces = [own] + [shifted(own, "yhi", 4 - u) for u in (1, 2, 3)]
+    n = own.shape[0]
+    least = jnp.array(-jnp.inf, own.dtype)
+    spaced = [lax.pad(v, least, ((k * n, (3 - k) * n, 0), (0, 0, 0))) for k, v in enumerate(pieces)]
+    return jnp.maximum(jnp.maximum(spaced[0], spaced[1]), jnp.maximum(spaced[2], spaced[3]))
 
 
 def wide(value):
@@ -77,9 +81,8 @@
     turns = [(k, (k + 2) % 8 if k % 2 == 0 else (k - 2) % 8) for k in range(8)]
     far = lax.ppermute(pick(4), "depth", turns)
     up = wide(pick(2)) + wide(near_up[1]) + jnp.where(even, wide(far), 0.0)
-    up, far = lax.optimization_barrier((up.astype(jnp.bfloat16), far))
     down = wide(pick(6)) + wide(near_down[1]) + jnp.where(even, 0.0, wide(far))
-    last_up = shifted(up, "depth", 2)
+    last_up = shifted(up.astype(jnp.bfloat16), "depth", 2)
     last_down = shifted(down.astype(jnp.bfloat16), "depth", 6)
     near = wide(pick(0)) + wide(near_up[0]) + wide(near_down[0])
     return near, last_up, last_down
@@ -124,7 +127,6 @@
     upper = contract_first(delta_other, flat(other[..., width:])) + upper_mine
     upper = upper.astype(jnp.bfloat16)
     near, last_up, last_down = depth_parts(upper.reshape(8, -1, upper.shape[1]))
-    near = lax.optimization_barrier(near)
 
     parts_mine = contract_last(delta_mine, weight_up).astype(jnp.bfloat16)
     parts_other = contract_last(delta_other, weight_up).astype(jnp.bfloat16)

time: 176 us -> 176 us (level)
  the two profiles are of different devices: /device:TPU:104 before, /device:TPU:8 now
where the time goes in v6:
time: 176 us; the launch traced here: 175 us
  starting transfers between devices  94.4 us (54%)
  waiting for transfers between devices  41.3 us (23%)
  other arithmetic  18.9 us (11%)
  matrix products  14.9 us (8%)
  local copies, waits for them, and re-layouts  4.27 us (2%)
    ppermute x11, starting transfers between devices, shifted(): lax.ppermute(value, axis, [(k, (k + by) % length) for k in range(length)])  56.8 us
    ppermute x11, waiting for transfers between devices, shifted(): lax.ppermute(value, axis, [(k, (k + by) % length) for k in range(length)])  21.9 us
    all_to_all x2, waiting for transfers between devices, spread(): return lax.all_to_all(copies, axis, split_axis=0, concat_axis=0, tiled=True)  14.1 us
    all_to_all x2, starting transfers between devices, spread(): return lax.all_to_all(copies, axis, split_axis=0, concat_axis=0, tiled=True)  13.5 us
    all_to_all x2, starting transfers between devices, exchanged(): return lax.all_to_all(value, axis, split_axis=0, concat_axis=0, tiled=True)  10.4 us
    dot_general x4, matrix products, contract_first(): lax.dot_general(left, right, (((0,), (0,)), ((), ())), preferred_element_...  10.1 us
    ppermute x2, starting transfers between devices, depth_parts(): far = lax.ppermute(pick(4), 'depth', turns)  7.99 us
    ppermute x3, starting transfers between devices, swapped(): return lax.ppermute(value, 'core', SWAP)  5.74 us
  transfers between devices with their start and end apart: 20, of which 6 were waited for; matrix products, arithmetic and copies ran while one was open for 17% of the time, Pallas kernels for 0%

profile of v6, /device:TPU:8, one launch (start us, length us, event | category | flops | bytes accessed | tf_op | source)
XLA Modules:
  0.0 174.9 jit_solution(2859328312358441246)
XLA Ops:
  2.9 9.3 %all-to-all-start = ((bf16[8,64,1280]{2,1,0:T(8,128)(2,1)}), bf16[8,64,1280]{2,1,0:T(8,128)(2,1)S(1)}, u32[]{:S(2)}, u32[]{:S(2)}) async-start(bf16[8,64,1280]{2,1,0:T(8,128)(2,1)} %broadcast_in_dim.17), calls=%async_computation | async-start | bytes 2621440 | tf_op jit(solution)/shard_map/all_to_all | solution.py:17
  12.2 13.5 %all-to-all-done = bf16[8,64,1280]{2,1,0:T(8,128)(2,1)S(1)} async-done(((bf16[8,64,1280]{2,1,0:T(8,128)(2,1)}), bf16[8,64,1280]{2,1,0:T(8,128)(2,1)S(1)}, u32[]{:S(2)}, u32[]{:S(2)}) %all-to-all-start) | async-done | bytes 1310752 | tf_op jit(solution)/shard_map/all_to_all | solution.py:17
  27.4 1.9 %collective-permute-start = (bf16[256,1280]{1,0:T(8,128)(2,1)S(1)}, bf16[256,1280]{1,0:T(8,128)(2,1)S(1)}, u32[]{:S(2)}, u32[]{:S(2)}) collective-permute-start(bf16[256,1280]{1,0:T(8,128)(2,1)S(1)} %convolution_convert_fusion), channel_id=1, source_target_pairs={{0,64},{64,0},{1,65},{65,1},{2,66},{66,2},{3,67},{67,3},{4,68},{68... | collective-permute-start | bytes 1966088 | tf_op jit(solution)/shard_map/ppermute | solution.py:56
  29.4 2.0 %collective-permute-done = bf16[256,1280]{1,0:T(8,128)(2,1)S(1)} collective-permute-done((bf16[256,1280]{1,0:T(8,128)(2,1)S(1)}, bf16[256,1280]{1,0:T(8,128)(2,1)S(1)}, u32[]{:S(2)}, u32[]{:S(2)}) %collective-permute-start) | collective-permute-done | bytes 655392 | tf_op jit(solution)/shard_map/ppermute | solution.py:56
  32.9 6.2 %all-to-all-start.1 = ((bf16[4,64,1280]{2,1,0:T(8,128)(2,1)}), bf16[4,64,1280]{2,1,0:T(8,128)(2,1)S(1)}, u32[]{:S(2)}, u32[]{:S(2)}) async-start(bf16[4,64,1280]{2,1,0:T(8,128)(2,1)} %bitcast.94), calls=%async_computation.1 | async-start | bytes 1310720 | tf_op jit(solution)/shard_map/all_to_all | solution.py:21
  40.3 4.8 %collective-permute-start.4 = (bf16[64,1280]{1,0:T(8,128)(2,1)S(1)}, bf16[64,1280]{1,0:T(8,128)(2,1)}, u32[]{:S(2)}, u32[]{:S(2)}) collective-permute-start(bf16[64,1280]{1,0:T(8,128)(2,1)S(1)} %get-tuple-element.9), channel_id=1, source_target_pairs={{0,128},{128,256},{256,384},{384,0},{1,129},{129,257},{257,385},{3... | collective-permute-start | bytes 491528 | tf_op jit(solution)/shard_map/ppermute | solution.py:52
  45.1 5.5 %collective-permute-start.3 = (bf16[64,1280]{1,0:T(8,128)(2,1)S(1)}, bf16[64,1280]{1,0:T(8,128)(2,1)}, u32[]{:S(2)}, u32[]{:S(2)}) collective-permute-start(bf16[64,1280]{1,0:T(8,128)(2,1)S(1)} %get-tuple-element.9), channel_id=1, source_target_pairs={{0,256},{128,384},{256,0},{384,128},{1,257},{129,385},{257,1},{385... | collective-permute-start | bytes 491528 | tf_op jit(solution)/shard_map/ppermute | solution.py:52
  50.6 5.5 %collective-permute-start.2 = (bf16[64,1280]{1,0:T(8,128)(2,1)S(1)}, bf16[64,1280]{1,0:T(8,128)(2,1)}, u32[]{:S(2)}, u32[]{:S(2)}) collective-permute-start(bf16[64,1280]{1,0:T(8,128)(2,1)S(1)} %get-tuple-element.9), channel_id=1, source_target_pairs={{0,384},{128,0},{256,128},{384,256},{1,385},{129,1},{257,129},{385... | collective-permute-start | bytes 491528 | tf_op jit(solution)/shard_map/ppermute | solution.py:52
  56.2 15.9 %collective-permute-done.4 = bf16[64,1280]{1,0:T(8,128)(2,1)} collective-permute-done((bf16[64,1280]{1,0:T(8,128)(2,1)S(1)}, bf16[64,1280]{1,0:T(8,128)(2,1)}, u32[]{:S(2)}, u32[]{:S(2)}) %collective-permute-start.4) | collective-permute-done | bytes 163872 | tf_op jit(solution)/shard_map/ppermute | solution.py:52
  72.1 2.0 %maximum_maximum_fusion = bf16[256,1280]{1,0:T(8,128)(2,1)} fusion(bf16[64,1280]{1,0:T(8,128)(2,1)} %collective-permute-done.4, bf16[64,1280]{1,0:T(8,128)(2,1)} %collective-permute-done.3, bf16[64,1280]{1,0:T(8,128)(2,1)} %collective-permute-done.2, bf16[64,1280]{1,0:T(8,128)(2,1)S(1)} %get-tuple-element.9), kind=kLoop, calls=%fused_computation.17 | loop fusion | flops 2621440 | bytes 1310720 | tf_op jit(solution)/shard_map/max | solution.py:68
  74.1 1.9 %collective-permute-start.5 = (bf16[256,1280]{1,0:T(8,128)(2,1)}, bf16[256,1280]{1,0:T(8,128)(2,1)}, u32[]{:S(2)}, u32[]{:S(2)}) collective-permute-start(bf16[256,1280]{1,0:T(8,128)(2,1)} %maximum_maximum_fusion), channel_id=1, source_target_pairs={{0,64},{64,0},{1,65},{65,1},{2,66},{66,2},{3,67},{67,3},{4,68},{68... | collective-permute-start | bytes 1966088 | tf_op jit(solution)/shard_map/ppermute | solution.py:56
  77.0 4.2 %all-to-all-start.2 = ((bf16[4,64,1280]{2,1,0:T(8,128)(2,1)}), bf16[4,64,1280]{2,1,0:T(8,128)(2,1)}, u32[]{:S(2)}, u32[]{:S(2)}) async-start(bf16[4,64,1280]{2,1,0:T(8,128)(2,1)} %broadcast_in_dim.18), calls=%async_computation.2 | async-start | bytes 1310720 | tf_op jit(solution)/shard_map/all_to_all | solution.py:17
  85.8 6.1 %collective-permute-start.8 = (bf16[160,640]{1,0:T(8,128)(2,1)}, bf16[160,640]{1,0:T(8,128)(2,1)}, u32[]{:S(2)}, u32[]{:S(2)}) collective-permute-start(bf16[160,640]{1,0:T(8,128)(2,1)} %get-tuple-element.23), channel_id=1, source_target_pairs={{0,2},{1,7},{2,4},{3,1},{4,6},{5,3},{6,0},{7,5},{8,10},{9,15},{10,... | collective-permute-start | bytes 614408 | tf_op jit(solution)/shard_map/ppermute | solution.py:82
  92.7 8.2 %collective-permute-start.6 = (bf16[2,160,640]{2,1,0:T(8,128)(2,1)}, bf16[2,160,640]{2,1,0:T(8,128)(2,1)}, u32[]{:S(2)}, u32[]{:S(2)}) collective-permute-start(bf16[2,160,640]{2,1,0:T(8,128)(2,1)} %pad_maximum_fusion.1), channel_id=1, source_target_pairs={{0,1},{1,2},{2,3},{3,4},{4,5},{5,6},{6,7},{7,0},{8,9},{9,10},{10,1... | collective-permute-start | bytes 1228808 | tf_op jit(solution)/shard_map/ppermute | solution.py:52
  101.4 1.9 %collective-permute-start.1 = (bf16[256,1280]{1,0:T(8,128)(2,1)}, bf16[256,1280]{1,0:T(8,128)(2,1)S(1)}, u32[]{:S(2)}, u32[]{:S(2)}) collective-permute-start(bf16[256,1280]{1,0:T(8,128)(2,1)} %bitcast.11), channel_id=1, source_target_pairs={{0,64},{64,0},{1,65},{65,1},{2,66},{66,2},{3,67},{67,3},{4,68},{68... | collective-permute-start | bytes 1966088 | tf_op jit(solution)/shard_map/ppermute | solution.py:56
  105.1 11.1 %collective-permute-start.7 = (bf16[2,160,640]{2,1,0:T(8,128)(2,1)}, bf16[2,160,640]{2,1,0:T(8,128)(2,1)}, u32[]{:S(2)}, u32[]{:S(2)}) collective-permute-start(bf16[2,160,640]{2,1,0:T(8,128)(2,1)} %pad_maximum_fusion.2), channel_id=1, source_target_pairs={{0,7},{1,0},{2,1},{3,2},{4,3},{5,4},{6,5},{7,6},{8,15},{9,8},{10,9... | collective-permute-start | bytes 1228808 | tf_op jit(solution)/shard_map/ppermute | solution.py:52
  116.2 3.6 %convolution_bitcast_fusion = f32[1280,640]{1,0:T(8,128)} fusion(bf16[4,64,1280]{2,1,0:T(8,128)(2,1)} %all-to-all-done.2, bf16[4,64,1280]{2,1,0:T(8,128)(2,1)} %copy-done.2), kind=kOutput, calls=%fused_computation.2 | convolution fusion | flops 419430400 | bytes 4259840 | tf_op jit(solution)/shard_map/dot_general | solution.py:45
  123.3 4.2 %all-to-all-start.3 = ((bf16[8,64,640]{2,1,0:T(8,128)(2,1)}), bf16[8,64,640]{2,1,0:T(8,128)(2,1)}, u32[]{:S(2)}, u32[]{:S(2)}) async-start(bf16[8,64,640]{2,1,0:T(8,128)(2,1)} %bitcast.93), calls=%async_computation.3 | async-start | bytes 1310720 | tf_op jit(solution)/shard_map/all_to_all | solution.py:21
  127.5 2.9 %fusion.1 = bf16[1280,640]{1,0:T(8,128)(2,1)S(1)} fusion(f32[1280,640]{1,0:T(8,128)} %convolution_bitcast_fusion, bf16[256,1280]{1,0:T(8,128)(2,1)} %copy-done.3, bf16[256,640]{1,0:T(8,128)(2,1)} %bitcast.95), kind=kOutput, calls=%fused_computation.4 | convolution fusion | flops 421068800 | bytes 5898240 | tf_op jit(solution)/shard_map/dot_general | solution.py:45
  131.6 2.5 %collective-permute-start.14 = (bf16[2,160,640]{2,1,0:T(8,128)(2,1)}, bf16[2,160,640]{2,1,0:T(8,128)(2,1)}, u32[]{:S(2)}, u32[]{:S(2)}) collective-permute-start(bf16[2,160,640]{2,1,0:T(8,128)(2,1)} %pad_maximum_fusion.4), channel_id=1, source_target_pairs={{0,7},{1,0},{2,1},{3,2},{4,3},{5,4},{6,5},{7,6},{8,15},{9,8},{10,9... | collective-permute-start | bytes 1228808 | tf_op jit(solution)/shard_map/ppermute | solution.py:52
  134.9 3.4 %collective-permute-start.11 = (bf16[2,160,640]{2,1,0:T(8,128)(2,1)}, bf16[2,160,640]{2,1,0:T(8,128)(2,1)}, u32[]{:S(2)}, u32[]{:S(2)}) collective-permute-start(bf16[2,160,640]{2,1,0:T(8,128)(2,1)} %pad_maximum_fusion.3), channel_id=1, source_target_pairs={{0,1},{1,2},{2,3},{3,4},{4,5},{5,6},{6,7},{7,0},{8,9},{9,10},{10,1... | collective-permute-start | bytes 1228808 | tf_op jit(solution)/shard_map/ppermute | solution.py:52
  138.3 1.9 %collective-permute-start.12 = (bf16[160,640]{1,0:T(8,128)(2,1)S(1)}, bf16[160,640]{1,0:T(8,128)(2,1)S(1)}, u32[]{:S(2)}, u32[]{:S(2)}) collective-permute-start(bf16[160,640]{1,0:T(8,128)(2,1)S(1)} %get-tuple-element.19), channel_id=1, source_target_pairs={{0,2},{1,7},{2,4},{3,1},{4,6},{5,3},{6,0},{7,5},{8,10},{9,15},{10,... | collective-permute-start | bytes 614408 | tf_op jit(solution)/shard_map/ppermute | solution.py:82
  141.6 6.0 %collective-permute-start.10 = (bf16[160,640]{1,0:T(8,128)(2,1)S(1)}, bf16[160,640]{1,0:T(8,128)(2,1)S(1)}, u32[]{:S(2)}, u32[]{:S(2)}) collective-permute-start(bf16[160,640]{1,0:T(8,128)(2,1)S(1)} %get-tuple-element.16), channel_id=1, source_target_pairs={{0,6},{1,7},{2,0},{3,1},{4,2},{5,3},{6,4},{7,5},{8,14},{9,15},{10,... | collective-permute-start | bytes 614408 | tf_op jit(solution)/shard_map/ppermute | solution.py:52
  147.6 1.9 %collective-permute-start.9 = (bf16[160,640]{1,0:T(8,128)(2,1)S(1)}, bf16[160,640]{1,0:T(8,128)(2,1)S(1)}, u32[]{:S(2)}, u32[]{:S(2)}) collective-permute-start(bf16[160,640]{1,0:T(8,128)(2,1)S(1)} %get-tuple-element.15), channel_id=1, source_target_pairs={{0,2},{1,3},{2,4},{3,5},{4,6},{5,7},{6,0},{7,1},{8,10},{9,11},{10,... | collective-permute-start | bytes 614408 | tf_op jit(solution)/shard_map/ppermute | solution.py:52
  149.5 3.3 %collective-permute-done.12 = bf16[160,640]{1,0:T(8,128)(2,1)S(1)} collective-permute-done((bf16[160,640]{1,0:T(8,128)(2,1)S(1)}, bf16[160,640]{1,0:T(8,128)(2,1)S(1)}, u32[]{:S(2)}, u32[]{:S(2)}) %collective-permute-start.12) | collective-permute-done | bytes 204832 | tf_op jit(solution)/shard_map/ppermute | solution.py:82
  152.8 6.0 %collective-permute-done.11 = bf16[2,160,640]{2,1,0:T(8,128)(2,1)} collective-permute-done((bf16[2,160,640]{2,1,0:T(8,128)(2,1)}, bf16[2,160,640]{2,1,0:T(8,128)(2,1)}, u32[]{:S(2)}, u32[]{:S(2)}) %collective-permute-start.11) | collective-permute-done | bytes 409632 | tf_op jit(solution)/shard_map/ppermute | solution.py:52
  158.9 2.1 %fusion.9 = (bf16[160,640]{1,0:T(8,128)(2,1)S(1)}, bf16[160,640]{1,0:T(8,128)(2,1)}) fusion(bf16[160,640]{1,0:T(8,128)(2,1)S(1)} %collective-permute-done.12, bf16[2,160,640]{2,1,0:T(8,128)(2,1)} %collective-permute-done.14, bf16[8,160,640]{2,1,0:T(8,128)(2,1)} %bitcast.88, s32[]{:T(128)S(6)} %select_n.203, pred[]{:T(512)S(6)} %eq.36, ...), kind=kLoop, calls=%fused_computation.31 | loop fusion | flops 1331200 | bytes 1433609 | tf_op jit(solution)/shard_map/convert_element_type | solution.py:86
  161.0 1.9 %collective-permute-start.13 = (bf16[160,640]{1,0:T(8,128)(2,1)}, bf16[160,640]{1,0:T(8,128)(2,1)}, u32[]{:S(2)}, u32[]{:S(2)}) collective-permute-start(bf16[160,640]{1,0:T(8,128)(2,1)} %get-tuple-element.14), channel_id=1, source_target_pairs={{0,2},{1,3},{2,4},{3,5},{4,6},{5,7},{6,0},{7,1},{8,10},{9,11},{10,... | collective-permute-start | bytes 614408 | tf_op jit(solution)/shard_map/ppermute | solution.py:52
  162.9 6.0 %collective-permute-start.15 = (bf16[160,640]{1,0:T(8,128)(2,1)S(1)}, bf16[160,640]{1,0:T(8,128)(2,1)}, u32[]{:S(2)}, u32[]{:S(2)}) collective-permute-start(bf16[160,640]{1,0:T(8,128)(2,1)S(1)} %get-tuple-element.13), channel_id=1, source_target_pairs={{0,6},{1,7},{2,0},{3,1},{4,2},{5,3},{6,4},{7,5},{8,14},{9,15},{10,... | collective-permute-start | bytes 614408 | tf_op jit(solution)/shard_map/ppermute | solution.py:52
  168.9 1.9 %fusion.12 = f32[160,640]{1,0:T(8,128)} fusion(bf16[160,640]{1,0:T(8,128)(2,1)S(1)} %collective-permute-done.10, bf16[160,640]{1,0:T(8,128)(2,1)S(1)} %collective-permute-done.9, bf16[2,160,640]{2,1,0:T(8,128)(2,1)} %collective-permute-done.7, bf16[2,160,640]{2,1,0:T(8,128)(2,1)} %collective-permute-done.6, bf16[8,160,640]{2,1,0:T(8,128)(2,1)S(1)} %bitcast.86, ...), kind=kLoop, calls=%fused_computation.40 | loop fusion | flops 921600 | bytes 1433604 | tf_op jit(solution)/shard_map/add | solution.py:93
  170.9 1.8 %reduce_sum.12 = bf16[64,640]{1,0:T(8,128)(2,1)} reduce(bf16[8,64,640]{2,1,0:T(8,128)(2,1)} %all-to-all-done.3, bf16[]{:T(256)} %constant.187.clone.1), dimensions={0}, to_apply=%region_0.1 | reduce | flops 286720 | bytes 737282 | tf_op jit(solution)/shard_map/reduce_sum | solution.py:25
  172.7 2.2 %fusion.11 = f32[640,160]{0,1:T(8,128)} fusion(bf16[160,640]{1,0:T(8,128)(2,1)} %collective-permute-done.15, bf16[160,640]{1,0:T(8,128)(2,1)} %collective-permute-done.13, bf16[2,160,640]{2,1,0:T(8,128)(2,1)} %collective-permute-done.14, bf16[2,160,640]{2,1,0:T(8,128)(2,1)} %collective-permute-done.11, bf16[8,160,640]{2,1,0:T(8,128)(2,1)} %bitcast.89, ...), kind=kLoop, calls=%fused_computation.38 | loop fusion | flops 921600 | bytes 1433604 | tf_op jit(solution)/shard_map/transpose | solution.py:141
  (49 shorter events, 22.1 us)
Async XLA Ops:
  0.6 26.0 %copy-start = (bf16[1280,640]{1,0:T(8,128)(2,1)S(1)}, bf16[1280,640]{1,0:T(8,128)(2,1)}, u32[]{:S(2)}) copy-start(bf16[1280,640]{1,0:T(8,128)(2,1)} %param.9) | copy-start | bytes 4915204
  2.9 22.8 %all-to-all-start = ((bf16[8,64,1280]{2,1,0:T(8,128)(2,1)}), bf16[8,64,1280]{2,1,0:T(8,128)(2,1)S(1)}, u32[]{:S(2)}, u32[]{:S(2)}) async-start(bf16[8,64,1280]{2,1,0:T(8,128)(2,1)} %broadcast_in_dim.17), calls=%async_computation | async-start | bytes 2621440 | tf_op jit(solution)/shard_map/all_to_all | solution.py:17
  25.8 3.5 %copy-start.2 = (bf16[4,64,1280]{2,1,0:T(8,128)(2,1)}, bf16[4,64,1280]{2,1,0:T(8,128)(2,1)S(1)}, u32[]{:S(2)}) copy-start(bf16[4,64,1280]{2,1,0:T(8,128)(2,1)S(1)} %get-tuple-element.28) | copy-start | bytes 1966084
  27.4 4.0 %collective-permute-start = (bf16[256,1280]{1,0:T(8,128)(2,1)S(1)}, bf16[256,1280]{1,0:T(8,128)(2,1)S(1)}, u32[]{:S(2)}, u32[]{:S(2)}) collective-permute-start(bf16[256,1280]{1,0:T(8,128)(2,1)S(1)} %convolution_convert_fusion), channel_id=1, source_target_pairs={{0,64},{64,0},{1,65},{65,1},{2,66},{66,2},{3,67},{67,3},{4,68},{68... | collective-permute-start | bytes 1966088 | tf_op jit(solution)/shard_map/ppermute | solution.py:56
  32.9 43.1 %all-to-all-start.1 = ((bf16[4,64,1280]{2,1,0:T(8,128)(2,1)}), bf16[4,64,1280]{2,1,0:T(8,128)(2,1)S(1)}, u32[]{:S(2)}, u32[]{:S(2)}) async-start(bf16[4,64,1280]{2,1,0:T(8,128)(2,1)} %bitcast.94), calls=%async_computation.1 | async-start | bytes 1310720 | tf_op jit(solution)/shard_map/all_to_all | solution.py:21
  40.3 31.8 %collective-permute-start.4 = (bf16[64,1280]{1,0:T(8,128)(2,1)S(1)}, bf16[64,1280]{1,0:T(8,128)(2,1)}, u32[]{:S(2)}, u32[]{:S(2)}) collective-permute-start(bf16[64,1280]{1,0:T(8,128)(2,1)S(1)} %get-tuple-element.9), channel_id=1, source_target_pairs={{0,128},{128,256},{256,384},{384,0},{1,129},{129,257},{257,385},{3... | collective-permute-start | bytes 491528 | tf_op jit(solution)/shard_map/ppermute | solution.py:52
  45.1 27.0 %collective-permute-start.3 = (bf16[64,1280]{1,0:T(8,128)(2,1)S(1)}, bf16[64,1280]{1,0:T(8,128)(2,1)}, u32[]{:S(2)}, u32[]{:S(2)}) collective-permute-start(bf16[64,1280]{1,0:T(8,128)(2,1)S(1)} %get-tuple-element.9), channel_id=1, source_target_pairs={{0,256},{128,384},{256,0},{384,128},{1,257},{129,385},{257,1},{385... | collective-permute-start | bytes 491528 | tf_op jit(solution)/shard_map/ppermute | solution.py:52
  50.6 21.5 %collective-permute-start.2 = (bf16[64,1280]{1,0:T(8,128)(2,1)S(1)}, bf16[64,1280]{1,0:T(8,128)(2,1)}, u32[]{:S(2)}, u32[]{:S(2)}) collective-permute-start(bf16[64,1280]{1,0:T(8,128)(2,1)S(1)} %get-tuple-element.9), channel_id=1, source_target_pairs={{0,384},{128,0},{256,128},{384,256},{1,385},{129,1},{257,129},{385... | collective-permute-start | bytes 491528 | tf_op jit(solution)/shard_map/ppermute | solution.py:52
  74.1 9.0 %collective-permute-start.5 = (bf16[256,1280]{1,0:T(8,128)(2,1)}, bf16[256,1280]{1,0:T(8,128)(2,1)}, u32[]{:S(2)}, u32[]{:S(2)}) collective-permute-start(bf16[256,1280]{1,0:T(8,128)(2,1)} %maximum_maximum_fusion), channel_id=1, source_target_pairs={{0,64},{64,0},{1,65},{65,1},{2,66},{66,2},{3,67},{67,3},{4,68},{68... | collective-permute-start | bytes 1966088 | tf_op jit(solution)/shard_map/ppermute | solution.py:56
  77.0 24.4 %all-to-all-start.2 = ((bf16[4,64,1280]{2,1,0:T(8,128)(2,1)}), bf16[4,64,1280]{2,1,0:T(8,128)(2,1)}, u32[]{:S(2)}, u32[]{:S(2)}) async-start(bf16[4,64,1280]{2,1,0:T(8,128)(2,1)} %broadcast_in_dim.18), calls=%async_computation.2 | async-start | bytes 1310720 | tf_op jit(solution)/shard_map/all_to_all | solution.py:17
  85.8 52.5 %collective-permute-start.8 = (bf16[160,640]{1,0:T(8,128)(2,1)}, bf16[160,640]{1,0:T(8,128)(2,1)}, u32[]{:S(2)}, u32[]{:S(2)}) collective-permute-start(bf16[160,640]{1,0:T(8,128)(2,1)} %get-tuple-element.23), channel_id=1, source_target_pairs={{0,2},{1,7},{2,4},{3,1},{4,6},{5,3},{6,0},{7,5},{8,10},{9,15},{10,... | collective-permute-start | bytes 614408 | tf_op jit(solution)/shard_map/ppermute | solution.py:82
  92.7 47.6 %collective-permute-start.6 = (bf16[2,160,640]{2,1,0:T(8,128)(2,1)}, bf16[2,160,640]{2,1,0:T(8,128)(2,1)}, u32[]{:S(2)}, u32[]{:S(2)}) collective-permute-start(bf16[2,160,640]{2,1,0:T(8,128)(2,1)} %pad_maximum_fusion.1), channel_id=1, source_target_pairs={{0,1},{1,2},{2,3},{3,4},{4,5},{5,6},{6,7},{7,0},{8,9},{9,10},{10,1... | collective-permute-start | bytes 1228808 | tf_op jit(solution)/shard_map/ppermute | solution.py:52
  101.4 20.1 %collective-permute-start.1 = (bf16[256,1280]{1,0:T(8,128)(2,1)}, bf16[256,1280]{1,0:T(8,128)(2,1)S(1)}, u32[]{:S(2)}, u32[]{:S(2)}) collective-permute-start(bf16[256,1280]{1,0:T(8,128)(2,1)} %bitcast.11), channel_id=1, source_target_pairs={{0,64},{64,0},{1,65},{65,1},{2,66},{66,2},{3,67},{67,3},{4,68},{68... | collective-permute-start | bytes 1966088 | tf_op jit(solution)/shard_map/ppermute | solution.py:56
  105.1 14.6 %copy-start.4 = (bf16[640,1280]{1,0:T(8,128)(2,1)S(1)}, bf16[640,1280]{1,0:T(8,128)(2,1)}, u32[]{:S(2)}) copy-start(bf16[640,1280]{1,0:T(8,128)(2,1)} %param.8) | copy-start | bytes 4915204
  105.1 35.2 %collective-permute-start.7 = (bf16[2,160,640]{2,1,0:T(8,128)(2,1)}, bf16[2,160,640]{2,1,0:T(8,128)(2,1)}, u32[]{:S(2)}, u32[]{:S(2)}) collective-permute-start(bf16[2,160,640]{2,1,0:T(8,128)(2,1)} %pad_maximum_fusion.2), channel_id=1, source_target_pairs={{0,7},{1,0},{2,1},{3,2},{4,3},{5,4},{6,5},{7,6},{8,15},{9,8},{10,9... | collective-permute-start | bytes 1228808 | tf_op jit(solution)/shard_map/ppermute | solution.py:52
  121.6 0.9 copy-start.3
  123.3 47.5 %all-to-all-start.3 = ((bf16[8,64,640]{2,1,0:T(8,128)(2,1)}), bf16[8,64,640]{2,1,0:T(8,128)(2,1)}, u32[]{:S(2)}, u32[]{:S(2)}) async-start(bf16[8,64,640]{2,1,0:T(8,128)(2,1)} %bitcast.93), calls=%async_computation.3 | async-start | bytes 1310720 | tf_op jit(solution)/shard_map/all_to_all | solution.py:21
  130.5 4.4 %copy-start.1 = (bf16[1280,640]{1,0:T(8,128)(2,1)}, bf16[1280,640]{1,0:T(8,128)(2,1)S(1)}, u32[]{:S(2)}) copy-start(bf16[1280,640]{1,0:T(8,128)(2,1)S(1)} %fusion.1) | copy-start | bytes 4915204
  131.6 21.2 %collective-permute-start.14 = (bf16[2,160,640]{2,1,0:T(8,128)(2,1)}, bf16[2,160,640]{2,1,0:T(8,128)(2,1)}, u32[]{:S(2)}, u32[]{:S(2)}) collective-permute-start(bf16[2,160,640]{2,1,0:T(8,128)(2,1)} %pad_maximum_fusion.4), channel_id=1, source_target_pairs={{0,7},{1,0},{2,1},{3,2},{4,3},{5,4},{6,5},{7,6},{8,15},{9,8},{10,9... | collective-permute-start | bytes 1228808 | tf_op jit(solution)/shard_map/ppermute | solution.py:52
  134.9 24.0 %collective-permute-start.11 = (bf16[2,160,640]{2,1,0:T(8,128)(2,1)}, bf16[2,160,640]{2,1,0:T(8,128)(2,1)}, u32[]{:S(2)}, u32[]{:S(2)}) collective-permute-start(bf16[2,160,640]{2,1,0:T(8,128)(2,1)} %pad_maximum_fusion.3), channel_id=1, source_target_pairs={{0,1},{1,2},{2,3},{3,4},{4,5},{5,6},{6,7},{7,0},{8,9},{9,10},{10,1... | collective-permute-start | bytes 1228808 | tf_op jit(solution)/shard_map/ppermute | solution.py:52
  138.3 14.5 %collective-permute-start.12 = (bf16[160,640]{1,0:T(8,128)(2,1)S(1)}, bf16[160,640]{1,0:T(8,128)(2,1)S(1)}, u32[]{:S(2)}, u32[]{:S(2)}) collective-permute-start(bf16[160,640]{1,0:T(8,128)(2,1)S(1)} %get-tuple-element.19), channel_id=1, source_target_pairs={{0,2},{1,7},{2,4},{3,1},{4,6},{5,3},{6,0},{7,5},{8,10},{9,15},{10,... | collective-permute-start | bytes 614408 | tf_op jit(solution)/shard_map/ppermute | solution.py:82
  141.6 27.4 %collective-permute-start.10 = (bf16[160,640]{1,0:T(8,128)(2,1)S(1)}, bf16[160,640]{1,0:T(8,128)(2,1)S(1)}, u32[]{:S(2)}, u32[]{:S(2)}) collective-permute-start(bf16[160,640]{1,0:T(8,128)(2,1)S(1)} %get-tuple-element.16), channel_id=1, source_target_pairs={{0,6},{1,7},{2,0},{3,1},{4,2},{5,3},{6,4},{7,5},{8,14},{9,15},{10,... | collective-permute-start | bytes 614408 | tf_op jit(solution)/shard_map/ppermute | solution.py:52
  147.6 21.3 %collective-permute-start.9 = (bf16[160,640]{1,0:T(8,128)(2,1)S(1)}, bf16[160,640]{1,0:T(8,128)(2,1)S(1)}, u32[]{:S(2)}, u32[]{:S(2)}) collective-permute-start(bf16[160,640]{1,0:T(8,128)(2,1)S(1)} %get-tuple-element.15), channel_id=1, source_target_pairs={{0,2},{1,3},{2,4},{3,5},{4,6},{5,7},{6,0},{7,1},{8,10},{9,11},{10,... | collective-permute-start | bytes 614408 | tf_op jit(solution)/shard_map/ppermute | solution.py:52
  161.0 11.7 %collective-permute-start.13 = (bf16[160,640]{1,0:T(8,128)(2,1)}, bf16[160,640]{1,0:T(8,128)(2,1)}, u32[]{:S(2)}, u32[]{:S(2)}) collective-permute-start(bf16[160,640]{1,0:T(8,128)(2,1)} %get-tuple-element.14), channel_id=1, source_target_pairs={{0,2},{1,3},{2,4},{3,5},{4,6},{5,7},{6,0},{7,1},{8,10},{9,11},{10,... | collective-permute-start | bytes 614408 | tf_op jit(solution)/shard_map/ppermute | solution.py:52
  162.9 9.8 %collective-permute-start.15 = (bf16[160,640]{1,0:T(8,128)(2,1)S(1)}, bf16[160,640]{1,0:T(8,128)(2,1)}, u32[]{:S(2)}, u32[]{:S(2)}) collective-permute-start(bf16[160,640]{1,0:T(8,128)(2,1)S(1)} %get-tuple-element.13), channel_id=1, source_target_pairs={{0,6},{1,7},{2,0},{3,1},{4,2},{5,3},{6,4},{7,5},{8,14},{9,15},{10,... | collective-permute-start | bytes 614408 | tf_op jit(solution)/shard_map/ppermute | solution.py:52

commit v7 on v6

--- a/solution.py
+++ b/solution.py
@@ -72,25 +72,28 @@
     return value.astype(jnp.float32)
 
 
-def depth_parts(blocks):
+def depth_parts(blocks, straight):
     here = lax.axis_index("depth")
     pick = lambda by: block_at(blocks, (here + by) % 8)
     even = here % 2 == 0
     near_up = shifted(jnp.stack([pick(1), pick(3)]), "depth", 1)
     near_down = shifted(jnp.stack([pick(7), pick(5)]), "depth", 7)
-    turns = [(k, (k + 2) % 8 if k % 2 == 0 else (k - 2) % 8) for k in range(8)]
-    far = lax.ppermute(pick(4), "depth", turns)
-    up = wide(pick(2)) + wide(near_up[1]) + jnp.where(even, wide(far), 0.0)
-    down = wide(pick(6)) + wide(near_down[1]) + jnp.where(even, 0.0, wide(far))
+    up = wide(pick(2)) + wide(near_up[1])
+    down = wide(pick(6)) + wide(near_down[1])
+    if straight:
+        far = [shifted(pick(4), "depth", 4)]
+    else:
+        turns = [(k, (k + 2) % 8 if k % 2 == 0 else (k - 2) % 8) for k in range(8)]
+        turn = wide(lax.ppermute(pick(4), "depth", turns))
+        up, down, far = up + jnp.where(even, turn, 0.0), down + jnp.where(even, 0.0, turn), []
     last_up = shifted(up.astype(jnp.bfloat16), "depth", 2)
     last_down = shifted(down.astype(jnp.bfloat16), "depth", 6)
     near = wide(pick(0)) + wide(near_up[0]) + wide(near_down[0])
-    return near, last_up, last_down
+    return near, last_up, last_down, *far
 
 
 def total(parts):
-    near, last_up, last_down = parts
-    return near + wide(last_up) + wide(last_down)
+    return sum(wide(part) for part in parts)
 
 
 def step(inputs, pre_act, grad_out, weight_up, weight_down):
@@ -117,7 +120,7 @@
     lower_mine = lax.optimization_barrier(contract_first(active_mine, turned(mine[..., :width])))
     lower = contract_first(active_other, turned(other[..., :width])) + lower_mine
     lower = lower.astype(jnp.bfloat16)
-    lower_parts = depth_parts(lower.reshape(8, -1, lower.shape[1]))
+    lower_parts = depth_parts(lower.reshape(8, -1, lower.shape[1]), True)
 
     delta_own = (sum(wide(came[k]) for k in range(4)) * slope).astype(jnp.bfloat16)
     delta_mine = flat(spread(delta_own, "yhi"))
@@ -126,7 +129,7 @@
     upper_mine = lax.optimization_barrier(contract_first(delta_mine, flat(mine[..., width:])))
     upper = contract_first(delta_other, flat(other[..., width:])) + upper_mine
     upper = upper.astype(jnp.bfloat16)
-    near, last_up, last_down = depth_parts(upper.reshape(8, -1, upper.shape[1]))
+    near, last_up, last_down = depth_parts(upper.reshape(8, -1, upper.shape[1]), False)
 
     parts_mine = contract_last(delta_mine, weight_up).astype(jnp.bfloat16)
     parts_other = contract_last(delta_other, weight_up).astype(jnp.bfloat16)

time: 176 us -> 186 us (1.057)
  the two profiles are of different devices: /device:TPU:8 before, /device:TPU:2 now
where the time goes in v7:
time: 186 us; the launch traced here: 184 us
  starting transfers between devices  93.8 us (50%)
  waiting for transfers between devices  51.6 us (28%)
  other arithmetic  18.7 us (10%)
  matrix products  14.9 us (8%)
  local copies, waits for them, and re-layouts  4.27 us (2%)
    ppermute x12, starting transfers between devices, shifted(): lax.ppermute(value, axis, [(k, (k + by) % length) for k in range(length)])  54.2 us
    all_to_all x2, waiting for transfers between devices, spread(): return lax.all_to_all(copies, axis, split_axis=0, concat_axis=0, tiled=True)  19.2 us
    ppermute x12, waiting for transfers between devices, shifted(): lax.ppermute(value, axis, [(k, (k + by) % length) for k in range(length)])  18.8 us
    all_to_all x2, starting transfers between devices, exchanged(): return lax.all_to_all(value, axis, split_axis=0, concat_axis=0, tiled=True)  15.5 us
    all_to_all x2, starting transfers between devices, spread(): return lax.all_to_all(copies, axis, split_axis=0, concat_axis=0, tiled=True)  13.5 us
    ppermute x1, waiting for transfers between devices, depth_parts(): turn = wide(lax.ppermute(pick(4), 'depth', turns))  11.5 us
    dot_general x4, matrix products, contract_first(): lax.dot_general(left, right, (((0,), (0,)), ((), ())), preferred_element_...  10.1 us
    ppermute x3, starting transfers between devices, swapped(): return lax.ppermute(value, 'core', SWAP)  5.74 us
  transfers between devices with their start and end apart: 20, of which 8 were waited for; matrix products, arithmetic and copies ran while one was open for 16% of the time, Pallas kernels for 0%

profile of v7, /device:TPU:2, one launch (start us, length us, event | category | flops | bytes accessed | tf_op | source)
XLA Modules:
  0.0 184.5 jit_solution(6614426492580972815)
XLA Ops:
  2.9 9.4 %all-to-all-start = ((bf16[8,64,1280]{2,1,0:T(8,128)(2,1)}), bf16[8,64,1280]{2,1,0:T(8,128)(2,1)S(1)}, u32[]{:S(2)}, u32[]{:S(2)}) async-start(bf16[8,64,1280]{2,1,0:T(8,128)(2,1)} %broadcast_in_dim.15), calls=%async_computation | async-start | bytes 2621440 | tf_op jit(solution)/shard_map/all_to_all | solution.py:17
  12.2 12.9 %all-to-all-done = bf16[8,64,1280]{2,1,0:T(8,128)(2,1)S(1)} async-done(((bf16[8,64,1280]{2,1,0:T(8,128)(2,1)}), bf16[8,64,1280]{2,1,0:T(8,128)(2,1)S(1)}, u32[]{:S(2)}, u32[]{:S(2)}) %all-to-all-start) | async-done | bytes 1310752 | tf_op jit(solution)/shard_map/all_to_all | solution.py:17
  26.9 1.9 %collective-permute-start = (bf16[256,1280]{1,0:T(8,128)(2,1)S(1)}, bf16[256,1280]{1,0:T(8,128)(2,1)S(1)}, u32[]{:S(2)}, u32[]{:S(2)}) collective-permute-start(bf16[256,1280]{1,0:T(8,128)(2,1)S(1)} %convolution_convert_fusion), channel_id=1, source_target_pairs={{0,64},{64,0},{1,65},{65,1},{2,66},{66,2},{3,67},{67,3},{4,68},{68... | collective-permute-start | bytes 1966088 | tf_op jit(solution)/shard_map/ppermute | solution.py:56
  28.8 2.0 %collective-permute-done = bf16[256,1280]{1,0:T(8,128)(2,1)S(1)} collective-permute-done((bf16[256,1280]{1,0:T(8,128)(2,1)S(1)}, bf16[256,1280]{1,0:T(8,128)(2,1)S(1)}, u32[]{:S(2)}, u32[]{:S(2)}) %collective-permute-start) | collective-permute-done | bytes 655392 | tf_op jit(solution)/shard_map/ppermute | solution.py:56
  32.4 6.2 %all-to-all-start.1 = ((bf16[4,64,1280]{2,1,0:T(8,128)(2,1)}), bf16[4,64,1280]{2,1,0:T(8,128)(2,1)S(1)}, u32[]{:S(2)}, u32[]{:S(2)}) async-start(bf16[4,64,1280]{2,1,0:T(8,128)(2,1)} %bitcast.96), calls=%async_computation.1 | async-start | bytes 1310720 | tf_op jit(solution)/shard_map/all_to_all | solution.py:21
  39.8 4.8 %collective-permute-start.4 = (bf16[64,1280]{1,0:T(8,128)(2,1)S(1)}, bf16[64,1280]{1,0:T(8,128)(2,1)}, u32[]{:S(2)}, u32[]{:S(2)}) collective-permute-start(bf16[64,1280]{1,0:T(8,128)(2,1)S(1)} %get-tuple-element.9), channel_id=1, source_target_pairs={{0,128},{128,256},{256,384},{384,0},{1,129},{129,257},{257,385},{3... | collective-permute-start | bytes 491528 | tf_op jit(solution)/shard_map/ppermute | solution.py:52
  44.6 5.5 %collective-permute-start.3 = (bf16[64,1280]{1,0:T(8,128)(2,1)S(1)}, bf16[64,1280]{1,0:T(8,128)(2,1)}, u32[]{:S(2)}, u32[]{:S(2)}) collective-permute-start(bf16[64,1280]{1,0:T(8,128)(2,1)S(1)} %get-tuple-element.9), channel_id=1, source_target_pairs={{0,256},{128,384},{256,0},{384,128},{1,257},{129,385},{257,1},{385... | collective-permute-start | bytes 491528 | tf_op jit(solution)/shard_map/ppermute | solution.py:52
  50.1 5.5 %collective-permute-start.2 = (bf16[64,1280]{1,0:T(8,128)(2,1)S(1)}, bf16[64,1280]{1,0:T(8,128)(2,1)}, u32[]{:S(2)}, u32[]{:S(2)}) collective-permute-start(bf16[64,1280]{1,0:T(8,128)(2,1)S(1)} %get-tuple-element.9), channel_id=1, source_target_pairs={{0,384},{128,0},{256,128},{384,256},{1,385},{129,1},{257,129},{385... | collective-permute-start | bytes 491528 | tf_op jit(solution)/shard_map/ppermute | solution.py:52
  55.7 3.5 %collective-permute-done.4 = bf16[64,1280]{1,0:T(8,128)(2,1)} collective-permute-done((bf16[64,1280]{1,0:T(8,128)(2,1)S(1)}, bf16[64,1280]{1,0:T(8,128)(2,1)}, u32[]{:S(2)}, u32[]{:S(2)}) %collective-permute-start.4) | collective-permute-done | bytes 163872 | tf_op jit(solution)/shard_map/ppermute | solution.py:52
  59.2 4.9 %collective-permute-done.3 = bf16[64,1280]{1,0:T(8,128)(2,1)} collective-permute-done((bf16[64,1280]{1,0:T(8,128)(2,1)S(1)}, bf16[64,1280]{1,0:T(8,128)(2,1)}, u32[]{:S(2)}, u32[]{:S(2)}) %collective-permute-start.3) | collective-permute-done | bytes 163872 | tf_op jit(solution)/shard_map/ppermute | solution.py:52
  64.1 7.3 %collective-permute-done.2 = bf16[64,1280]{1,0:T(8,128)(2,1)} collective-permute-done((bf16[64,1280]{1,0:T(8,128)(2,1)S(1)}, bf16[64,1280]{1,0:T(8,128)(2,1)}, u32[]{:S(2)}, u32[]{:S(2)}) %collective-permute-start.2) | collective-permute-done | bytes 163872 | tf_op jit(solution)/shard_map/ppermute | solution.py:52
  71.4 2.0 %maximum_maximum_fusion = bf16[256,1280]{1,0:T(8,128)(2,1)} fusion(bf16[64,1280]{1,0:T(8,128)(2,1)} %collective-permute-done.4, bf16[64,1280]{1,0:T(8,128)(2,1)} %collective-permute-done.3, bf16[64,1280]{1,0:T(8,128)(2,1)} %collective-permute-done.2, bf16[64,1280]{1,0:T(8,128)(2,1)S(1)} %get-tuple-element.9), kind=kLoop, calls=%fused_computation.17 | loop fusion | flops 2621440 | bytes 1310720 | tf_op jit(solution)/shard_map/max | solution.py:68
  73.3 1.9 %collective-permute-start.5 = (bf16[256,1280]{1,0:T(8,128)(2,1)}, bf16[256,1280]{1,0:T(8,128)(2,1)}, u32[]{:S(2)}, u32[]{:S(2)}) collective-permute-start(bf16[256,1280]{1,0:T(8,128)(2,1)} %maximum_maximum_fusion), channel_id=1, source_target_pairs={{0,64},{64,0},{1,65},{65,1},{2,66},{66,2},{3,67},{67,3},{4,68},{68... | collective-permute-start | bytes 1966088 | tf_op jit(solution)/shard_map/ppermute | solution.py:56
  76.3 4.2 %all-to-all-start.2 = ((bf16[4,64,1280]{2,1,0:T(8,128)(2,1)}), bf16[4,64,1280]{2,1,0:T(8,128)(2,1)}, u32[]{:S(2)}, u32[]{:S(2)}) async-start(bf16[4,64,1280]{2,1,0:T(8,128)(2,1)} %broadcast_in_dim.16), calls=%async_computation.2 | async-start | bytes 1310720 | tf_op jit(solution)/shard_map/all_to_all | solution.py:17
  85.8 4.3 %collective-permute-start.6 = (bf16[2,160,640]{2,1,0:T(8,128)(2,1)}, bf16[2,160,640]{2,1,0:T(8,128)(2,1)}, u32[]{:S(2)}, u32[]{:S(2)}) collective-permute-start(bf16[2,160,640]{2,1,0:T(8,128)(2,1)} %pad_maximum_fusion.1), channel_id=1, source_target_pairs={{0,1},{1,2},{2,3},{3,4},{4,5},{5,6},{6,7},{7,0},{8,9},{9,10},{10,1... | collective-permute-start | bytes 1228808 | tf_op jit(solution)/shard_map/ppermute | solution.py:52
  90.1 6.3 %all-to-all-done.2 = bf16[4,64,1280]{2,1,0:T(8,128)(2,1)} async-done(((bf16[4,64,1280]{2,1,0:T(8,128)(2,1)}), bf16[4,64,1280]{2,1,0:T(8,128)(2,1)}, u32[]{:S(2)}, u32[]{:S(2)}) %all-to-all-start.2) | async-done | bytes 655392 | tf_op jit(solution)/shard_map/all_to_all | solution.py:17
  100.0 11.1 %collective-permute-start.7 = (bf16[2,160,640]{2,1,0:T(8,128)(2,1)}, bf16[2,160,640]{2,1,0:T(8,128)(2,1)}, u32[]{:S(2)}, u32[]{:S(2)}) collective-permute-start(bf16[2,160,640]{2,1,0:T(8,128)(2,1)} %pad_maximum_fusion.2), channel_id=1, source_target_pairs={{0,7},{1,0},{2,1},{3,2},{4,3},{5,4},{6,5},{7,6},{8,15},{9,8},{10,9... | collective-permute-start | bytes 1228808 | tf_op jit(solution)/shard_map/ppermute | solution.py:52
  111.1 3.6 %convolution_bitcast_fusion = f32[1280,640]{1,0:T(8,128)} fusion(bf16[4,64,1280]{2,1,0:T(8,128)(2,1)} %all-to-all-done.2, bf16[4,64,1280]{2,1,0:T(8,128)(2,1)} %copy-done.2), kind=kOutput, calls=%fused_computation.2 | convolution fusion | flops 419430400 | bytes 4259840 | tf_op jit(solution)/shard_map/dot_general | solution.py:45
  118.3 9.3 %all-to-all-start.3 = ((bf16[8,64,640]{2,1,0:T(8,128)(2,1)}), bf16[8,64,640]{2,1,0:T(8,128)(2,1)}, u32[]{:S(2)}, u32[]{:S(2)}) async-start(bf16[8,64,640]{2,1,0:T(8,128)(2,1)} %bitcast.95), calls=%async_computation.3 | async-start | bytes 1310720 | tf_op jit(solution)/shard_map/all_to_all | solution.py:21
  127.6 2.9 %fusion.1 = bf16[1280,640]{1,0:T(8,128)(2,1)S(1)} fusion(f32[1280,640]{1,0:T(8,128)} %convolution_bitcast_fusion, bf16[256,1280]{1,0:T(8,128)(2,1)} %copy-done.3, bf16[256,640]{1,0:T(8,128)(2,1)} %bitcast.97), kind=kOutput, calls=%fused_computation.4 | convolution fusion | flops 421068800 | bytes 5898240 | tf_op jit(solution)/shard_map/dot_general | solution.py:45
  131.7 2.5 %collective-permute-start.14 = (bf16[2,160,640]{2,1,0:T(8,128)(2,1)}, bf16[2,160,640]{2,1,0:T(8,128)(2,1)}, u32[]{:S(2)}, u32[]{:S(2)}) collective-permute-start(bf16[2,160,640]{2,1,0:T(8,128)(2,1)} %pad_maximum_fusion.4), channel_id=1, source_target_pairs={{0,7},{1,0},{2,1},{3,2},{4,3},{5,4},{6,5},{7,6},{8,15},{9,8},{10,9... | collective-permute-start | bytes 1228808 | tf_op jit(solution)/shard_map/ppermute | solution.py:52
  135.0 3.4 %collective-permute-start.11 = (bf16[2,160,640]{2,1,0:T(8,128)(2,1)}, bf16[2,160,640]{2,1,0:T(8,128)(2,1)}, u32[]{:S(2)}, u32[]{:S(2)}) collective-permute-start(bf16[2,160,640]{2,1,0:T(8,128)(2,1)} %pad_maximum_fusion.3), channel_id=1, source_target_pairs={{0,1},{1,2},{2,3},{3,4},{4,5},{5,6},{6,7},{7,0},{8,9},{9,10},{10,1... | collective-permute-start | bytes 1228808 | tf_op jit(solution)/shard_map/ppermute | solution.py:52
  138.4 1.9 %collective-permute-start.10 = (bf16[160,640]{1,0:T(8,128)(2,1)}, bf16[160,640]{1,0:T(8,128)(2,1)S(1)}, u32[]{:S(2)}, u32[]{:S(2)}) collective-permute-start(bf16[160,640]{1,0:T(8,128)(2,1)} %get-tuple-element.23), channel_id=1, source_target_pairs={{0,4},{1,5},{2,6},{3,7},{4,0},{5,1},{6,2},{7,3},{8,12},{9,13},{10,... | collective-permute-start | bytes 614408 | tf_op jit(solution)/shard_map/ppermute | solution.py:52
  140.3 4.8 %collective-permute-start.12 = (bf16[160,640]{1,0:T(8,128)(2,1)S(1)}, bf16[160,640]{1,0:T(8,128)(2,1)S(1)}, u32[]{:S(2)}, u32[]{:S(2)}) collective-permute-start(bf16[160,640]{1,0:T(8,128)(2,1)S(1)} %get-tuple-element.17), channel_id=1, source_target_pairs={{0,2},{1,7},{2,4},{3,1},{4,6},{5,3},{6,0},{7,5},{8,10},{9,15},{10,... | collective-permute-start | bytes 614408 | tf_op jit(solution)/shard_map/ppermute | solution.py:87
  146.3 3.1 %collective-permute-start.9 = (bf16[160,640]{1,0:T(8,128)(2,1)S(1)}, bf16[160,640]{1,0:T(8,128)(2,1)S(1)}, u32[]{:S(2)}, u32[]{:S(2)}) collective-permute-start(bf16[160,640]{1,0:T(8,128)(2,1)S(1)} %get-tuple-element.21), channel_id=1, source_target_pairs={{0,6},{1,7},{2,0},{3,1},{4,2},{5,3},{6,4},{7,5},{8,14},{9,15},{10,... | collective-permute-start | bytes 614408 | tf_op jit(solution)/shard_map/ppermute | solution.py:52
  149.5 11.5 %collective-permute-done.12 = bf16[160,640]{1,0:T(8,128)(2,1)S(1)} collective-permute-done((bf16[160,640]{1,0:T(8,128)(2,1)S(1)}, bf16[160,640]{1,0:T(8,128)(2,1)S(1)}, u32[]{:S(2)}, u32[]{:S(2)}) %collective-permute-start.12) | collective-permute-done | bytes 204832 | tf_op jit(solution)/shard_map/ppermute | solution.py:87
  161.0 4.3 %collective-permute-start.8 = (bf16[160,640]{1,0:T(8,128)(2,1)S(1)}, bf16[160,640]{1,0:T(8,128)(2,1)S(1)}, u32[]{:S(2)}, u32[]{:S(2)}) collective-permute-start(bf16[160,640]{1,0:T(8,128)(2,1)S(1)} %get-tuple-element.20), channel_id=1, source_target_pairs={{0,2},{1,3},{2,4},{3,5},{4,6},{5,7},{6,0},{7,1},{8,10},{9,11},{10,... | collective-permute-start | bytes 614408 | tf_op jit(solution)/shard_map/ppermute | solution.py:52
  165.3 2.1 %fusion.5 = (bf16[160,640]{1,0:T(8,128)(2,1)S(1)}, bf16[160,640]{1,0:T(8,128)(2,1)}) fusion(bf16[160,640]{1,0:T(8,128)(2,1)S(1)} %collective-permute-done.12, bf16[2,160,640]{2,1,0:T(8,128)(2,1)} %collective-permute-done.14, bf16[8,160,640]{2,1,0:T(8,128)(2,1)} %bitcast.90, s32[]{:T(128)S(6)} %select_n.188, pred[]{:T(512)S(6)} %eq.34, ...), kind=kLoop, calls=%fused_computation.25 | loop fusion | flops 1331200 | bytes 1433609 | tf_op jit(solution)/shard_map/convert_element_type | solution.py:90
  169.3 6.0 %collective-permute-start.15 = (bf16[160,640]{1,0:T(8,128)(2,1)S(1)}, bf16[160,640]{1,0:T(8,128)(2,1)}, u32[]{:S(2)}, u32[]{:S(2)}) collective-permute-start(bf16[160,640]{1,0:T(8,128)(2,1)S(1)} %get-tuple-element.13), channel_id=1, source_target_pairs={{0,6},{1,7},{2,0},{3,1},{4,2},{5,3},{6,4},{7,5},{8,14},{9,15},{10,... | collective-permute-start | bytes 614408 | tf_op jit(solution)/shard_map/ppermute | solution.py:52
  175.4 1.9 %fusion.9 = f32[160,640]{1,0:T(8,128)} fusion(bf16[160,640]{1,0:T(8,128)(2,1)S(1)} %collective-permute-done.10, bf16[160,640]{1,0:T(8,128)(2,1)S(1)} %collective-permute-done.9, bf16[160,640]{1,0:T(8,128)(2,1)S(1)} %collective-permute-done.8, bf16[2,160,640]{2,1,0:T(8,128)(2,1)} %collective-permute-done.7, bf16[2,160,640]{2,1,0:T(8,128)(2,1)} %collective-permute-done.6, ...), kind=kLoop, calls=%fused_computation.35 | loop fusion | flops 1126400 | bytes 1638404 | tf_op jit(solution)/shard_map/add | solution.py:96
  179.2 3.1 %collective-permute-done.13 = bf16[160,640]{1,0:T(8,128)(2,1)} collective-permute-done((bf16[160,640]{1,0:T(8,128)(2,1)}, bf16[160,640]{1,0:T(8,128)(2,1)}, u32[]{:S(2)}, u32[]{:S(2)}) %collective-permute-start.13) | collective-permute-done | bytes 204832 | tf_op jit(solution)/shard_map/ppermute | solution.py:52
  182.3 2.2 %fusion.7 = f32[640,160]{0,1:T(8,128)} fusion(bf16[160,640]{1,0:T(8,128)(2,1)} %collective-permute-done.15, bf16[160,640]{1,0:T(8,128)(2,1)} %collective-permute-done.13, bf16[2,160,640]{2,1,0:T(8,128)(2,1)} %collective-permute-done.14, bf16[2,160,640]{2,1,0:T(8,128)(2,1)} %collective-permute-done.11, bf16[8,160,640]{2,1,0:T(8,128)(2,1)} %bitcast.91, ...), kind=kLoop, calls=%fused_computation.32 | loop fusion | flops 921600 | bytes 1433604 | tf_op jit(solution)/shard_map/transpose | solution.py:144
  (49 shorter events, 27.0 us)
Async XLA Ops:
  0.6 25.5 %copy-start = (bf16[1280,640]{1,0:T(8,128)(2,1)S(1)}, bf16[1280,640]{1,0:T(8,128)(2,1)}, u32[]{:S(2)}) copy-start(bf16[1280,640]{1,0:T(8,128)(2,1)} %param.9) | copy-start | bytes 4915204
  2.9 22.3 %all-to-all-start = ((bf16[8,64,1280]{2,1,0:T(8,128)(2,1)}), bf16[8,64,1280]{2,1,0:T(8,128)(2,1)S(1)}, u32[]{:S(2)}, u32[]{:S(2)}) async-start(bf16[8,64,1280]{2,1,0:T(8,128)(2,1)} %broadcast_in_dim.15), calls=%async_computation | async-start | bytes 2621440 | tf_op jit(solution)/shard_map/all_to_all | solution.py:17
  25.3 3.5 %copy-start.2 = (bf16[4,64,1280]{2,1,0:T(8,128)(2,1)}, bf16[4,64,1280]{2,1,0:T(8,128)(2,1)S(1)}, u32[]{:S(2)}) copy-start(bf16[4,64,1280]{2,1,0:T(8,128)(2,1)S(1)} %get-tuple-element.28) | copy-start | bytes 1966084
  26.9 4.0 %collective-permute-start = (bf16[256,1280]{1,0:T(8,128)(2,1)S(1)}, bf16[256,1280]{1,0:T(8,128)(2,1)S(1)}, u32[]{:S(2)}, u32[]{:S(2)}) collective-permute-start(bf16[256,1280]{1,0:T(8,128)(2,1)S(1)} %convolution_convert_fusion), channel_id=1, source_target_pairs={{0,64},{64,0},{1,65},{65,1},{2,66},{66,2},{3,67},{67,3},{4,68},{68... | collective-permute-start | bytes 1966088 | tf_op jit(solution)/shard_map/ppermute | solution.py:56
  32.4 42.8 %all-to-all-start.1 = ((bf16[4,64,1280]{2,1,0:T(8,128)(2,1)}), bf16[4,64,1280]{2,1,0:T(8,128)(2,1)S(1)}, u32[]{:S(2)}, u32[]{:S(2)}) async-start(bf16[4,64,1280]{2,1,0:T(8,128)(2,1)} %bitcast.96), calls=%async_computation.1 | async-start | bytes 1310720 | tf_op jit(solution)/shard_map/all_to_all | solution.py:21
  39.8 19.4 %collective-permute-start.4 = (bf16[64,1280]{1,0:T(8,128)(2,1)S(1)}, bf16[64,1280]{1,0:T(8,128)(2,1)}, u32[]{:S(2)}, u32[]{:S(2)}) collective-permute-start(bf16[64,1280]{1,0:T(8,128)(2,1)S(1)} %get-tuple-element.9), channel_id=1, source_target_pairs={{0,128},{128,256},{256,384},{384,0},{1,129},{129,257},{257,385},{3... | collective-permute-start | bytes 491528 | tf_op jit(solution)/shard_map/ppermute | solution.py:52
  44.6 19.5 %collective-permute-start.3 = (bf16[64,1280]{1,0:T(8,128)(2,1)S(1)}, bf16[64,1280]{1,0:T(8,128)(2,1)}, u32[]{:S(2)}, u32[]{:S(2)}) collective-permute-start(bf16[64,1280]{1,0:T(8,128)(2,1)S(1)} %get-tuple-element.9), channel_id=1, source_target_pairs={{0,256},{128,384},{256,0},{384,128},{1,257},{129,385},{257,1},{385... | collective-permute-start | bytes 491528 | tf_op jit(solution)/shard_map/ppermute | solution.py:52
  50.1 21.3 %collective-permute-start.2 = (bf16[64,1280]{1,0:T(8,128)(2,1)S(1)}, bf16[64,1280]{1,0:T(8,128)(2,1)}, u32[]{:S(2)}, u32[]{:S(2)}) collective-permute-start(bf16[64,1280]{1,0:T(8,128)(2,1)S(1)} %get-tuple-element.9), channel_id=1, source_target_pairs={{0,384},{128,0},{256,128},{384,256},{1,385},{129,1},{257,129},{385... | collective-permute-start | bytes 491528 | tf_op jit(solution)/shard_map/ppermute | solution.py:52
  73.3 9.0 %collective-permute-start.5 = (bf16[256,1280]{1,0:T(8,128)(2,1)}, bf16[256,1280]{1,0:T(8,128)(2,1)}, u32[]{:S(2)}, u32[]{:S(2)}) collective-permute-start(bf16[256,1280]{1,0:T(8,128)(2,1)} %maximum_maximum_fusion), channel_id=1, source_target_pairs={{0,64},{64,0},{1,65},{65,1},{2,66},{66,2},{3,67},{67,3},{4,68},{68... | collective-permute-start | bytes 1966088 | tf_op jit(solution)/shard_map/ppermute | solution.py:56
  76.3 20.1 %all-to-all-start.2 = ((bf16[4,64,1280]{2,1,0:T(8,128)(2,1)}), bf16[4,64,1280]{2,1,0:T(8,128)(2,1)}, u32[]{:S(2)}, u32[]{:S(2)}) async-start(bf16[4,64,1280]{2,1,0:T(8,128)(2,1)} %broadcast_in_dim.16), calls=%async_computation.2 | async-start | bytes 1310720 | tf_op jit(solution)/shard_map/all_to_all | solution.py:17
  85.8 54.5 %collective-permute-start.6 = (bf16[2,160,640]{2,1,0:T(8,128)(2,1)}, bf16[2,160,640]{2,1,0:T(8,128)(2,1)}, u32[]{:S(2)}, u32[]{:S(2)}) collective-permute-start(bf16[2,160,640]{2,1,0:T(8,128)(2,1)} %pad_maximum_fusion.1), channel_id=1, source_target_pairs={{0,1},{1,2},{2,3},{3,4},{4,5},{5,6},{6,7},{7,0},{8,9},{9,10},{10,1... | collective-permute-start | bytes 1228808 | tf_op jit(solution)/shard_map/ppermute | solution.py:52
  96.4 20.1 %collective-permute-start.1 = (bf16[256,1280]{1,0:T(8,128)(2,1)}, bf16[256,1280]{1,0:T(8,128)(2,1)S(1)}, u32[]{:S(2)}, u32[]{:S(2)}) collective-permute-start(bf16[256,1280]{1,0:T(8,128)(2,1)} %bitcast.11), channel_id=1, source_target_pairs={{0,64},{64,0},{1,65},{65,1},{2,66},{66,2},{3,67},{67,3},{4,68},{68... | collective-permute-start | bytes 1966088 | tf_op jit(solution)/shard_map/ppermute | solution.py:56
  100.0 14.7 %copy-start.4 = (bf16[640,1280]{1,0:T(8,128)(2,1)S(1)}, bf16[640,1280]{1,0:T(8,128)(2,1)}, u32[]{:S(2)}) copy-start(bf16[640,1280]{1,0:T(8,128)(2,1)} %param.8) | copy-start | bytes 4915204
  100.0 45.1 %collective-permute-start.7 = (bf16[2,160,640]{2,1,0:T(8,128)(2,1)}, bf16[2,160,640]{2,1,0:T(8,128)(2,1)}, u32[]{:S(2)}, u32[]{:S(2)}) collective-permute-start(bf16[2,160,640]{2,1,0:T(8,128)(2,1)} %pad_maximum_fusion.2), channel_id=1, source_target_pairs={{0,7},{1,0},{2,1},{3,2},{4,3},{5,4},{6,5},{7,6},{8,15},{9,8},{10,9... | collective-permute-start | bytes 1228808 | tf_op jit(solution)/shard_map/ppermute | solution.py:52
  116.5 0.9 copy-start.3
  118.3 59.0 %all-to-all-start.3 = ((bf16[8,64,640]{2,1,0:T(8,128)(2,1)}), bf16[8,64,640]{2,1,0:T(8,128)(2,1)}, u32[]{:S(2)}, u32[]{:S(2)}) async-start(bf16[8,64,640]{2,1,0:T(8,128)(2,1)} %bitcast.95), calls=%async_computation.3 | async-start | bytes 1310720 | tf_op jit(solution)/shard_map/all_to_all | solution.py:21
  130.6 4.4 %copy-start.1 = (bf16[1280,640]{1,0:T(8,128)(2,1)}, bf16[1280,640]{1,0:T(8,128)(2,1)S(1)}, u32[]{:S(2)}) copy-start(bf16[1280,640]{1,0:T(8,128)(2,1)S(1)} %fusion.1) | copy-start | bytes 4915204
  131.7 33.6 %collective-permute-start.14 = (bf16[2,160,640]{2,1,0:T(8,128)(2,1)}, bf16[2,160,640]{2,1,0:T(8,128)(2,1)}, u32[]{:S(2)}, u32[]{:S(2)}) collective-permute-start(bf16[2,160,640]{2,1,0:T(8,128)(2,1)} %pad_maximum_fusion.4), channel_id=1, source_target_pairs={{0,7},{1,0},{2,1},{3,2},{4,3},{5,4},{6,5},{7,6},{8,15},{9,8},{10,9... | collective-permute-start | bytes 1228808 | tf_op jit(solution)/shard_map/ppermute | solution.py:52
  135.0 30.3 %collective-permute-start.11 = (bf16[2,160,640]{2,1,0:T(8,128)(2,1)}, bf16[2,160,640]{2,1,0:T(8,128)(2,1)}, u32[]{:S(2)}, u32[]{:S(2)}) collective-permute-start(bf16[2,160,640]{2,1,0:T(8,128)(2,1)} %pad_maximum_fusion.3), channel_id=1, source_target_pairs={{0,1},{1,2},{2,3},{3,4},{4,5},{5,6},{6,7},{7,0},{8,9},{9,10},{10,1... | collective-permute-start | bytes 1228808 | tf_op jit(solution)/shard_map/ppermute | solution.py:52
  138.4 37.0 %collective-permute-start.10 = (bf16[160,640]{1,0:T(8,128)(2,1)}, bf16[160,640]{1,0:T(8,128)(2,1)S(1)}, u32[]{:S(2)}, u32[]{:S(2)}) collective-permute-start(bf16[160,640]{1,0:T(8,128)(2,1)} %get-tuple-element.23), channel_id=1, source_target_pairs={{0,4},{1,5},{2,6},{3,7},{4,0},{5,1},{6,2},{7,3},{8,12},{9,13},{10,... | collective-permute-start | bytes 614408 | tf_op jit(solution)/shard_map/ppermute | solution.py:52
  140.3 20.7 %collective-permute-start.12 = (bf16[160,640]{1,0:T(8,128)(2,1)S(1)}, bf16[160,640]{1,0:T(8,128)(2,1)S(1)}, u32[]{:S(2)}, u32[]{:S(2)}) collective-permute-start(bf16[160,640]{1,0:T(8,128)(2,1)S(1)} %get-tuple-element.17), channel_id=1, source_target_pairs={{0,2},{1,7},{2,4},{3,1},{4,6},{5,3},{6,0},{7,5},{8,10},{9,15},{10,... | collective-permute-start | bytes 614408 | tf_op jit(solution)/shard_map/ppermute | solution.py:87
  146.3 29.0 %collective-permute-start.9 = (bf16[160,640]{1,0:T(8,128)(2,1)S(1)}, bf16[160,640]{1,0:T(8,128)(2,1)S(1)}, u32[]{:S(2)}, u32[]{:S(2)}) collective-permute-start(bf16[160,640]{1,0:T(8,128)(2,1)S(1)} %get-tuple-element.21), channel_id=1, source_target_pairs={{0,6},{1,7},{2,0},{3,1},{4,2},{5,3},{6,4},{7,5},{8,14},{9,15},{10,... | collective-permute-start | bytes 614408 | tf_op jit(solution)/shard_map/ppermute | solution.py:52
  161.0 14.4 %collective-permute-start.8 = (bf16[160,640]{1,0:T(8,128)(2,1)S(1)}, bf16[160,640]{1,0:T(8,128)(2,1)S(1)}, u32[]{:S(2)}, u32[]{:S(2)}) collective-permute-start(bf16[160,640]{1,0:T(8,128)(2,1)S(1)} %get-tuple-element.20), channel_id=1, source_target_pairs={{0,2},{1,3},{2,4},{3,5},{4,6},{5,7},{6,0},{7,1},{8,10},{9,11},{10,... | collective-permute-start | bytes 614408 | tf_op jit(solution)/shard_map/ppermute | solution.py:52
  167.4 14.9 %collective-permute-start.13 = (bf16[160,640]{1,0:T(8,128)(2,1)}, bf16[160,640]{1,0:T(8,128)(2,1)}, u32[]{:S(2)}, u32[]{:S(2)}) collective-permute-start(bf16[160,640]{1,0:T(8,128)(2,1)} %get-tuple-element.14), channel_id=1, source_target_pairs={{0,2},{1,3},{2,4},{3,5},{4,6},{5,7},{6,0},{7,1},{8,10},{9,11},{10,... | collective-permute-start | bytes 614408 | tf_op jit(solution)/shard_map/ppermute | solution.py:52
  169.3 13.0 %collective-permute-start.15 = (bf16[160,640]{1,0:T(8,128)(2,1)S(1)}, bf16[160,640]{1,0:T(8,128)(2,1)}, u32[]{:S(2)}, u32[]{:S(2)}) collective-permute-start(bf16[160,640]{1,0:T(8,128)(2,1)S(1)} %get-tuple-element.13), channel_id=1, source_target_pairs={{0,6},{1,7},{2,0},{3,1},{4,2},{5,3},{6,4},{7,5},{8,14},{9,15},{10,... | collective-permute-start | bytes 614408 | tf_op jit(solution)/shard_map/ppermute | solution.py:52

commit v8 on v6

--- a/solution.py
+++ b/solution.py
@@ -61,10 +61,12 @@
 
 
 def gathered(own):
-    pieces = [own] + [shifted(own, "yhi", 4 - u) for u in (1, 2, 3)]
+    after, before = shifted(own, "yhi", 3), shifted(own, "yhi", 1)
+    across = shifted(own, "yhi", 2)
     n = own.shape[0]
     least = jnp.array(-jnp.inf, own.dtype)
-    spaced = [lax.pad(v, least, ((k * n, (3 - k) * n, 0), (0, 0, 0))) for k, v in enumerate(pieces)]
+    pieces = enumerate((own, after, across, before))
+    spaced = [lax.pad(v, least, ((k * n, (3 - k) * n, 0), (0, 0, 0))) for k, v in pieces]
     return jnp.maximum(jnp.maximum(spaced[0], spaced[1]), jnp.maximum(spaced[2], spaced[3]))
 
 
@@ -75,22 +77,19 @@
 def depth_parts(blocks):
     here = lax.axis_index("depth")
     pick = lambda by: block_at(blocks, (here + by) % 8)
-    even = here % 2 == 0
     near_up = shifted(jnp.stack([pick(1), pick(3)]), "depth", 1)
     near_down = shifted(jnp.stack([pick(7), pick(5)]), "depth", 7)
-    turns = [(k, (k + 2) % 8 if k % 2 == 0 else (k - 2) % 8) for k in range(8)]
-    far = lax.ppermute(pick(4), "depth", turns)
-    up = wide(pick(2)) + wide(near_up[1]) + jnp.where(even, wide(far), 0.0)
-    down = wide(pick(6)) + wide(near_down[1]) + jnp.where(even, 0.0, wide(far))
+    far = shifted(pick(4), "depth", 4)
+    up = wide(pick(2)) + wide(near_up[1])
+    down = wide(pick(6)) + wide(near_down[1])
     last_up = shifted(up.astype(jnp.bfloat16), "depth", 2)
     last_down = shifted(down.astype(jnp.bfloat16), "depth", 6)
     near = wide(pick(0)) + wide(near_up[0]) + wide(near_down[0])
-    return near, last_up, last_down
+    return near, last_up, last_down, far
 
 
 def total(parts):
-    near, last_up, last_down = parts
-    return near + wide(last_up) + wide(last_down)
+    return sum(wide(part) for part in parts)
 
 
 def step(inputs, pre_act, grad_out, weight_up, weight_down):
@@ -126,7 +125,7 @@
     upper_mine = lax.optimization_barrier(contract_first(delta_mine, flat(mine[..., width:])))
     upper = contract_first(delta_other, flat(other[..., width:])) + upper_mine
     upper = upper.astype(jnp.bfloat16)
-    near, last_up, last_down = depth_parts(upper.reshape(8, -1, upper.shape[1]))
+    near, last_up, *rest = depth_parts(upper.reshape(8, -1, upper.shape[1]))
 
     parts_mine = contract_last(delta_mine, weight_up).astype(jnp.bfloat16)
     parts_other = contract_last(delta_other, weight_up).astype(jnp.bfloat16)
@@ -137,7 +136,7 @@
     grad_inputs = summed(parts).astype(jnp.bfloat16)[None]
     grad_down = total(lower_parts)
     grad_inputs, grad_down, last_up = lax.optimization_barrier((grad_inputs, grad_down, last_up))
-    grad_up = total((near, last_up, last_down))
+    grad_up = total((near, last_up, *rest))
     return (grad_inputs, grad_up.T, grad_down)
 
 

time: 176 us -> 193 us (1.097)
  waiting for transfers between devices: 41.3 us -> 60.7 us
  starting transfers between devices: 94.4 us -> 91 us
    ppermute x11 -> x13, waiting for transfers between devices: 21.9 us -> 34.6 us  [shifted(): lax.ppermute(value, axis, [(k, (k + by) % length) for k in range(length)])]
    all_to_all x2, waiting for transfers between devices: 14.1 us -> 24.1 us  [spread(): return lax.all_to_all(copies, axis, split_axis=0, concat_axis=0, tiled=True)]
    ppermute x2 -> x0, starting transfers between devices: 7.99 us -> none  [depth_parts(): far = lax.ppermute(pick(4), 'depth', turns)]
    ppermute x11 -> x13, starting transfers between devices: 56.8 us -> 61.4 us  [shifted(): lax.ppermute(value, axis, [(k, (k + by) % length) for k in range(length)])]
    ppermute x2 -> x0, waiting for transfers between devices: 3.29 us -> none  [depth_parts(): far = lax.ppermute(pick(4), 'depth', turns)]
  transfers between devices with their start and end apart: 20 -> 20, of which waited for: 6 -> 5; matrix products, arithmetic and copies ran while one was open for 17% -> 16% of each run, Pallas kernels for 0% -> 0%
where the time goes in v8:
time: 193 us; the launch traced here: 191 us
  starting transfers between devices  91 us (47%)
  waiting for transfers between devices  60.7 us (31%)
  other arithmetic  18.6 us (10%)
  matrix products  14.9 us (8%)
  local copies, waits for them, and re-layouts  5.08 us (3%)
    ppermute x13, starting transfers between devices, shifted(): lax.ppermute(value, axis, [(k, (k + by) % length) for k in range(length)])  61.4 us
    ppermute x13, waiting for transfers between devices, shifted(): lax.ppermute(value, axis, [(k, (k + by) % length) for k in range(length)])  34.6 us
    all_to_all x2, waiting for transfers between devices, spread(): return lax.all_to_all(copies, axis, split_axis=0, concat_axis=0, tiled=True)  24.1 us
    all_to_all x2, starting transfers between devices, spread(): return lax.all_to_all(copies, axis, split_axis=0, concat_axis=0, tiled=True)  13.5 us
    all_to_all x2, starting transfers between devices, exchanged(): return lax.all_to_all(value, axis, split_axis=0, concat_axis=0, tiled=True)  10.4 us
    dot_general x4, matrix products, contract_first(): lax.dot_general(left, right, (((0,), (0,)), ((), ())), preferred_element_...  10.1 us
    ppermute x3, starting transfers between devices, swapped(): return lax.ppermute(value, 'core', SWAP)  5.74 us
    dot_general x4, matrix products, contract_last(): lax.dot_general(left, right, (((1,), (1,)), ((), ())), preferred_element_...  4.79 us
  transfers between devices with their start and end apart: 20, of which 5 were waited for; matrix products, arithmetic and copies ran while one was open for 16% of the time, Pallas kernels for 0%

profile of v8, /device:TPU:8, one launch (start us, length us, event | category | flops | bytes accessed | tf_op | source)
XLA Modules:
  0.0 191.4 jit_solution(4830020843041538674)
XLA Ops:
  2.9 9.3 %all-to-all-start = ((bf16[8,64,1280]{2,1,0:T(8,128)(2,1)}), bf16[8,64,1280]{2,1,0:T(8,128)(2,1)S(1)}, u32[]{:S(2)}, u32[]{:S(2)}) async-start(bf16[8,64,1280]{2,1,0:T(8,128)(2,1)} %broadcast_in_dim.9), calls=%async_computation | async-start | bytes 2621440 | tf_op jit(solution)/shard_map/all_to_all | solution.py:17
  12.2 13.5 %all-to-all-done = bf16[8,64,1280]{2,1,0:T(8,128)(2,1)S(1)} async-done(((bf16[8,64,1280]{2,1,0:T(8,128)(2,1)}), bf16[8,64,1280]{2,1,0:T(8,128)(2,1)S(1)}, u32[]{:S(2)}, u32[]{:S(2)}) %all-to-all-start) | async-done | bytes 1310752 | tf_op jit(solution)/shard_map/all_to_all | solution.py:17
  27.4 1.9 %collective-permute-start = (bf16[256,1280]{1,0:T(8,128)(2,1)S(1)}, bf16[256,1280]{1,0:T(8,128)(2,1)S(1)}, u32[]{:S(2)}, u32[]{:S(2)}) collective-permute-start(bf16[256,1280]{1,0:T(8,128)(2,1)S(1)} %convolution_convert_fusion), channel_id=1, source_target_pairs={{0,64},{64,0},{1,65},{65,1},{2,66},{66,2},{3,67},{67,3},{4,68},{68... | collective-permute-start | bytes 1966088 | tf_op jit(solution)/shard_map/ppermute | solution.py:56
  29.4 2.0 %collective-permute-done = bf16[256,1280]{1,0:T(8,128)(2,1)S(1)} collective-permute-done((bf16[256,1280]{1,0:T(8,128)(2,1)S(1)}, bf16[256,1280]{1,0:T(8,128)(2,1)S(1)}, u32[]{:S(2)}, u32[]{:S(2)}) %collective-permute-start) | collective-permute-done | bytes 655392 | tf_op jit(solution)/shard_map/ppermute | solution.py:56
  32.9 6.2 %all-to-all-start.1 = ((bf16[4,64,1280]{2,1,0:T(8,128)(2,1)}), bf16[4,64,1280]{2,1,0:T(8,128)(2,1)S(1)}, u32[]{:S(2)}, u32[]{:S(2)}) async-start(bf16[4,64,1280]{2,1,0:T(8,128)(2,1)} %bitcast.98), calls=%async_computation.1 | async-start | bytes 1310720 | tf_op jit(solution)/shard_map/all_to_all | solution.py:21
  40.3 4.8 %collective-permute-start.4 = (bf16[64,1280]{1,0:T(8,128)(2,1)S(1)}, bf16[64,1280]{1,0:T(8,128)(2,1)}, u32[]{:S(2)}, u32[]{:S(2)}) collective-permute-start(bf16[64,1280]{1,0:T(8,128)(2,1)S(1)} %get-tuple-element.9), channel_id=1, source_target_pairs={{0,128},{128,256},{256,384},{384,0},{1,129},{129,257},{257,385},{3... | collective-permute-start | bytes 491528 | tf_op jit(solution)/shard_map/ppermute | solution.py:52
  45.1 5.5 %collective-permute-start.3 = (bf16[64,1280]{1,0:T(8,128)(2,1)S(1)}, bf16[64,1280]{1,0:T(8,128)(2,1)}, u32[]{:S(2)}, u32[]{:S(2)}) collective-permute-start(bf16[64,1280]{1,0:T(8,128)(2,1)S(1)} %get-tuple-element.9), channel_id=1, source_target_pairs={{0,256},{128,384},{256,0},{384,128},{1,257},{129,385},{257,1},{385... | collective-permute-start | bytes 491528 | tf_op jit(solution)/shard_map/ppermute | solution.py:52
  50.6 5.5 %collective-permute-start.2 = (bf16[64,1280]{1,0:T(8,128)(2,1)S(1)}, bf16[64,1280]{1,0:T(8,128)(2,1)}, u32[]{:S(2)}, u32[]{:S(2)}) collective-permute-start(bf16[64,1280]{1,0:T(8,128)(2,1)S(1)} %get-tuple-element.9), channel_id=1, source_target_pairs={{0,384},{128,0},{256,128},{384,256},{1,385},{129,1},{257,129},{385... | collective-permute-start | bytes 491528 | tf_op jit(solution)/shard_map/ppermute | solution.py:52
  56.2 15.9 %collective-permute-done.4 = bf16[64,1280]{1,0:T(8,128)(2,1)} collective-permute-done((bf16[64,1280]{1,0:T(8,128)(2,1)S(1)}, bf16[64,1280]{1,0:T(8,128)(2,1)}, u32[]{:S(2)}, u32[]{:S(2)}) %collective-permute-start.4) | collective-permute-done | bytes 163872 | tf_op jit(solution)/shard_map/ppermute | solution.py:52
  72.1 2.0 %maximum_maximum_fusion = bf16[256,1280]{1,0:T(8,128)(2,1)} fusion(bf16[64,1280]{1,0:T(8,128)(2,1)} %collective-permute-done.4, bf16[64,1280]{1,0:T(8,128)(2,1)} %collective-permute-done.3, bf16[64,1280]{1,0:T(8,128)(2,1)} %collective-permute-done.2, bf16[64,1280]{1,0:T(8,128)(2,1)S(1)} %get-tuple-element.9), kind=kLoop, calls=%fused_computation.17 | loop fusion | flops 2621440 | bytes 1310720 | tf_op jit(solution)/shard_map/max | solution.py:70
  74.1 1.9 collective-permute-start.5
  77.0 4.2 %all-to-all-start.2 = ((bf16[4,64,1280]{2,1,0:T(8,128)(2,1)}), bf16[4,64,1280]{2,1,0:T(8,128)(2,1)}, u32[]{:S(2)}, u32[]{:S(2)}) async-start(bf16[4,64,1280]{2,1,0:T(8,128)(2,1)} %broadcast_in_dim.10), calls=%async_computation.2 | async-start | bytes 1310720 | tf_op jit(solution)/shard_map/all_to_all | solution.py:17
  86.6 4.3 %collective-permute-start.6 = (bf16[2,160,640]{2,1,0:T(8,128)(2,1)}, bf16[2,160,640]{2,1,0:T(8,128)(2,1)}, u32[]{:S(2)}, u32[]{:S(2)}) collective-permute-start(bf16[2,160,640]{2,1,0:T(8,128)(2,1)} %pad_maximum_fusion.1), channel_id=1, source_target_pairs={{0,1},{1,2},{2,3},{3,4},{4,5},{5,6},{6,7},{7,0},{8,9},{9,10},{10,1... | collective-permute-start | bytes 1228808 | tf_op jit(solution)/shard_map/ppermute | solution.py:52
  90.9 10.6 %all-to-all-done.2 = bf16[4,64,1280]{2,1,0:T(8,128)(2,1)} async-done(((bf16[4,64,1280]{2,1,0:T(8,128)(2,1)}), bf16[4,64,1280]{2,1,0:T(8,128)(2,1)}, u32[]{:S(2)}, u32[]{:S(2)}) %all-to-all-start.2) | async-done | bytes 655392 | tf_op jit(solution)/shard_map/all_to_all | solution.py:17
  101.4 1.9 collective-permute-start.1
  105.1 11.1 %collective-permute-start.7 = (bf16[2,160,640]{2,1,0:T(8,128)(2,1)}, bf16[2,160,640]{2,1,0:T(8,128)(2,1)}, u32[]{:S(2)}, u32[]{:S(2)}) collective-permute-start(bf16[2,160,640]{2,1,0:T(8,128)(2,1)} %pad_maximum_fusion.2), channel_id=1, source_target_pairs={{0,7},{1,0},{2,1},{3,2},{4,3},{5,4},{6,5},{7,6},{8,15},{9,8},{10,9... | collective-permute-start | bytes 1228808 | tf_op jit(solution)/shard_map/ppermute | solution.py:52
  116.2 3.6 %convolution_bitcast_fusion = f32[1280,640]{1,0:T(8,128)} fusion(bf16[4,64,1280]{2,1,0:T(8,128)(2,1)} %all-to-all-done.2, bf16[4,64,1280]{2,1,0:T(8,128)(2,1)} %copy-done.2), kind=kOutput, calls=%fused_computation.2 | convolution fusion | flops 419430400 | bytes 4259840 | tf_op jit(solution)/shard_map/dot_general | solution.py:45
  123.3 4.2 %all-to-all-start.3 = ((bf16[8,64,640]{2,1,0:T(8,128)(2,1)}), bf16[8,64,640]{2,1,0:T(8,128)(2,1)}, u32[]{:S(2)}, u32[]{:S(2)}) async-start(bf16[8,64,640]{2,1,0:T(8,128)(2,1)} %bitcast.97), calls=%async_computation.3 | async-start | bytes 1310720 | tf_op jit(solution)/shard_map/all_to_all | solution.py:21
  127.5 2.9 %fusion.1 = bf16[1280,640]{1,0:T(8,128)(2,1)S(1)} fusion(f32[1280,640]{1,0:T(8,128)} %convolution_bitcast_fusion, bf16[256,1280]{1,0:T(8,128)(2,1)} %copy-done.3, bf16[256,640]{1,0:T(8,128)(2,1)} %bitcast.99), kind=kOutput, calls=%fused_computation.4 | convolution fusion | flops 421068800 | bytes 5898240 | tf_op jit(solution)/shard_map/dot_general | solution.py:45
  132.2 2.5 %collective-permute-start.13 = (bf16[2,160,640]{2,1,0:T(8,128)(2,1)}, bf16[2,160,640]{2,1,0:T(8,128)(2,1)}, u32[]{:S(2)}, u32[]{:S(2)}) collective-permute-start(bf16[2,160,640]{2,1,0:T(8,128)(2,1)} %pad_maximum_fusion.4), channel_id=1, source_target_pairs={{0,7},{1,0},{2,1},{3,2},{4,3},{5,4},{6,5},{7,6},{8,15},{9,8},{10,9... | collective-permute-start | bytes 1228808 | tf_op jit(solution)/shard_map/ppermute | solution.py:52
  135.5 3.4 %collective-permute-start.11 = (bf16[2,160,640]{2,1,0:T(8,128)(2,1)}, bf16[2,160,640]{2,1,0:T(8,128)(2,1)}, u32[]{:S(2)}, u32[]{:S(2)}) collective-permute-start(bf16[2,160,640]{2,1,0:T(8,128)(2,1)} %pad_maximum_fusion.3), channel_id=1, source_target_pairs={{0,1},{1,2},{2,3},{3,4},{4,5},{5,6},{6,7},{7,0},{8,9},{9,10},{10,1... | collective-permute-start | bytes 1228808 | tf_op jit(solution)/shard_map/ppermute | solution.py:52
  138.9 1.9 %collective-permute-start.10 = (bf16[160,640]{1,0:T(8,128)(2,1)}, bf16[160,640]{1,0:T(8,128)(2,1)S(1)}, u32[]{:S(2)}, u32[]{:S(2)}) collective-permute-start(bf16[160,640]{1,0:T(8,128)(2,1)} %get-tuple-element.23), channel_id=1, source_target_pairs={{0,4},{1,5},{2,6},{3,7},{4,0},{5,1},{6,2},{7,3},{8,12},{9,13},{10,... | collective-permute-start | bytes 614408 | tf_op jit(solution)/shard_map/ppermute | solution.py:52
  142.0 2.5 %collective-permute-start.9 = (bf16[160,640]{1,0:T(8,128)(2,1)S(1)}, bf16[160,640]{1,0:T(8,128)(2,1)S(1)}, u32[]{:S(2)}, u32[]{:S(2)}) collective-permute-start(bf16[160,640]{1,0:T(8,128)(2,1)S(1)} %get-tuple-element.21), channel_id=1, source_target_pairs={{0,6},{1,7},{2,0},{3,1},{4,2},{5,3},{6,4},{7,5},{8,14},{9,15},{10,... | collective-permute-start | bytes 614408 | tf_op jit(solution)/shard_map/ppermute | solution.py:52
  144.5 4.3 %collective-permute-start.8 = (bf16[160,640]{1,0:T(8,128)(2,1)S(1)}, bf16[160,640]{1,0:T(8,128)(2,1)S(1)}, u32[]{:S(2)}, u32[]{:S(2)}) collective-permute-start(bf16[160,640]{1,0:T(8,128)(2,1)S(1)} %get-tuple-element.20), channel_id=1, source_target_pairs={{0,2},{1,3},{2,4},{3,5},{4,6},{5,7},{6,0},{7,1},{8,10},{9,11},{10,... | collective-permute-start | bytes 614408 | tf_op jit(solution)/shard_map/ppermute | solution.py:52
  148.8 7.8 %collective-permute-start.15 = (bf16[160,640]{1,0:T(8,128)(2,1)}, bf16[160,640]{1,0:T(8,128)(2,1)S(1)}, u32[]{:S(2)}, u32[]{:S(2)}) collective-permute-start(bf16[160,640]{1,0:T(8,128)(2,1)} %get-tuple-element.16), channel_id=1, source_target_pairs={{0,4},{1,5},{2,6},{3,7},{4,0},{5,1},{6,2},{7,3},{8,12},{9,13},{10,... | collective-permute-start | bytes 614408 | tf_op jit(solution)/shard_map/ppermute | solution.py:52
  156.6 18.7 %collective-permute-done.11 = bf16[2,160,640]{2,1,0:T(8,128)(2,1)} collective-permute-done((bf16[2,160,640]{2,1,0:T(8,128)(2,1)}, bf16[2,160,640]{2,1,0:T(8,128)(2,1)}, u32[]{:S(2)}, u32[]{:S(2)}) %collective-permute-start.11) | collective-permute-done | bytes 409632 | tf_op jit(solution)/shard_map/ppermute | solution.py:52
  175.3 2.1 %fusion.36 = (bf16[160,640]{1,0:T(8,128)(2,1)}, bf16[160,640]{1,0:T(8,128)(2,1)}) fusion(bf16[2,160,640]{2,1,0:T(8,128)(2,1)} %collective-permute-done.13, bf16[8,160,640]{2,1,0:T(8,128)(2,1)} %bitcast.92, s32[]{:T(128)S(6)} %select_n.170, bf16[2,160,640]{2,1,0:T(8,128)(2,1)} %collective-permute-done.11, s32[]{:T(128)S(6)} %select_n.168), kind=kLoop, calls=%fused_computation.67 | loop fusion | flops 819200 | bytes 1228808 | tf_op jit(solution)/shard_map/convert_element_type | solution.py:86
  177.4 1.9 collective-permute-start.12
  179.4 6.0 %collective-permute-start.14 = (bf16[160,640]{1,0:T(8,128)(2,1)}, bf16[160,640]{1,0:T(8,128)(2,1)}, u32[]{:S(2)}, u32[]{:S(2)}) collective-permute-start(bf16[160,640]{1,0:T(8,128)(2,1)} %get-tuple-element.13), channel_id=1, source_target_pairs={{0,6},{1,7},{2,0},{3,1},{4,2},{5,3},{6,4},{7,5},{8,14},{9,15},{10,... | collective-permute-start | bytes 614408 | tf_op jit(solution)/shard_map/ppermute | solution.py:52
  185.4 1.9 %fusion.6 = f32[160,640]{1,0:T(8,128)} fusion(bf16[160,640]{1,0:T(8,128)(2,1)S(1)} %collective-permute-done.10, bf16[160,640]{1,0:T(8,128)(2,1)S(1)} %collective-permute-done.9, bf16[160,640]{1,0:T(8,128)(2,1)S(1)} %collective-permute-done.8, bf16[2,160,640]{2,1,0:T(8,128)(2,1)} %collective-permute-done.7, bf16[2,160,640]{2,1,0:T(8,128)(2,1)} %collective-permute-done.6, ...), kind=kLoop, calls=%fused_computation.30 | loop fusion | flops 1126400 | bytes 1638404 | tf_op jit(solution)/shard_map/add | solution.py:92
  187.4 1.8 reduce_sum.12
  189.2 2.2 %fusion.4 = f32[640,160]{0,1:T(8,128)} fusion(bf16[160,640]{1,0:T(8,128)(2,1)S(1)} %collective-permute-done.15, bf16[160,640]{1,0:T(8,128)(2,1)} %collective-permute-done.14, bf16[160,640]{1,0:T(8,128)(2,1)} %collective-permute-done.12, bf16[2,160,640]{2,1,0:T(8,128)(2,1)} %collective-permute-done.13, bf16[2,160,640]{2,1,0:T(8,128)(2,1)} %collective-permute-done.11, ...), kind=kLoop, calls=%fused_computation.27 | loop fusion | flops 1126400 | bytes 1638404 | tf_op jit(solution)/shard_map/transpose | solution.py:140
  (49 shorter events, 22.0 us)
Async XLA Ops:
  0.6 26.0 %copy-start = (bf16[1280,640]{1,0:T(8,128)(2,1)S(1)}, bf16[1280,640]{1,0:T(8,128)(2,1)}, u32[]{:S(2)}) copy-start(bf16[1280,640]{1,0:T(8,128)(2,1)} %param.9) | copy-start | bytes 4915204
  2.9 22.8 %all-to-all-start = ((bf16[8,64,1280]{2,1,0:T(8,128)(2,1)}), bf16[8,64,1280]{2,1,0:T(8,128)(2,1)S(1)}, u32[]{:S(2)}, u32[]{:S(2)}) async-start(bf16[8,64,1280]{2,1,0:T(8,128)(2,1)} %broadcast_in_dim.9), calls=%async_computation | async-start | bytes 2621440 | tf_op jit(solution)/shard_map/all_to_all | solution.py:17
  25.8 3.5 %copy-start.2 = (bf16[4,64,1280]{2,1,0:T(8,128)(2,1)}, bf16[4,64,1280]{2,1,0:T(8,128)(2,1)S(1)}, u32[]{:S(2)}) copy-start(bf16[4,64,1280]{2,1,0:T(8,128)(2,1)S(1)} %get-tuple-element.28) | copy-start | bytes 1966084
  27.4 4.0 %collective-permute-start = (bf16[256,1280]{1,0:T(8,128)(2,1)S(1)}, bf16[256,1280]{1,0:T(8,128)(2,1)S(1)}, u32[]{:S(2)}, u32[]{:S(2)}) collective-permute-start(bf16[256,1280]{1,0:T(8,128)(2,1)S(1)} %convolution_convert_fusion), channel_id=1, source_target_pairs={{0,64},{64,0},{1,65},{65,1},{2,66},{66,2},{3,67},{67,3},{4,68},{68... | collective-permute-start | bytes 1966088 | tf_op jit(solution)/shard_map/ppermute | solution.py:56
  32.9 43.1 %all-to-all-start.1 = ((bf16[4,64,1280]{2,1,0:T(8,128)(2,1)}), bf16[4,64,1280]{2,1,0:T(8,128)(2,1)S(1)}, u32[]{:S(2)}, u32[]{:S(2)}) async-start(bf16[4,64,1280]{2,1,0:T(8,128)(2,1)} %bitcast.98), calls=%async_computation.1 | async-start | bytes 1310720 | tf_op jit(solution)/shard_map/all_to_all | solution.py:21
  40.3 31.8 %collective-permute-start.4 = (bf16[64,1280]{1,0:T(8,128)(2,1)S(1)}, bf16[64,1280]{1,0:T(8,128)(2,1)}, u32[]{:S(2)}, u32[]{:S(2)}) collective-permute-start(bf16[64,1280]{1,0:T(8,128)(2,1)S(1)} %get-tuple-element.9), channel_id=1, source_target_pairs={{0,128},{128,256},{256,384},{384,0},{1,129},{129,257},{257,385},{3... | collective-permute-start | bytes 491528 | tf_op jit(solution)/shard_map/ppermute | solution.py:52
  45.1 27.0 %collective-permute-start.3 = (bf16[64,1280]{1,0:T(8,128)(2,1)S(1)}, bf16[64,1280]{1,0:T(8,128)(2,1)}, u32[]{:S(2)}, u32[]{:S(2)}) collective-permute-start(bf16[64,1280]{1,0:T(8,128)(2,1)S(1)} %get-tuple-element.9), channel_id=1, source_target_pairs={{0,256},{128,384},{256,0},{384,128},{1,257},{129,385},{257,1},{385... | collective-permute-start | bytes 491528 | tf_op jit(solution)/shard_map/ppermute | solution.py:52
  50.6 21.5 %collective-permute-start.2 = (bf16[64,1280]{1,0:T(8,128)(2,1)S(1)}, bf16[64,1280]{1,0:T(8,128)(2,1)}, u32[]{:S(2)}, u32[]{:S(2)}) collective-permute-start(bf16[64,1280]{1,0:T(8,128)(2,1)S(1)} %get-tuple-element.9), channel_id=1, source_target_pairs={{0,384},{128,0},{256,128},{384,256},{1,385},{129,1},{257,129},{385... | collective-permute-start | bytes 491528 | tf_op jit(solution)/shard_map/ppermute | solution.py:52
  74.1 9.0 %collective-permute-start.5 = (bf16[256,1280]{1,0:T(8,128)(2,1)}, bf16[256,1280]{1,0:T(8,128)(2,1)}, u32[]{:S(2)}, u32[]{:S(2)}) collective-permute-start(bf16[256,1280]{1,0:T(8,128)(2,1)} %maximum_maximum_fusion), channel_id=1, source_target_pairs={{0,64},{64,0},{1,65},{65,1},{2,66},{66,2},{3,67},{67,3},{4,68},{68... | collective-permute-start | bytes 1966088 | tf_op jit(solution)/shard_map/ppermute | solution.py:56
  77.0 24.4 %all-to-all-start.2 = ((bf16[4,64,1280]{2,1,0:T(8,128)(2,1)}), bf16[4,64,1280]{2,1,0:T(8,128)(2,1)}, u32[]{:S(2)}, u32[]{:S(2)}) async-start(bf16[4,64,1280]{2,1,0:T(8,128)(2,1)} %broadcast_in_dim.10), calls=%async_computation.2 | async-start | bytes 1310720 | tf_op jit(solution)/shard_map/all_to_all | solution.py:17
  86.6 54.2 %collective-permute-start.6 = (bf16[2,160,640]{2,1,0:T(8,128)(2,1)}, bf16[2,160,640]{2,1,0:T(8,128)(2,1)}, u32[]{:S(2)}, u32[]{:S(2)}) collective-permute-start(bf16[2,160,640]{2,1,0:T(8,128)(2,1)} %pad_maximum_fusion.1), channel_id=1, source_target_pairs={{0,1},{1,2},{2,3},{3,4},{4,5},{5,6},{6,7},{7,0},{8,9},{9,10},{10,1... | collective-permute-start | bytes 1228808 | tf_op jit(solution)/shard_map/ppermute | solution.py:52
  101.4 20.1 %collective-permute-start.1 = (bf16[256,1280]{1,0:T(8,128)(2,1)}, bf16[256,1280]{1,0:T(8,128)(2,1)S(1)}, u32[]{:S(2)}, u32[]{:S(2)}) collective-permute-start(bf16[256,1280]{1,0:T(8,128)(2,1)} %bitcast.11), channel_id=1, source_target_pairs={{0,64},{64,0},{1,65},{65,1},{2,66},{66,2},{3,67},{67,3},{4,68},{68... | collective-permute-start | bytes 1966088 | tf_op jit(solution)/shard_map/ppermute | solution.py:56
  105.1 14.6 %copy-start.4 = (bf16[640,1280]{1,0:T(8,128)(2,1)S(1)}, bf16[640,1280]{1,0:T(8,128)(2,1)}, u32[]{:S(2)}) copy-start(bf16[640,1280]{1,0:T(8,128)(2,1)} %param.8) | copy-start | bytes 4915204
  105.1 35.8 %collective-permute-start.7 = (bf16[2,160,640]{2,1,0:T(8,128)(2,1)}, bf16[2,160,640]{2,1,0:T(8,128)(2,1)}, u32[]{:S(2)}, u32[]{:S(2)}) collective-permute-start(bf16[2,160,640]{2,1,0:T(8,128)(2,1)} %pad_maximum_fusion.2), channel_id=1, source_target_pairs={{0,7},{1,0},{2,1},{3,2},{4,3},{5,4},{6,5},{7,6},{8,15},{9,8},{10,9... | collective-permute-start | bytes 1228808 | tf_op jit(solution)/shard_map/ppermute | solution.py:52
  121.6 0.9 copy-start.3
  123.3 64.0 %all-to-all-start.3 = ((bf16[8,64,640]{2,1,0:T(8,128)(2,1)}), bf16[8,64,640]{2,1,0:T(8,128)(2,1)}, u32[]{:S(2)}, u32[]{:S(2)}) async-start(bf16[8,64,640]{2,1,0:T(8,128)(2,1)} %bitcast.97), calls=%async_computation.3 | async-start | bytes 1310720 | tf_op jit(solution)/shard_map/all_to_all | solution.py:21
  130.5 5.0 %copy-start.1 = (bf16[1280,640]{1,0:T(8,128)(2,1)}, bf16[1280,640]{1,0:T(8,128)(2,1)S(1)}, u32[]{:S(2)}) copy-start(bf16[1280,640]{1,0:T(8,128)(2,1)S(1)} %fusion.1) | copy-start | bytes 4915204
  132.2 16.5 %collective-permute-start.13 = (bf16[2,160,640]{2,1,0:T(8,128)(2,1)}, bf16[2,160,640]{2,1,0:T(8,128)(2,1)}, u32[]{:S(2)}, u32[]{:S(2)}) collective-permute-start(bf16[2,160,640]{2,1,0:T(8,128)(2,1)} %pad_maximum_fusion.4), channel_id=1, source_target_pairs={{0,7},{1,0},{2,1},{3,2},{4,3},{5,4},{6,5},{7,6},{8,15},{9,8},{10,9... | collective-permute-start | bytes 1228808 | tf_op jit(solution)/shard_map/ppermute | solution.py:52
  135.5 39.8 %collective-permute-start.11 = (bf16[2,160,640]{2,1,0:T(8,128)(2,1)}, bf16[2,160,640]{2,1,0:T(8,128)(2,1)}, u32[]{:S(2)}, u32[]{:S(2)}) collective-permute-start(bf16[2,160,640]{2,1,0:T(8,128)(2,1)} %pad_maximum_fusion.3), channel_id=1, source_target_pairs={{0,1},{1,2},{2,3},{3,4},{4,5},{5,6},{6,7},{7,0},{8,9},{9,10},{10,1... | collective-permute-start | bytes 1228808 | tf_op jit(solution)/shard_map/ppermute | solution.py:52
  138.9 40.4 %collective-permute-start.10 = (bf16[160,640]{1,0:T(8,128)(2,1)}, bf16[160,640]{1,0:T(8,128)(2,1)S(1)}, u32[]{:S(2)}, u32[]{:S(2)}) collective-permute-start(bf16[160,640]{1,0:T(8,128)(2,1)} %get-tuple-element.23), channel_id=1, source_target_pairs={{0,4},{1,5},{2,6},{3,7},{4,0},{5,1},{6,2},{7,3},{8,12},{9,13},{10,... | collective-permute-start | bytes 614408 | tf_op jit(solution)/shard_map/ppermute | solution.py:52
  142.0 43.4 %collective-permute-start.9 = (bf16[160,640]{1,0:T(8,128)(2,1)S(1)}, bf16[160,640]{1,0:T(8,128)(2,1)S(1)}, u32[]{:S(2)}, u32[]{:S(2)}) collective-permute-start(bf16[160,640]{1,0:T(8,128)(2,1)S(1)} %get-tuple-element.21), channel_id=1, source_target_pairs={{0,6},{1,7},{2,0},{3,1},{4,2},{5,3},{6,4},{7,5},{8,14},{9,15},{10,... | collective-permute-start | bytes 614408 | tf_op jit(solution)/shard_map/ppermute | solution.py:52
  144.5 40.9 %collective-permute-start.8 = (bf16[160,640]{1,0:T(8,128)(2,1)S(1)}, bf16[160,640]{1,0:T(8,128)(2,1)S(1)}, u32[]{:S(2)}, u32[]{:S(2)}) collective-permute-start(bf16[160,640]{1,0:T(8,128)(2,1)S(1)} %get-tuple-element.20), channel_id=1, source_target_pairs={{0,2},{1,3},{2,4},{3,5},{4,6},{5,7},{6,0},{7,1},{8,10},{9,11},{10,... | collective-permute-start | bytes 614408 | tf_op jit(solution)/shard_map/ppermute | solution.py:52
  148.8 40.4 %collective-permute-start.15 = (bf16[160,640]{1,0:T(8,128)(2,1)}, bf16[160,640]{1,0:T(8,128)(2,1)S(1)}, u32[]{:S(2)}, u32[]{:S(2)}) collective-permute-start(bf16[160,640]{1,0:T(8,128)(2,1)} %get-tuple-element.16), channel_id=1, source_target_pairs={{0,4},{1,5},{2,6},{3,7},{4,0},{5,1},{6,2},{7,3},{8,12},{9,13},{10,... | collective-permute-start | bytes 614408 | tf_op jit(solution)/shard_map/ppermute | solution.py:52
  177.4 11.8 %collective-permute-start.12 = (bf16[160,640]{1,0:T(8,128)(2,1)}, bf16[160,640]{1,0:T(8,128)(2,1)}, u32[]{:S(2)}, u32[]{:S(2)}) collective-permute-start(bf16[160,640]{1,0:T(8,128)(2,1)} %get-tuple-element.14), channel_id=1, source_target_pairs={{0,2},{1,3},{2,4},{3,5},{4,6},{5,7},{6,0},{7,1},{8,10},{9,11},{10,... | collective-permute-start | bytes 614408 | tf_op jit(solution)/shard_map/ppermute | solution.py:52
  179.4 9.8 %collective-permute-start.14 = (bf16[160,640]{1,0:T(8,128)(2,1)}, bf16[160,640]{1,0:T(8,128)(2,1)}, u32[]{:S(2)}, u32[]{:S(2)}) collective-permute-start(bf16[160,640]{1,0:T(8,128)(2,1)} %get-tuple-element.13), channel_id=1, source_target_pairs={{0,6},{1,7},{2,0},{3,1},{4,2},{5,3},{6,4},{7,5},{8,14},{9,15},{10,... | collective-permute-start | bytes 614408 | tf_op jit(solution)/shard_map/ppermute | solution.py:52

commit v9 on v7

--- a/solution.py
+++ b/solution.py
@@ -103,22 +103,24 @@
     active, slope = lax.optimization_barrier((active.astype(jnp.bfloat16), slope))
     active_mine = gathered(active)
 
-    both = spread(jnp.concatenate([grad_out[0], inputs[0]], axis=1), COL)
-    width = inputs.shape[2]
-    both = both.reshape(4, 2, *both.shape[1:])
-    of = lambda c: lax.dynamic_index_in_dim(both, c, 1, keepdims=False)
-    mine, other = of(core), of(1 - core)
+    by_core = lambda blocks: blocks.reshape(4, 2, *blocks.shape[1:])
+    of = lambda blocks, c: lax.dynamic_index_in_dim(blocks, c, 1, keepdims=False)
     flat = lambda blocks: blocks.reshape(-1, blocks.shape[-1])
-    away = contract_last(flat(other[..., :width]), weight_down).astype(jnp.bfloat16)
+    layer_grads = by_core(spread(grad_out[0], COL))
+    layer_inputs = by_core(spread(inputs[0], COL))
+    grads_mine, grads_other = of(layer_grads, core), of(layer_grads, 1 - core)
+    away = contract_last(flat(grads_other), weight_down).astype(jnp.bfloat16)
     back = swapped(away)
-    kept = contract_last(flat(mine[..., :width]), weight_down)
+    kept = contract_last(flat(grads_mine), weight_down)
     pair = (kept + wide(back)).astype(jnp.bfloat16).reshape(4, 64, -1)
     came = exchanged(pair, "yhi")
+    layer_inputs, _ = lax.optimization_barrier((layer_inputs, pair))
+    inputs_mine, inputs_other = of(layer_inputs, core), of(layer_inputs, 1 - core)
 
     active_other = swapped(active_mine)
     turned = lambda blocks: jnp.concatenate([block_at(blocks, (high + u) % 4) for u in range(4)], axis=0)
-    lower_mine = lax.optimization_barrier(contract_first(active_mine, turned(mine[..., :width])))
-    lower = contract_first(active_other, turned(other[..., :width])) + lower_mine
+    lower_mine = lax.optimization_barrier(contract_first(active_mine, turned(grads_mine)))
+    lower = contract_first(active_other, turned(grads_other)) + lower_mine
     lower = lower.astype(jnp.bfloat16)
     lower_parts = depth_parts(lower.reshape(8, -1, lower.shape[1]), True)
 
@@ -126,8 +128,8 @@
     delta_mine = flat(spread(delta_own, "yhi"))
     delta_other = swapped(delta_mine)
 
-    upper_mine = lax.optimization_barrier(contract_first(delta_mine, flat(mine[..., width:])))
-    upper = contract_first(delta_other, flat(other[..., width:])) + upper_mine
+    upper_mine = lax.optimization_barrier(contract_first(delta_mine, flat(inputs_mine)))
+    upper = contract_first(delta_other, flat(inputs_other)) + upper_mine
     upper = upper.astype(jnp.bfloat16)
     near, last_up, last_down = depth_parts(upper.reshape(8, -1, upper.shape[1]), False)
 

time: 186 us -> 190 us (1.022)
  the two profiles are of different devices: /device:TPU:2 before, /device:TPU:1 now
where the time goes in v9:
time: 190 us; the launch traced here: 189 us
  starting transfers between devices  88.9 us (47%)
  waiting for transfers between devices  39.3 us (21%)
  blocking collectives  20 us (11%)
  other arithmetic  17.4 us (9%)
  matrix products  14.1 us (7%)
  local copies, waits for them, and re-layouts  7.89 us (4%)
    ppermute x12, starting transfers between devices, shifted(): lax.ppermute(value, axis, [(k, (k + by) % length) for k in range(length)])  52.2 us
    all_to_all x1, blocking collectives, exchanged(): return lax.all_to_all(value, axis, split_axis=0, concat_axis=0, tiled=True)  20 us
    ppermute x12, waiting for transfers between devices, shifted(): lax.ppermute(value, axis, [(k, (k + by) % length) for k in range(length)])  17.8 us
    all_to_all x3, starting transfers between devices, spread(): return lax.all_to_all(copies, axis, split_axis=0, concat_axis=0, tiled=True)  16.2 us
    ppermute x3, starting transfers between devices, swapped(): return lax.ppermute(value, 'core', SWAP)  12.2 us
    ppermute x1, waiting for transfers between devices, depth_parts(): turn = wide(lax.ppermute(pick(4), 'depth', turns))  12.1 us
    dot_general x4, matrix products, contract_first(): lax.dot_general(left, right, (((0,), (0,)), ((), ())), preferred_element_...  10.2 us
    all_to_all x3, waiting for transfers between devices, spread(): return lax.all_to_all(copies, axis, split_axis=0, concat_axis=0, tiled=True)  7.66 us
  transfers between devices with their start and end apart: 20, of which 7 were waited for; matrix products, arithmetic and copies ran while one was open for 17% of the time, Pallas kernels for 0%

profile of v9, /device:TPU:1, one launch (start us, length us, event | category | flops | bytes accessed | tf_op | source)
XLA Modules:
  0.0 188.8 jit_solution(735113991895759283)
XLA Ops:
  2.6 5.9 %all-to-all-start = ((bf16[8,64,640]{2,1,0:T(8,128)(2,1)}), bf16[8,64,640]{2,1,0:T(8,128)(2,1)S(1)}, u32[]{:S(2)}, u32[]{:S(2)}) async-start(bf16[8,64,640]{2,1,0:T(8,128)(2,1)} %broadcast_in_dim.18), calls=%async_computation | async-start | bytes 1310720 | tf_op jit(solution)/shard_map/all_to_all | solution.py:17
  8.4 7.7 %all-to-all-done = bf16[8,64,640]{2,1,0:T(8,128)(2,1)S(1)} async-done(((bf16[8,64,640]{2,1,0:T(8,128)(2,1)}), bf16[8,64,640]{2,1,0:T(8,128)(2,1)S(1)}, u32[]{:S(2)}, u32[]{:S(2)}) %all-to-all-start) | async-done | bytes 655392 | tf_op jit(solution)/shard_map/all_to_all | solution.py:17
  16.9 7.5 %collective-permute-start = (bf16[256,1280]{1,0:T(8,128)(2,1)S(1)}, bf16[256,1280]{1,0:T(8,128)(2,1)S(1)}, u32[]{:S(2)}, u32[]{:S(2)}) collective-permute-start(bf16[256,1280]{1,0:T(8,128)(2,1)S(1)} %convolution_convert_fusion), channel_id=1, source_target_pairs={{0,64},{64,0},{1,65},{65,1},{2,66},{66,2},{3,67},{67,3},{4,68},{68... | collective-permute-start | bytes 1966088 | tf_op jit(solution)/shard_map/ppermute | solution.py:56
  26.8 20.0 %all_to_all.25 = bf16[4,64,1280]{2,1,0:T(8,128)(2,1)} all-to-all(bf16[4,64,1280]{2,1,0:T(8,128)(2,1)S(1)} %bitcast.93), channel_id=1, replica_groups=mesh['yhi'=4,'core'=2,'ylo'=2,'x'=4,'depth'=8] {'yhi'}, dimensions={0} | all-to-all | bytes 1310720 | tf_op jit(solution)/shard_map/all_to_all | solution.py:21
  47.7 6.2 %all-to-all-start.4 = ((bf16[8,64,640]{2,1,0:T(8,128)(2,1)}), bf16[8,64,640]{2,1,0:T(8,128)(2,1)S(1)}, u32[]{:S(2)}, u32[]{:S(2)}) async-start(bf16[8,64,640]{2,1,0:T(8,128)(2,1)} %broadcast_in_dim.21), calls=%async_computation.4 | async-start | bytes 1310720 | tf_op jit(solution)/shard_map/all_to_all | solution.py:17
  55.1 3.3 %collective-permute-start.4 = (bf16[64,1280]{1,0:T(8,128)(2,1)S(1)}, bf16[64,1280]{1,0:T(8,128)(2,1)}, u32[]{:S(2)}, u32[]{:S(2)}) collective-permute-start(bf16[64,1280]{1,0:T(8,128)(2,1)S(1)} %get-tuple-element.10), channel_id=1, source_target_pairs={{0,128},{128,256},{256,384},{384,0},{1,129},{129,257},{257,385},{3... | collective-permute-start | bytes 491528 | tf_op jit(solution)/shard_map/ppermute | solution.py:52
  58.4 4.6 %collective-permute-start.3 = (bf16[64,1280]{1,0:T(8,128)(2,1)S(1)}, bf16[64,1280]{1,0:T(8,128)(2,1)}, u32[]{:S(2)}, u32[]{:S(2)}) collective-permute-start(bf16[64,1280]{1,0:T(8,128)(2,1)S(1)} %get-tuple-element.10), channel_id=1, source_target_pairs={{0,256},{128,384},{256,0},{384,128},{1,257},{129,385},{257,1},{385... | collective-permute-start | bytes 491528 | tf_op jit(solution)/shard_map/ppermute | solution.py:52
  63.0 3.4 %collective-permute-start.2 = (bf16[64,1280]{1,0:T(8,128)(2,1)S(1)}, bf16[64,1280]{1,0:T(8,128)(2,1)}, u32[]{:S(2)}, u32[]{:S(2)}) collective-permute-start(bf16[64,1280]{1,0:T(8,128)(2,1)S(1)} %get-tuple-element.10), channel_id=1, source_target_pairs={{0,384},{128,0},{256,128},{384,256},{1,385},{129,1},{257,129},{385... | collective-permute-start | bytes 491528 | tf_op jit(solution)/shard_map/ppermute | solution.py:52
  66.6 4.0 %collective-permute-done.4 = bf16[64,1280]{1,0:T(8,128)(2,1)} collective-permute-done((bf16[64,1280]{1,0:T(8,128)(2,1)S(1)}, bf16[64,1280]{1,0:T(8,128)(2,1)}, u32[]{:S(2)}, u32[]{:S(2)}) %collective-permute-start.4) | collective-permute-done | bytes 163872 | tf_op jit(solution)/shard_map/ppermute | solution.py:52
  70.6 3.6 %collective-permute-done.3 = bf16[64,1280]{1,0:T(8,128)(2,1)} collective-permute-done((bf16[64,1280]{1,0:T(8,128)(2,1)S(1)}, bf16[64,1280]{1,0:T(8,128)(2,1)}, u32[]{:S(2)}, u32[]{:S(2)}) %collective-permute-start.3) | collective-permute-done | bytes 163872 | tf_op jit(solution)/shard_map/ppermute | solution.py:52
  74.2 6.7 %collective-permute-done.2 = bf16[64,1280]{1,0:T(8,128)(2,1)} collective-permute-done((bf16[64,1280]{1,0:T(8,128)(2,1)S(1)}, bf16[64,1280]{1,0:T(8,128)(2,1)}, u32[]{:S(2)}, u32[]{:S(2)}) %collective-permute-start.2) | collective-permute-done | bytes 163872 | tf_op jit(solution)/shard_map/ppermute | solution.py:52
  80.9 2.0 %maximum_maximum_fusion = bf16[256,1280]{1,0:T(8,128)(2,1)} fusion(bf16[64,1280]{1,0:T(8,128)(2,1)} %collective-permute-done.4, bf16[64,1280]{1,0:T(8,128)(2,1)} %collective-permute-done.3, bf16[64,1280]{1,0:T(8,128)(2,1)} %collective-permute-done.2, bf16[64,1280]{1,0:T(8,128)(2,1)S(1)} %get-tuple-element.10), kind=kLoop, calls=%fused_computation.16 | loop fusion | flops 2621440 | bytes 1310720 | tf_op jit(solution)/shard_map/max | solution.py:68
  82.9 2.5 %collective-permute-start.5 = (bf16[256,1280]{1,0:T(8,128)(2,1)}, bf16[256,1280]{1,0:T(8,128)(2,1)}, u32[]{:S(2)}, u32[]{:S(2)}) collective-permute-start(bf16[256,1280]{1,0:T(8,128)(2,1)} %maximum_maximum_fusion), channel_id=1, source_target_pairs={{0,64},{64,0},{1,65},{65,1},{2,66},{66,2},{3,67},{67,3},{4,68},{68... | collective-permute-start | bytes 1966088 | tf_op jit(solution)/shard_map/ppermute | solution.py:56
  86.2 2.0 %broadcast_in_dim.19 = bf16[4,64,1280]{2,1,0:T(8,128)(2,1)} broadcast(bf16[64,1280]{1,0:T(8,128)(2,1)} %fusion.34), dimensions={1,2} | broadcast | bytes 819200 | tf_op jit(solution)/shard_map/broadcast_in_dim | solution.py:16
  88.2 4.2 %all-to-all-start.2 = ((bf16[4,64,1280]{2,1,0:T(8,128)(2,1)}), bf16[4,64,1280]{2,1,0:T(8,128)(2,1)}, u32[]{:S(2)}, u32[]{:S(2)}) async-start(bf16[4,64,1280]{2,1,0:T(8,128)(2,1)} %broadcast_in_dim.19), calls=%async_computation.2 | async-start | bytes 1310720 | tf_op jit(solution)/shard_map/all_to_all | solution.py:17
  97.7 3.9 %collective-permute-start.6 = (bf16[2,160,640]{2,1,0:T(8,128)(2,1)}, bf16[2,160,640]{2,1,0:T(8,128)(2,1)}, u32[]{:S(2)}, u32[]{:S(2)}) collective-permute-start(bf16[2,160,640]{2,1,0:T(8,128)(2,1)} %pad_maximum_fusion.1), channel_id=1, source_target_pairs={{0,1},{1,2},{2,3},{3,4},{4,5},{5,6},{6,7},{7,0},{8,9},{9,10},{10,1... | collective-permute-start | bytes 1228808 | tf_op jit(solution)/shard_map/ppermute | solution.py:52
  102.4 8.6 %collective-permute-start.7 = (bf16[2,160,640]{2,1,0:T(8,128)(2,1)}, bf16[2,160,640]{2,1,0:T(8,128)(2,1)}, u32[]{:S(2)}, u32[]{:S(2)}) collective-permute-start(bf16[2,160,640]{2,1,0:T(8,128)(2,1)} %pad_maximum_fusion.2), channel_id=1, source_target_pairs={{0,7},{1,0},{2,1},{3,2},{4,3},{5,4},{6,5},{7,6},{8,15},{9,8},{10,9... | collective-permute-start | bytes 1228808 | tf_op jit(solution)/shard_map/ppermute | solution.py:52
  111.0 2.2 %collective-permute-start.1 = (bf16[256,1280]{1,0:T(8,128)(2,1)}, bf16[256,1280]{1,0:T(8,128)(2,1)S(1)}, u32[]{:S(2)}, u32[]{:S(2)}) collective-permute-start(bf16[256,1280]{1,0:T(8,128)(2,1)} %bitcast.8), channel_id=1, source_target_pairs={{0,64},{64,0},{1,65},{65,1},{2,66},{66,2},{3,67},{67,3},{4,68},{68... | collective-permute-start | bytes 1966088 | tf_op jit(solution)/shard_map/ppermute | solution.py:56
  115.1 3.6 %fusion.39 = f32[1280,640]{1,0:T(8,128)} fusion(bf16[256,1280]{1,0:T(8,128)(2,1)} %bitcast.8, bf16[256,640]{1,0:T(8,128)(2,1)S(1)} %bitcast.95), kind=kOutput, calls=%fused_computation.89 | convolution fusion | flops 419430400 | bytes 4259840 | tf_op jit(solution)/shard_map/dot_general | solution.py:45
  122.3 4.2 %all-to-all-start.3 = ((bf16[8,64,640]{2,1,0:T(8,128)(2,1)}), bf16[8,64,640]{2,1,0:T(8,128)(2,1)}, u32[]{:S(2)}, u32[]{:S(2)}) async-start(bf16[8,64,640]{2,1,0:T(8,128)(2,1)} %bitcast.92), calls=%async_computation.3 | async-start | bytes 1310720 | tf_op jit(solution)/shard_map/all_to_all | solution.py:21
  126.5 3.0 %fusion.1 = bf16[1280,640]{1,0:T(8,128)(2,1)S(1)} fusion(f32[1280,640]{1,0:T(8,128)} %fusion.39, bf16[256,1280]{1,0:T(8,128)(2,1)} %copy-done.4, bf16[256,640]{1,0:T(8,128)(2,1)} %bitcast.94), kind=kOutput, calls=%fused_computation.3 | convolution fusion | flops 421068800 | bytes 5898240 | tf_op jit(solution)/shard_map/dot_general | solution.py:45
  130.6 9.5 %collective-permute-start.14 = (bf16[2,160,640]{2,1,0:T(8,128)(2,1)}, bf16[2,160,640]{2,1,0:T(8,128)(2,1)}, u32[]{:S(2)}, u32[]{:S(2)}) collective-permute-start(bf16[2,160,640]{2,1,0:T(8,128)(2,1)} %pad_maximum_fusion.4), channel_id=1, source_target_pairs={{0,7},{1,0},{2,1},{3,2},{4,3},{5,4},{6,5},{7,6},{8,15},{9,8},{10,9... | collective-permute-start | bytes 1228808 | tf_op jit(solution)/shard_map/ppermute | solution.py:52
  142.8 3.3 %collective-permute-start.10 = (bf16[160,640]{1,0:T(8,128)(2,1)}, bf16[160,640]{1,0:T(8,128)(2,1)S(1)}, u32[]{:S(2)}, u32[]{:S(2)}) collective-permute-start(bf16[160,640]{1,0:T(8,128)(2,1)} %get-tuple-element.25), channel_id=1, source_target_pairs={{0,4},{1,5},{2,6},{3,7},{4,0},{5,1},{6,2},{7,3},{8,12},{9,13},{10,... | collective-permute-start | bytes 614408 | tf_op jit(solution)/shard_map/ppermute | solution.py:52
  146.2 4.0 %collective-permute-start.12 = (bf16[160,640]{1,0:T(8,128)(2,1)S(1)}, bf16[160,640]{1,0:T(8,128)(2,1)S(1)}, u32[]{:S(2)}, u32[]{:S(2)}) collective-permute-start(bf16[160,640]{1,0:T(8,128)(2,1)S(1)} %get-tuple-element.19), channel_id=1, source_target_pairs={{0,2},{1,7},{2,4},{3,1},{4,6},{5,3},{6,0},{7,5},{8,10},{9,15},{10,... | collective-permute-start | bytes 614408 | tf_op jit(solution)/shard_map/ppermute | solution.py:87
  151.4 3.4 %collective-permute-start.9 = (bf16[160,640]{1,0:T(8,128)(2,1)S(1)}, bf16[160,640]{1,0:T(8,128)(2,1)S(1)}, u32[]{:S(2)}, u32[]{:S(2)}) collective-permute-start(bf16[160,640]{1,0:T(8,128)(2,1)S(1)} %get-tuple-element.23), channel_id=1, source_target_pairs={{0,6},{1,7},{2,0},{3,1},{4,2},{5,3},{6,4},{7,5},{8,14},{9,15},{10,... | collective-permute-start | bytes 614408 | tf_op jit(solution)/shard_map/ppermute | solution.py:52
  154.8 12.1 %collective-permute-done.12 = bf16[160,640]{1,0:T(8,128)(2,1)S(1)} collective-permute-done((bf16[160,640]{1,0:T(8,128)(2,1)S(1)}, bf16[160,640]{1,0:T(8,128)(2,1)S(1)}, u32[]{:S(2)}, u32[]{:S(2)}) %collective-permute-start.12) | collective-permute-done | bytes 204832 | tf_op jit(solution)/shard_map/ppermute | solution.py:87
  166.9 3.0 %collective-permute-start.8 = (bf16[160,640]{1,0:T(8,128)(2,1)S(1)}, bf16[160,640]{1,0:T(8,128)(2,1)S(1)}, u32[]{:S(2)}, u32[]{:S(2)}) collective-permute-start(bf16[160,640]{1,0:T(8,128)(2,1)S(1)} %get-tuple-element.22), channel_id=1, source_target_pairs={{0,2},{1,3},{2,4},{3,5},{4,6},{5,7},{6,0},{7,1},{8,10},{9,11},{10,... | collective-permute-start | bytes 614408 | tf_op jit(solution)/shard_map/ppermute | solution.py:52
  169.9 2.1 %fusion.5 = (bf16[160,640]{1,0:T(8,128)(2,1)S(1)}, bf16[160,640]{1,0:T(8,128)(2,1)}) fusion(bf16[160,640]{1,0:T(8,128)(2,1)S(1)} %collective-permute-done.12, bf16[2,160,640]{2,1,0:T(8,128)(2,1)} %collective-permute-done.14, bf16[8,160,640]{2,1,0:T(8,128)(2,1)} %bitcast.87, s32[]{:T(128)S(6)} %select_n.208, pred[]{:T(512)S(6)} %eq.34, ...), kind=kLoop, calls=%fused_computation.22 | loop fusion | flops 1331200 | bytes 1433609 | tf_op jit(solution)/shard_map/convert_element_type | solution.py:90
  173.9 5.5 %collective-permute-start.15 = (bf16[160,640]{1,0:T(8,128)(2,1)S(1)}, bf16[160,640]{1,0:T(8,128)(2,1)}, u32[]{:S(2)}, u32[]{:S(2)}) collective-permute-start(bf16[160,640]{1,0:T(8,128)(2,1)S(1)} %get-tuple-element.15), channel_id=1, source_target_pairs={{0,6},{1,7},{2,0},{3,1},{4,2},{5,3},{6,4},{7,5},{8,14},{9,15},{10,... | collective-permute-start | bytes 614408 | tf_op jit(solution)/shard_map/ppermute | solution.py:52
  179.4 1.9 %fusion.9 = f32[160,640]{1,0:T(8,128)} fusion(bf16[160,640]{1,0:T(8,128)(2,1)S(1)} %collective-permute-done.10, bf16[160,640]{1,0:T(8,128)(2,1)S(1)} %collective-permute-done.9, bf16[160,640]{1,0:T(8,128)(2,1)S(1)} %collective-permute-done.8, bf16[2,160,640]{2,1,0:T(8,128)(2,1)} %collective-permute-done.7, bf16[2,160,640]{2,1,0:T(8,128)(2,1)} %collective-permute-done.6, ...), kind=kLoop, calls=%fused_computation.32 | loop fusion | flops 1126400 | bytes 1638404 | tf_op jit(solution)/shard_map/add | solution.py:96
  183.2 3.4 %collective-permute-done.15 = bf16[160,640]{1,0:T(8,128)(2,1)} collective-permute-done((bf16[160,640]{1,0:T(8,128)(2,1)S(1)}, bf16[160,640]{1,0:T(8,128)(2,1)}, u32[]{:S(2)}, u32[]{:S(2)}) %collective-permute-start.15) | collective-permute-done | bytes 204832 | tf_op jit(solution)/shard_map/ppermute | solution.py:52
  186.6 2.2 %fusion.7 = f32[640,160]{0,1:T(8,128)} fusion(bf16[160,640]{1,0:T(8,128)(2,1)} %collective-permute-done.15, bf16[160,640]{1,0:T(8,128)(2,1)} %collective-permute-done.13, bf16[2,160,640]{2,1,0:T(8,128)(2,1)} %collective-permute-done.14, bf16[2,160,640]{2,1,0:T(8,128)(2,1)} %collective-permute-done.11, bf16[8,160,640]{2,1,0:T(8,128)(2,1)} %bitcast.88, ...), kind=kLoop, calls=%fused_computation.29 | loop fusion | flops 921600 | bytes 1433604 | tf_op jit(solution)/shard_map/transpose | solution.py:146
  (52 shorter events, 28.2 us)
Async XLA Ops:
  0.6 15.5 %copy-start = (bf16[1280,640]{1,0:T(8,128)(2,1)S(1)}, bf16[1280,640]{1,0:T(8,128)(2,1)}, u32[]{:S(2)}) copy-start(bf16[1280,640]{1,0:T(8,128)(2,1)} %param.9) | copy-start | bytes 4915204
  2.6 13.5 %all-to-all-start = ((bf16[8,64,640]{2,1,0:T(8,128)(2,1)}), bf16[8,64,640]{2,1,0:T(8,128)(2,1)S(1)}, u32[]{:S(2)}, u32[]{:S(2)}) async-start(bf16[8,64,640]{2,1,0:T(8,128)(2,1)} %broadcast_in_dim.18), calls=%async_computation | async-start | bytes 1310720 | tf_op jit(solution)/shard_map/all_to_all | solution.py:17
  16.9 9.2 %collective-permute-start = (bf16[256,1280]{1,0:T(8,128)(2,1)S(1)}, bf16[256,1280]{1,0:T(8,128)(2,1)S(1)}, u32[]{:S(2)}, u32[]{:S(2)}) collective-permute-start(bf16[256,1280]{1,0:T(8,128)(2,1)S(1)} %convolution_convert_fusion), channel_id=1, source_target_pairs={{0,64},{64,0},{1,65},{65,1},{2,66},{66,2},{3,67},{67,3},{4,68},{68... | collective-permute-start | bytes 1966088 | tf_op jit(solution)/shard_map/ppermute | solution.py:56
  26.1 20.7 %copy-start.5 = (bf16[1,64,640]{2,1,0:T(8,128)(2,1)S(1)}, bf16[1,64,640]{2,1,0:T(8,128)(2,1)}, u32[]{:S(2)}) copy-start(bf16[1,64,640]{2,1,0:T(8,128)(2,1)} %param.5) | copy-start | bytes 245764
  47.7 38.5 %all-to-all-start.4 = ((bf16[8,64,640]{2,1,0:T(8,128)(2,1)}), bf16[8,64,640]{2,1,0:T(8,128)(2,1)S(1)}, u32[]{:S(2)}, u32[]{:S(2)}) async-start(bf16[8,64,640]{2,1,0:T(8,128)(2,1)} %broadcast_in_dim.21), calls=%async_computation.4 | async-start | bytes 1310720 | tf_op jit(solution)/shard_map/all_to_all | solution.py:17
  55.1 15.5 %collective-permute-start.4 = (bf16[64,1280]{1,0:T(8,128)(2,1)S(1)}, bf16[64,1280]{1,0:T(8,128)(2,1)}, u32[]{:S(2)}, u32[]{:S(2)}) collective-permute-start(bf16[64,1280]{1,0:T(8,128)(2,1)S(1)} %get-tuple-element.10), channel_id=1, source_target_pairs={{0,128},{128,256},{256,384},{384,0},{1,129},{129,257},{257,385},{3... | collective-permute-start | bytes 491528 | tf_op jit(solution)/shard_map/ppermute | solution.py:52
  58.4 15.8 %collective-permute-start.3 = (bf16[64,1280]{1,0:T(8,128)(2,1)S(1)}, bf16[64,1280]{1,0:T(8,128)(2,1)}, u32[]{:S(2)}, u32[]{:S(2)}) collective-permute-start(bf16[64,1280]{1,0:T(8,128)(2,1)S(1)} %get-tuple-element.10), channel_id=1, source_target_pairs={{0,256},{128,384},{256,0},{384,128},{1,257},{129,385},{257,1},{385... | collective-permute-start | bytes 491528 | tf_op jit(solution)/shard_map/ppermute | solution.py:52
  63.0 17.9 %collective-permute-start.2 = (bf16[64,1280]{1,0:T(8,128)(2,1)S(1)}, bf16[64,1280]{1,0:T(8,128)(2,1)}, u32[]{:S(2)}, u32[]{:S(2)}) collective-permute-start(bf16[64,1280]{1,0:T(8,128)(2,1)S(1)} %get-tuple-element.10), channel_id=1, source_target_pairs={{0,384},{128,0},{256,128},{384,256},{1,385},{129,1},{257,129},{385... | collective-permute-start | bytes 491528 | tf_op jit(solution)/shard_map/ppermute | solution.py:52
  66.6 18.8 %copy-start.3 = (bf16[4,64,1280]{2,1,0:T(8,128)(2,1)S(1)}, bf16[4,64,1280]{2,1,0:T(8,128)(2,1)}, u32[]{:S(2)}) copy-start(bf16[4,64,1280]{2,1,0:T(8,128)(2,1)} %all_to_all.25) | copy-start | bytes 1966084
  82.9 11.3 %collective-permute-start.5 = (bf16[256,1280]{1,0:T(8,128)(2,1)}, bf16[256,1280]{1,0:T(8,128)(2,1)}, u32[]{:S(2)}, u32[]{:S(2)}) collective-permute-start(bf16[256,1280]{1,0:T(8,128)(2,1)} %maximum_maximum_fusion), channel_id=1, source_target_pairs={{0,64},{64,0},{1,65},{65,1},{2,66},{66,2},{3,67},{67,3},{4,68},{68... | collective-permute-start | bytes 1966088 | tf_op jit(solution)/shard_map/ppermute | solution.py:56
  86.2 8.0 %copy-start.2 = (bf16[8,64,640]{2,1,0:T(8,128)(2,1)}, bf16[8,64,640]{2,1,0:T(8,128)(2,1)S(1)}, u32[]{:S(2)}) copy-start(bf16[8,64,640]{2,1,0:T(8,128)(2,1)S(1)} %all-to-all-done.4) | copy-start | bytes 1966084
  88.2 22.8 %all-to-all-start.2 = ((bf16[4,64,1280]{2,1,0:T(8,128)(2,1)}), bf16[4,64,1280]{2,1,0:T(8,128)(2,1)}, u32[]{:S(2)}, u32[]{:S(2)}) async-start(bf16[4,64,1280]{2,1,0:T(8,128)(2,1)} %broadcast_in_dim.19), calls=%async_computation.2 | async-start | bytes 1310720 | tf_op jit(solution)/shard_map/all_to_all | solution.py:17
  97.7 48.5 %collective-permute-start.6 = (bf16[2,160,640]{2,1,0:T(8,128)(2,1)}, bf16[2,160,640]{2,1,0:T(8,128)(2,1)}, u32[]{:S(2)}, u32[]{:S(2)}) collective-permute-start(bf16[2,160,640]{2,1,0:T(8,128)(2,1)} %pad_maximum_fusion.1), channel_id=1, source_target_pairs={{0,1},{1,2},{2,3},{3,4},{4,5},{5,6},{6,7},{7,0},{8,9},{9,10},{10,1... | collective-permute-start | bytes 1228808 | tf_op jit(solution)/shard_map/ppermute | solution.py:52
  102.4 47.8 %collective-permute-start.7 = (bf16[2,160,640]{2,1,0:T(8,128)(2,1)}, bf16[2,160,640]{2,1,0:T(8,128)(2,1)}, u32[]{:S(2)}, u32[]{:S(2)}) collective-permute-start(bf16[2,160,640]{2,1,0:T(8,128)(2,1)} %pad_maximum_fusion.2), channel_id=1, source_target_pairs={{0,7},{1,0},{2,1},{3,2},{4,3},{5,4},{6,5},{7,6},{8,15},{9,8},{10,9... | collective-permute-start | bytes 1228808 | tf_op jit(solution)/shard_map/ppermute | solution.py:52
  111.0 9.5 %collective-permute-start.1 = (bf16[256,1280]{1,0:T(8,128)(2,1)}, bf16[256,1280]{1,0:T(8,128)(2,1)S(1)}, u32[]{:S(2)}, u32[]{:S(2)}) collective-permute-start(bf16[256,1280]{1,0:T(8,128)(2,1)} %bitcast.8), channel_id=1, source_target_pairs={{0,64},{64,0},{1,65},{65,1},{2,66},{66,2},{3,67},{67,3},{4,68},{68... | collective-permute-start | bytes 1966088 | tf_op jit(solution)/shard_map/ppermute | solution.py:56
  115.1 3.6 %copy-start.6 = (bf16[640,1280]{1,0:T(8,128)(2,1)S(1)}, bf16[640,1280]{1,0:T(8,128)(2,1)}, u32[]{:S(2)}) copy-start(bf16[640,1280]{1,0:T(8,128)(2,1)} %param.8) | copy-start | bytes 4915204
  120.5 0.8 copy-start.4
  122.3 59.1 %all-to-all-start.3 = ((bf16[8,64,640]{2,1,0:T(8,128)(2,1)}), bf16[8,64,640]{2,1,0:T(8,128)(2,1)}, u32[]{:S(2)}, u32[]{:S(2)}) async-start(bf16[8,64,640]{2,1,0:T(8,128)(2,1)} %bitcast.92), calls=%async_computation.3 | async-start | bytes 1310720 | tf_op jit(solution)/shard_map/all_to_all | solution.py:21
  129.5 11.4 %copy-start.1 = (bf16[1280,640]{1,0:T(8,128)(2,1)}, bf16[1280,640]{1,0:T(8,128)(2,1)S(1)}, u32[]{:S(2)}) copy-start(bf16[1280,640]{1,0:T(8,128)(2,1)S(1)} %fusion.1) | copy-start | bytes 4915204
  130.6 39.3 %collective-permute-start.14 = (bf16[2,160,640]{2,1,0:T(8,128)(2,1)}, bf16[2,160,640]{2,1,0:T(8,128)(2,1)}, u32[]{:S(2)}, u32[]{:S(2)}) collective-permute-start(bf16[2,160,640]{2,1,0:T(8,128)(2,1)} %pad_maximum_fusion.4), channel_id=1, source_target_pairs={{0,7},{1,0},{2,1},{3,2},{4,3},{5,4},{6,5},{7,6},{8,15},{9,8},{10,9... | collective-permute-start | bytes 1228808 | tf_op jit(solution)/shard_map/ppermute | solution.py:52
  140.9 29.0 %collective-permute-start.11 = (bf16[2,160,640]{2,1,0:T(8,128)(2,1)}, bf16[2,160,640]{2,1,0:T(8,128)(2,1)}, u32[]{:S(2)}, u32[]{:S(2)}) collective-permute-start(bf16[2,160,640]{2,1,0:T(8,128)(2,1)} %pad_maximum_fusion.3), channel_id=1, source_target_pairs={{0,1},{1,2},{2,3},{3,4},{4,5},{5,6},{6,7},{7,0},{8,9},{9,10},{10,1... | collective-permute-start | bytes 1228808 | tf_op jit(solution)/shard_map/ppermute | solution.py:52
  142.8 36.6 %collective-permute-start.10 = (bf16[160,640]{1,0:T(8,128)(2,1)}, bf16[160,640]{1,0:T(8,128)(2,1)S(1)}, u32[]{:S(2)}, u32[]{:S(2)}) collective-permute-start(bf16[160,640]{1,0:T(8,128)(2,1)} %get-tuple-element.25), channel_id=1, source_target_pairs={{0,4},{1,5},{2,6},{3,7},{4,0},{5,1},{6,2},{7,3},{8,12},{9,13},{10,... | collective-permute-start | bytes 614408 | tf_op jit(solution)/shard_map/ppermute | solution.py:52
  146.2 20.7 %collective-permute-start.12 = (bf16[160,640]{1,0:T(8,128)(2,1)S(1)}, bf16[160,640]{1,0:T(8,128)(2,1)S(1)}, u32[]{:S(2)}, u32[]{:S(2)}) collective-permute-start(bf16[160,640]{1,0:T(8,128)(2,1)S(1)} %get-tuple-element.19), channel_id=1, source_target_pairs={{0,2},{1,7},{2,4},{3,1},{4,6},{5,3},{6,0},{7,5},{8,10},{9,15},{10,... | collective-permute-start | bytes 614408 | tf_op jit(solution)/shard_map/ppermute | solution.py:87
  151.4 28.0 %collective-permute-start.9 = (bf16[160,640]{1,0:T(8,128)(2,1)S(1)}, bf16[160,640]{1,0:T(8,128)(2,1)S(1)}, u32[]{:S(2)}, u32[]{:S(2)}) collective-permute-start(bf16[160,640]{1,0:T(8,128)(2,1)S(1)} %get-tuple-element.23), channel_id=1, source_target_pairs={{0,6},{1,7},{2,0},{3,1},{4,2},{5,3},{6,4},{7,5},{8,14},{9,15},{10,... | collective-permute-start | bytes 614408 | tf_op jit(solution)/shard_map/ppermute | solution.py:52
  166.9 12.5 %collective-permute-start.8 = (bf16[160,640]{1,0:T(8,128)(2,1)S(1)}, bf16[160,640]{1,0:T(8,128)(2,1)S(1)}, u32[]{:S(2)}, u32[]{:S(2)}) collective-permute-start(bf16[160,640]{1,0:T(8,128)(2,1)S(1)} %get-tuple-element.22), channel_id=1, source_target_pairs={{0,2},{1,3},{2,4},{3,5},{4,6},{5,7},{6,0},{7,1},{8,10},{9,11},{10,... | collective-permute-start | bytes 614408 | tf_op jit(solution)/shard_map/ppermute | solution.py:52
  172.0 11.2 %collective-permute-start.13 = (bf16[160,640]{1,0:T(8,128)(2,1)}, bf16[160,640]{1,0:T(8,128)(2,1)}, u32[]{:S(2)}, u32[]{:S(2)}) collective-permute-start(bf16[160,640]{1,0:T(8,128)(2,1)} %get-tuple-element.16), channel_id=1, source_target_pairs={{0,2},{1,3},{2,4},{3,5},{4,6},{5,7},{6,0},{7,1},{8,10},{9,11},{10,... | collective-permute-start | bytes 614408 | tf_op jit(solution)/shard_map/ppermute | solution.py:52
  173.9 12.7 %collective-permute-start.15 = (bf16[160,640]{1,0:T(8,128)(2,1)S(1)}, bf16[160,640]{1,0:T(8,128)(2,1)}, u32[]{:S(2)}, u32[]{:S(2)}) collective-permute-start(bf16[160,640]{1,0:T(8,128)(2,1)S(1)} %get-tuple-element.15), channel_id=1, source_target_pairs={{0,6},{1,7},{2,0},{3,1},{4,2},{5,3},{6,4},{7,5},{8,14},{9,15},{10,... | collective-permute-start | bytes 614408 | tf_op jit(solution)/shard_map/ppermute | solution.py:52

commit v10 on v7

--- a/solution.py
+++ b/solution.py
@@ -1,6 +1,8 @@
 import jax
 import jax.numpy as jnp
 from jax import lax
+from jax.experimental import pallas as pl
+from jax.experimental.pallas import tpu as pltpu
 from jax.sharding import Mesh, PartitionSpec as P
 
 
@@ -72,22 +74,49 @@
     return value.astype(jnp.float32)
 
 
+def onward_kernel(spot, own_up, own_down, near_up, near_down, *rest):
+    *turn, up, down = rest
+    upward = wide(own_up[0]) + wide(near_up[0])
+    downward = wide(own_down[0]) + wide(near_down[0])
+    if turn:
+        came = wide(turn[0][...])
+        upward = upward + jnp.where(spot[2] == 1, came, 0.0)
+        downward = downward + jnp.where(spot[2] == 1, 0.0, came)
+    up[...] = upward.astype(up.dtype)
+    down[...] = downward.astype(down.dtype)
+
+
+def onward(blocks, near_up, near_down, *turn):
+    here = lax.axis_index("depth")
+    spot = jnp.stack([(here + 2) % 8, (here + 6) % 8, 1 - here % 2]).astype(jnp.int32)
+    shape = blocks.shape[1:]
+    block = lambda pick: pl.BlockSpec((1, *shape), pick)
+    specs = [block(lambda i, s: (s[0], 0, 0)), block(lambda i, s: (s[1], 0, 0))]
+    specs += [block(lambda i, s: (1, 0, 0))] * 2 + [pl.BlockSpec(shape, lambda i, s: (0, 0))] * len(turn)
+    whole = pl.BlockSpec(memory_space=pltpu.VMEM)
+    return pl.pallas_call(
+        onward_kernel,
+        out_shape=[pltpu.VMEM(shape, blocks.dtype)] * 2,
+        grid_spec=pltpu.PrefetchScalarGridSpec(
+            num_scalar_prefetch=1, grid=(1,), in_specs=specs, out_specs=[whole] * 2
+        ),
+        name="onward",
+    )(spot, blocks, blocks, near_up, near_down, *turn)
+
+
 def depth_parts(blocks, straight):
     here = lax.axis_index("depth")
     pick = lambda by: block_at(blocks, (here + by) % 8)
-    even = here % 2 == 0
     near_up = shifted(jnp.stack([pick(1), pick(3)]), "depth", 1)
     near_down = shifted(jnp.stack([pick(7), pick(5)]), "depth", 7)
-    up = wide(pick(2)) + wide(near_up[1])
-    down = wide(pick(6)) + wide(near_down[1])
     if straight:
-        far = [shifted(pick(4), "depth", 4)]
+        far, turn = [shifted(pick(4), "depth", 4)], []
     else:
         turns = [(k, (k + 2) % 8 if k % 2 == 0 else (k - 2) % 8) for k in range(8)]
-        turn = wide(lax.ppermute(pick(4), "depth", turns))
-        up, down, far = up + jnp.where(even, turn, 0.0), down + jnp.where(even, 0.0, turn), []
-    last_up = shifted(up.astype(jnp.bfloat16), "depth", 2)
-    last_down = shifted(down.astype(jnp.bfloat16), "depth", 6)
+        far, turn = [], [lax.ppermute(pick(4), "depth", turns)]
+    up, down = onward(blocks, near_up, near_down, *turn)
+    last_up = shifted(up, "depth", 2)
+    last_down = shifted(down, "depth", 6)
     near = wide(pick(0)) + wide(near_up[0]) + wide(near_down[0])
     return near, last_up, last_down, *far
 

time: 186 us -> 184 us (0.989)
  Pallas kernels: 0 us -> 4.14 us
  other arithmetic: 18.7 us -> 15 us
  waiting for transfers between devices: 51.6 us -> 49.6 us
    ppermute x1, waiting for transfers between devices: 11.5 us -> 4.18 us  [depth_parts(): far, turn = ([], [lax.ppermute(pick(4), 'depth', turns)])]
    ppermute x12, waiting for transfers between devices: 18.8 us -> 25.3 us  [shifted(): lax.ppermute(value, axis, [(k, (k + by) % length) for k in range(length)])]
    pallas_call x0 -> x2, Pallas kernels: none -> 4.14 us  [onward(): pl.pallas_call(onward_kernel, out_shape=[pltpu.VMEM(shape, blocks.dtype)]...]
    convert_element_type x2 -> x0, other arithmetic: 3.23 us -> none  [the longest x1 2.1 us: depth_parts(): last_down = shifted(down.astype(jnp.bfloat16), 'depth', 6)]
    ppermute x1, starting transfers between devices: 4.82 us -> 1.92 us  [depth_parts(): far, turn = ([], [lax.ppermute(pick(4), 'depth', turns)])]
    ppermute x12, starting transfers between devices: 54.2 us -> 56.1 us  [shifted(): lax.ppermute(value, axis, [(k, (k + by) % length) for k in range(length)])]
  transfers between devices with their start and end apart: 20 -> 20, of which waited for: 8 -> 11; matrix products, arithmetic and copies ran while one was open for 16% -> 15% of each run, Pallas kernels for 0% -> 2%
where the time goes in v10:
time: 184 us; the launch traced here: 183 us
  starting transfers between devices  92.9 us (50%)
  waiting for transfers between devices  49.6 us (27%)
  other arithmetic  15 us (8%)
  matrix products  14.5 us (8%)
  local copies, waits for them, and re-layouts  5.41 us (3%)
  Pallas kernels  4.14 us (2%)
    ppermute x12, starting transfers between devices, shifted(): lax.ppermute(value, axis, [(k, (k + by) % length) for k in range(length)])  56.1 us
    ppermute x12, waiting for transfers between devices, shifted(): lax.ppermute(value, axis, [(k, (k + by) % length) for k in range(length)])  25.3 us
    all_to_all x2, waiting for transfers between devices, spread(): return lax.all_to_all(copies, axis, split_axis=0, concat_axis=0, tiled=True)  18.1 us
    all_to_all x2, starting transfers between devices, exchanged(): return lax.all_to_all(value, axis, split_axis=0, concat_axis=0, tiled=True)  15.6 us
    all_to_all x2, starting transfers between devices, spread(): return lax.all_to_all(copies, axis, split_axis=0, concat_axis=0, tiled=True)  13.5 us
    dot_general x4, matrix products, contract_first(): lax.dot_general(left, right, (((0,), (0,)), ((), ())), preferred_element_...  9.7 us
    ppermute x3, starting transfers between devices, swapped(): return lax.ppermute(value, 'core', SWAP)  5.74 us
    dot_general x4, matrix products, contract_last(): lax.dot_general(left, right, (((1,), (1,)), ((), ())), preferred_element_...  4.82 us
  transfers between devices with their start and end apart: 20, of which 11 were waited for; matrix products, arithmetic and copies ran while one was open for 15% of the time, Pallas kernels for 2%

profile of v10, /device:TPU:2, one launch (start us, length us, event | category | flops | bytes accessed | tf_op | source)
XLA Modules:
  0.0 182.7 jit_solution(15501322616074070984)
XLA Ops:
  2.9 9.4 %all-to-all-start = ((bf16[8,64,1280]{2,1,0:T(8,128)(2,1)}), bf16[8,64,1280]{2,1,0:T(8,128)(2,1)S(1)}, u32[]{:S(2)}, u32[]{:S(2)}) async-start(bf16[8,64,1280]{2,1,0:T(8,128)(2,1)} %broadcast_in_dim.9), calls=%async_computation | async-start | bytes 2621440 | tf_op jit(solution)/shard_map/all_to_all | solution.py:19
  12.2 12.9 %all-to-all-done = bf16[8,64,1280]{2,1,0:T(8,128)(2,1)S(1)} async-done(((bf16[8,64,1280]{2,1,0:T(8,128)(2,1)}), bf16[8,64,1280]{2,1,0:T(8,128)(2,1)S(1)}, u32[]{:S(2)}, u32[]{:S(2)}) %all-to-all-start) | async-done | bytes 1310752 | tf_op jit(solution)/shard_map/all_to_all | solution.py:19
  28.1 2.0 %collective-permute-done = bf16[256,1280]{1,0:T(8,128)(2,1)S(1)} collective-permute-done((bf16[256,1280]{1,0:T(8,128)(2,1)S(1)}, bf16[256,1280]{1,0:T(8,128)(2,1)S(1)}, u32[]{:S(2)}, u32[]{:S(2)}) %collective-permute-start) | collective-permute-done | bytes 655392 | tf_op jit(solution)/shard_map/ppermute | solution.py:58
  31.7 6.2 %all-to-all-start.1 = ((bf16[4,64,1280]{2,1,0:T(8,128)(2,1)}), bf16[4,64,1280]{2,1,0:T(8,128)(2,1)S(1)}, u32[]{:S(2)}, u32[]{:S(2)}) async-start(bf16[4,64,1280]{2,1,0:T(8,128)(2,1)} %bitcast.92), calls=%async_computation.1 | async-start | bytes 1310720 | tf_op jit(solution)/shard_map/all_to_all | solution.py:23
  39.7 4.8 %collective-permute-start.4 = (bf16[64,1280]{1,0:T(8,128)(2,1)S(1)}, bf16[64,1280]{1,0:T(8,128)(2,1)}, u32[]{:S(2)}, u32[]{:S(2)}) collective-permute-start(bf16[64,1280]{1,0:T(8,128)(2,1)S(1)} %get-tuple-element.13), channel_id=1, source_target_pairs={{0,128},{128,256},{256,384},{384,0},{1,129},{129,257},{257,385},{3... | collective-permute-start | bytes 491528 | tf_op jit(solution)/shard_map/ppermute | solution.py:54
  44.5 5.5 %collective-permute-start.3 = (bf16[64,1280]{1,0:T(8,128)(2,1)S(1)}, bf16[64,1280]{1,0:T(8,128)(2,1)}, u32[]{:S(2)}, u32[]{:S(2)}) collective-permute-start(bf16[64,1280]{1,0:T(8,128)(2,1)S(1)} %get-tuple-element.13), channel_id=1, source_target_pairs={{0,256},{128,384},{256,0},{384,128},{1,257},{129,385},{257,1},{385... | collective-permute-start | bytes 491528 | tf_op jit(solution)/shard_map/ppermute | solution.py:54
  50.0 5.5 %collective-permute-start.2 = (bf16[64,1280]{1,0:T(8,128)(2,1)S(1)}, bf16[64,1280]{1,0:T(8,128)(2,1)}, u32[]{:S(2)}, u32[]{:S(2)}) collective-permute-start(bf16[64,1280]{1,0:T(8,128)(2,1)S(1)} %get-tuple-element.13), channel_id=1, source_target_pairs={{0,384},{128,0},{256,128},{384,256},{1,385},{129,1},{257,129},{385... | collective-permute-start | bytes 491528 | tf_op jit(solution)/shard_map/ppermute | solution.py:54
  55.7 2.8 %collective-permute-done.4 = bf16[64,1280]{1,0:T(8,128)(2,1)} collective-permute-done((bf16[64,1280]{1,0:T(8,128)(2,1)S(1)}, bf16[64,1280]{1,0:T(8,128)(2,1)}, u32[]{:S(2)}, u32[]{:S(2)}) %collective-permute-start.4) | collective-permute-done | bytes 163872 | tf_op jit(solution)/shard_map/ppermute | solution.py:54
  58.4 5.1 %collective-permute-done.3 = bf16[64,1280]{1,0:T(8,128)(2,1)} collective-permute-done((bf16[64,1280]{1,0:T(8,128)(2,1)S(1)}, bf16[64,1280]{1,0:T(8,128)(2,1)}, u32[]{:S(2)}, u32[]{:S(2)}) %collective-permute-start.3) | collective-permute-done | bytes 163872 | tf_op jit(solution)/shard_map/ppermute | solution.py:54
  63.5 7.1 %collective-permute-done.2 = bf16[64,1280]{1,0:T(8,128)(2,1)} collective-permute-done((bf16[64,1280]{1,0:T(8,128)(2,1)S(1)}, bf16[64,1280]{1,0:T(8,128)(2,1)}, u32[]{:S(2)}, u32[]{:S(2)}) %collective-permute-start.2) | collective-permute-done | bytes 163872 | tf_op jit(solution)/shard_map/ppermute | solution.py:54
  70.6 2.0 %maximum_maximum_fusion = bf16[256,1280]{1,0:T(8,128)(2,1)} fusion(bf16[64,1280]{1,0:T(8,128)(2,1)} %collective-permute-done.4, bf16[64,1280]{1,0:T(8,128)(2,1)} %collective-permute-done.3, bf16[64,1280]{1,0:T(8,128)(2,1)} %collective-permute-done.2, bf16[64,1280]{1,0:T(8,128)(2,1)S(1)} %get-tuple-element.13), kind=kLoop, calls=%fused_computation.17 | loop fusion | flops 2621440 | bytes 1310720 | tf_op jit(solution)/shard_map/max | solution.py:70
  76.5 4.2 %all-to-all-start.2 = ((bf16[4,64,1280]{2,1,0:T(8,128)(2,1)}), bf16[4,64,1280]{2,1,0:T(8,128)(2,1)}, u32[]{:S(2)}, u32[]{:S(2)}) async-start(bf16[4,64,1280]{2,1,0:T(8,128)(2,1)} %broadcast_in_dim.10), calls=%async_computation.2 | async-start | bytes 1310720 | tf_op jit(solution)/shard_map/all_to_all | solution.py:19
  87.1 4.3 %collective-permute-start.6 = (bf16[2,160,640]{2,1,0:T(8,128)(2,1)}, bf16[2,160,640]{2,1,0:T(8,128)(2,1)}, u32[]{:S(2)}, u32[]{:S(2)}) collective-permute-start(bf16[2,160,640]{2,1,0:T(8,128)(2,1)} %pad_maximum_fusion.1), channel_id=1, source_target_pairs={{0,1},{1,2},{2,3},{3,4},{4,5},{5,6},{6,7},{7,0},{8,9},{9,10},{10,1... | collective-permute-start | bytes 1228808 | tf_op jit(solution)/shard_map/ppermute | solution.py:54
  91.4 5.2 %all-to-all-done.2 = bf16[4,64,1280]{2,1,0:T(8,128)(2,1)} async-done(((bf16[4,64,1280]{2,1,0:T(8,128)(2,1)}), bf16[4,64,1280]{2,1,0:T(8,128)(2,1)}, u32[]{:S(2)}, u32[]{:S(2)}) %all-to-all-start.2) | async-done | bytes 655392 | tf_op jit(solution)/shard_map/all_to_all | solution.py:19
  99.3 11.1 %collective-permute-start.7 = (bf16[2,160,640]{2,1,0:T(8,128)(2,1)}, bf16[2,160,640]{2,1,0:T(8,128)(2,1)}, u32[]{:S(2)}, u32[]{:S(2)}) collective-permute-start(bf16[2,160,640]{2,1,0:T(8,128)(2,1)} %pad_maximum_fusion.2), channel_id=1, source_target_pairs={{0,7},{1,0},{2,1},{3,2},{4,3},{5,4},{6,5},{7,6},{8,15},{9,8},{10,9... | collective-permute-start | bytes 1228808 | tf_op jit(solution)/shard_map/ppermute | solution.py:54
  110.4 3.5 %convolution_bitcast_fusion = f32[1280,640]{1,0:T(8,128)} fusion(bf16[4,64,1280]{2,1,0:T(8,128)(2,1)} %all-to-all-done.2, bf16[4,64,1280]{2,1,0:T(8,128)(2,1)S(1)} %copy-done.4), kind=kOutput, calls=%fused_computation.2 | convolution fusion | flops 419430400 | bytes 4259840 | tf_op jit(solution)/shard_map/dot_general | solution.py:47
  117.4 9.4 %all-to-all-start.3 = ((bf16[8,64,640]{2,1,0:T(8,128)(2,1)}), bf16[8,64,640]{2,1,0:T(8,128)(2,1)S(1)}, u32[]{:S(2)}, u32[]{:S(2)}) async-start(bf16[8,64,640]{2,1,0:T(8,128)(2,1)} %bitcast.16), calls=%async_computation.3 | async-start | bytes 1310720 | tf_op jit(solution)/shard_map/all_to_all | solution.py:23
  126.8 2.6 %fusion.1 = bf16[1280,640]{1,0:T(8,128)(2,1)S(1)} fusion(f32[1280,640]{1,0:T(8,128)} %convolution_bitcast_fusion, bf16[256,1280]{1,0:T(8,128)(2,1)S(1)} %copy-done.8, bf16[256,640]{1,0:T(8,128)(2,1)S(1)} %bitcast.93), kind=kOutput, calls=%fused_computation.4 | convolution fusion | flops 421068800 | bytes 5898240 | tf_op jit(solution)/shard_map/dot_general | solution.py:47
  130.4 1.9 %collective-permute-start.11 = (bf16[2,160,640]{2,1,0:T(8,128)(2,1)S(1)}, bf16[2,160,640]{2,1,0:T(8,128)(2,1)S(1)}, u32[]{:S(2)}, u32[]{:S(2)}) collective-permute-start(bf16[2,160,640]{2,1,0:T(8,128)(2,1)S(1)} %pad_maximum_fusion.3), channel_id=1, source_target_pairs={{0,1},{1,2},{2,3},{3,4},{4,5},{5,6},{6,7},{7,0},{8,9},{9,10},{10,1... | collective-permute-start | bytes 1228808 | tf_op jit(solution)/shard_map/ppermute | solution.py:54
  133.2 5.1 %collective-permute-start.12 = (bf16[2,160,640]{2,1,0:T(8,128)(2,1)}, bf16[2,160,640]{2,1,0:T(8,128)(2,1)}, u32[]{:S(2)}, u32[]{:S(2)}) collective-permute-start(bf16[2,160,640]{2,1,0:T(8,128)(2,1)} %pad_maximum_fusion.4), channel_id=1, source_target_pairs={{0,7},{1,0},{2,1},{3,2},{4,3},{5,4},{6,5},{7,6},{8,15},{9,8},{10,9... | collective-permute-start | bytes 1228808 | tf_op jit(solution)/shard_map/ppermute | solution.py:54
  138.3 1.9 %collective-permute-start.13 = (bf16[160,640]{1,0:T(8,128)(2,1)}, bf16[160,640]{1,0:T(8,128)(2,1)}, u32[]{:S(2)}, u32[]{:S(2)}) collective-permute-start(bf16[160,640]{1,0:T(8,128)(2,1)} %get-tuple-element.21), channel_id=1, source_target_pairs={{0,2},{1,7},{2,4},{3,1},{4,6},{5,3},{6,0},{7,5},{8,10},{9,15},{10,... | collective-permute-start | bytes 614408 | tf_op jit(solution)/shard_map/ppermute | solution.py:116
  140.8 3.6 %collective-permute-start.10 = (bf16[160,640]{1,0:T(8,128)(2,1)}, bf16[160,640]{1,0:T(8,128)(2,1)}, u32[]{:S(2)}, u32[]{:S(2)}) collective-permute-start(bf16[160,640]{1,0:T(8,128)(2,1)} %get-tuple-element.27), channel_id=1, source_target_pairs={{0,4},{1,5},{2,6},{3,7},{4,0},{5,1},{6,2},{7,3},{8,12},{9,13},{10,... | collective-permute-start | bytes 614408 | tf_op jit(solution)/shard_map/ppermute | solution.py:54
  144.4 2.0 %onward.2 = (bf16[160,640]{1,0:T(8,128)(2,1)S(1)}, bf16[160,640]{1,0:T(8,128)(2,1)S(1)}) custom-call(s32[3]{0:T(128)} %pad_add_fusion.spot, bf16[8,160,640]{2,1,0:T(8,128)(2,1)} %bitcast.82, bf16[8,160,640]{2,1,0:T(8,128)(2,1)} %bitcast.83, bf16[2,160,640]{2,1,0:T(8,128)(2,1)} %collective-permute-done.6.near_up, ...), custom_call_target="tpu_custom_call" | custom-call | tf_op jit(solution)/shard_map/onward/pallas_call | solution.py:97
  146.4 4.4 %collective-permute-start.9 = (bf16[160,640]{1,0:T(8,128)(2,1)S(1)}, bf16[160,640]{1,0:T(8,128)(2,1)}, u32[]{:S(2)}, u32[]{:S(2)}) collective-permute-start(bf16[160,640]{1,0:T(8,128)(2,1)S(1)} %get-tuple-element.15), channel_id=1, source_target_pairs={{0,6},{1,7},{2,0},{3,1},{4,2},{5,3},{6,4},{7,5},{8,14},{9,15},{10,... | collective-permute-start | bytes 614408 | tf_op jit(solution)/shard_map/ppermute | solution.py:54
  150.8 4.2 %collective-permute-done.13.rest_0_ = bf16[160,640]{1,0:T(8,128)(2,1)} collective-permute-done((bf16[160,640]{1,0:T(8,128)(2,1)}, bf16[160,640]{1,0:T(8,128)(2,1)}, u32[]{:S(2)}, u32[]{:S(2)}) %collective-permute-start.13) | collective-permute-done | bytes 204832 | tf_op jit(solution)/shard_map/ppermute | solution.py:116
  156.9 3.3 %collective-permute-done.11.near_up = bf16[2,160,640]{2,1,0:T(8,128)(2,1)S(1)} collective-permute-done((bf16[2,160,640]{2,1,0:T(8,128)(2,1)S(1)}, bf16[2,160,640]{2,1,0:T(8,128)(2,1)S(1)}, u32[]{:S(2)}, u32[]{:S(2)}) %collective-permute-start.11) | collective-permute-done | bytes 409632 | tf_op jit(solution)/shard_map/ppermute | solution.py:54
  160.2 4.4 %collective-permute-done.12.near_down = bf16[2,160,640]{2,1,0:T(8,128)(2,1)} collective-permute-done((bf16[2,160,640]{2,1,0:T(8,128)(2,1)}, bf16[2,160,640]{2,1,0:T(8,128)(2,1)}, u32[]{:S(2)}, u32[]{:S(2)}) %collective-permute-start.12) | collective-permute-done | bytes 409632 | tf_op jit(solution)/shard_map/ppermute | solution.py:54
  164.7 2.1 %onward.3 = (bf16[160,640]{1,0:T(8,128)(2,1)S(1)}, bf16[160,640]{1,0:T(8,128)(2,1)S(1)}) custom-call(s32[3]{0:T(128)} %pad_add_fusion.spot, bf16[8,160,640]{2,1,0:T(8,128)(2,1)} %bitcast.86, bf16[8,160,640]{2,1,0:T(8,128)(2,1)} %bitcast.87, bf16[2,160,640]{2,1,0:T(8,128)(2,1)} %copy-done.5, bf16[2,160,640]{2,1,0:T(8,128)(2,1)} %collective-permute-done.12.near_down, ...), custom_call_target="tpu_custom_call" | custom-call | tf_op jit(solution)/shard_map/onward/pallas_call | solution.py:97
  166.8 2.1 %collective-permute-start.14 = (bf16[160,640]{1,0:T(8,128)(2,1)S(1)}, bf16[160,640]{1,0:T(8,128)(2,1)}, u32[]{:S(2)}, u32[]{:S(2)}) collective-permute-start(bf16[160,640]{1,0:T(8,128)(2,1)S(1)} %get-tuple-element.16), channel_id=1, source_target_pairs={{0,2},{1,3},{2,4},{3,5},{4,6},{5,7},{6,0},{7,1},{8,10},{9,11},{10,... | collective-permute-start | bytes 614408 | tf_op jit(solution)/shard_map/ppermute | solution.py:54
  168.9 6.0 %collective-permute-start.15 = (bf16[160,640]{1,0:T(8,128)(2,1)S(1)}, bf16[160,640]{1,0:T(8,128)(2,1)}, u32[]{:S(2)}, u32[]{:S(2)}) collective-permute-start(bf16[160,640]{1,0:T(8,128)(2,1)S(1)} %get-tuple-element.19), channel_id=1, source_target_pairs={{0,6},{1,7},{2,0},{3,1},{4,2},{5,3},{6,4},{7,5},{8,14},{9,15},{10,... | collective-permute-start | bytes 614408 | tf_op jit(solution)/shard_map/ppermute | solution.py:54
  174.9 2.3 %fusion.5 = f32[160,640]{1,0:T(8,128)} fusion(bf16[160,640]{1,0:T(8,128)(2,1)} %collective-permute-done.10, bf16[160,640]{1,0:T(8,128)(2,1)} %collective-permute-done.9, bf16[160,640]{1,0:T(8,128)(2,1)} %collective-permute-done.8, bf16[2,160,640]{2,1,0:T(8,128)(2,1)} %collective-permute-done.7.near_down, ...), kind=kLoop, calls=%fused_computation.29 | loop fusion | flops 1126400 | bytes 1638404 | tf_op jit(solution)/shard_map/add | solution.py:125
  180.6 2.1 %fusion.3 = f32[640,160]{0,1:T(8,128)} fusion(bf16[160,640]{1,0:T(8,128)(2,1)} %collective-permute-done.15, bf16[160,640]{1,0:T(8,128)(2,1)} %collective-permute-done.14, bf16[2,160,640]{2,1,0:T(8,128)(2,1)} %collective-permute-done.12.near_down, bf16[2,160,640]{2,1,0:T(8,128)(2,1)S(1)} %copy-done.6, bf16[8,160,640]{2,1,0:T(8,128)(2,1)} %bitcast.88, ...), kind=kLoop, calls=%fused_computation.26 | loop fusion | flops 921600 | bytes 1433604 | tf_op jit(solution)/shard_map/transpose | solution.py:173
  (60 shorter events, 32.8 us)
Async XLA Ops:
  0.6 24.7 %copy-start = (bf16[1280,640]{1,0:T(8,128)(2,1)S(1)}, bf16[1280,640]{1,0:T(8,128)(2,1)}, u32[]{:S(2)}) copy-start(bf16[1280,640]{1,0:T(8,128)(2,1)} %param.9) | copy-start | bytes 4915204
  2.9 22.3 %all-to-all-start = ((bf16[8,64,1280]{2,1,0:T(8,128)(2,1)}), bf16[8,64,1280]{2,1,0:T(8,128)(2,1)S(1)}, u32[]{:S(2)}, u32[]{:S(2)}) async-start(bf16[8,64,1280]{2,1,0:T(8,128)(2,1)} %broadcast_in_dim.9), calls=%async_computation | async-start | bytes 2621440 | tf_op jit(solution)/shard_map/all_to_all | solution.py:19
  25.3 2.7 %copy-start.3 = (bf16[4,64,1280]{2,1,0:T(8,128)(2,1)}, bf16[4,64,1280]{2,1,0:T(8,128)(2,1)S(1)}, u32[]{:S(2)}) copy-start(bf16[4,64,1280]{2,1,0:T(8,128)(2,1)S(1)} %get-tuple-element.32) | copy-start | bytes 1966084
  26.1 4.0 %collective-permute-start = (bf16[256,1280]{1,0:T(8,128)(2,1)S(1)}, bf16[256,1280]{1,0:T(8,128)(2,1)S(1)}, u32[]{:S(2)}, u32[]{:S(2)}) collective-permute-start(bf16[256,1280]{1,0:T(8,128)(2,1)S(1)} %convolution_convert_fusion), channel_id=1, source_target_pairs={{0,64},{64,0},{1,65},{65,1},{2,66},{66,2},{3,67},{67,3},{4,68},{68... | collective-permute-start | bytes 1966088 | tf_op jit(solution)/shard_map/ppermute | solution.py:58
  31.7 42.8 %all-to-all-start.1 = ((bf16[4,64,1280]{2,1,0:T(8,128)(2,1)}), bf16[4,64,1280]{2,1,0:T(8,128)(2,1)S(1)}, u32[]{:S(2)}, u32[]{:S(2)}) async-start(bf16[4,64,1280]{2,1,0:T(8,128)(2,1)} %bitcast.92), calls=%async_computation.1 | async-start | bytes 1310720 | tf_op jit(solution)/shard_map/all_to_all | solution.py:23
  39.7 18.7 %collective-permute-start.4 = (bf16[64,1280]{1,0:T(8,128)(2,1)S(1)}, bf16[64,1280]{1,0:T(8,128)(2,1)}, u32[]{:S(2)}, u32[]{:S(2)}) collective-permute-start(bf16[64,1280]{1,0:T(8,128)(2,1)S(1)} %get-tuple-element.13), channel_id=1, source_target_pairs={{0,128},{128,256},{256,384},{384,0},{1,129},{129,257},{257,385},{3... | collective-permute-start | bytes 491528 | tf_op jit(solution)/shard_map/ppermute | solution.py:54
  44.5 18.9 %collective-permute-start.3 = (bf16[64,1280]{1,0:T(8,128)(2,1)S(1)}, bf16[64,1280]{1,0:T(8,128)(2,1)}, u32[]{:S(2)}, u32[]{:S(2)}) collective-permute-start(bf16[64,1280]{1,0:T(8,128)(2,1)S(1)} %get-tuple-element.13), channel_id=1, source_target_pairs={{0,256},{128,384},{256,0},{384,128},{1,257},{129,385},{257,1},{385... | collective-permute-start | bytes 491528 | tf_op jit(solution)/shard_map/ppermute | solution.py:54
  50.0 20.5 %collective-permute-start.2 = (bf16[64,1280]{1,0:T(8,128)(2,1)S(1)}, bf16[64,1280]{1,0:T(8,128)(2,1)}, u32[]{:S(2)}, u32[]{:S(2)}) collective-permute-start(bf16[64,1280]{1,0:T(8,128)(2,1)S(1)} %get-tuple-element.13), channel_id=1, source_target_pairs={{0,384},{128,0},{256,128},{384,256},{1,385},{129,1},{257,129},{385... | collective-permute-start | bytes 491528 | tf_op jit(solution)/shard_map/ppermute | solution.py:54
  72.5 10.0 %collective-permute-start.5 = (bf16[256,1280]{1,0:T(8,128)(2,1)}, bf16[256,1280]{1,0:T(8,128)(2,1)}, u32[]{:S(2)}, u32[]{:S(2)}) collective-permute-start(bf16[256,1280]{1,0:T(8,128)(2,1)} %maximum_maximum_fusion), channel_id=1, source_target_pairs={{0,64},{64,0},{1,65},{65,1},{2,66},{66,2},{3,67},{67,3},{4,68},{68... | collective-permute-start | bytes 1966088 | tf_op jit(solution)/shard_map/ppermute | solution.py:58
  76.5 20.1 %all-to-all-start.2 = ((bf16[4,64,1280]{2,1,0:T(8,128)(2,1)}), bf16[4,64,1280]{2,1,0:T(8,128)(2,1)}, u32[]{:S(2)}, u32[]{:S(2)}) async-start(bf16[4,64,1280]{2,1,0:T(8,128)(2,1)} %broadcast_in_dim.10), calls=%async_computation.2 | async-start | bytes 1310720 | tf_op jit(solution)/shard_map/all_to_all | solution.py:19
  84.3 1.2 copy-start.1
  85.5 24.8 %copy-start.4 = (bf16[4,64,1280]{2,1,0:T(8,128)(2,1)S(1)}, bf16[4,64,1280]{2,1,0:T(8,128)(2,1)}, u32[]{:S(2)}) copy-start(bf16[4,64,1280]{2,1,0:T(8,128)(2,1)} %copy-done.3) | copy-start | bytes 1966084
  87.1 53.7 %collective-permute-start.6 = (bf16[2,160,640]{2,1,0:T(8,128)(2,1)}, bf16[2,160,640]{2,1,0:T(8,128)(2,1)}, u32[]{:S(2)}, u32[]{:S(2)}) collective-permute-start(bf16[2,160,640]{2,1,0:T(8,128)(2,1)} %pad_maximum_fusion.1), channel_id=1, source_target_pairs={{0,1},{1,2},{2,3},{3,4},{4,5},{5,6},{6,7},{7,0},{8,9},{9,10},{10,1... | collective-permute-start | bytes 1228808 | tf_op jit(solution)/shard_map/ppermute | solution.py:54
  96.6 19.1 %collective-permute-start.1 = (bf16[256,1280]{1,0:T(8,128)(2,1)}, bf16[256,1280]{1,0:T(8,128)(2,1)S(1)}, u32[]{:S(2)}, u32[]{:S(2)}) collective-permute-start(bf16[256,1280]{1,0:T(8,128)(2,1)} %bitcast.11), channel_id=1, source_target_pairs={{0,64},{64,0},{1,65},{65,1},{2,66},{66,2},{3,67},{67,3},{4,68},{68... | collective-permute-start | bytes 1966088 | tf_op jit(solution)/shard_map/ppermute | solution.py:58
  99.3 14.6 %copy-start.9 = (bf16[640,1280]{1,0:T(8,128)(2,1)S(1)}, bf16[640,1280]{1,0:T(8,128)(2,1)}, u32[]{:S(2)}) copy-start(bf16[640,1280]{1,0:T(8,128)(2,1)} %param.8) | copy-start | bytes 4915204
  99.3 45.1 %collective-permute-start.7 = (bf16[2,160,640]{2,1,0:T(8,128)(2,1)}, bf16[2,160,640]{2,1,0:T(8,128)(2,1)}, u32[]{:S(2)}, u32[]{:S(2)}) collective-permute-start(bf16[2,160,640]{2,1,0:T(8,128)(2,1)} %pad_maximum_fusion.2), channel_id=1, source_target_pairs={{0,7},{1,0},{2,1},{3,2},{4,3},{5,4},{6,5},{7,6},{8,15},{9,8},{10,9... | collective-permute-start | bytes 1228808 | tf_op jit(solution)/shard_map/ppermute | solution.py:54
  115.7 0.8 copy-start.7
  116.5 10.3 %copy-start.8 = (bf16[256,1280]{1,0:T(8,128)(2,1)S(1)}, bf16[256,1280]{1,0:T(8,128)(2,1)}, u32[]{:S(2)}) copy-start(bf16[256,1280]{1,0:T(8,128)(2,1)} %copy-done.7) | copy-start | bytes 1966084
  117.4 59.8 %all-to-all-start.3 = ((bf16[8,64,640]{2,1,0:T(8,128)(2,1)}), bf16[8,64,640]{2,1,0:T(8,128)(2,1)S(1)}, u32[]{:S(2)}, u32[]{:S(2)}) async-start(bf16[8,64,640]{2,1,0:T(8,128)(2,1)} %bitcast.16), calls=%async_computation.3 | async-start | bytes 1310720 | tf_op jit(solution)/shard_map/all_to_all | solution.py:23
  129.4 3.7 %copy-start.2 = (bf16[1280,640]{1,0:T(8,128)(2,1)}, bf16[1280,640]{1,0:T(8,128)(2,1)S(1)}, u32[]{:S(2)}) copy-start(bf16[1280,640]{1,0:T(8,128)(2,1)S(1)} %fusion.1) | copy-start | bytes 4915204
  130.4 29.8 %collective-permute-start.11 = (bf16[2,160,640]{2,1,0:T(8,128)(2,1)S(1)}, bf16[2,160,640]{2,1,0:T(8,128)(2,1)S(1)}, u32[]{:S(2)}, u32[]{:S(2)}) collective-permute-start(bf16[2,160,640]{2,1,0:T(8,128)(2,1)S(1)} %pad_maximum_fusion.3), channel_id=1, source_target_pairs={{0,1},{1,2},{2,3},{3,4},{4,5},{5,6},{6,7},{7,0},{8,9},{9,10},{10,1... | collective-permute-start | bytes 1228808 | tf_op jit(solution)/shard_map/ppermute | solution.py:54
  133.2 31.5 %collective-permute-start.12 = (bf16[2,160,640]{2,1,0:T(8,128)(2,1)}, bf16[2,160,640]{2,1,0:T(8,128)(2,1)}, u32[]{:S(2)}, u32[]{:S(2)}) collective-permute-start(bf16[2,160,640]{2,1,0:T(8,128)(2,1)} %pad_maximum_fusion.4), channel_id=1, source_target_pairs={{0,7},{1,0},{2,1},{3,2},{4,3},{5,4},{6,5},{7,6},{8,15},{9,8},{10,9... | collective-permute-start | bytes 1228808 | tf_op jit(solution)/shard_map/ppermute | solution.py:54
  138.3 16.7 %collective-permute-start.13 = (bf16[160,640]{1,0:T(8,128)(2,1)}, bf16[160,640]{1,0:T(8,128)(2,1)}, u32[]{:S(2)}, u32[]{:S(2)}) collective-permute-start(bf16[160,640]{1,0:T(8,128)(2,1)} %get-tuple-element.21), channel_id=1, source_target_pairs={{0,2},{1,7},{2,4},{3,1},{4,6},{5,3},{6,0},{7,5},{8,10},{9,15},{10,... | collective-permute-start | bytes 614408 | tf_op jit(solution)/shard_map/ppermute | solution.py:116
  140.8 34.1 %collective-permute-start.10 = (bf16[160,640]{1,0:T(8,128)(2,1)}, bf16[160,640]{1,0:T(8,128)(2,1)}, u32[]{:S(2)}, u32[]{:S(2)}) collective-permute-start(bf16[160,640]{1,0:T(8,128)(2,1)} %get-tuple-element.27), channel_id=1, source_target_pairs={{0,4},{1,5},{2,6},{3,7},{4,0},{5,1},{6,2},{7,3},{8,12},{9,13},{10,... | collective-permute-start | bytes 614408 | tf_op jit(solution)/shard_map/ppermute | solution.py:54
  146.4 28.5 %collective-permute-start.9 = (bf16[160,640]{1,0:T(8,128)(2,1)S(1)}, bf16[160,640]{1,0:T(8,128)(2,1)}, u32[]{:S(2)}, u32[]{:S(2)}) collective-permute-start(bf16[160,640]{1,0:T(8,128)(2,1)S(1)} %get-tuple-element.15), channel_id=1, source_target_pairs={{0,6},{1,7},{2,0},{3,1},{4,2},{5,3},{6,4},{7,5},{8,14},{9,15},{10,... | collective-permute-start | bytes 614408 | tf_op jit(solution)/shard_map/ppermute | solution.py:54
  155.0 19.9 %collective-permute-start.8 = (bf16[160,640]{1,0:T(8,128)(2,1)S(1)}, bf16[160,640]{1,0:T(8,128)(2,1)}, u32[]{:S(2)}, u32[]{:S(2)}) collective-permute-start(bf16[160,640]{1,0:T(8,128)(2,1)S(1)} %get-tuple-element.14), channel_id=1, source_target_pairs={{0,2},{1,3},{2,4},{3,5},{4,6},{5,7},{6,0},{7,1},{8,10},{9,11},{10,... | collective-permute-start | bytes 614408 | tf_op jit(solution)/shard_map/ppermute | solution.py:54
  160.2 4.4 %copy-start.5 = (bf16[2,160,640]{2,1,0:T(8,128)(2,1)}, bf16[2,160,640]{2,1,0:T(8,128)(2,1)S(1)}, u32[]{:S(2)}) copy-start(bf16[2,160,640]{2,1,0:T(8,128)(2,1)S(1)} %collective-permute-done.11.near_up) | copy-start | bytes 1228804
  166.8 13.8 %copy-start.6 = (bf16[2,160,640]{2,1,0:T(8,128)(2,1)S(1)}, bf16[2,160,640]{2,1,0:T(8,128)(2,1)}, u32[]{:S(2)}) copy-start(bf16[2,160,640]{2,1,0:T(8,128)(2,1)} %copy-done.5) | copy-start | bytes 1228804
  166.8 12.5 %collective-permute-start.14 = (bf16[160,640]{1,0:T(8,128)(2,1)S(1)}, bf16[160,640]{1,0:T(8,128)(2,1)}, u32[]{:S(2)}, u32[]{:S(2)}) collective-permute-start(bf16[160,640]{1,0:T(8,128)(2,1)S(1)} %get-tuple-element.16), channel_id=1, source_target_pairs={{0,2},{1,3},{2,4},{3,5},{4,6},{5,7},{6,0},{7,1},{8,10},{9,11},{10,... | collective-permute-start | bytes 614408 | tf_op jit(solution)/shard_map/ppermute | solution.py:54
  168.9 11.7 %collective-permute-start.15 = (bf16[160,640]{1,0:T(8,128)(2,1)S(1)}, bf16[160,640]{1,0:T(8,128)(2,1)}, u32[]{:S(2)}, u32[]{:S(2)}) collective-permute-start(bf16[160,640]{1,0:T(8,128)(2,1)S(1)} %get-tuple-element.19), channel_id=1, source_target_pairs={{0,6},{1,7},{2,0},{3,1},{4,2},{5,3},{6,4},{7,5},{8,14},{9,15},{10,... | collective-permute-start | bytes 614408 | tf_op jit(solution)/shard_map/ppermute | solution.py:54

commit v11 on v10

--- a/solution.py
+++ b/solution.py
@@ -104,16 +104,46 @@
     )(spot, blocks, blocks, near_up, near_down, *turn)
 
 
+def leaving_kernel(spot, first, third, seventh, fifth, fourth, to_up, to_down, across):
+    to_up[0] = first[0]
+    to_up[1] = third[0]
+    to_down[0] = seventh[0]
+    to_down[1] = fifth[0]
+    across[...] = fourth[0]
+
+
+def leaving(blocks):
+    here = lax.axis_index("depth")
+    spot = jnp.stack([(here + by) % 8 for by in (1, 3, 7, 5, 4)]).astype(jnp.int32)
+    shape = blocks.shape[1:]
+    specs = [pl.BlockSpec((1, *shape), lambda i, s, k=k: (s[k], 0, 0)) for k in range(5)]
+    whole = pl.BlockSpec(memory_space=pltpu.VMEM)
+    pair = pltpu.VMEM((2, *shape), blocks.dtype)
+    return pl.pallas_call(
+        leaving_kernel,
+        out_shape=[pair, pair, pltpu.VMEM(shape, blocks.dtype)],
+        grid_spec=pltpu.PrefetchScalarGridSpec(
+            num_scalar_prefetch=1, grid=(1,), in_specs=specs, out_specs=[whole] * 3
+        ),
+        name="leaving",
+    )(spot, *[blocks] * 5)
+
+
 def depth_parts(blocks, straight):
     here = lax.axis_index("depth")
     pick = lambda by: block_at(blocks, (here + by) % 8)
-    near_up = shifted(jnp.stack([pick(1), pick(3)]), "depth", 1)
-    near_down = shifted(jnp.stack([pick(7), pick(5)]), "depth", 7)
     if straight:
-        far, turn = [shifted(pick(4), "depth", 4)], []
+        to_up, to_down = jnp.stack([pick(1), pick(3)]), jnp.stack([pick(7), pick(5)])
+        across = pick(4)
+    else:
+        to_up, to_down, across = leaving(blocks)
+    near_up = shifted(to_up, "depth", 1)
+    near_down = shifted(to_down, "depth", 7)
+    if straight:
+        far, turn = [shifted(across, "depth", 4)], []
     else:
         turns = [(k, (k + 2) % 8 if k % 2 == 0 else (k - 2) % 8) for k in range(8)]
-        far, turn = [], [lax.ppermute(pick(4), "depth", turns)]
+        far, turn = [], [lax.ppermute(across, "depth", turns)]
     up, down = onward(blocks, near_up, near_down, *turn)
     last_up = shifted(up, "depth", 2)
     last_down = shifted(down, "depth", 6)

time: 184 us -> 186 us (1.011)
  the two profiles are of different devices: /device:TPU:2 before, /device:TPU:72 now
where the time goes in v11:
time: 186 us; the launch traced here: 185 us
  starting transfers between devices  89.2 us (48%)
  waiting for transfers between devices  59.4 us (32%)
  other arithmetic  12.3 us (7%)
  matrix products  11.1 us (6%)
  Pallas kernels  6.18 us (3%)
  local copies, waits for them, and re-layouts  5.58 us (3%)
    ppermute x12, starting transfers between devices, shifted(): lax.ppermute(value, axis, [(k, (k + by) % length) for k in range(length)])  57.7 us
    all_to_all x2, waiting for transfers between devices, spread(): return lax.all_to_all(copies, axis, split_axis=0, concat_axis=0, tiled=True)  33.7 us
    ppermute x12, waiting for transfers between devices, shifted(): lax.ppermute(value, axis, [(k, (k + by) % length) for k in range(length)])  20.3 us
    all_to_all x2, starting transfers between devices, exchanged(): return lax.all_to_all(value, axis, split_axis=0, concat_axis=0, tiled=True)  10.4 us
    all_to_all x2, starting transfers between devices, spread(): return lax.all_to_all(copies, axis, split_axis=0, concat_axis=0, tiled=True)  9.93 us
    dot_general x4, matrix products, contract_first(): lax.dot_general(left, right, (((0,), (0,)), ((), ())), preferred_element_...  6.28 us
    ppermute x3, starting transfers between devices, swapped(): return lax.ppermute(value, 'core', SWAP)  5.75 us
    ppermute x1, starting transfers between devices, depth_parts(): far, turn = ([], [lax.ppermute(across, 'depth', turns)])  5.38 us
  transfers between devices with their start and end apart: 20, of which 6 were waited for; matrix products, arithmetic and copies ran while one was open for 11% of the time, Pallas kernels for 3%

profile of v11, /device:TPU:72, one launch (start us, length us, event | category | flops | bytes accessed | tf_op | source)
XLA Modules:
  0.0 185.0 jit_solution(6345185821863395716)
XLA Ops:
  2.9 5.8 %all-to-all-start = ((bf16[8,64,1280]{2,1,0:T(8,128)(2,1)}), bf16[8,64,1280]{2,1,0:T(8,128)(2,1)S(1)}, u32[]{:S(2)}, u32[]{:S(2)}) async-start(bf16[8,64,1280]{2,1,0:T(8,128)(2,1)} %broadcast_in_dim.9), calls=%async_computation | async-start | bytes 2621440 | tf_op jit(solution)/shard_map/all_to_all | solution.py:19
  8.7 17.1 %all-to-all-done = bf16[8,64,1280]{2,1,0:T(8,128)(2,1)S(1)} async-done(((bf16[8,64,1280]{2,1,0:T(8,128)(2,1)}), bf16[8,64,1280]{2,1,0:T(8,128)(2,1)S(1)}, u32[]{:S(2)}, u32[]{:S(2)}) %all-to-all-start) | async-done | bytes 1310752 | tf_op jit(solution)/shard_map/all_to_all | solution.py:19
  27.4 1.9 %collective-permute-start = (bf16[256,1280]{1,0:T(8,128)(2,1)S(1)}, bf16[256,1280]{1,0:T(8,128)(2,1)S(1)}, u32[]{:S(2)}, u32[]{:S(2)}) collective-permute-start(bf16[256,1280]{1,0:T(8,128)(2,1)S(1)} %convolution_convert_fusion), channel_id=1, source_target_pairs={{0,64},{64,0},{1,65},{65,1},{2,66},{66,2},{3,67},{67,3},{4,68},{68... | collective-permute-start | bytes 1966088 | tf_op jit(solution)/shard_map/ppermute | solution.py:58
  29.4 2.0 %collective-permute-done = bf16[256,1280]{1,0:T(8,128)(2,1)S(1)} collective-permute-done((bf16[256,1280]{1,0:T(8,128)(2,1)S(1)}, bf16[256,1280]{1,0:T(8,128)(2,1)S(1)}, u32[]{:S(2)}, u32[]{:S(2)}) %collective-permute-start) | collective-permute-done | bytes 655392 | tf_op jit(solution)/shard_map/ppermute | solution.py:58
  33.0 6.2 %all-to-all-start.1 = ((bf16[4,64,1280]{2,1,0:T(8,128)(2,1)}), bf16[4,64,1280]{2,1,0:T(8,128)(2,1)S(1)}, u32[]{:S(2)}, u32[]{:S(2)}) async-start(bf16[4,64,1280]{2,1,0:T(8,128)(2,1)} %bitcast.99), calls=%async_computation.1 | async-start | bytes 1310720 | tf_op jit(solution)/shard_map/all_to_all | solution.py:23
  40.3 4.8 %collective-permute-start.4 = (bf16[64,1280]{1,0:T(8,128)(2,1)S(1)}, bf16[64,1280]{1,0:T(8,128)(2,1)S(1)}, u32[]{:S(2)}, u32[]{:S(2)}) collective-permute-start(bf16[64,1280]{1,0:T(8,128)(2,1)S(1)} %get-tuple-element.16), channel_id=1, source_target_pairs={{0,128},{128,256},{256,384},{384,0},{1,129},{129,257},{257,385},{3... | collective-permute-start | bytes 491528 | tf_op jit(solution)/shard_map/ppermute | solution.py:54
  45.2 5.5 %collective-permute-start.3 = (bf16[64,1280]{1,0:T(8,128)(2,1)S(1)}, bf16[64,1280]{1,0:T(8,128)(2,1)S(1)}, u32[]{:S(2)}, u32[]{:S(2)}) collective-permute-start(bf16[64,1280]{1,0:T(8,128)(2,1)S(1)} %get-tuple-element.16), channel_id=1, source_target_pairs={{0,256},{128,384},{256,0},{384,128},{1,257},{129,385},{257,1},{385... | collective-permute-start | bytes 491528 | tf_op jit(solution)/shard_map/ppermute | solution.py:54
  50.6 5.5 %collective-permute-start.2 = (bf16[64,1280]{1,0:T(8,128)(2,1)S(1)}, bf16[64,1280]{1,0:T(8,128)(2,1)S(1)}, u32[]{:S(2)}, u32[]{:S(2)}) collective-permute-start(bf16[64,1280]{1,0:T(8,128)(2,1)S(1)} %get-tuple-element.16), channel_id=1, source_target_pairs={{0,384},{128,0},{256,128},{384,256},{1,385},{129,1},{257,129},{385... | collective-permute-start | bytes 491528 | tf_op jit(solution)/shard_map/ppermute | solution.py:54
  56.1 15.9 %collective-permute-done.4 = bf16[64,1280]{1,0:T(8,128)(2,1)S(1)} collective-permute-done((bf16[64,1280]{1,0:T(8,128)(2,1)S(1)}, bf16[64,1280]{1,0:T(8,128)(2,1)S(1)}, u32[]{:S(2)}, u32[]{:S(2)}) %collective-permute-start.4) | collective-permute-done | bytes 163872 | tf_op jit(solution)/shard_map/ppermute | solution.py:54
  73.0 1.9 %collective-permute-start.5 = (bf16[256,1280]{1,0:T(8,128)(2,1)}, bf16[256,1280]{1,0:T(8,128)(2,1)}, u32[]{:S(2)}, u32[]{:S(2)}) collective-permute-start(bf16[256,1280]{1,0:T(8,128)(2,1)} %maximum_maximum_fusion), channel_id=1, source_target_pairs={{0,64},{64,0},{1,65},{65,1},{2,66},{66,2},{3,67},{67,3},{4,68},{68... | collective-permute-start | bytes 1966088 | tf_op jit(solution)/shard_map/ppermute | solution.py:58
  76.0 4.2 %all-to-all-start.2 = ((bf16[4,64,1280]{2,1,0:T(8,128)(2,1)}), bf16[4,64,1280]{2,1,0:T(8,128)(2,1)}, u32[]{:S(2)}, u32[]{:S(2)}) async-start(bf16[4,64,1280]{2,1,0:T(8,128)(2,1)} %broadcast_in_dim.10), calls=%async_computation.2 | async-start | bytes 1310720 | tf_op jit(solution)/shard_map/all_to_all | solution.py:19
  83.6 16.7 %all-to-all-done.2 = bf16[4,64,1280]{2,1,0:T(8,128)(2,1)} async-done(((bf16[4,64,1280]{2,1,0:T(8,128)(2,1)}), bf16[4,64,1280]{2,1,0:T(8,128)(2,1)}, u32[]{:S(2)}, u32[]{:S(2)}) %all-to-all-start.2) | async-done | bytes 655392 | tf_op jit(solution)/shard_map/all_to_all | solution.py:19
  100.3 1.9 %collective-permute-start.1 = (bf16[256,1280]{1,0:T(8,128)(2,1)}, bf16[256,1280]{1,0:T(8,128)(2,1)S(1)}, u32[]{:S(2)}, u32[]{:S(2)}) collective-permute-start(bf16[256,1280]{1,0:T(8,128)(2,1)} %bitcast.11), channel_id=1, source_target_pairs={{0,64},{64,0},{1,65},{65,1},{2,66},{66,2},{3,67},{67,3},{4,68},{68... | collective-permute-start | bytes 1966088 | tf_op jit(solution)/shard_map/ppermute | solution.py:58
  103.8 4.3 %collective-permute-start.6 = (bf16[2,160,640]{2,1,0:T(8,128)(2,1)}, bf16[2,160,640]{2,1,0:T(8,128)(2,1)}, u32[]{:S(2)}, u32[]{:S(2)}) collective-permute-start(bf16[2,160,640]{2,1,0:T(8,128)(2,1)} %pad_maximum_fusion.1), channel_id=1, source_target_pairs={{0,1},{1,2},{2,3},{3,4},{4,5},{5,6},{6,7},{7,0},{8,9},{9,10},{10,1... | collective-permute-start | bytes 1228808 | tf_op jit(solution)/shard_map/ppermute | solution.py:54
  108.9 1.9 %collective-permute-start.7 = (bf16[2,160,640]{2,1,0:T(8,128)(2,1)}, bf16[2,160,640]{2,1,0:T(8,128)(2,1)}, u32[]{:S(2)}, u32[]{:S(2)}) collective-permute-start(bf16[2,160,640]{2,1,0:T(8,128)(2,1)} %pad_maximum_fusion.2), channel_id=1, source_target_pairs={{0,7},{1,0},{2,1},{3,2},{4,3},{5,4},{6,5},{7,6},{8,15},{9,8},{10,9... | collective-permute-start | bytes 1228808 | tf_op jit(solution)/shard_map/ppermute | solution.py:54
  114.5 4.2 %all-to-all-start.3 = ((bf16[8,64,640]{2,1,0:T(8,128)(2,1)}), bf16[8,64,640]{2,1,0:T(8,128)(2,1)}, u32[]{:S(2)}, u32[]{:S(2)}) async-start(bf16[8,64,640]{2,1,0:T(8,128)(2,1)} %bitcast.16), calls=%async_computation.3 | async-start | bytes 1310720 | tf_op jit(solution)/shard_map/all_to_all | solution.py:23
  120.7 1.9 %fusion.1 = bf16[1280,640]{1,0:T(8,128)(2,1)} fusion(f32[1280,640]{1,0:T(8,128)S(1)} %convolution_bitcast_fusion, bf16[256,1280]{1,0:T(8,128)(2,1)S(1)} %copy-done.8, bf16[256,640]{1,0:T(8,128)(2,1)S(1)} %bitcast.100), kind=kOutput, calls=%fused_computation.4 | convolution fusion | flops 421068800 | bytes 5898240 | tf_op jit(solution)/shard_map/dot_general | solution.py:47
  122.5 2.0 %leaving.1 = (bf16[2,160,640]{2,1,0:T(8,128)(2,1)S(1)}, bf16[2,160,640]{2,1,0:T(8,128)(2,1)S(1)}, bf16[160,640]{1,0:T(8,128)(2,1)S(1)}) custom-call(s32[5]{0:T(128)} %stack.59.spot, bf16[8,160,640]{2,1,0:T(8,128)(2,1)} %bitcast.84, bf16[8,160,640]{2,1,0:T(8,128)(2,1)} %bitcast.85, bf16[8,160,640]{2,1,0:T(8,128)(2,1)} %bitcast.86, ...), custom_call_target="tpu_custom_call" | custom-call | tf_op jit(solution)/shard_map/leaving/pallas_call | solution.py:122
  124.6 4.2 %collective-permute-start.11 = (bf16[2,160,640]{2,1,0:T(8,128)(2,1)S(1)}, bf16[2,160,640]{2,1,0:T(8,128)(2,1)S(1)}, u32[]{:S(2)}, u32[]{:S(2)}) collective-permute-start(bf16[2,160,640]{2,1,0:T(8,128)(2,1)S(1)} %get-tuple-element.19), channel_id=1, source_target_pairs={{0,1},{1,2},{2,3},{3,4},{4,5},{5,6},{6,7},{7,0},{8,9},{9,10},{10,1... | collective-permute-start | bytes 1228808 | tf_op jit(solution)/shard_map/ppermute | solution.py:54
  128.8 5.9 %collective-permute-start.12 = (bf16[2,160,640]{2,1,0:T(8,128)(2,1)S(1)}, bf16[2,160,640]{2,1,0:T(8,128)(2,1)}, u32[]{:S(2)}, u32[]{:S(2)}) collective-permute-start(bf16[2,160,640]{2,1,0:T(8,128)(2,1)S(1)} %get-tuple-element.20), channel_id=1, source_target_pairs={{0,7},{1,0},{2,1},{3,2},{4,3},{5,4},{6,5},{7,6},{8,15},{9,8},{10,9... | collective-permute-start | bytes 1228808 | tf_op jit(solution)/shard_map/ppermute | solution.py:54
  134.7 5.4 %collective-permute-start.13 = (bf16[160,640]{1,0:T(8,128)(2,1)S(1)}, bf16[160,640]{1,0:T(8,128)(2,1)}, u32[]{:S(2)}, u32[]{:S(2)}) collective-permute-start(bf16[160,640]{1,0:T(8,128)(2,1)S(1)} %get-tuple-element.21), channel_id=1, source_target_pairs={{0,2},{1,7},{2,4},{3,1},{4,6},{5,3},{6,0},{7,5},{8,10},{9,15},{10,... | collective-permute-start | bytes 614408 | tf_op jit(solution)/shard_map/ppermute | solution.py:146
  140.7 4.3 %collective-permute-start.10 = (bf16[160,640]{1,0:T(8,128)(2,1)}, bf16[160,640]{1,0:T(8,128)(2,1)}, u32[]{:S(2)}, u32[]{:S(2)}) collective-permute-start(bf16[160,640]{1,0:T(8,128)(2,1)} %get-tuple-element.28), channel_id=1, source_target_pairs={{0,4},{1,5},{2,6},{3,7},{4,0},{5,1},{6,2},{7,3},{8,12},{9,13},{10,... | collective-permute-start | bytes 614408 | tf_op jit(solution)/shard_map/ppermute | solution.py:54
  145.0 2.0 %onward.2 = (bf16[160,640]{1,0:T(8,128)(2,1)S(1)}, bf16[160,640]{1,0:T(8,128)(2,1)S(1)}) custom-call(s32[3]{0:T(128)} %pad_add_fusion.spot, bf16[8,160,640]{2,1,0:T(8,128)(2,1)} %bitcast.93, bf16[8,160,640]{2,1,0:T(8,128)(2,1)} %bitcast.94, bf16[2,160,640]{2,1,0:T(8,128)(2,1)} %collective-permute-done.6.near_up, ...), custom_call_target="tpu_custom_call" | custom-call | tf_op jit(solution)/shard_map/onward/pallas_call | solution.py:97
  147.0 2.5 %collective-permute-start.9 = (bf16[160,640]{1,0:T(8,128)(2,1)S(1)}, bf16[160,640]{1,0:T(8,128)(2,1)}, u32[]{:S(2)}, u32[]{:S(2)}) collective-permute-start(bf16[160,640]{1,0:T(8,128)(2,1)S(1)} %get-tuple-element.18), channel_id=1, source_target_pairs={{0,6},{1,7},{2,0},{3,1},{4,2},{5,3},{6,4},{7,5},{8,14},{9,15},{10,... | collective-permute-start | bytes 614408 | tf_op jit(solution)/shard_map/ppermute | solution.py:54
  149.6 3.4 %collective-permute-done.13.rest_0_ = bf16[160,640]{1,0:T(8,128)(2,1)} collective-permute-done((bf16[160,640]{1,0:T(8,128)(2,1)S(1)}, bf16[160,640]{1,0:T(8,128)(2,1)}, u32[]{:S(2)}, u32[]{:S(2)}) %collective-permute-start.13) | collective-permute-done | bytes 204832 | tf_op jit(solution)/shard_map/ppermute | solution.py:146
  152.9 3.3 %collective-permute-start.8 = (bf16[160,640]{1,0:T(8,128)(2,1)S(1)}, bf16[160,640]{1,0:T(8,128)(2,1)S(1)}, u32[]{:S(2)}, u32[]{:S(2)}) collective-permute-start(bf16[160,640]{1,0:T(8,128)(2,1)S(1)} %get-tuple-element.17), channel_id=1, source_target_pairs={{0,2},{1,3},{2,4},{3,5},{4,6},{5,7},{6,0},{7,1},{8,10},{9,11},{10,... | collective-permute-start | bytes 614408 | tf_op jit(solution)/shard_map/ppermute | solution.py:54
  157.0 2.1 %onward.3 = (bf16[160,640]{1,0:T(8,128)(2,1)S(1)}, bf16[160,640]{1,0:T(8,128)(2,1)S(1)}) custom-call(s32[3]{0:T(128)} %pad_add_fusion.spot, bf16[8,160,640]{2,1,0:T(8,128)(2,1)} %bitcast.89, bf16[8,160,640]{2,1,0:T(8,128)(2,1)} %bitcast.90, bf16[2,160,640]{2,1,0:T(8,128)(2,1)} %copy-done.5, bf16[2,160,640]{2,1,0:T(8,128)(2,1)} %collective-permute-done.12.near_down, ...), custom_call_target="tpu_custom_call" | custom-call | tf_op jit(solution)/shard_map/onward/pallas_call | solution.py:97
  159.2 13.1 %collective-permute-start.14 = (bf16[160,640]{1,0:T(8,128)(2,1)S(1)}, bf16[160,640]{1,0:T(8,128)(2,1)S(1)}, u32[]{:S(2)}, u32[]{:S(2)}) collective-permute-start(bf16[160,640]{1,0:T(8,128)(2,1)S(1)} %get-tuple-element.22), channel_id=1, source_target_pairs={{0,2},{1,3},{2,4},{3,5},{4,6},{5,7},{6,0},{7,1},{8,10},{9,11},{10,... | collective-permute-start | bytes 614408 | tf_op jit(solution)/shard_map/ppermute | solution.py:54
  172.3 2.3 %collective-permute-start.15 = (bf16[160,640]{1,0:T(8,128)(2,1)S(1)}, bf16[160,640]{1,0:T(8,128)(2,1)S(1)}, u32[]{:S(2)}, u32[]{:S(2)}) collective-permute-start(bf16[160,640]{1,0:T(8,128)(2,1)S(1)} %get-tuple-element.25), channel_id=1, source_target_pairs={{0,6},{1,7},{2,0},{3,1},{4,2},{5,3},{6,4},{7,5},{8,14},{9,15},{10,... | collective-permute-start | bytes 614408 | tf_op jit(solution)/shard_map/ppermute | solution.py:54
  174.7 2.2 %fusion.5 = f32[160,640]{1,0:T(8,128)} fusion(bf16[160,640]{1,0:T(8,128)(2,1)} %collective-permute-done.10, bf16[160,640]{1,0:T(8,128)(2,1)} %collective-permute-done.9, bf16[160,640]{1,0:T(8,128)(2,1)S(1)} %collective-permute-done.8, bf16[2,160,640]{2,1,0:T(8,128)(2,1)} %collective-permute-done.7.near_down, ...), kind=kLoop, calls=%fused_computation.27 | loop fusion | flops 1126400 | bytes 1638404 | tf_op jit(solution)/shard_map/add | solution.py:155
  178.7 4.3 %collective-permute-done.15 = bf16[160,640]{1,0:T(8,128)(2,1)S(1)} collective-permute-done((bf16[160,640]{1,0:T(8,128)(2,1)S(1)}, bf16[160,640]{1,0:T(8,128)(2,1)S(1)}, u32[]{:S(2)}, u32[]{:S(2)}) %collective-permute-start.15) | collective-permute-done | bytes 204832 | tf_op jit(solution)/shard_map/ppermute | solution.py:54
  183.1 1.9 %fusion.3 = f32[640,160]{0,1:T(8,128)} fusion(bf16[160,640]{1,0:T(8,128)(2,1)S(1)} %collective-permute-done.15, bf16[160,640]{1,0:T(8,128)(2,1)S(1)} %collective-permute-done.14, bf16[2,160,640]{2,1,0:T(8,128)(2,1)} %collective-permute-done.12.near_down, bf16[2,160,640]{2,1,0:T(8,128)(2,1)S(1)} %copy-done.6, bf16[8,160,640]{2,1,0:T(8,128)(2,1)} %bitcast.91, ...), kind=kLoop, calls=%fused_computation.24 | loop fusion | flops 921600 | bytes 1433604 | tf_op jit(solution)/shard_map/transpose | solution.py:203
  (71 shorter events, 23.0 us)
Async XLA Ops:
  0.6 26.1 %copy-start = (bf16[1280,640]{1,0:T(8,128)(2,1)S(1)}, bf16[1280,640]{1,0:T(8,128)(2,1)}, u32[]{:S(2)}) copy-start(bf16[1280,640]{1,0:T(8,128)(2,1)} %param.9) | copy-start | bytes 4915204
  2.9 22.8 %all-to-all-start = ((bf16[8,64,1280]{2,1,0:T(8,128)(2,1)}), bf16[8,64,1280]{2,1,0:T(8,128)(2,1)S(1)}, u32[]{:S(2)}, u32[]{:S(2)}) async-start(bf16[8,64,1280]{2,1,0:T(8,128)(2,1)} %broadcast_in_dim.9), calls=%async_computation | async-start | bytes 2621440 | tf_op jit(solution)/shard_map/all_to_all | solution.py:19
  25.8 3.5 %copy-start.2 = (bf16[4,64,1280]{2,1,0:T(8,128)(2,1)}, bf16[4,64,1280]{2,1,0:T(8,128)(2,1)S(1)}, u32[]{:S(2)}) copy-start(bf16[4,64,1280]{2,1,0:T(8,128)(2,1)S(1)} %get-tuple-element.33) | copy-start | bytes 1966084
  27.4 4.0 %collective-permute-start = (bf16[256,1280]{1,0:T(8,128)(2,1)S(1)}, bf16[256,1280]{1,0:T(8,128)(2,1)S(1)}, u32[]{:S(2)}, u32[]{:S(2)}) collective-permute-start(bf16[256,1280]{1,0:T(8,128)(2,1)S(1)} %convolution_convert_fusion), channel_id=1, source_target_pairs={{0,64},{64,0},{1,65},{65,1},{2,66},{66,2},{3,67},{67,3},{4,68},{68... | collective-permute-start | bytes 1966088 | tf_op jit(solution)/shard_map/ppermute | solution.py:58
  33.0 42.0 %all-to-all-start.1 = ((bf16[4,64,1280]{2,1,0:T(8,128)(2,1)}), bf16[4,64,1280]{2,1,0:T(8,128)(2,1)S(1)}, u32[]{:S(2)}, u32[]{:S(2)}) async-start(bf16[4,64,1280]{2,1,0:T(8,128)(2,1)} %bitcast.99), calls=%async_computation.1 | async-start | bytes 1310720 | tf_op jit(solution)/shard_map/all_to_all | solution.py:23
  40.3 31.7 %collective-permute-start.4 = (bf16[64,1280]{1,0:T(8,128)(2,1)S(1)}, bf16[64,1280]{1,0:T(8,128)(2,1)S(1)}, u32[]{:S(2)}, u32[]{:S(2)}) collective-permute-start(bf16[64,1280]{1,0:T(8,128)(2,1)S(1)} %get-tuple-element.16), channel_id=1, source_target_pairs={{0,128},{128,256},{256,384},{384,0},{1,129},{129,257},{257,385},{3... | collective-permute-start | bytes 491528 | tf_op jit(solution)/shard_map/ppermute | solution.py:54
  45.2 26.9 %collective-permute-start.3 = (bf16[64,1280]{1,0:T(8,128)(2,1)S(1)}, bf16[64,1280]{1,0:T(8,128)(2,1)S(1)}, u32[]{:S(2)}, u32[]{:S(2)}) collective-permute-start(bf16[64,1280]{1,0:T(8,128)(2,1)S(1)} %get-tuple-element.16), channel_id=1, source_target_pairs={{0,256},{128,384},{256,0},{384,128},{1,257},{129,385},{257,1},{385... | collective-permute-start | bytes 491528 | tf_op jit(solution)/shard_map/ppermute | solution.py:54
  50.6 21.4 %collective-permute-start.2 = (bf16[64,1280]{1,0:T(8,128)(2,1)S(1)}, bf16[64,1280]{1,0:T(8,128)(2,1)S(1)}, u32[]{:S(2)}, u32[]{:S(2)}) collective-permute-start(bf16[64,1280]{1,0:T(8,128)(2,1)S(1)} %get-tuple-element.16), channel_id=1, source_target_pairs={{0,384},{128,0},{256,128},{384,256},{1,385},{129,1},{257,129},{385... | collective-permute-start | bytes 491528 | tf_op jit(solution)/shard_map/ppermute | solution.py:54
  72.0 1.0 copy-start.9
  73.0 8.8 %collective-permute-start.5 = (bf16[256,1280]{1,0:T(8,128)(2,1)}, bf16[256,1280]{1,0:T(8,128)(2,1)}, u32[]{:S(2)}, u32[]{:S(2)}) collective-permute-start(bf16[256,1280]{1,0:T(8,128)(2,1)} %maximum_maximum_fusion), channel_id=1, source_target_pairs={{0,64},{64,0},{1,65},{65,1},{2,66},{66,2},{3,67},{67,3},{4,68},{68... | collective-permute-start | bytes 1966088 | tf_op jit(solution)/shard_map/ppermute | solution.py:58
  75.1 5.9 %copy-start.10 = (bf16[64,1280]{1,0:T(8,128)(2,1)S(1)}, bf16[64,1280]{1,0:T(8,128)(2,1)}, u32[]{:S(2)}) copy-start(bf16[64,1280]{1,0:T(8,128)(2,1)} %copy-done.9) | copy-start | bytes 491524
  75.1 5.9 %copy-start.12 = (bf16[64,1280]{1,0:T(8,128)(2,1)S(1)}, bf16[64,1280]{1,0:T(8,128)(2,1)}, u32[]{:S(2)}) copy-start(bf16[64,1280]{1,0:T(8,128)(2,1)} %copy-done.11) | copy-start | bytes 491524
  75.1 5.9 %copy-start.14 = (bf16[64,1280]{1,0:T(8,128)(2,1)S(1)}, bf16[64,1280]{1,0:T(8,128)(2,1)}, u32[]{:S(2)}) copy-start(bf16[64,1280]{1,0:T(8,128)(2,1)} %copy-done.13) | copy-start | bytes 491524
  76.0 24.3 %all-to-all-start.2 = ((bf16[4,64,1280]{2,1,0:T(8,128)(2,1)}), bf16[4,64,1280]{2,1,0:T(8,128)(2,1)}, u32[]{:S(2)}, u32[]{:S(2)}) async-start(bf16[4,64,1280]{2,1,0:T(8,128)(2,1)} %broadcast_in_dim.10), calls=%async_computation.2 | async-start | bytes 1310720 | tf_op jit(solution)/shard_map/all_to_all | solution.py:19
  83.6 25.3 %copy-start.1 = (bf16[1280,640]{1,0:T(8,128)(2,1)}, bf16[1280,640]{1,0:T(8,128)(2,1)S(1)}, u32[]{:S(2)}) copy-start(bf16[1280,640]{1,0:T(8,128)(2,1)S(1)} %fusion) | copy-start | bytes 4915204
  100.3 12.4 %collective-permute-start.1 = (bf16[256,1280]{1,0:T(8,128)(2,1)}, bf16[256,1280]{1,0:T(8,128)(2,1)S(1)}, u32[]{:S(2)}, u32[]{:S(2)}) collective-permute-start(bf16[256,1280]{1,0:T(8,128)(2,1)} %bitcast.11), channel_id=1, source_target_pairs={{0,64},{64,0},{1,65},{65,1},{2,66},{66,2},{3,67},{67,3},{4,68},{68... | collective-permute-start | bytes 1966088 | tf_op jit(solution)/shard_map/ppermute | solution.py:58
  102.2 8.6 %copy-start.15 = (bf16[640,1280]{1,0:T(8,128)(2,1)S(1)}, bf16[640,1280]{1,0:T(8,128)(2,1)}, u32[]{:S(2)}) copy-start(bf16[640,1280]{1,0:T(8,128)(2,1)} %param.8) | copy-start | bytes 4915204
  103.8 36.9 %collective-permute-start.6 = (bf16[2,160,640]{2,1,0:T(8,128)(2,1)}, bf16[2,160,640]{2,1,0:T(8,128)(2,1)}, u32[]{:S(2)}, u32[]{:S(2)}) collective-permute-start(bf16[2,160,640]{2,1,0:T(8,128)(2,1)} %pad_maximum_fusion.1), channel_id=1, source_target_pairs={{0,1},{1,2},{2,3},{3,4},{4,5},{5,6},{6,7},{7,0},{8,9},{9,10},{10,1... | collective-permute-start | bytes 1228808 | tf_op jit(solution)/shard_map/ppermute | solution.py:54
  108.9 36.1 %collective-permute-start.7 = (bf16[2,160,640]{2,1,0:T(8,128)(2,1)}, bf16[2,160,640]{2,1,0:T(8,128)(2,1)}, u32[]{:S(2)}, u32[]{:S(2)}) collective-permute-start(bf16[2,160,640]{2,1,0:T(8,128)(2,1)} %pad_maximum_fusion.2), channel_id=1, source_target_pairs={{0,7},{1,0},{2,1},{3,2},{4,3},{5,4},{6,5},{7,6},{8,15},{9,8},{10,9... | collective-permute-start | bytes 1228808 | tf_op jit(solution)/shard_map/ppermute | solution.py:54
  113.6 5.2 %copy-start.3 = (bf16[4,64,1280]{2,1,0:T(8,128)(2,1)S(1)}, bf16[4,64,1280]{2,1,0:T(8,128)(2,1)}, u32[]{:S(2)}) copy-start(bf16[4,64,1280]{2,1,0:T(8,128)(2,1)} %copy-done.2) | copy-start | bytes 1966084
  114.5 62.4 %all-to-all-start.3 = ((bf16[8,64,640]{2,1,0:T(8,128)(2,1)}), bf16[8,64,640]{2,1,0:T(8,128)(2,1)}, u32[]{:S(2)}, u32[]{:S(2)}) async-start(bf16[8,64,640]{2,1,0:T(8,128)(2,1)} %bitcast.16), calls=%async_computation.3 | async-start | bytes 1310720 | tf_op jit(solution)/shard_map/all_to_all | solution.py:23
  118.7 1.9 %copy-start.4 = (bf16[4,64,640]{2,1,0:T(8,128)(2,1)S(1)}, bf16[4,64,640]{2,1,0:T(8,128)(2,1)}, u32[]{:S(2)}) copy-start(bf16[4,64,640]{2,1,0:T(8,128)(2,1)} %get-tuple-element.34) | copy-start | bytes 983044
  118.7 1.9 %copy-start.8 = (bf16[256,1280]{1,0:T(8,128)(2,1)S(1)}, bf16[256,1280]{1,0:T(8,128)(2,1)}, u32[]{:S(2)}) copy-start(bf16[256,1280]{1,0:T(8,128)(2,1)} %copy-done.7) | copy-start | bytes 1966084
  124.6 31.7 %collective-permute-start.11 = (bf16[2,160,640]{2,1,0:T(8,128)(2,1)S(1)}, bf16[2,160,640]{2,1,0:T(8,128)(2,1)S(1)}, u32[]{:S(2)}, u32[]{:S(2)}) collective-permute-start(bf16[2,160,640]{2,1,0:T(8,128)(2,1)S(1)} %get-tuple-element.19), channel_id=1, source_target_pairs={{0,1},{1,2},{2,3},{3,4},{4,5},{5,6},{6,7},{7,0},{8,9},{9,10},{10,1... | collective-permute-start | bytes 1228808 | tf_op jit(solution)/shard_map/ppermute | solution.py:54
  128.8 27.5 %collective-permute-start.12 = (bf16[2,160,640]{2,1,0:T(8,128)(2,1)S(1)}, bf16[2,160,640]{2,1,0:T(8,128)(2,1)}, u32[]{:S(2)}, u32[]{:S(2)}) collective-permute-start(bf16[2,160,640]{2,1,0:T(8,128)(2,1)S(1)} %get-tuple-element.20), channel_id=1, source_target_pairs={{0,7},{1,0},{2,1},{3,2},{4,3},{5,4},{6,5},{7,6},{8,15},{9,8},{10,9... | collective-permute-start | bytes 1228808 | tf_op jit(solution)/shard_map/ppermute | solution.py:54
  134.7 18.3 %collective-permute-start.13 = (bf16[160,640]{1,0:T(8,128)(2,1)S(1)}, bf16[160,640]{1,0:T(8,128)(2,1)}, u32[]{:S(2)}, u32[]{:S(2)}) collective-permute-start(bf16[160,640]{1,0:T(8,128)(2,1)S(1)} %get-tuple-element.21), channel_id=1, source_target_pairs={{0,2},{1,7},{2,4},{3,1},{4,6},{5,3},{6,0},{7,5},{8,10},{9,15},{10,... | collective-permute-start | bytes 614408 | tf_op jit(solution)/shard_map/ppermute | solution.py:146
  140.7 34.0 %collective-permute-start.10 = (bf16[160,640]{1,0:T(8,128)(2,1)}, bf16[160,640]{1,0:T(8,128)(2,1)}, u32[]{:S(2)}, u32[]{:S(2)}) collective-permute-start(bf16[160,640]{1,0:T(8,128)(2,1)} %get-tuple-element.28), channel_id=1, source_target_pairs={{0,4},{1,5},{2,6},{3,7},{4,0},{5,1},{6,2},{7,3},{8,12},{9,13},{10,... | collective-permute-start | bytes 614408 | tf_op jit(solution)/shard_map/ppermute | solution.py:54
  147.0 27.6 %collective-permute-start.9 = (bf16[160,640]{1,0:T(8,128)(2,1)S(1)}, bf16[160,640]{1,0:T(8,128)(2,1)}, u32[]{:S(2)}, u32[]{:S(2)}) collective-permute-start(bf16[160,640]{1,0:T(8,128)(2,1)S(1)} %get-tuple-element.18), channel_id=1, source_target_pairs={{0,6},{1,7},{2,0},{3,1},{4,2},{5,3},{6,4},{7,5},{8,14},{9,15},{10,... | collective-permute-start | bytes 614408 | tf_op jit(solution)/shard_map/ppermute | solution.py:54
  152.9 21.7 %collective-permute-start.8 = (bf16[160,640]{1,0:T(8,128)(2,1)S(1)}, bf16[160,640]{1,0:T(8,128)(2,1)S(1)}, u32[]{:S(2)}, u32[]{:S(2)}) collective-permute-start(bf16[160,640]{1,0:T(8,128)(2,1)S(1)} %get-tuple-element.17), channel_id=1, source_target_pairs={{0,2},{1,3},{2,4},{3,5},{4,6},{5,7},{6,0},{7,1},{8,10},{9,11},{10,... | collective-permute-start | bytes 614408 | tf_op jit(solution)/shard_map/ppermute | solution.py:54
  159.2 23.9 %copy-start.6 = (bf16[2,160,640]{2,1,0:T(8,128)(2,1)S(1)}, bf16[2,160,640]{2,1,0:T(8,128)(2,1)}, u32[]{:S(2)}) copy-start(bf16[2,160,640]{2,1,0:T(8,128)(2,1)} %copy-done.5) | copy-start | bytes 1228804
  159.2 19.5 %collective-permute-start.14 = (bf16[160,640]{1,0:T(8,128)(2,1)S(1)}, bf16[160,640]{1,0:T(8,128)(2,1)S(1)}, u32[]{:S(2)}, u32[]{:S(2)}) collective-permute-start(bf16[160,640]{1,0:T(8,128)(2,1)S(1)} %get-tuple-element.22), channel_id=1, source_target_pairs={{0,2},{1,3},{2,4},{3,5},{4,6},{5,7},{6,0},{7,1},{8,10},{9,11},{10,... | collective-permute-start | bytes 614408 | tf_op jit(solution)/shard_map/ppermute | solution.py:54
  172.3 10.7 %collective-permute-start.15 = (bf16[160,640]{1,0:T(8,128)(2,1)S(1)}, bf16[160,640]{1,0:T(8,128)(2,1)S(1)}, u32[]{:S(2)}, u32[]{:S(2)}) collective-permute-start(bf16[160,640]{1,0:T(8,128)(2,1)S(1)} %get-tuple-element.25), channel_id=1, source_target_pairs={{0,6},{1,7},{2,0},{3,1},{4,2},{5,3},{6,4},{7,5},{8,14},{9,15},{10,... | collective-permute-start | bytes 614408 | tf_op jit(solution)/shard_map/ppermute | solution.py:54
  (4 other events, 3.6 us)

commit v12 on v10

--- a/solution.py
+++ b/solution.py
@@ -140,7 +140,7 @@
     flat = lambda blocks: blocks.reshape(-1, blocks.shape[-1])
     away = contract_last(flat(other[..., :width]), weight_down).astype(jnp.bfloat16)
     back = swapped(away)
-    kept = contract_last(flat(mine[..., :width]), weight_down)
+    kept = lax.optimization_barrier(contract_last(flat(mine[..., :width]), weight_down))
     pair = (kept + wide(back)).astype(jnp.bfloat16).reshape(4, 64, -1)
     came = exchanged(pair, "yhi")
 
@@ -155,8 +155,10 @@
     delta_mine = flat(spread(delta_own, "yhi"))
     delta_other = swapped(delta_mine)
 
+    late, _ = lax.optimization_barrier((other, pair))
+    inputs_other = lax.optimization_barrier(late[..., width:])
     upper_mine = lax.optimization_barrier(contract_first(delta_mine, flat(mine[..., width:])))
-    upper = contract_first(delta_other, flat(other[..., width:])) + upper_mine
+    upper = contract_first(delta_other, flat(inputs_other)) + upper_mine
     upper = upper.astype(jnp.bfloat16)
     near, last_up, last_down = depth_parts(upper.reshape(8, -1, upper.shape[1]), False)
 

time: 184 us -> 182 us (0.989)
  waiting for transfers between devices: 49.6 us -> 47.3 us
  starting transfers between devices: 92.9 us -> 95 us
    ppermute x1, waiting for transfers between devices: 4.18 us -> 1.58 us  [depth_parts(): far, turn = ([], [lax.ppermute(pick(4), 'depth', turns)])]
    ppermute x12, starting transfers between devices: 56.1 us -> 58.3 us  [shifted(): lax.ppermute(value, axis, [(k, (k + by) % length) for k in range(length)])]
  transfers between devices with their start and end apart: 20 -> 20, of which waited for: 11 -> 11; matrix products, arithmetic and copies ran while one was open for 15% -> 14% of each run, Pallas kernels for 2% -> 2%
where the time goes in v12:
time: 182 us; the launch traced here: 181 us
  starting transfers between devices  95 us (52%)
  waiting for transfers between devices  47.3 us (26%)
  other arithmetic  14.3 us (8%)
  matrix products  13.8 us (8%)
  local copies, waits for them, and re-layouts  5.52 us (3%)
  Pallas kernels  4.14 us (2%)
    ppermute x12, starting transfers between devices, shifted(): lax.ppermute(value, axis, [(k, (k + by) % length) for k in range(length)])  58.3 us
    ppermute x12, waiting for transfers between devices, shifted(): lax.ppermute(value, axis, [(k, (k + by) % length) for k in range(length)])  26.3 us
    all_to_all x2, waiting for transfers between devices, spread(): return lax.all_to_all(copies, axis, split_axis=0, concat_axis=0, tiled=True)  18.1 us
    all_to_all x2, starting transfers between devices, exchanged(): return lax.all_to_all(value, axis, split_axis=0, concat_axis=0, tiled=True)  15.5 us
    all_to_all x2, starting transfers between devices, spread(): return lax.all_to_all(copies, axis, split_axis=0, concat_axis=0, tiled=True)  13.5 us
    dot_general x4, matrix products, contract_first(): lax.dot_general(left, right, (((0,), (0,)), ((), ())), preferred_element_...  9.83 us
    ppermute x3, starting transfers between devices, swapped(): return lax.ppermute(value, 'core', SWAP)  5.73 us
    pallas_call x2, Pallas kernels, onward(): pl.pallas_call(onward_kernel, out_shape=[pltpu.VMEM(shape, blocks.dtype)]...  4.14 us
  transfers between devices with their start and end apart: 20, of which 11 were waited for; matrix products, arithmetic and copies ran while one was open for 14% of the time, Pallas kernels for 2%

profile of v12, /device:TPU:2, one launch (start us, length us, event | category | flops | bytes accessed | tf_op | source)
XLA Modules:
  0.0 181.3 jit_solution(10854729916770975709)
XLA Ops:
  2.9 9.4 %all-to-all-start = ((bf16[8,64,1280]{2,1,0:T(8,128)(2,1)}), bf16[8,64,1280]{2,1,0:T(8,128)(2,1)S(1)}, u32[]{:S(2)}, u32[]{:S(2)}) async-start(bf16[8,64,1280]{2,1,0:T(8,128)(2,1)} %broadcast_in_dim.9), calls=%async_computation | async-start | bytes 2621440 | tf_op jit(solution)/shard_map/all_to_all | solution.py:19
  12.3 12.9 %all-to-all-done = bf16[8,64,1280]{2,1,0:T(8,128)(2,1)S(1)} async-done(((bf16[8,64,1280]{2,1,0:T(8,128)(2,1)}), bf16[8,64,1280]{2,1,0:T(8,128)(2,1)S(1)}, u32[]{:S(2)}, u32[]{:S(2)}) %all-to-all-start) | async-done | bytes 1310752 | tf_op jit(solution)/shard_map/all_to_all | solution.py:19
  31.1 6.2 %all-to-all-start.1 = ((bf16[4,64,1280]{2,1,0:T(8,128)(2,1)}), bf16[4,64,1280]{2,1,0:T(8,128)(2,1)S(1)}, u32[]{:S(2)}, u32[]{:S(2)}) async-start(bf16[4,64,1280]{2,1,0:T(8,128)(2,1)} %bitcast.7), calls=%async_computation.1 | async-start | bytes 1310720 | tf_op jit(solution)/shard_map/all_to_all | solution.py:23
  38.4 4.8 %collective-permute-start.4 = (bf16[64,1280]{1,0:T(8,128)(2,1)S(1)}, bf16[64,1280]{1,0:T(8,128)(2,1)}, u32[]{:S(2)}, u32[]{:S(2)}) collective-permute-start(bf16[64,1280]{1,0:T(8,128)(2,1)S(1)} %get-tuple-element.14), channel_id=1, source_target_pairs={{0,128},{128,256},{256,384},{384,0},{1,129},{129,257},{257,385},{3... | collective-permute-start | bytes 491528 | tf_op jit(solution)/shard_map/ppermute | solution.py:54
  43.3 5.5 %collective-permute-start.3 = (bf16[64,1280]{1,0:T(8,128)(2,1)S(1)}, bf16[64,1280]{1,0:T(8,128)(2,1)}, u32[]{:S(2)}, u32[]{:S(2)}) collective-permute-start(bf16[64,1280]{1,0:T(8,128)(2,1)S(1)} %get-tuple-element.14), channel_id=1, source_target_pairs={{0,256},{128,384},{256,0},{384,128},{1,257},{129,385},{257,1},{385... | collective-permute-start | bytes 491528 | tf_op jit(solution)/shard_map/ppermute | solution.py:54
  48.8 5.5 %collective-permute-start.2 = (bf16[64,1280]{1,0:T(8,128)(2,1)S(1)}, bf16[64,1280]{1,0:T(8,128)(2,1)}, u32[]{:S(2)}, u32[]{:S(2)}) collective-permute-start(bf16[64,1280]{1,0:T(8,128)(2,1)S(1)} %get-tuple-element.14), channel_id=1, source_target_pairs={{0,384},{128,0},{256,128},{384,256},{1,385},{129,1},{257,129},{385... | collective-permute-start | bytes 491528 | tf_op jit(solution)/shard_map/ppermute | solution.py:54
  54.4 3.5 %collective-permute-done.4 = bf16[64,1280]{1,0:T(8,128)(2,1)} collective-permute-done((bf16[64,1280]{1,0:T(8,128)(2,1)S(1)}, bf16[64,1280]{1,0:T(8,128)(2,1)}, u32[]{:S(2)}, u32[]{:S(2)}) %collective-permute-start.4) | collective-permute-done | bytes 163872 | tf_op jit(solution)/shard_map/ppermute | solution.py:54
  57.9 4.9 %collective-permute-done.3 = bf16[64,1280]{1,0:T(8,128)(2,1)} collective-permute-done((bf16[64,1280]{1,0:T(8,128)(2,1)S(1)}, bf16[64,1280]{1,0:T(8,128)(2,1)}, u32[]{:S(2)}, u32[]{:S(2)}) %collective-permute-start.3) | collective-permute-done | bytes 163872 | tf_op jit(solution)/shard_map/ppermute | solution.py:54
  62.8 7.3 %collective-permute-done.2 = bf16[64,1280]{1,0:T(8,128)(2,1)} collective-permute-done((bf16[64,1280]{1,0:T(8,128)(2,1)S(1)}, bf16[64,1280]{1,0:T(8,128)(2,1)}, u32[]{:S(2)}, u32[]{:S(2)}) %collective-permute-start.2) | collective-permute-done | bytes 163872 | tf_op jit(solution)/shard_map/ppermute | solution.py:54
  70.0 2.0 %maximum_maximum_fusion = bf16[256,1280]{1,0:T(8,128)(2,1)} fusion(bf16[64,1280]{1,0:T(8,128)(2,1)} %collective-permute-done.4, bf16[64,1280]{1,0:T(8,128)(2,1)} %collective-permute-done.3, bf16[64,1280]{1,0:T(8,128)(2,1)} %collective-permute-done.2, bf16[64,1280]{1,0:T(8,128)(2,1)S(1)} %get-tuple-element.14), kind=kLoop, calls=%fused_computation.17 | loop fusion | flops 2621440 | bytes 1310720 | tf_op jit(solution)/shard_map/max | solution.py:70
  72.0 1.9 %collective-permute-start.5 = (bf16[256,1280]{1,0:T(8,128)(2,1)}, bf16[256,1280]{1,0:T(8,128)(2,1)}, u32[]{:S(2)}, u32[]{:S(2)}) collective-permute-start(bf16[256,1280]{1,0:T(8,128)(2,1)} %maximum_maximum_fusion), channel_id=1, source_target_pairs={{0,64},{64,0},{1,65},{65,1},{2,66},{66,2},{3,67},{67,3},{4,68},{68... | collective-permute-start | bytes 1966088 | tf_op jit(solution)/shard_map/ppermute | solution.py:58
  74.9 4.2 %all-to-all-start.2 = ((bf16[4,64,1280]{2,1,0:T(8,128)(2,1)}), bf16[4,64,1280]{2,1,0:T(8,128)(2,1)}, u32[]{:S(2)}, u32[]{:S(2)}) async-start(bf16[4,64,1280]{2,1,0:T(8,128)(2,1)} %broadcast_in_dim.10), calls=%async_computation.2 | async-start | bytes 1310720 | tf_op jit(solution)/shard_map/all_to_all | solution.py:19
  85.6 4.3 %collective-permute-start.6 = (bf16[2,160,640]{2,1,0:T(8,128)(2,1)}, bf16[2,160,640]{2,1,0:T(8,128)(2,1)}, u32[]{:S(2)}, u32[]{:S(2)}) collective-permute-start(bf16[2,160,640]{2,1,0:T(8,128)(2,1)} %pad_maximum_fusion.1), channel_id=1, source_target_pairs={{0,1},{1,2},{2,3},{3,4},{4,5},{5,6},{6,7},{7,0},{8,9},{9,10},{10,1... | collective-permute-start | bytes 1228808 | tf_op jit(solution)/shard_map/ppermute | solution.py:54
  89.9 5.2 %all-to-all-done.2 = bf16[4,64,1280]{2,1,0:T(8,128)(2,1)} async-done(((bf16[4,64,1280]{2,1,0:T(8,128)(2,1)}), bf16[4,64,1280]{2,1,0:T(8,128)(2,1)}, u32[]{:S(2)}, u32[]{:S(2)}) %all-to-all-start.2) | async-done | bytes 655392 | tf_op jit(solution)/shard_map/all_to_all | solution.py:19
  97.7 10.9 %collective-permute-start.7 = (bf16[2,160,640]{2,1,0:T(8,128)(2,1)}, bf16[2,160,640]{2,1,0:T(8,128)(2,1)}, u32[]{:S(2)}, u32[]{:S(2)}) collective-permute-start(bf16[2,160,640]{2,1,0:T(8,128)(2,1)} %pad_maximum_fusion.2), channel_id=1, source_target_pairs={{0,7},{1,0},{2,1},{3,2},{4,3},{5,4},{6,5},{7,6},{8,15},{9,8},{10,9... | collective-permute-start | bytes 1228808 | tf_op jit(solution)/shard_map/ppermute | solution.py:54
  108.8 3.6 %convolution_bitcast_fusion = f32[1280,640]{1,0:T(8,128)} fusion(bf16[4,64,1280]{2,1,0:T(8,128)(2,1)} %all-to-all-done.2, bf16[4,64,1280]{2,1,0:T(8,128)(2,1)S(1)} %copy-done.6), kind=kOutput, calls=%fused_computation.2 | convolution fusion | flops 419430400 | bytes 4259840 | tf_op jit(solution)/shard_map/dot_general | solution.py:47
  116.0 9.3 %all-to-all-start.3 = ((bf16[8,64,640]{2,1,0:T(8,128)(2,1)}), bf16[8,64,640]{2,1,0:T(8,128)(2,1)S(1)}, u32[]{:S(2)}, u32[]{:S(2)}) async-start(bf16[8,64,640]{2,1,0:T(8,128)(2,1)} %bitcast.16), calls=%async_computation.3 | async-start | bytes 1310720 | tf_op jit(solution)/shard_map/all_to_all | solution.py:23
  125.3 2.6 %fusion.1 = bf16[1280,640]{1,0:T(8,128)(2,1)S(1)} fusion(f32[1280,640]{1,0:T(8,128)} %convolution_bitcast_fusion, bf16[256,1280]{1,0:T(8,128)(2,1)S(1)} %copy-done.10, bf16[256,640]{1,0:T(8,128)(2,1)S(1)} %bitcast.92), kind=kOutput, calls=%fused_computation.4 | convolution fusion | flops 421068800 | bytes 5898240 | tf_op jit(solution)/shard_map/dot_general | solution.py:47
  129.0 1.9 %collective-permute-start.11 = (bf16[2,160,640]{2,1,0:T(8,128)(2,1)S(1)}, bf16[2,160,640]{2,1,0:T(8,128)(2,1)S(1)}, u32[]{:S(2)}, u32[]{:S(2)}) collective-permute-start(bf16[2,160,640]{2,1,0:T(8,128)(2,1)S(1)} %pad_maximum_fusion.3), channel_id=1, source_target_pairs={{0,1},{1,2},{2,3},{3,4},{4,5},{5,6},{6,7},{7,0},{8,9},{9,10},{10,1... | collective-permute-start | bytes 1228808 | tf_op jit(solution)/shard_map/ppermute | solution.py:54
  131.7 5.1 %collective-permute-start.12 = (bf16[2,160,640]{2,1,0:T(8,128)(2,1)}, bf16[2,160,640]{2,1,0:T(8,128)(2,1)}, u32[]{:S(2)}, u32[]{:S(2)}) collective-permute-start(bf16[2,160,640]{2,1,0:T(8,128)(2,1)} %pad_maximum_fusion.4), channel_id=1, source_target_pairs={{0,7},{1,0},{2,1},{3,2},{4,3},{5,4},{6,5},{7,6},{8,15},{9,8},{10,9... | collective-permute-start | bytes 1228808 | tf_op jit(solution)/shard_map/ppermute | solution.py:54
  136.8 1.9 %collective-permute-start.13 = (bf16[160,640]{1,0:T(8,128)(2,1)}, bf16[160,640]{1,0:T(8,128)(2,1)}, u32[]{:S(2)}, u32[]{:S(2)}) collective-permute-start(bf16[160,640]{1,0:T(8,128)(2,1)} %get-tuple-element.23), channel_id=1, source_target_pairs={{0,2},{1,7},{2,4},{3,1},{4,6},{5,3},{6,0},{7,5},{8,10},{9,15},{10,... | collective-permute-start | bytes 614408 | tf_op jit(solution)/shard_map/ppermute | solution.py:116
  139.4 3.6 %collective-permute-start.10 = (bf16[160,640]{1,0:T(8,128)(2,1)}, bf16[160,640]{1,0:T(8,128)(2,1)}, u32[]{:S(2)}, u32[]{:S(2)}) collective-permute-start(bf16[160,640]{1,0:T(8,128)(2,1)} %get-tuple-element.29), channel_id=1, source_target_pairs={{0,4},{1,5},{2,6},{3,7},{4,0},{5,1},{6,2},{7,3},{8,12},{9,13},{10,... | collective-permute-start | bytes 614408 | tf_op jit(solution)/shard_map/ppermute | solution.py:54
  143.0 2.0 %onward.2 = (bf16[160,640]{1,0:T(8,128)(2,1)S(1)}, bf16[160,640]{1,0:T(8,128)(2,1)S(1)}) custom-call(s32[3]{0:T(128)} %pad_add_fusion.spot, bf16[8,160,640]{2,1,0:T(8,128)(2,1)} %bitcast.82, bf16[8,160,640]{2,1,0:T(8,128)(2,1)} %bitcast.83, bf16[2,160,640]{2,1,0:T(8,128)(2,1)} %collective-permute-done.6.near_up, ...), custom_call_target="tpu_custom_call" | custom-call | tf_op jit(solution)/shard_map/onward/pallas_call | solution.py:97
  145.0 6.7 %collective-permute-start.8 = (bf16[160,640]{1,0:T(8,128)(2,1)S(1)}, bf16[160,640]{1,0:T(8,128)(2,1)}, u32[]{:S(2)}, u32[]{:S(2)}) collective-permute-start(bf16[160,640]{1,0:T(8,128)(2,1)S(1)} %get-tuple-element.15), channel_id=1, source_target_pairs={{0,2},{1,3},{2,4},{3,5},{4,6},{5,7},{6,0},{7,1},{8,10},{9,11},{10,... | collective-permute-start | bytes 614408 | tf_op jit(solution)/shard_map/ppermute | solution.py:54
  153.3 1.9 %collective-permute-start.9 = (bf16[160,640]{1,0:T(8,128)(2,1)S(1)}, bf16[160,640]{1,0:T(8,128)(2,1)}, u32[]{:S(2)}, u32[]{:S(2)}) collective-permute-start(bf16[160,640]{1,0:T(8,128)(2,1)S(1)} %get-tuple-element.16), channel_id=1, source_target_pairs={{0,6},{1,7},{2,0},{3,1},{4,2},{5,3},{6,4},{7,5},{8,14},{9,15},{10,... | collective-permute-start | bytes 614408 | tf_op jit(solution)/shard_map/ppermute | solution.py:54
  156.5 5.5 %collective-permute-done.12.near_down = bf16[2,160,640]{2,1,0:T(8,128)(2,1)} collective-permute-done((bf16[2,160,640]{2,1,0:T(8,128)(2,1)}, bf16[2,160,640]{2,1,0:T(8,128)(2,1)}, u32[]{:S(2)}, u32[]{:S(2)}) %collective-permute-start.12) | collective-permute-done | bytes 409632 | tf_op jit(solution)/shard_map/ppermute | solution.py:54
  162.1 2.1 %onward.3 = (bf16[160,640]{1,0:T(8,128)(2,1)S(1)}, bf16[160,640]{1,0:T(8,128)(2,1)S(1)}) custom-call(s32[3]{0:T(128)} %pad_add_fusion.spot, bf16[8,160,640]{2,1,0:T(8,128)(2,1)} %bitcast.86, bf16[8,160,640]{2,1,0:T(8,128)(2,1)} %bitcast.87, bf16[2,160,640]{2,1,0:T(8,128)(2,1)} %copy-done.7, bf16[2,160,640]{2,1,0:T(8,128)(2,1)} %collective-permute-done.12.near_down, ...), custom_call_target="tpu_custom_call" | custom-call | tf_op jit(solution)/shard_map/onward/pallas_call | solution.py:97
  164.2 2.1 %collective-permute-start.14 = (bf16[160,640]{1,0:T(8,128)(2,1)S(1)}, bf16[160,640]{1,0:T(8,128)(2,1)}, u32[]{:S(2)}, u32[]{:S(2)}) collective-permute-start(bf16[160,640]{1,0:T(8,128)(2,1)S(1)} %get-tuple-element.18), channel_id=1, source_target_pairs={{0,2},{1,3},{2,4},{3,5},{4,6},{5,7},{6,0},{7,1},{8,10},{9,11},{10,... | collective-permute-start | bytes 614408 | tf_op jit(solution)/shard_map/ppermute | solution.py:54
  166.3 6.0 %collective-permute-start.15 = (bf16[160,640]{1,0:T(8,128)(2,1)S(1)}, bf16[160,640]{1,0:T(8,128)(2,1)}, u32[]{:S(2)}, u32[]{:S(2)}) collective-permute-start(bf16[160,640]{1,0:T(8,128)(2,1)S(1)} %get-tuple-element.21), channel_id=1, source_target_pairs={{0,6},{1,7},{2,0},{3,1},{4,2},{5,3},{6,4},{7,5},{8,14},{9,15},{10,... | collective-permute-start | bytes 614408 | tf_op jit(solution)/shard_map/ppermute | solution.py:54
  172.4 2.3 %fusion.5 = f32[160,640]{1,0:T(8,128)} fusion(bf16[160,640]{1,0:T(8,128)(2,1)} %collective-permute-done.10, bf16[160,640]{1,0:T(8,128)(2,1)} %collective-permute-done.9, bf16[160,640]{1,0:T(8,128)(2,1)} %collective-permute-done.8, bf16[2,160,640]{2,1,0:T(8,128)(2,1)} %collective-permute-done.7.near_down, ...), kind=kLoop, calls=%fused_computation.29 | loop fusion | flops 1126400 | bytes 1638404 | tf_op jit(solution)/shard_map/add | solution.py:125
  176.5 2.7 %collective-permute-done.15 = bf16[160,640]{1,0:T(8,128)(2,1)} collective-permute-done((bf16[160,640]{1,0:T(8,128)(2,1)S(1)}, bf16[160,640]{1,0:T(8,128)(2,1)}, u32[]{:S(2)}, u32[]{:S(2)}) %collective-permute-start.15) | collective-permute-done | bytes 204832 | tf_op jit(solution)/shard_map/ppermute | solution.py:54
  179.2 2.1 %fusion.3 = f32[640,160]{0,1:T(8,128)} fusion(bf16[160,640]{1,0:T(8,128)(2,1)} %collective-permute-done.15, bf16[160,640]{1,0:T(8,128)(2,1)} %collective-permute-done.14, bf16[2,160,640]{2,1,0:T(8,128)(2,1)} %collective-permute-done.12.near_down, bf16[2,160,640]{2,1,0:T(8,128)(2,1)S(1)} %copy-done.8, bf16[8,160,640]{2,1,0:T(8,128)(2,1)} %bitcast.88, ...), kind=kLoop, calls=%fused_computation.26 | loop fusion | flops 921600 | bytes 1433604 | tf_op jit(solution)/shard_map/transpose | solution.py:175
  (66 shorter events, 30.1 us)
Async XLA Ops:
  0.6 24.7 %copy-start = (bf16[1280,640]{1,0:T(8,128)(2,1)S(1)}, bf16[1280,640]{1,0:T(8,128)(2,1)}, u32[]{:S(2)}) copy-start(bf16[1280,640]{1,0:T(8,128)(2,1)} %param.9) | copy-start | bytes 4915204
  2.9 22.3 %all-to-all-start = ((bf16[8,64,1280]{2,1,0:T(8,128)(2,1)}), bf16[8,64,1280]{2,1,0:T(8,128)(2,1)S(1)}, u32[]{:S(2)}, u32[]{:S(2)}) async-start(bf16[8,64,1280]{2,1,0:T(8,128)(2,1)} %broadcast_in_dim.9), calls=%async_computation | async-start | bytes 2621440 | tf_op jit(solution)/shard_map/all_to_all | solution.py:19
  25.3 0.9 copy-start.3
  25.3 2.8 %copy-start.5 = (bf16[4,64,1280]{2,1,0:T(8,128)(2,1)}, bf16[4,64,1280]{2,1,0:T(8,128)(2,1)S(1)}, u32[]{:S(2)}) copy-start(bf16[4,64,1280]{2,1,0:T(8,128)(2,1)S(1)} %get-tuple-element.34) | copy-start | bytes 1966084
  26.2 4.0 %collective-permute-start = (bf16[256,1280]{1,0:T(8,128)(2,1)S(1)}, bf16[256,1280]{1,0:T(8,128)(2,1)S(1)}, u32[]{:S(2)}, u32[]{:S(2)}) collective-permute-start(bf16[256,1280]{1,0:T(8,128)(2,1)S(1)} %convolution_convert_fusion), channel_id=1, source_target_pairs={{0,64},{64,0},{1,65},{65,1},{2,66},{66,2},{3,67},{67,3},{4,68},{68... | collective-permute-start | bytes 1966088 | tf_op jit(solution)/shard_map/ppermute | solution.py:58
  31.1 42.8 %all-to-all-start.1 = ((bf16[4,64,1280]{2,1,0:T(8,128)(2,1)}), bf16[4,64,1280]{2,1,0:T(8,128)(2,1)S(1)}, u32[]{:S(2)}, u32[]{:S(2)}) async-start(bf16[4,64,1280]{2,1,0:T(8,128)(2,1)} %bitcast.7), calls=%async_computation.1 | async-start | bytes 1310720 | tf_op jit(solution)/shard_map/all_to_all | solution.py:23
  38.4 19.4 %collective-permute-start.4 = (bf16[64,1280]{1,0:T(8,128)(2,1)S(1)}, bf16[64,1280]{1,0:T(8,128)(2,1)}, u32[]{:S(2)}, u32[]{:S(2)}) collective-permute-start(bf16[64,1280]{1,0:T(8,128)(2,1)S(1)} %get-tuple-element.14), channel_id=1, source_target_pairs={{0,128},{128,256},{256,384},{384,0},{1,129},{129,257},{257,385},{3... | collective-permute-start | bytes 491528 | tf_op jit(solution)/shard_map/ppermute | solution.py:54
  43.3 19.5 %collective-permute-start.3 = (bf16[64,1280]{1,0:T(8,128)(2,1)S(1)}, bf16[64,1280]{1,0:T(8,128)(2,1)}, u32[]{:S(2)}, u32[]{:S(2)}) collective-permute-start(bf16[64,1280]{1,0:T(8,128)(2,1)S(1)} %get-tuple-element.14), channel_id=1, source_target_pairs={{0,256},{128,384},{256,0},{384,128},{1,257},{129,385},{257,1},{385... | collective-permute-start | bytes 491528 | tf_op jit(solution)/shard_map/ppermute | solution.py:54
  48.8 21.3 %collective-permute-start.2 = (bf16[64,1280]{1,0:T(8,128)(2,1)S(1)}, bf16[64,1280]{1,0:T(8,128)(2,1)}, u32[]{:S(2)}, u32[]{:S(2)}) collective-permute-start(bf16[64,1280]{1,0:T(8,128)(2,1)S(1)} %get-tuple-element.14), channel_id=1, source_target_pairs={{0,384},{128,0},{256,128},{384,256},{1,385},{129,1},{257,129},{385... | collective-permute-start | bytes 491528 | tf_op jit(solution)/shard_map/ppermute | solution.py:54
  72.0 9.0 %collective-permute-start.5 = (bf16[256,1280]{1,0:T(8,128)(2,1)}, bf16[256,1280]{1,0:T(8,128)(2,1)}, u32[]{:S(2)}, u32[]{:S(2)}) collective-permute-start(bf16[256,1280]{1,0:T(8,128)(2,1)} %maximum_maximum_fusion), channel_id=1, source_target_pairs={{0,64},{64,0},{1,65},{65,1},{2,66},{66,2},{3,67},{67,3},{4,68},{68... | collective-permute-start | bytes 1966088 | tf_op jit(solution)/shard_map/ppermute | solution.py:58
  74.9 20.1 %all-to-all-start.2 = ((bf16[4,64,1280]{2,1,0:T(8,128)(2,1)}), bf16[4,64,1280]{2,1,0:T(8,128)(2,1)}, u32[]{:S(2)}, u32[]{:S(2)}) async-start(bf16[4,64,1280]{2,1,0:T(8,128)(2,1)} %broadcast_in_dim.10), calls=%async_computation.2 | async-start | bytes 1310720 | tf_op jit(solution)/shard_map/all_to_all | solution.py:19
  82.8 1.2 copy-start.1
  84.0 24.7 %copy-start.4 = (bf16[4,64,1280]{2,1,0:T(8,128)(2,1)S(1)}, bf16[4,64,1280]{2,1,0:T(8,128)(2,1)}, u32[]{:S(2)}) copy-start(bf16[4,64,1280]{2,1,0:T(8,128)(2,1)} %copy-done.3) | copy-start | bytes 1966084
  84.8 23.9 %copy-start.6 = (bf16[4,64,1280]{2,1,0:T(8,128)(2,1)S(1)}, bf16[4,64,1280]{2,1,0:T(8,128)(2,1)}, u32[]{:S(2)}) copy-start(bf16[4,64,1280]{2,1,0:T(8,128)(2,1)} %copy-done.5) | copy-start | bytes 1966084
  85.6 53.8 %collective-permute-start.6 = (bf16[2,160,640]{2,1,0:T(8,128)(2,1)}, bf16[2,160,640]{2,1,0:T(8,128)(2,1)}, u32[]{:S(2)}, u32[]{:S(2)}) collective-permute-start(bf16[2,160,640]{2,1,0:T(8,128)(2,1)} %pad_maximum_fusion.1), channel_id=1, source_target_pairs={{0,1},{1,2},{2,3},{3,4},{4,5},{5,6},{6,7},{7,0},{8,9},{9,10},{10,1... | collective-permute-start | bytes 1228808 | tf_op jit(solution)/shard_map/ppermute | solution.py:54
  95.0 19.1 %collective-permute-start.1 = (bf16[256,1280]{1,0:T(8,128)(2,1)}, bf16[256,1280]{1,0:T(8,128)(2,1)S(1)}, u32[]{:S(2)}, u32[]{:S(2)}) collective-permute-start(bf16[256,1280]{1,0:T(8,128)(2,1)} %bitcast.11), channel_id=1, source_target_pairs={{0,64},{64,0},{1,65},{65,1},{2,66},{66,2},{3,67},{67,3},{4,68},{68... | collective-permute-start | bytes 1966088 | tf_op jit(solution)/shard_map/ppermute | solution.py:58
  97.7 45.2 %collective-permute-start.7 = (bf16[2,160,640]{2,1,0:T(8,128)(2,1)}, bf16[2,160,640]{2,1,0:T(8,128)(2,1)}, u32[]{:S(2)}, u32[]{:S(2)}) collective-permute-start(bf16[2,160,640]{2,1,0:T(8,128)(2,1)} %pad_maximum_fusion.2), channel_id=1, source_target_pairs={{0,7},{1,0},{2,1},{3,2},{4,3},{5,4},{6,5},{7,6},{8,15},{9,8},{10,9... | collective-permute-start | bytes 1228808 | tf_op jit(solution)/shard_map/ppermute | solution.py:54
  108.8 3.6 %copy-start.11 = (bf16[640,1280]{1,0:T(8,128)(2,1)S(1)}, bf16[640,1280]{1,0:T(8,128)(2,1)}, u32[]{:S(2)}) copy-start(bf16[640,1280]{1,0:T(8,128)(2,1)} %param.8) | copy-start | bytes 4915204
  114.2 0.9 copy-start.9
  115.0 10.3 %copy-start.10 = (bf16[256,1280]{1,0:T(8,128)(2,1)S(1)}, bf16[256,1280]{1,0:T(8,128)(2,1)}, u32[]{:S(2)}) copy-start(bf16[256,1280]{1,0:T(8,128)(2,1)} %copy-done.9) | copy-start | bytes 1966084
  116.0 58.7 %all-to-all-start.3 = ((bf16[8,64,640]{2,1,0:T(8,128)(2,1)}), bf16[8,64,640]{2,1,0:T(8,128)(2,1)S(1)}, u32[]{:S(2)}, u32[]{:S(2)}) async-start(bf16[8,64,640]{2,1,0:T(8,128)(2,1)} %bitcast.16), calls=%async_computation.3 | async-start | bytes 1310720 | tf_op jit(solution)/shard_map/all_to_all | solution.py:23
  127.9 3.7 %copy-start.2 = (bf16[1280,640]{1,0:T(8,128)(2,1)}, bf16[1280,640]{1,0:T(8,128)(2,1)S(1)}, u32[]{:S(2)}) copy-start(bf16[1280,640]{1,0:T(8,128)(2,1)S(1)} %fusion.1) | copy-start | bytes 4915204
  129.0 27.6 %collective-permute-start.11 = (bf16[2,160,640]{2,1,0:T(8,128)(2,1)S(1)}, bf16[2,160,640]{2,1,0:T(8,128)(2,1)S(1)}, u32[]{:S(2)}, u32[]{:S(2)}) collective-permute-start(bf16[2,160,640]{2,1,0:T(8,128)(2,1)S(1)} %pad_maximum_fusion.3), channel_id=1, source_target_pairs={{0,1},{1,2},{2,3},{3,4},{4,5},{5,6},{6,7},{7,0},{8,9},{9,10},{10,1... | collective-permute-start | bytes 1228808 | tf_op jit(solution)/shard_map/ppermute | solution.py:54
  131.7 30.4 %collective-permute-start.12 = (bf16[2,160,640]{2,1,0:T(8,128)(2,1)}, bf16[2,160,640]{2,1,0:T(8,128)(2,1)}, u32[]{:S(2)}, u32[]{:S(2)}) collective-permute-start(bf16[2,160,640]{2,1,0:T(8,128)(2,1)} %pad_maximum_fusion.4), channel_id=1, source_target_pairs={{0,7},{1,0},{2,1},{3,2},{4,3},{5,4},{6,5},{7,6},{8,15},{9,8},{10,9... | collective-permute-start | bytes 1228808 | tf_op jit(solution)/shard_map/ppermute | solution.py:54
  136.8 16.5 %collective-permute-start.13 = (bf16[160,640]{1,0:T(8,128)(2,1)}, bf16[160,640]{1,0:T(8,128)(2,1)}, u32[]{:S(2)}, u32[]{:S(2)}) collective-permute-start(bf16[160,640]{1,0:T(8,128)(2,1)} %get-tuple-element.23), channel_id=1, source_target_pairs={{0,2},{1,7},{2,4},{3,1},{4,6},{5,3},{6,0},{7,5},{8,10},{9,15},{10,... | collective-permute-start | bytes 614408 | tf_op jit(solution)/shard_map/ppermute | solution.py:116
  139.4 33.0 %collective-permute-start.10 = (bf16[160,640]{1,0:T(8,128)(2,1)}, bf16[160,640]{1,0:T(8,128)(2,1)}, u32[]{:S(2)}, u32[]{:S(2)}) collective-permute-start(bf16[160,640]{1,0:T(8,128)(2,1)} %get-tuple-element.29), channel_id=1, source_target_pairs={{0,4},{1,5},{2,6},{3,7},{4,0},{5,1},{6,2},{7,3},{8,12},{9,13},{10,... | collective-permute-start | bytes 614408 | tf_op jit(solution)/shard_map/ppermute | solution.py:54
  145.0 27.4 %collective-permute-start.8 = (bf16[160,640]{1,0:T(8,128)(2,1)S(1)}, bf16[160,640]{1,0:T(8,128)(2,1)}, u32[]{:S(2)}, u32[]{:S(2)}) collective-permute-start(bf16[160,640]{1,0:T(8,128)(2,1)S(1)} %get-tuple-element.15), channel_id=1, source_target_pairs={{0,2},{1,3},{2,4},{3,5},{4,6},{5,7},{6,0},{7,1},{8,10},{9,11},{10,... | collective-permute-start | bytes 614408 | tf_op jit(solution)/shard_map/ppermute | solution.py:54
  153.3 19.1 %collective-permute-start.9 = (bf16[160,640]{1,0:T(8,128)(2,1)S(1)}, bf16[160,640]{1,0:T(8,128)(2,1)}, u32[]{:S(2)}, u32[]{:S(2)}) collective-permute-start(bf16[160,640]{1,0:T(8,128)(2,1)S(1)} %get-tuple-element.16), channel_id=1, source_target_pairs={{0,6},{1,7},{2,0},{3,1},{4,2},{5,3},{6,4},{7,5},{8,14},{9,15},{10,... | collective-permute-start | bytes 614408 | tf_op jit(solution)/shard_map/ppermute | solution.py:54
  156.5 5.5 %copy-start.7 = (bf16[2,160,640]{2,1,0:T(8,128)(2,1)}, bf16[2,160,640]{2,1,0:T(8,128)(2,1)S(1)}, u32[]{:S(2)}) copy-start(bf16[2,160,640]{2,1,0:T(8,128)(2,1)S(1)} %collective-permute-done.11.near_up) | copy-start | bytes 1228804
  164.2 14.9 %copy-start.8 = (bf16[2,160,640]{2,1,0:T(8,128)(2,1)S(1)}, bf16[2,160,640]{2,1,0:T(8,128)(2,1)}, u32[]{:S(2)}) copy-start(bf16[2,160,640]{2,1,0:T(8,128)(2,1)} %copy-done.7) | copy-start | bytes 1228804
  164.2 12.2 %collective-permute-start.14 = (bf16[160,640]{1,0:T(8,128)(2,1)S(1)}, bf16[160,640]{1,0:T(8,128)(2,1)}, u32[]{:S(2)}, u32[]{:S(2)}) collective-permute-start(bf16[160,640]{1,0:T(8,128)(2,1)S(1)} %get-tuple-element.18), channel_id=1, source_target_pairs={{0,2},{1,3},{2,4},{3,5},{4,6},{5,7},{6,0},{7,1},{8,10},{9,11},{10,... | collective-permute-start | bytes 614408 | tf_op jit(solution)/shard_map/ppermute | solution.py:54
  166.3 12.9 %collective-permute-start.15 = (bf16[160,640]{1,0:T(8,128)(2,1)S(1)}, bf16[160,640]{1,0:T(8,128)(2,1)}, u32[]{:S(2)}, u32[]{:S(2)}) collective-permute-start(bf16[160,640]{1,0:T(8,128)(2,1)S(1)} %get-tuple-element.21), channel_id=1, source_target_pairs={{0,6},{1,7},{2,0},{3,1},{4,2},{5,3},{6,4},{7,5},{8,14},{9,15},{10,... | collective-permute-start | bytes 614408 | tf_op jit(solution)/shard_map/ppermute | solution.py:54
